TPU v7x, 32 devices: a whole 2x2x4 slice. The times are simulated.
32 devices in a mesh: dp: 2 (over y), expert: 4 (over z), shard: 4 (over x, core).
Axes of the slice: x: 2, y: 2, z: 4, core: 2. Of those that a mesh axis runs over, the one named last changes fastest.
Arguments:
- tokens: bfloat16 [32768, 768], P(('dp', 'expert', 'shard')), may hold values from -6 to 6
- lengths: int32 [32], P(('dp', 'expert', 'shard')), may hold values from 256 to 1024, as said below
- routes: int32 [32768, 2], P(('dp', 'expert', 'shard')), may hold values from 0 to 7, all different within a row; in each aligned block of 1024 rows (0 to 1023, 1024 to 2047, ...) at most 288 rows name the same one
- route_gates: float32 [32768, 2], P(('dp', 'expert', 'shard')), may hold values from 0.2 to 1
- cotangent: bfloat16 [32768, 768], P(('dp', 'expert', 'shard')), may hold values from -6 to 6
- norm_gains: bfloat16 [2, 768], P(None, ('dp', 'shard')), may hold values from 0.25 to 1.75
- w_qkv: bfloat16 [768, 2304], P(('dp', 'shard')), may hold values from -0.21875 to 0.21875
- w_out: bfloat16 [768, 768], P(('dp', 'shard')), may hold values from -1.75 to 1.75
- w_shared_gu: bfloat16 [768, 4096], P(('dp', 'shard')), may hold values from -0.21875 to 0.21875
- w_shared_down: bfloat16 [2048, 768], P(('dp', 'shard')), may hold values from -0.125 to 0.125
- w_expert_gu: bfloat16 [8, 768, 4096], P('expert'), may hold values from -0.21875 to 0.21875
- w_expert_down: bfloat16 [8, 2048, 768], P('expert'), may hold values from -0.125 to 0.125
Outputs:
- layer_out: bfloat16 [32768, 768], P(('dp', 'expert', 'shard'))
- input_grad: float32 [32768, 768], P(('dp', 'expert', 'shard'))
- gains_grad: float32 [2, 768], P(None, ('dp', 'shard'))
- qkv_grad: float32 [768, 2304], P(('dp', 'shard'))
- out_proj_grad: float32 [768, 768], P(('dp', 'shard'))
- shared_gu_grad: float32 [768, 4096], P(('dp', 'shard'))
- shared_down_grad: float32 [2048, 768], P(('dp', 'shard'))
- expert_gu_grad: float32 [8, 768, 4096], P('expert', None, ('dp', 'shard'))
- expert_down_grad: float32 [8, 2048, 768], P('expert', ('dp', 'shard'))
Inputs may be any that keep to these rules, and one draw needn't show every extreme that they name: `lengths`: each sequence has at least a quarter of its slots live, and some sequence is full. `routes`: each row names 2 different experts; in the rows of one device (aligned blocks of 1024 rows, padded positions included) no expert is named by more than 288 rows.
All inputs are finite; a program needn't handle non-finite values.
Results may differ from a plain program's by a relative error of at most 0.014.
Values may be sent and summed in bfloat16 or wider, within the bound.
A program may use at most 384 MiB of HBM per device.

v0:
```python
import math

import jax
import jax.numpy as jnp
from jax import lax
from jax.sharding import PartitionSpec as P

HEADS = 12


epsilon = 1e-05


def rotary_tables(length, head_dim):
    half_dim = head_dim // 2
    position = lax.iota(jnp.float32, length)[:, None]
    frequency = jnp.exp(lax.iota(jnp.float32, half_dim) * (-2.0 * math.log(10000.0) / head_dim))
    angle_table = position * frequency[None, :]
    return (jnp.cos(angle_table)[:, None, :], jnp.sin(angle_table)[:, None, :])


def rotate(values, cosine_table, sine_table):
    half_dim = values.shape[-1] // 2
    front_half = values[..., :half_dim]
    back_half = values[..., half_dim:]
    return jnp.concatenate(
        [
            front_half * cosine_table - back_half * sine_table,
            back_half * cosine_table + front_half * sine_table,
        ],
        axis=-1,
    )


def contract_rows(left_side, right_side):
    return lax.dot_general(
        left_side, right_side, (((0,), (0,)), ((), ())), preferred_element_type=jnp.float32
    )


def contract_cols(left_side, right_side):
    return lax.dot_general(
        left_side, right_side, (((1,), (1,)), ((), ())), preferred_element_type=jnp.float32
    )


def silu_parts(pre_act):
    sigmoid_v = jax.nn.sigmoid(pre_act)
    return (pre_act * sigmoid_v, sigmoid_v * (1.0 + pre_act * (1.0 - sigmoid_v)))


def causal_mask(first_row, block_rows, last_row):
    return (
        lax.iota(jnp.int32, block_rows)[:, None] + first_row
        >= lax.iota(jnp.int32, last_row)[None, :]
    )


def attend_forward(packed):
    queries, keys_rot, values_h = packed
    length = queries.shape[0]
    block_rows = min(512, length)
    mixed_blocks = []
    log_totals = []
    for first_row in range(0, length, block_rows):
        last_row = first_row + block_rows
        scores = jnp.einsum(
            "qhd,khd->hqk",
            queries[first_row:last_row],
            keys_rot[:last_row],
            preferred_element_type=jnp.float32,
        )
        scores = jnp.where(causal_mask(first_row, block_rows, last_row), scores, -1e30)
        row_peak = jnp.max(scores, axis=2, keepdims=True)
        row_expo = jnp.exp(scores - row_peak)
        row_total = jnp.sum(row_expo, axis=2, keepdims=True)
        probs_b = (row_expo / row_total).astype(jnp.bfloat16)
        mixed_out = jnp.einsum(
            "hqk,khd->qhd", probs_b, values_h[:last_row], preferred_element_type=jnp.float32
        )
        mixed_blocks.append(mixed_out.astype(jnp.bfloat16))
        log_totals.append(row_peak + jnp.log(row_total))
    return (jnp.concatenate(mixed_blocks, axis=0), jnp.concatenate(log_totals, axis=1))


def attend_backward(packed):
    queries, keys_rot, values_h, grad_mixed, log_total = packed
    length = queries.shape[0]
    block_rows = min(512, length)
    grad_keys = jnp.zeros(keys_rot.shape, jnp.float32)
    grad_values = jnp.zeros(values_h.shape, jnp.float32)
    query_blocks = []
    for first_row in range(0, length, block_rows):
        last_row = first_row + block_rows
        scores = jnp.einsum(
            "qhd,khd->hqk",
            queries[first_row:last_row],
            keys_rot[:last_row],
            preferred_element_type=jnp.float32,
        )
        scores = jnp.where(causal_mask(first_row, block_rows, last_row), scores, -1e30)
        probs_full = jnp.exp(scores - log_total[:, first_row:last_row, :])
        grad_probs = jnp.einsum(
            "qhd,khd->hqk",
            grad_mixed[first_row:last_row],
            values_h[:last_row],
            preferred_element_type=jnp.float32,
        )
        row_inner = jnp.sum(grad_probs * probs_full, axis=2, keepdims=True)
        grad_scores = (probs_full * (grad_probs - row_inner)).astype(jnp.bfloat16)
        query_blocks.append(
            jnp.einsum(
                "hqk,khd->qhd", grad_scores, keys_rot[:last_row], preferred_element_type=jnp.float32
            )
        )
        grad_keys = grad_keys.at[:last_row].add(
            jnp.einsum(
                "hqk,qhd->khd",
                grad_scores,
                queries[first_row:last_row],
                preferred_element_type=jnp.float32,
            )
        )
        grad_values = grad_values.at[:last_row].add(
            jnp.einsum(
                "hqk,qhd->khd",
                probs_full.astype(jnp.bfloat16),
                grad_mixed[first_row:last_row],
                preferred_element_type=jnp.float32,
            )
        )
    return (jnp.concatenate(query_blocks, axis=0), grad_keys, grad_values)


def local(
    tokens,
    lengths,
    routes,
    route_gates,
    cotangent,
    norm_gains,
    w_qkv,
    w_out,
    w_shared_gu,
    w_shared_down,
    w_expert_gu,
    w_expert_down,
):
    tok_count, model_width = tokens.shape
    seq_count = lengths.shape[0]
    length = tok_count // seq_count
    local_experts = w_expert_gu.shape[0]
    hidden_units = w_expert_down.shape[1]
    owner_count = lax.axis_size("expert")
    experts = local_experts * owner_count
    top_count = routes.shape[1]
    capacity = tok_count * top_count * 9 // (8 * experts)
    head_count = HEADS
    head_dim = model_width // head_count
    query_scale = 1.0 / math.sqrt(head_dim)
    gains_full, qkv_weight, out_weight, sgu_weight, sdown_weight = (
        lax.all_gather(norm_gains, ("dp", "shard"), axis=1, tiled=True),
        lax.all_gather(w_qkv, ("dp", "shard"), axis=0, tiled=True),
        lax.all_gather(w_out, ("dp", "shard"), axis=0, tiled=True),
        lax.all_gather(w_shared_gu, ("dp", "shard"), axis=0, tiled=True),
        lax.all_gather(w_shared_down, ("dp", "shard"), axis=0, tiled=True),
    )
    shared_units = sdown_weight.shape[0]
    gain_one = gains_full[0].astype(jnp.float32)
    gain_two = gains_full[1].astype(jnp.float32)
    source = tokens.astype(jnp.float32)
    live_bool = lax.iota(jnp.int32, tok_count) % length < jnp.repeat(lengths, length)
    live_mask = live_bool.astype(jnp.float32)[:, None]
    scale_one = lax.rsqrt(jnp.mean(source * source, axis=1, keepdims=True) + epsilon)
    normed_one = (source * scale_one * gain_one).astype(jnp.bfloat16)
    qkv_proj = jnp.dot(normed_one, qkv_weight, preferred_element_type=jnp.float32)
    shaped = qkv_proj.reshape(seq_count, length, 3, head_count, head_dim)
    cosine_table, sine_table = rotary_tables(length, head_dim)
    queries = (rotate(shaped[:, :, 0], cosine_table, sine_table) * query_scale).astype(jnp.bfloat16)
    keys_rot = rotate(shaped[:, :, 1], cosine_table, sine_table).astype(jnp.bfloat16)
    values_h = shaped[:, :, 2].astype(jnp.bfloat16)
    mixed_out, log_total = lax.map(attend_forward, (queries, keys_rot, values_h))
    attn_mix = mixed_out.reshape(tok_count, model_width)
    first_sum = source + jnp.dot(attn_mix, out_weight, preferred_element_type=jnp.float32)
    scale_two = lax.rsqrt(jnp.mean(first_sum * first_sum, axis=1, keepdims=True) + epsilon)
    normed_two = (first_sum * scale_two * gain_two).astype(jnp.bfloat16)
    shared_gu = jnp.dot(normed_two, sgu_weight, preferred_element_type=jnp.float32)
    shared_gate = shared_gu[:, :shared_units]
    shared_up = shared_gu[:, shared_units:]
    gate_value, gate_slope = silu_parts(shared_gate)
    shared_hidden = (gate_value * shared_up).astype(jnp.bfloat16)
    shared_out = jnp.dot(shared_hidden, sdown_weight, preferred_element_type=jnp.float32)
    row_count = tok_count * top_count
    slot_total = experts * capacity
    flat_expert = routes.reshape(row_count)
    live_row = jnp.repeat(live_bool, top_count)
    onehot = (
        (flat_expert[:, None] == lax.iota(jnp.int32, experts)[None, :]) & live_row[:, None]
    ).astype(jnp.int32)
    slot_index = jnp.sum(onehot * jnp.cumsum(onehot, axis=0), axis=1) - 1
    destination = jnp.where(live_row, flat_expert * capacity + slot_index, slot_total)
    slot_row = (
        jnp.full((slot_total,), row_count, jnp.int32)
        .at[destination]
        .set(lax.iota(jnp.int32, row_count), mode="drop")
    )
    slot_token = slot_row // top_count
    slot_gate = jnp.take(
        jnp.concatenate([route_gates.reshape(row_count), jnp.zeros((1,), jnp.float32)]), slot_row
    )
    padded_normed = jnp.concatenate([normed_two, jnp.zeros((1, model_width), jnp.bfloat16)], axis=0)
    send_rows = jnp.take(padded_normed, slot_token, axis=0).reshape(experts, capacity, model_width)
    received = lax.all_to_all(send_rows, "expert", split_axis=0, concat_axis=0, tiled=True)
    grouped = received.reshape(-1, local_experts, received.shape[1], model_width)
    gate_up = jnp.einsum("sexd,edf->sexf", grouped, w_expert_gu, preferred_element_type=jnp.float32)
    activated = (jax.nn.silu(gate_up[..., :hidden_units]) * gate_up[..., hidden_units:]).astype(
        jnp.bfloat16
    )
    result = jnp.einsum(
        "sexf,efd->sexd", activated, w_expert_down, preferred_element_type=jnp.float32
    )
    expert_result = result.astype(jnp.bfloat16).reshape(received.shape)
    expert_gate_up = gate_up.reshape(received.shape[0], received.shape[1], 2 * hidden_units)
    returned = lax.all_to_all(expert_result, "expert", split_axis=0, concat_axis=0, tiled=True)
    padded_return = jnp.concatenate(
        [returned.reshape(slot_total, model_width), jnp.zeros((1, model_width), jnp.bfloat16)],
        axis=0,
    )
    picked = (
        jnp.take(padded_return, destination, axis=0)
        .astype(jnp.float32)
        .reshape(tok_count, top_count, model_width)
    )
    moe_out = jnp.sum(picked * route_gates[:, :, None], axis=1)
    layer_out = (live_mask * (first_sum + shared_out + moe_out)).astype(jnp.bfloat16)
    grad_out = cotangent.astype(jnp.float32) * live_mask
    grad_b = grad_out.astype(jnp.bfloat16)
    grad_sdown_weight = contract_rows(shared_hidden, grad_b)
    grad_hidden = contract_cols(grad_b, sdown_weight)
    grad_shared_gu = jnp.concatenate(
        [grad_hidden * shared_up * gate_slope, grad_hidden * gate_value], axis=1
    ).astype(jnp.bfloat16)
    grad_sgu_weight = contract_rows(normed_two, grad_shared_gu)
    grad_normed_two = contract_cols(grad_shared_gu, sgu_weight)
    padded_grad = jnp.concatenate([grad_out, jnp.zeros((1, model_width), jnp.float32)], axis=0)
    send_grad = (
        (jnp.take(padded_grad, slot_token, axis=0) * slot_gate[:, None])
        .astype(jnp.bfloat16)
        .reshape(experts, capacity, model_width)
    )
    received_grad = lax.all_to_all(send_grad, "expert", split_axis=0, concat_axis=0, tiled=True)
    grouped_grad = received_grad.reshape(-1, local_experts, capacity, model_width)
    grouped_input = received.reshape(-1, local_experts, capacity, model_width)
    grouped_gu = expert_gate_up.reshape(-1, local_experts, capacity, 2 * hidden_units)
    expert_gate = grouped_gu[..., :hidden_units]
    expert_up = grouped_gu[..., hidden_units:]
    act_value, act_slope = silu_parts(expert_gate)
    activated = (act_value * expert_up).astype(jnp.bfloat16)
    grad_activated = jnp.einsum(
        "sexd,efd->sexf", grouped_grad, w_expert_down, preferred_element_type=jnp.float32
    )
    grad_expert_gu = jnp.concatenate(
        [grad_activated * expert_up * act_slope, grad_activated * act_value], axis=-1
    ).astype(jnp.bfloat16)
    grad_edown_weight = jnp.einsum(
        "sexf,sexd->efd", activated, grouped_grad, preferred_element_type=jnp.float32
    )
    grad_egu_weight = jnp.einsum(
        "sexd,sexf->edf", grouped_input, grad_expert_gu, preferred_element_type=jnp.float32
    )
    grad_rows = (
        jnp.einsum(
            "sexf,edf->sexd", grad_expert_gu, w_expert_gu, preferred_element_type=jnp.float32
        )
        .astype(jnp.bfloat16)
        .reshape(experts, capacity, model_width)
    )
    back_rows = lax.all_to_all(grad_rows, "expert", split_axis=0, concat_axis=0, tiled=True)
    padded_back = jnp.concatenate(
        [back_rows.reshape(slot_total, model_width), jnp.zeros((1, model_width), jnp.bfloat16)],
        axis=0,
    )
    grad_expert_in = (
        jnp.take(padded_back, destination, axis=0)
        .astype(jnp.float32)
        .reshape(tok_count, top_count, model_width)
    )
    grad_normed_two = grad_normed_two + jnp.sum(grad_expert_in, axis=1)
    weighted_two = grad_normed_two * gain_two
    grad_first = (
        grad_out
        + scale_two * weighted_two
        - first_sum * scale_two**3 * jnp.mean(first_sum * weighted_two, axis=1, keepdims=True)
    )
    grad_gain_two = jnp.sum(grad_normed_two * first_sum * scale_two, axis=0)
    grad_attn = grad_first.astype(jnp.bfloat16)
    grad_out_weight = contract_rows(attn_mix, grad_attn)
    grad_mixed = (
        contract_cols(grad_attn, out_weight)
        .astype(jnp.bfloat16)
        .reshape(seq_count, length, head_count, head_dim)
    )
    grad_queries, grad_keys, grad_values = lax.map(
        attend_backward, (queries, keys_rot, values_h, grad_mixed, log_total)
    )
    grad_qkv = jnp.concatenate(
        [
            rotate(grad_queries * query_scale, cosine_table, -sine_table).reshape(
                tok_count, model_width
            ),
            rotate(grad_keys, cosine_table, -sine_table).reshape(tok_count, model_width),
            grad_values.reshape(tok_count, model_width),
        ],
        axis=1,
    ).astype(jnp.bfloat16)
    grad_qkv_weight = contract_rows(normed_one, grad_qkv)
    grad_normed_one = contract_cols(grad_qkv, qkv_weight)
    weighted_one = grad_normed_one * gain_one
    input_grad = (
        grad_first
        + scale_one * weighted_one
        - source * scale_one**3 * jnp.mean(source * weighted_one, axis=1, keepdims=True)
    )
    grad_gain_one = jnp.sum(grad_normed_one * source * scale_one, axis=0)
    grad_gains = jnp.stack([grad_gain_one, grad_gain_two], axis=0)
    bucket_shares = (
        lax.psum_scatter(grad_gains, ("dp", "shard"), scatter_dimension=1, tiled=True),
        lax.psum_scatter(grad_qkv_weight, ("dp", "shard"), scatter_dimension=0, tiled=True),
        lax.psum_scatter(grad_out_weight, ("dp", "shard"), scatter_dimension=0, tiled=True),
        lax.psum_scatter(grad_sgu_weight, ("dp", "shard"), scatter_dimension=0, tiled=True),
        lax.psum_scatter(grad_sdown_weight, ("dp", "shard"), scatter_dimension=0, tiled=True),
        lax.psum_scatter(grad_egu_weight, ("dp", "shard"), scatter_dimension=2, tiled=True),
        lax.psum_scatter(grad_edown_weight, ("dp", "shard"), scatter_dimension=1, tiled=True),
    )
    mixer_shares = bucket_shares[:5]
    expert_shares = bucket_shares[5:]
    totals = lax.psum(
        (mixer_shares[0], mixer_shares[1], mixer_shares[2], mixer_shares[3], mixer_shares[4]),
        "expert",
    )
    return (
        layer_out,
        input_grad,
        totals[0],
        totals[1],
        totals[2],
        totals[3],
        totals[4],
        expert_shares[0],
        expert_shares[1],
    )


def solution(mesh):
    in_specs = (
        P(("dp", "expert", "shard"), None),
        P(("dp", "expert", "shard")),
        P(("dp", "expert", "shard"), None),
        P(("dp", "expert", "shard"), None),
        P(("dp", "expert", "shard"), None),
        P(None, ("dp", "shard")),
        P(("dp", "shard"), None),
        P(("dp", "shard"), None),
        P(("dp", "shard"), None),
        P(("dp", "shard"), None),
        P("expert", None, None),
        P("expert", None, None),
    )
    out_specs = (
        P(("dp", "expert", "shard"), None),
        P(("dp", "expert", "shard"), None),
        P(None, ("dp", "shard")),
        P(("dp", "shard"), None),
        P(("dp", "shard"), None),
        P(("dp", "shard"), None),
        P(("dp", "shard"), None),
        P("expert", None, ("dp", "shard")),
        P("expert", ("dp", "shard"), None),
    )
    return jax.shard_map(local, mesh=mesh, in_specs=in_specs, out_specs=out_specs, check_vma=False)
```

profile of v0, /device:TPU:0, one launch (start us, length us, event | category | flops | bytes accessed | tf_op | source)
XLA Modules:
  0.0 1319.8 jit_solution(1891437139479731110)
XLA Ops:
  86.6 12.4 fusion.68
  141.1 12.3 gather_fusion.2
  167.4 51.7 %all-to-all-done = bf16[8,288,768]{2,1,0:T(8,128)(2,1)} async-done(((bf16[8,288,768]{2,1,0:T(8,128)(2,1)}), bf16[8,288,768]{2,1,0:T(8,128)(2,1)}, u32[]{:S(2)}, u32[]{:S(2)}) %all-to-all-start) | async-done | bytes 3538976 | tf_op jit(solution)/shard_map/all_to_all | solution.py:213
  223.3 24.7 %convolution_bitcast_fusion = f32[4,2,288,4096]{3,2,0,1:T(8,128)} fusion(bf16[2,768,4096]{2,1,0:T(8,128)(2,1)} %param.36, bf16[4,2,288,768]{3,2,1,0:T(8,128)(2,1)} %bitcast.22), kind=kOutput, calls=%fused_computation.25 | convolution fusion | flops 14495514624 | bytes 53870592 | tf_op jit(solution)/shard_map/sexd,edf->sexf/dot_general | solution.py:215
  248.0 54.1 %all-to-all-done.2 = bf16[8,288,768]{2,1,0:T(8,128)(2,1)S(1)} async-done(((bf16[8,288,768]{2,1,0:T(8,128)(2,1)}), bf16[8,288,768]{2,1,0:T(8,128)(2,1)S(1)}, u32[]{:S(2)}, u32[]{:S(2)}) %all-to-all-start.2) | async-done | bytes 3538976 | tf_op jit(solution)/shard_map/all_to_all | solution.py:251
  302.1 28.3 %fusion.2 = (bf16[4,2,288,2048]{3,2,0,1:T(8,128)(2,1)}, bf16[4,2,288,2048]{3,2,0,1:T(8,128)(2,1)}, bf16[4,2,288,2048]{3,2,0,1:T(8,128)(2,1)}) fusion(f32[4,2,288,4096]{3,2,0,1:T(8,128)} %convolution_bitcast_fusion, bf16[2,2048,768]{2,1,0:T(8,128)(2,1)} %param.37, bf16[4,2,288,768]{3,2,1,0:T(8,128)(2,1)S(1)} %bitcast.199), kind=kOutput, calls=%fused_computation.17 | convolution fusion | flops 7318536192 | bytes 75890688 | tf_op jit(solution)/shard_map/sexd,efd->sexf/dot_general | solution.py:259
  348.6 22.6 %convert_bitcast_fusion = bf16[4,2,288,768]{3,2,0,1:T(8,128)(2,1)} fusion(bf16[2,768,4096]{2,1,0:T(8,128)(2,1)} %param.36, bf16[4,2,288,2048]{3,2,0,1:T(8,128)(2,1)} %get-tuple-element.152, bf16[4,2,288,2048]{3,2,0,1:T(8,128)(2,1)} %get-tuple-element.151), kind=kOutput, calls=%fused_computation.71 | convolution fusion | flops 14535032832 | bytes 34996224 | tf_op jit(solution)/shard_map/sexf,edf->sexd/dot_general | solution.py:272
  375.3 51.4 %all-to-all-done.1 = bf16[8,288,768]{2,1,0:T(8,128)(2,1)S(1)} async-done(((bf16[8,288,768]{2,1,0:T(8,128)(2,1)}), bf16[8,288,768]{2,1,0:T(8,128)(2,1)S(1)}, u32[]{:S(2)}, u32[]{:S(2)}) %all-to-all-start.1) | async-done | bytes 3538976 | tf_op jit(solution)/shard_map/all_to_all | solution.py:224
  434.4 12.6 fusion.125
  447.1 15.6 %multiply_convert_fusion.4 = (bf16[1024,2048]{1,0:T(8,128)(2,1)}, bf16[1024,2048]{1,0:T(8,128)(2,1)}, bf16[1024,2048]{1,0:T(8,128)(2,1)}) fusion(f32[1024,4096]{1,0:T(8,128)} %fusion.125, bf16[2048,768]{1,0:T(8,128)(2,1)} %all-gather.12.cloned.1.call-done, f32[1024]{0:T(1024)S(1)} %copy-done.64, bf16[1024,768]{1,0:T(8,128)(2,1)S(1)} %copy-done.24), kind=kOutput, calls=%fused_computation.44 | convolution fusion | flops 3255042048 | bytes 34082816 | tf_op jit(solution)/shard_map/dot_general | solution.py:42
  463.0 48.9 %all-to-all-done.3 = bf16[8,288,768]{2,1,0:T(8,128)(2,1)} async-done(((bf16[8,288,768]{2,1,0:T(8,128)(2,1)}), bf16[8,288,768]{2,1,0:T(8,128)(2,1)}, u32[]{:S(2)}, u32[]{:S(2)}) %all-to-all-start.3) | async-done | bytes 3538976 | tf_op jit(solution)/shard_map/all_to_all | solution.py:278
  526.1 13.3 %gather_fusion.4 = bf16[2048,768]{1,0:T(8,128)(2,1)} fusion(bf16[2305,768]{1,0:T(8,128)(2,1)} %concatenate.109, s32[2048]{0:T(1024)} %get-tuple-element.173), kind=kCustom, calls=%fused_computation.1.clone | custom fusion | bytes 6299648 | tf_op jit(solution)/shard_map/jit(_take)/gather | solution.py:284
  609.6 20.3 %multiply_reduce_fusion = (f32[12,512]{1,0:T(8,128)S(1)}, f32[12,512,1024]{2,1,0:T(8,128)}) fusion(f32[12,512,1024]{2,1,0:T(8,128)} %get-tuple-element.185, f32[12,512]{1,0:T(8,128)S(1)} %log_add_fusion, pred[512,1024]{1,0:T(8,128)(4,1)S(1)} %copy-done.10, bf16[512,12,64]{0,2,1:T(8,128)(2,1)S(1)} %bitcast.201, f32[1,1024,3,12,64]{1,4,3,2,0:T(8,128)} %bitcast.196), kind=kOutput, calls=%fused_computation.7 | convolution fusion | flops 830466048 | bytes 53264384 | tf_op jit(solution)/shard_map/while/body/eval_jaxpr/qhd,khd->hqk/dot_general | solution.py:103
  630.0 14.8 %multiply_convert_fusion.2 = bf16[12,512,512]{1,2,0:T(8,128)(2,1)} fusion(f32[12,512,512]{1,2,0:T(8,128)} %get-tuple-element.194, f32[12,512,512]{1,2,0:T(8,128)} %get-tuple-element.187, f32[12,512]{1,0:T(8,128)S(1)} %get-tuple-element.193, f32[12,512]{1,0:T(8,128)S(1)} %log_add_fusion.1, pred[512,512]{0,1:T(8,128)(4,1)S(1)} %copy-done.20), kind=kLoop, calls=%fused_computation.31 | loop fusion | flops 15728640 | bytes 31768576 | tf_op jit(solution)/shard_map/while/body/eval_jaxpr/convert_element_type | solution.py:110
  653.8 15.8 %multiply_convert_fusion = bf16[12,512,1024]{2,1,0:T(8,128)(2,1)} fusion(f32[12,512,1024]{2,1,0:T(8,128)} %get-tuple-element.192, f32[12,512,1024]{2,1,0:T(8,128)S(1)} %bitcast.181, f32[12,512]{1,0:T(8,128)S(1)} %get-tuple-element.191, f32[12,512]{1,0:T(8,128)S(1)} %log_add_fusion, pred[512,1024]{1,0:T(8,128)(4,1)S(1)} %copy-done.10), kind=kLoop, calls=%fused_computation.6 | loop fusion | flops 31457280 | bytes 63488000 | tf_op jit(solution)/shard_map/while/body/eval_jaxpr/convert_element_type | solution.py:110
  716.4 13.4 %fusion.33 = f32[768,4096]{1,0:T(8,128)} fusion(bf16[1024,768]{1,0:T(8,128)(2,1)S(1)} %copy-done.28, bf16[1024,2048]{1,0:T(8,128)(2,1)} %get-tuple-element.155, bf16[1024,2048]{1,0:T(8,128)(2,1)} %get-tuple-element.154), kind=kOutput, calls=%fused_computation.66 | convolution fusion | flops 6459228160 | bytes 22544384 | tf_op jit(solution)/shard_map/dot_general | solution.py:36
  741.2 14.7 %convolution_bitcast_fusion.1 = f32[2,2048,768]{2,1,0:T(8,128)} fusion(bf16[4,2,288,2048]{3,2,0,1:T(8,128)(2,1)} %get-tuple-element.153, bf16[4,2,288,768]{3,2,1,0:T(8,128)(2,1)} %bitcast.200), kind=kOutput, calls=%fused_computation.68 | convolution fusion | flops 7247757312 | bytes 25559040 | tf_op jit(solution)/shard_map/sexf,sexd->efd/dot_general | solution.py:265
  756.0 24.3 %reduce-scatter.10.cloned.1.call-done = f32[96,2304]{1,0:T(8,128)} async-done(((f32[768,2304]{1,0:T(8,128)}), f32[96,2304]{1,0:T(8,128)}) %reduce-scatter.10.cloned.1.call-update) | async-done | bytes 884752 | tf_op jit(solution)/shard_map/reduce_scatter | solution.py:328
  780.3 95.8 %reduce-scatter.14.cloned.1.call-done = f32[96,4096]{1,0:T(8,128)} async-done(((f32[768,4096]{1,0:T(8,128)}), f32[96,4096]{1,0:T(8,128)}) %reduce-scatter.14.cloned.1.call-update) | async-done | bytes 1572880 | tf_op jit(solution)/shard_map/reduce_scatter | solution.py:330
  876.2 24.0 %fusion.18 = f32[2,768,4096]{2,1,0:T(8,128)} fusion(bf16[4,2,288,768]{3,2,1,0:T(8,128)(2,1)} %bitcast.22, bf16[4,2,288,2048]{3,2,0,1:T(8,128)(2,1)} %get-tuple-element.152, bf16[4,2,288,2048]{3,2,0,1:T(8,128)(2,1)} %get-tuple-element.151), kind=kOutput, calls=%fused_computation.40 | convolution fusion | flops 14533263360 | bytes 47579136 | tf_op jit(solution)/shard_map/sexd,sexf->edf/dot_general | solution.py:268
  914.1 29.7 %multiply_reduce_fusion.2 = f32[1024,768]{1,0:T(8,128)S(1)} fusion(f32[1024,2,768]{2,1,0:T(2,128)S(1)} %copy-done, f32[1024,2]{1,0:T(8,128)S(1)} %copy-done.33), kind=kLoop, calls=%fused_computation.62 | loop fusion | flops 2359296 | bytes 9445376 | tf_op jit(solution)/shard_map/reduce_sum | solution.py:234
  961.6 48.2 %reduce-scatter.20.cloned.1.call-done = f32[2,256,768]{2,1,0:T(8,128)} async-done(((f32[2,2048,768]{2,1,0:T(8,128)}), f32[2,256,768]{2,1,0:T(8,128)}) %reduce-scatter.20.cloned.1.call-update) | async-done | bytes 1572880 | tf_op jit(solution)/shard_map/reduce_scatter | solution.py:333
  1009.8 136.5 %all-reduce.9.cloned.1.call-done = (f32[96,2304]{1,0:T(8,128)}, f32[96,768]{1,0:T(8,128)}, f32[96,4096]{1,0:T(8,128)}, f32[256,768]{1,0:T(8,128)}) async-done(((f32[96,2304]{1,0:T(8,128)}, f32[96,768]{1,0:T(8,128)}, f32[96,4096]{1,0:T(8,128)}, f32[256,768]{1,0:T(8,128)}), (f32[96,2304]{1,0:T(8,128)}, f32[96,768]{1,0:T(8,128)}, f32[96,4096]{1,0:T(8,128)}, f32[256,768]{1,0:T(8,128)})) %all-reduce.9.cloned.1.call-update) | async-done | bytes 3538960 | tf_op jit(solution)/shard_map/psum | solution.py:337
  1146.3 159.1 %reduce-scatter.18.cloned.1.call-done = f32[2,768,512]{2,1,0:T(8,128)} async-done(((f32[2,768,4096]{2,1,0:T(8,128)}), f32[2,768,512]{2,1,0:T(8,128)}) %reduce-scatter.18.cloned.1.call-update) | async-done | bytes 3145744 | tf_op jit(solution)/shard_map/reduce_scatter | solution.py:332
  (330 shorter events, 358.7 us)
Async XLA Ops:
  7.2 39.3 %all-gather.6.cloned.1.call-start = ((), (), s32[]{:S(2)}) async-start(), calls=%async_computation.11 | async-start | bytes 3981312 | tf_op jit(solution)/shard_map/all_gather | solution.py:163
  7.9 108.5 %all-gather.8.cloned.1.call-start = ((), (), s32[]{:S(2)}) async-start(), calls=%async_computation.12 | async-start | bytes 1327104 | tf_op jit(solution)/shard_map/all_gather | solution.py:164
  8.8 99.2 %copy-start.19 = (pred[512,512]{0,1:T(8,128)(4,1)}, pred[512,512]{0,1:T(8,128)(4,1)S(1)}, u32[]{:S(2)}) copy-start(pred[512,512]{0,1:T(8,128)(4,1)S(1)} %iota_compare_fusion.1) | copy-start | bytes 786436
  23.1 97.4 %copy-start.59 = (f32[768]{0:T(1024)}, f32[768]{0:T(1024)S(1)}, u32[]{:S(2)}) copy-start(f32[768]{0:T(1024)S(1)} %get-tuple-element.143) | copy-start | bytes 9220
  25.3 31.0 %copy-start.43 = (f32[1024,32]{0,1:T(8,128)}, f32[1024,32]{0,1:T(8,128)S(1)}, u32[]{:S(2)}) copy-start(f32[1024,32]{0,1:T(8,128)S(1)} %get-tuple-element.183) | copy-start | bytes 393220
  25.7 60.9 %copy-start.9 = (pred[512,1024]{1,0:T(8,128)(4,1)}, pred[512,1024]{1,0:T(8,128)(4,1)S(1)}, u32[]{:S(2)}) copy-start(pred[512,1024]{1,0:T(8,128)(4,1)S(1)} %iota_compare_fusion) | copy-start | bytes 1572868
  64.3 43.6 %copy-start.47 = (f32[12,512]{1,0:T(8,128)}, f32[12,512]{1,0:T(8,128)S(1)}, u32[]{:S(2)}) copy-start(f32[12,512]{1,0:T(8,128)S(1)} %get-tuple-element.186) | copy-start | bytes 73732
  134.4 84.7 %all-to-all-start = ((bf16[8,288,768]{2,1,0:T(8,128)(2,1)}), bf16[8,288,768]{2,1,0:T(8,128)(2,1)}, u32[]{:S(2)}, u32[]{:S(2)}) async-start(bf16[8,288,768]{2,1,0:T(8,128)(2,1)} %broadcast_select_fusion), calls=%async_computation | async-start | bytes 7077888 | tf_op jit(solution)/shard_map/all_to_all | solution.py:213
  139.3 295.1 %all-gather.10.cloned.1.call-start = ((), (), s32[]{:S(2)}) async-start(), calls=%async_computation.13 | async-start | bytes 7077888 | tf_op jit(solution)/shard_map/all_gather | solution.py:165
  219.1 83.0 %all-to-all-start.2 = ((bf16[8,288,768]{2,1,0:T(8,128)(2,1)}), bf16[8,288,768]{2,1,0:T(8,128)(2,1)S(1)}, u32[]{:S(2)}, u32[]{:S(2)}) async-start(bf16[8,288,768]{2,1,0:T(8,128)(2,1)} %multiply_convert_fusion.6), calls=%async_computation.2 | async-start | bytes 7077888 | tf_op jit(solution)/shard_map/all_to_all | solution.py:251
  344.3 82.4 %all-to-all-start.1 = ((bf16[8,288,768]{2,1,0:T(8,128)(2,1)}), bf16[8,288,768]{2,1,0:T(8,128)(2,1)S(1)}, u32[]{:S(2)}, u32[]{:S(2)}) async-start(bf16[8,288,768]{2,1,0:T(8,128)(2,1)} %bitcast.29), calls=%async_computation.1 | async-start | bytes 7077888 | tf_op jit(solution)/shard_map/all_to_all | solution.py:224
  348.0 99.1 %all-gather.12.cloned.1.call-start = ((), (), s32[]{:S(2)}) async-start(), calls=%async_computation.14 | async-start | bytes 3538944 | tf_op jit(solution)/shard_map/all_gather | solution.py:166
  428.4 83.5 %all-to-all-start.3 = ((bf16[8,288,768]{2,1,0:T(8,128)(2,1)}), bf16[8,288,768]{2,1,0:T(8,128)(2,1)}, u32[]{:S(2)}, u32[]{:S(2)}) async-start(bf16[8,288,768]{2,1,0:T(8,128)(2,1)} %bitcast.37), calls=%async_computation.3 | async-start | bytes 7077888 | tf_op jit(solution)/shard_map/all_to_all | solution.py:278
  433.2 322.8 %reduce-scatter.12.cloned.1.call-start = ((), (), s32[]{:S(2)}) async-start(), calls=%async_computation.16 | async-start | bytes 2654208 | tf_op jit(solution)/shard_map/reduce_scatter | solution.py:329
  584.7 171.4 %reduce-scatter.16.cloned.1.call-start = ((), (), s32[]{:S(2)}) async-start(), calls=%async_computation.18 | async-start | bytes 7077888 | tf_op jit(solution)/shard_map/reduce_scatter | solution.py:331
  593.3 187.0 %reduce-scatter.10.cloned.1.call-start = ((), (), s32[]{:S(2)}) async-start(), calls=%async_computation.15 | async-start | bytes 7962624 | tf_op jit(solution)/shard_map/reduce_scatter | solution.py:328
  715.0 161.1 %reduce-scatter.14.cloned.1.call-start = ((), (), s32[]{:S(2)}) async-start(), calls=%async_computation.17 | async-start | bytes 14155776 | tf_op jit(solution)/shard_map/reduce_scatter | solution.py:330
  729.8 218.6 %reduce-scatter.22.cloned.1.call-start = ((), (), s32[]{:S(2)}) async-start(), calls=%async_computation.21 | async-start | bytes 442368
  741.1 268.7 %reduce-scatter.20.cloned.1.call-start = ((), (), s32[]{:S(2)}) async-start(), calls=%async_computation.20 | async-start | bytes 14155776 | tf_op jit(solution)/shard_map/reduce_scatter | solution.py:333
  755.9 390.4 %all-reduce.9.cloned.1.call-start = ((), (), s32[]{:S(2)}) async-start(), calls=%async_computation.22 | async-start | bytes 7077888 | tf_op jit(solution)/shard_map/psum | solution.py:337
  876.2 429.2 %reduce-scatter.18.cloned.1.call-start = ((), (), s32[]{:S(2)}) async-start(), calls=%async_computation.19 | async-start | bytes 28311552 | tf_op jit(solution)/shard_map/reduce_scatter | solution.py:332
  908.6 35.2 %copy-start.77 = (bf16[1024,2048]{1,0:T(8,128)(2,1)S(1)}, bf16[1024,2048]{1,0:T(8,128)(2,1)}, u32[]{:S(2)}) copy-start(bf16[1024,2048]{1,0:T(8,128)(2,1)} %get-tuple-element.156) | copy-start | bytes 12582916
  914.1 29.8 %copy-start.75 = (bf16[2048,768]{1,0:T(8,128)(2,1)S(1)}, bf16[2048,768]{1,0:T(8,128)(2,1)}, u32[]{:S(2)}) copy-start(bf16[2048,768]{1,0:T(8,128)(2,1)} %all-gather.12.cloned.1.call-done) | copy-start | bytes 9437188
  1146.3 165.6 %copy-start.45 = (f32[256,768]{1,0:T(8,128)S(1)}, f32[256,768]{1,0:T(8,128)}, u32[]{:S(2)}) copy-start(f32[256,768]{1,0:T(8,128)} %get-tuple-element.204) | copy-start | bytes 2359300
  (82 other events, 805.1 us)
Sparse Core Ops, SparseCore 0:
  9.9 36.5 all-gather.5
  48.4 23.9 all-gather.7
  142.0 45.8 all-gather.9
  350.4 32.6 all-gather.11
  584.8 40.4 reduce-scatter.11
  628.5 61.7 reduce-scatter.15
  715.1 65.1 reduce-scatter.9
  783.8 92.2 reduce-scatter.13
  879.8 33.8 reduce-scatter.21
  917.6 92.1 reduce-scatter.19
  1012.4 133.7 all-reduce.8
  1150.3 154.9 reduce-scatter.17
where the time goes:
time: 1330 us; the launch traced here: 1320 us
  waiting for transfers between devices  680 us (51%)
  matrix products  328 us (25%)
  local copies, waits for them, and re-layouts  128 us (10%)
  other arithmetic  127 us (10%)
  blocking collectives  22.7 us (2%)
  starting transfers between devices  18 us (1%)
  between operations  16.4 us (1%)
    reduce_scatter x1, waiting for transfers between devices, local(): lax.psum_scatter(grad_egu_weight, ('dp', 'shard'), scatter_dimension=2, t...  159 us
    psum x1, waiting for transfers between devices, local(): lax.psum((mixer_shares[0], mixer_shares[1], mixer_shares[2], mixer_shares...  136 us
    reduce_scatter x1, waiting for transfers between devices, local(): lax.psum_scatter(grad_sgu_weight, ('dp', 'shard'), scatter_dimension=0, t...  95.8 us
    all_to_all x1, waiting for transfers between devices, local(): lax.all_to_all(send_grad, 'expert', split_axis=0, concat_axis=0, tiled=True)  54.1 us
    all_to_all x1, waiting for transfers between devices, local(): lax.all_to_all(send_rows, 'expert', split_axis=0, concat_axis=0, tiled=True)  51.7 us
    all_to_all x1, waiting for transfers between devices, local(): lax.all_to_all(expert_result, 'expert', split_axis=0, concat_axis=0, tile...  51.4 us
    all_to_all x1, waiting for transfers between devices, local(): lax.all_to_all(grad_rows, 'expert', split_axis=0, concat_axis=0, tiled=True)  48.9 us
    reduce_scatter x1, waiting for transfers between devices, local(): lax.psum_scatter(grad_edown_weight, ('dp', 'shard'), scatter_dimension=1,...  48.2 us
  transfers between devices with their start and end apart: 16, of which 10 were waited for; matrix products, arithmetic and copies ran while one was open for 35% of the time, Pallas kernels for 0%

commit v1 on v0

v1 whole, which is shorter than its diff:
```python
import functools
import math

import jax
import jax.numpy as jnp
from jax import lax
from jax.experimental import pallas as pl
from jax.experimental.pallas import tpu as pltpu
from jax.sharding import PartitionSpec as P


HEADS = 12
LANES = 128
EPSILON = 1e-05
VMEM_BYTES = 60 * 1024 * 1024
BF16 = jnp.bfloat16
F32 = jnp.float32


def call(kernel, grid, in_specs, out_specs, out_shape, scratch=(), flops=0, moved=0, trans=0):
    return pl.pallas_call(
        kernel,
        grid_spec=pltpu.PrefetchScalarGridSpec(
            num_scalar_prefetch=0,
            grid=grid,
            in_specs=in_specs,
            out_specs=out_specs,
            scratch_shapes=list(scratch),
        ),
        out_shape=out_shape,
        compiler_params=pltpu.CompilerParams(
            dimension_semantics=("arbitrary",) * len(grid), vmem_limit_bytes=VMEM_BYTES
        ),
        cost_estimate=pl.CostEstimate(flops=flops, bytes_accessed=moved, transcendentals=trans),
    )


def shape_of(shape, dtype):
    return jax.ShapeDtypeStruct(shape, dtype)


def whole(shape):
    return pl.BlockSpec(shape, lambda *_: (0,) * len(shape), pipeline_mode=pl.Buffered(1))


def dot_nn(left, right):
    return lax.dot_general(left, right, (((1,), (0,)), ((), ())), preferred_element_type=F32)


def dot_nt(left, right):
    return lax.dot_general(left, right, (((1,), (1,)), ((), ())), preferred_element_type=F32)


def dot_tn(left, right):
    return lax.dot_general(left, right, (((0,), (0,)), ((), ())), preferred_element_type=F32)


def rotary_tables(length, head_dim):
    half_dim = head_dim // 2
    position = lax.iota(F32, length)[:, None]
    frequency = jnp.exp(lax.iota(F32, half_dim) * (-2.0 * math.log(10000.0) / head_dim))
    angle_table = position * frequency[None, :]
    cosine, sine = jnp.cos(angle_table), jnp.sin(angle_table)
    repeats = LANES // head_dim
    return (
        jnp.tile(jnp.concatenate([cosine, cosine], axis=1), (1, repeats)),
        jnp.tile(jnp.concatenate([-sine, sine], axis=1), (1, repeats)),
    )


def turn(values, cosine, signed_sine, head_dim):
    lane = lax.broadcasted_iota(jnp.int32, values.shape, 1)
    half = head_dim // 2
    other = jnp.where(
        lane % head_dim < half,
        pltpu.roll(values, LANES - half, 1),
        pltpu.roll(values, half, 1),
    )
    return values * cosine + other * signed_sine


def attend_forward_kernel(
    head_dim, block, x_ref, wq_ref, wk_ref, wv_ref, cos_ref, sin_ref, q_ref, k_ref, v_ref, o_ref, lse_ref, lse_tile
):
    length = x_ref.shape[0]
    heads = LANES // head_dim
    x = x_ref[...]
    cosine, sine = cos_ref[...], sin_ref[...]
    scale = 1.0 / math.sqrt(head_dim)
    q_ref[...] = (turn(dot_nn(x, wq_ref[...]), cosine, sine, head_dim) * scale).astype(BF16)
    k_ref[...] = turn(dot_nn(x, wk_ref[...]), cosine, sine, head_dim).astype(BF16)
    v_ref[...] = dot_nn(x, wv_ref[...]).astype(BF16)
    lane = lax.broadcasted_iota(jnp.int32, (1, LANES), 1)
    own_lane = lax.broadcasted_iota(jnp.int32, (block, LANES), 1) // head_dim
    below = lax.broadcasted_iota(jnp.int32, (block, block), 0) >= lax.broadcasted_iota(
        jnp.int32, (block, block), 1
    )
    for first in range(0, length, block):
        rows = pl.ds(first, block)
        mixed = None
        logs = None
        for head in range(heads):
            select = (lane // head_dim == head).astype(F32).astype(BF16)
            queries = q_ref[rows, :] * select
            near = jnp.where(below, dot_nt(queries, k_ref[rows, :]), -1e30)
            peak = jnp.max(near, axis=1, keepdims=True)
            if first:
                far = dot_nt(queries, k_ref[pl.ds(0, first), :])
                peak = jnp.maximum(peak, jnp.max(far, axis=1, keepdims=True))
            near = jnp.exp(near - peak)
            total = jnp.sum(near, axis=1, keepdims=True)
            part = dot_nn(near.astype(BF16), v_ref[rows, :])
            if first:
                far = jnp.exp(far - peak)
                total = total + jnp.sum(far, axis=1, keepdims=True)
                part = part + dot_nn(far.astype(BF16), v_ref[pl.ds(0, first), :])
            part = part * (1.0 / total)
            log_total = jnp.broadcast_to(peak + jnp.log(total), (block, LANES))
            mixed = part if head == 0 else jnp.where(own_lane == head, part, mixed)
            logs = log_total if head == 0 else jnp.where(own_lane == head, log_total, logs)
        o_ref[rows, :] = mixed.astype(BF16)
        lse_tile[rows, :] = logs
    turned = lse_tile[...].T
    for head in range(heads):
        lse_ref[pl.ds(head * 8, 8), :] = turned[head * head_dim : head * head_dim + 8, :]


def attend_forward(normed, w_qkv, cosine, sine, length, head_dim):
    tokens, width = normed.shape
    seqs, pairs, heads = tokens // length, width // LANES, LANES // head_dim
    block = min(256, length)
    rows = pl.BlockSpec((length, LANES), lambda s, p: (s, p))

    def weight(part):
        return pl.BlockSpec((width, LANES), lambda s, p: (0, part * pairs + p))

    table = whole((length, LANES))
    return call(
        functools.partial(attend_forward_kernel, head_dim, block),
        (seqs, pairs),
        [pl.BlockSpec((length, width), lambda s, p: (s, 0)), weight(0), weight(1), weight(2), table, table],
        [rows, rows, rows, rows, pl.BlockSpec((8 * heads, length), lambda s, p: (s * pairs + p, 0))],
        [shape_of((tokens, width), BF16)] * 4 + [shape_of((seqs * pairs * 8 * heads, length), F32)],
        scratch=[pltpu.VMEM((length, LANES), F32)],
        flops=6 * tokens * width * width + 4 * tokens * length * width,
        moved=16 * tokens * width,
        trans=tokens * length * width // head_dim // 2,
    )(normed, w_qkv, w_qkv, w_qkv, cosine, sine)


def attend_backward_kernel(
    head_dim, block, q_ref, k_ref, v_ref, o_ref, g_ref, lse_ref, cos_ref, sin_ref, gq_ref, gk_ref, gv_ref, gq_acc
):
    length = q_ref.shape[0]
    heads = LANES // head_dim
    scale = 1.0 / math.sqrt(head_dim)
    product = (g_ref[...].astype(F32) * o_ref[...].astype(F32)).T
    inner = [
        jnp.sum(product[head * head_dim : (head + 1) * head_dim, :], axis=0, keepdims=True)
        for head in range(heads)
    ]
    gq_acc[...] = jnp.zeros_like(gq_acc)
    lane = lax.broadcasted_iota(jnp.int32, (1, LANES), 1)
    own_lane = lax.broadcasted_iota(jnp.int32, (block, LANES), 1) // head_dim
    above = lax.broadcasted_iota(jnp.int32, (block, block), 1) >= lax.broadcasted_iota(
        jnp.int32, (block, block), 0
    )
    for first in range(0, length, block):
        rows = pl.ds(first, block)
        keys_grad = None
        values_grad = None
        for head in range(heads):
            select = (lane // head_dim == head).astype(F32).astype(BF16)
            keys = k_ref[rows, :] * select
            values = v_ref[rows, :] * select
            log_total = lse_ref[pl.ds(head * 8, 1), :]
            pieces = [(first, block, True)]
            if first + block < length:
                pieces.append((first + block, length - first - block, False))
            keys_part = None
            values_part = None
            for start, count, diagonal in pieces:
                span = pl.ds(start, count)
                queries, grads = q_ref[span, :], g_ref[span, :]
                scores = dot_nt(keys, queries)
                probs = jnp.exp(scores - log_total[:, start : start + count])
                if diagonal:
                    probs = jnp.where(above, probs, 0.0)
                grad_probs = dot_nt(values, grads)
                grad_scores = (probs * (grad_probs - inner[head][:, start : start + count])).astype(BF16)
                piece_values = dot_nn(probs.astype(BF16), grads)
                piece_keys = dot_nn(grad_scores, queries)
                values_part = piece_values if values_part is None else values_part + piece_values
                keys_part = piece_keys if keys_part is None else keys_part + piece_keys
                gq_acc[span, :] += dot_tn(grad_scores, keys)
            keys_grad = keys_part if head == 0 else jnp.where(own_lane == head, keys_part, keys_grad)
            values_grad = values_part if head == 0 else jnp.where(own_lane == head, values_part, values_grad)
        gk_ref[rows, :] = turn(keys_grad, cos_ref[rows, :], -sin_ref[rows, :], head_dim).astype(BF16)
        gv_ref[rows, :] = values_grad.astype(BF16)
    gq_ref[...] = turn(gq_acc[...] * scale, cos_ref[...], -sin_ref[...], head_dim).astype(BF16)


def attend_backward(queries, keys, values, mixed, grad_mixed, lse, cosine, sine, length, head_dim):
    tokens, width = queries.shape
    seqs, pairs, heads = tokens // length, width // LANES, LANES // head_dim
    block = min(256, length)
    rows = pl.BlockSpec((length, LANES), lambda s, p: (s, p))
    table = whole((length, LANES))
    return call(
        functools.partial(attend_backward_kernel, head_dim, block),
        (seqs, pairs),
        [rows] * 5 + [pl.BlockSpec((8 * heads, length), lambda s, p: (s * pairs + p, 0)), table, table],
        [rows] * 3,
        [shape_of((tokens, width), BF16)] * 3,
        scratch=[pltpu.VMEM((length, LANES), F32)],
        flops=10 * tokens * length * width,
        moved=16 * tokens * width,
        trans=tokens * length * width // head_dim // 2,
    )(queries, keys, values, mixed, grad_mixed, lse, cosine, sine)


def norm_one_kernel(x_ref, gain_ref, out_ref):
    x = x_ref[...].astype(F32)
    scale = lax.rsqrt(jnp.mean(x * x, axis=1, keepdims=True) + EPSILON)
    out_ref[...] = (x * scale * gain_ref[...]).astype(BF16)


def norm_one(tokens, gain):
    rows, width = tokens.shape
    block = min(256, rows)
    blocked = pl.BlockSpec((block, width), lambda i: (i, 0))
    return call(
        norm_one_kernel, (rows // block,), [blocked, whole((1, width))], blocked, shape_of((rows, width), BF16),
        flops=5 * rows * width, moved=4 * rows * width,
    )(tokens, gain)


def norm_two_kernel(mixed_ref, tokens_ref, weight_ref, gain_ref, sum_ref, normed_ref):
    first_sum = tokens_ref[...].astype(F32) + dot_nn(mixed_ref[...], weight_ref[...])
    sum_ref[...] = first_sum
    scale = lax.rsqrt(jnp.mean(first_sum * first_sum, axis=1, keepdims=True) + EPSILON)
    normed_ref[...] = (first_sum * scale * gain_ref[...]).astype(BF16)


def norm_two(mixed, tokens, weight, gain):
    rows, width = tokens.shape
    block = min(256, rows)
    blocked = pl.BlockSpec((block, width), lambda i: (i, 0))
    return call(
        norm_two_kernel, (rows // block,), [blocked, blocked, whole((width, width)), whole((1, width))],
        [blocked, blocked], [shape_of((rows, width), F32), shape_of((rows, width), BF16)],
        flops=2 * rows * width * width, moved=10 * rows * width,
    )(mixed, tokens, weight, gain)


def slots_kernel(experts, capacity, routes_ref, live_ref, dest_ref):
    top, tokens = routes_ref.shape
    live = live_ref[...]
    number = lax.broadcasted_iota(jnp.int32, (experts, tokens), 0)
    hits = [
        jnp.where((routes_ref[pl.ds(k, 1), :] == number) & (live > 0), 1.0, 0.0) for k in range(top)
    ]
    earlier = jnp.where(
        lax.broadcasted_iota(jnp.int32, (tokens, tokens), 0)
        <= lax.broadcasted_iota(jnp.int32, (tokens, tokens), 1),
        1.0,
        0.0,
    ).astype(BF16)
    ranks = dot_nn(jnp.concatenate(hits, axis=0).astype(BF16), earlier)
    before = jnp.zeros((experts, 1), F32)
    for k in range(top):
        rank = ranks[k * experts : (k + 1) * experts, :]
        place = number.astype(F32) * capacity + before + rank - 1.0
        slot = jnp.sum(hits[k] * place, axis=0, keepdims=True).astype(jnp.int32)
        dest_ref[pl.ds(k, 1), :] = jnp.where(live > 0, slot, experts * capacity)
        before = before + jnp.sum(hits[k], axis=1, keepdims=True)


def slots_of(routes_t, live_row, experts, capacity):
    top, tokens = routes_t.shape
    return call(
        functools.partial(slots_kernel, experts, capacity), (1,),
        [whole((top, tokens)), whole((1, tokens))], whole((top, tokens)), shape_of((top, tokens), jnp.int32),
        flops=2 * top * experts * tokens * tokens, moved=16 * tokens,
    )(routes_t, live_row)


def dispatch_kernel(gated, first, dest_ref, gates_ref, x_ref, out_ref):
    top, tokens = dest_ref.shape
    capacity = out_ref.shape[0]
    slot = lax.broadcasted_iota(jnp.int32, (capacity, tokens), 0) + (first + pl.program_id(0)) * capacity
    hits = [slot == dest_ref[pl.ds(k, 1), :] for k in range(top)]
    chosen = functools.reduce(jnp.logical_or, hits)
    rows = dot_nn(jnp.where(chosen, 1.0, 0.0).astype(BF16), x_ref[...])
    if gated:
        weights = jnp.zeros((capacity, tokens), F32)
        for k in range(top):
            weights = jnp.where(hits[k], gates_ref[pl.ds(k, 1), :], weights)
        rows = rows * jnp.sum(weights, axis=1, keepdims=True)
    out_ref[...] = rows.astype(BF16)


def dispatch(dest_t, gates_t, x, experts, capacity, gated, first):
    top, tokens = dest_t.shape
    width = x.shape[1]
    return call(
        functools.partial(dispatch_kernel, gated, first), (experts,),
        [whole((top, tokens)), whole((top, tokens)), whole((tokens, width))],
        pl.BlockSpec((capacity, width), lambda e: (e, 0)),
        shape_of((experts * capacity, width), BF16),
        flops=2 * experts * capacity * tokens * width, moved=2 * (experts * capacity + tokens) * width,
    )(dest_t, gates_t, x)


def combine_kernel(parts, dest_ref, gates_ref, live_ref, sum_ref, shared_ref, *rest):
    y_refs, out_ref = rest[:parts], rest[parts]
    block, top = dest_ref.shape
    total = sum_ref[...] + shared_ref[...]
    dest = dest_ref[...]
    gates = gates_ref[...]
    for index, y_ref in enumerate(y_refs):
        y = y_ref[...]
        slot = slot_numbers(block, y_ref.shape[0], index)
        for k in range(top):
            hit = jnp.where(slot == dest[:, k : k + 1], 1.0, 0.0).astype(BF16)
            total = total + dot_nn(hit, y) * gates[:, k : k + 1]
    out_ref[...] = (live_ref[...] * total).astype(BF16)


def slot_numbers(block, slots, index):
    return lax.broadcasted_iota(jnp.int32, (block, slots), 1) + index * slots


def combine(dest, gates, live, first_sum, shared_out, returned):
    rows, width = first_sum.shape
    top = dest.shape[1]
    block = min(256, rows)
    parts = len(returned)
    blocked = pl.BlockSpec((block, width), lambda i: (i, 0))
    narrow = pl.BlockSpec((block, top), lambda i: (i, 0))
    slots = sum(y.shape[0] for y in returned)
    return call(
        functools.partial(combine_kernel, parts), (rows // block,),
        [narrow, narrow, pl.BlockSpec((block, 1), lambda i: (i, 0)), blocked, blocked]
        + [whole(y.shape) for y in returned],
        blocked, shape_of((rows, width), BF16),
        flops=4 * rows * slots * width, moved=10 * rows * width + 2 * slots * width,
    )(dest, gates, live, first_sum, shared_out, *returned)


def norm_two_back_kernel(parts, dest_ref, live_ref, cot_ref, sum_ref, shared_ref, gain_ref, *rest):
    y_refs = rest[:parts]
    first_ref, attn_ref, gain_grad_ref = rest[parts:]
    block, top = dest_ref.shape
    grad_normed = shared_ref[...]
    dest = dest_ref[...]
    for index, y_ref in enumerate(y_refs):
        slot = slot_numbers(block, y_ref.shape[0], index)
        hit = functools.reduce(jnp.logical_or, [slot == dest[:, k : k + 1] for k in range(top)])
        grad_normed = grad_normed + dot_nn(jnp.where(hit, 1.0, 0.0).astype(BF16), y_ref[...])
    first_sum = sum_ref[...]
    scale = lax.rsqrt(jnp.mean(first_sum * first_sum, axis=1, keepdims=True) + EPSILON)
    weighted = grad_normed * gain_ref[...]
    inner = jnp.mean(first_sum * weighted, axis=1, keepdims=True)
    grad_first = (
        cot_ref[...].astype(F32) * live_ref[...] + scale * weighted - first_sum * (scale * scale * scale * inner)
    )
    first_ref[...] = grad_first
    attn_ref[...] = grad_first.astype(BF16)

    @pl.when(pl.program_id(0) == 0)
    def _():
        gain_grad_ref[...] = jnp.zeros_like(gain_grad_ref)

    gain_grad_ref[...] += jnp.sum(grad_normed * first_sum * scale, axis=0, keepdims=True)


def norm_two_back(dest, live, cotangent, first_sum, grad_shared, gain, returned):
    rows, width = first_sum.shape
    top = dest.shape[1]
    block = min(256, rows)
    parts = len(returned)
    blocked = pl.BlockSpec((block, width), lambda i: (i, 0))
    slots = sum(y.shape[0] for y in returned)
    return call(
        functools.partial(norm_two_back_kernel, parts), (rows // block,),
        [pl.BlockSpec((block, top), lambda i: (i, 0)), pl.BlockSpec((block, 1), lambda i: (i, 0)), blocked, blocked,
         blocked, whole((1, width))]
        + [whole(y.shape) for y in returned],
        [blocked, blocked, pl.BlockSpec((1, width), lambda i: (0, 0))],
        [shape_of((rows, width), F32), shape_of((rows, width), BF16), shape_of((1, width), F32)],
        flops=2 * rows * slots * width, moved=16 * rows * width + 2 * slots * width,
    )(dest, live, cotangent, first_sum, grad_shared, gain, *returned)


def norm_one_back_kernel(gq_ref, gk_ref, gv_ref, wq_ref, wk_ref, wv_ref, tokens_ref, first_ref, gain_ref, out_ref, gain_grad_ref):
    grad_normed = (
        dot_nt(gq_ref[...], wq_ref[...]) + dot_nt(gk_ref[...], wk_ref[...]) + dot_nt(gv_ref[...], wv_ref[...])
    )
    source = tokens_ref[...].astype(F32)
    scale = lax.rsqrt(jnp.mean(source * source, axis=1, keepdims=True) + EPSILON)
    weighted = grad_normed * gain_ref[...]
    inner = jnp.mean(source * weighted, axis=1, keepdims=True)
    out_ref[...] = first_ref[...] + scale * weighted - source * (scale * scale * scale * inner)

    @pl.when(pl.program_id(0) == 0)
    def _():
        gain_grad_ref[...] = jnp.zeros_like(gain_grad_ref)

    gain_grad_ref[...] += jnp.sum(grad_normed * source * scale, axis=0, keepdims=True)


def norm_one_back(grads, w_qkv, tokens, grad_first, gain):
    rows, width = tokens.shape
    block = min(256, rows)
    blocked = pl.BlockSpec((block, width), lambda i: (i, 0))

    def weight(part):
        return pl.BlockSpec((width, width), lambda i: (0, part), pipeline_mode=pl.Buffered(1))

    return call(
        norm_one_back_kernel, (rows // block,),
        [blocked] * 3 + [weight(0), weight(1), weight(2), blocked, blocked, whole((1, width))],
        [blocked, pl.BlockSpec((1, width), lambda i: (0, 0))],
        [shape_of((rows, width), F32), shape_of((1, width), F32)],
        flops=6 * rows * width * width, moved=22 * rows * width,
    )(*grads, w_qkv, w_qkv, w_qkv, tokens, grad_first, gain)


def copies_of(layout, block, width, step, stage_g, stage_u, stage_d, slot, packed_ref, sems):
    by_rows, owners, hidden = layout
    panels = block // LANES
    rows_down = hidden // owners
    out = []

    def add(source, target):
        out.append(pltpu.make_async_copy(source, target, sems.at[slot, len(out)]))

    if by_rows:
        rows = width // owners
        for half, stage in enumerate((stage_g, stage_u)):
            for p in range(panels):
                panel = half * (hidden // LANES) + step * panels + p
                add(
                    stage.at[slot, :, :, pl.ds(p * LANES, LANES)],
                    packed_ref.at[:, pl.ds(pl.multiple_of(panel * rows, 8), rows), :],
                )
        start = 2 * hidden // LANES * rows
    else:
        columns = 2 * hidden // owners
        for half, stage in enumerate((stage_g, stage_u)):
            for p in range(panels):
                column = half * hidden + step * block + p * LANES
                owner, panel = column // columns, (column % columns) // LANES
                add(
                    stage.at[slot, :, pl.ds(p * LANES, LANES)],
                    packed_ref.at[owner, pl.ds(pl.multiple_of(panel * width, 8), width), :],
                )
        start = columns // LANES * width
    for q in range(block // rows_down):
        owner = step * (block // rows_down) + q
        for c in range(width // LANES):
            add(
                stage_d.at[slot, pl.ds(q * rows_down, rows_down), pl.ds(c * LANES, LANES)],
                packed_ref.at[owner, pl.ds(start + c * rows_down, rows_down), :],
            )
    return out


def packed_rows(width, hidden, owners):
    return 3 * width * hidden // owners // LANES


def ffn_kernel(out_type, layout, block, x_ref, gy_ref, wg_ref, wu_ref, wd_ref, y_ref, gx_ref, packed_ref, xt, y_acc, gx_acc,
               stage_g, stage_u, stage_d, sems):
    step = pl.program_id(0)
    steps = layout[2] // block
    width = x_ref.shape[1]
    slot = step % 2
    copies = functools.partial(copies_of, layout, block, width)

    @pl.when(step == 0)
    def _():
        xt[...] = x_ref[...].T
        y_acc[...] = jnp.zeros_like(y_acc)
        gx_acc[...] = jnp.zeros_like(gx_acc)

    @pl.when(step >= 2)
    def _():
        for copy in copies(step - 2, stage_g, stage_u, stage_d, slot, packed_ref, sems):
            copy.wait()

    x, gy = x_ref[...], gy_ref[...].reshape(x_ref.shape)
    wg, wu, wd = wg_ref[...], wu_ref[...], wd_ref[...]
    gate, up = dot_nn(x, wg), dot_nn(x, wu)
    grad_hidden = dot_nt(gy, wd)
    sigmoid = jax.nn.sigmoid(gate)
    value = gate * sigmoid
    hidden = (value * up).astype(BF16)
    grad_up = (grad_hidden * value).astype(BF16)
    grad_gate = (grad_hidden * up * (sigmoid * (1.0 + gate * (1.0 - sigmoid)))).astype(BF16)
    y_acc[...] += dot_nn(hidden, wd)
    gx_acc[...] += dot_nt(grad_gate, wg) + dot_nt(grad_up, wu)
    stage_g[slot] = dot_nn(xt[...], grad_gate).astype(BF16).reshape(stage_g.shape[1:])
    stage_u[slot] = dot_nn(xt[...], grad_up).astype(BF16).reshape(stage_u.shape[1:])
    stage_d[slot] = dot_tn(hidden, gy).astype(BF16)
    for copy in copies(step, stage_g, stage_u, stage_d, slot, packed_ref, sems):
        copy.start()

    @pl.when(step == steps - 1)
    def _():
        y_ref[...] = y_acc[...].astype(out_type)
        gx_ref[...] = gx_acc[...].astype(out_type)
        for back in (1, 0):
            if steps > back:
                for copy in copies(steps - 1 - back, stage_g, stage_u, stage_d, (steps - 1 - back) % 2, packed_ref, sems):
                    copy.wait()


def ffn_both(x, gy, w_gu, w_down, expert, owners, out_type):
    rows, width = x.shape
    hidden = w_down.shape[-2]
    block = min(256, hidden)
    steps = hidden // block
    by_rows = expert is None
    if by_rows:
        gate = pl.BlockSpec((width, block), lambda f: (0, f))
        up = pl.BlockSpec((width, block), lambda f: (0, steps + f))
        down = pl.BlockSpec((block, width), lambda f: (f, 0))
        stage = (2, owners, width // owners, block)
    else:
        gate = pl.BlockSpec((None, width, block), lambda f: (expert, 0, f))
        up = pl.BlockSpec((None, width, block), lambda f: (expert, 0, steps + f))
        down = pl.BlockSpec((None, block, width), lambda f: (expert, f, 0))
        stage = (2, width, block)
    if by_rows:
        grads = whole((rows, width))
    else:
        grads = pl.BlockSpec(
            (gy.shape[0], rows // gy.shape[0], width), lambda f: (0, expert, 0), pipeline_mode=pl.Buffered(1)
        )
    out_rows = whole((rows, width))
    layout = (by_rows, owners, hidden)
    copies = 2 * (block // LANES) + block // (hidden // owners) * (width // LANES)
    return call(
        functools.partial(ffn_kernel, out_type, layout, block), (steps,),
        [whole((rows, width)), grads, gate, up, down],
        [out_rows, out_rows, pl.BlockSpec(memory_space=pl.ANY)],
        [shape_of((rows, width), out_type), shape_of((rows, width), out_type),
         shape_of((owners, packed_rows(width, hidden, owners), LANES), BF16)],
        scratch=[pltpu.VMEM((width, rows), BF16), pltpu.VMEM((rows, width), F32), pltpu.VMEM((rows, width), F32),
                 pltpu.VMEM(stage, BF16), pltpu.VMEM(stage, BF16), pltpu.VMEM((2, block, width), BF16),
                 pltpu.SemaphoreType.DMA((2, copies))],
        flops=18 * rows * width * hidden, moved=12 * width * hidden + 16 * rows * width, trans=rows * hidden,
    )(x, gy, w_gu, w_gu, w_down)


def panels_to(rows_array, rows, panels):
    return jnp.transpose(rows_array.reshape(panels, rows, LANES), (1, 0, 2)).reshape(rows, panels * LANES)


def attention_weights_kernel(per, normed_ref, mixed_ref, gq_ref, gk_ref, gv_ref, ga_ref, gains_ref, out_ref, xt):
    step = pl.program_id(0)
    owners, rows = out_ref.shape[0], out_ref.shape[1] // (out_ref.shape[1] // (normed_ref.shape[1] // out_ref.shape[0]))
    panels = out_ref.shape[1] // rows

    @pl.when(step == 0)
    def _():
        xt[...] = normed_ref[...].T

    @pl.when(step == 3 * per)
    def _():
        xt[...] = mixed_ref[...].T

    for index, grad_ref in enumerate((gq_ref, gk_ref, gv_ref, ga_ref)):

        @pl.when((step >= index * per) & (step < (index + 1) * per))
        def _():
            product = dot_nn(xt[...], grad_ref[...]).astype(BF16)
            for p in range(panels):
                out_ref[:, pl.ds(p * rows, rows), :] = product[:, p * LANES : (p + 1) * LANES].reshape(owners, rows, LANES)

    @pl.when(step == 4 * per)
    def _():
        out_ref[...] = jnp.zeros_like(out_ref)
        out_ref[:, pl.ds(0, gains_ref.shape[1]), :] = gains_ref[...]


def attention_weights(normed, mixed, grads, grad_attn, gains, owners):
    tokens, width = normed.shape
    rows = width // owners
    block = 256
    panels, per = block // LANES, width // block

    def columns(index):
        return pl.BlockSpec((tokens, block), lambda i: (0, jnp.clip(i - index * per, 0, per - 1)))

    return call(
        functools.partial(attention_weights_kernel, per), (4 * per + 1,),
        [whole((tokens, width)), whole((tokens, width))] + [columns(index) for index in range(4)] + [whole(gains.shape)],
        pl.BlockSpec((owners, panels * rows, LANES), lambda i: (0, i, 0)),
        shape_of((owners, (4 * per + 1) * panels * rows, LANES), BF16),
        scratch=[pltpu.VMEM((width, tokens), BF16)],
        flops=8 * tokens * width * width, moved=16 * tokens * width,
    )(normed, mixed, *grads, grad_attn, gains)


GROUP = ("dp", "shard")


def local(
    tokens,
    lengths,
    routes,
    route_gates,
    cotangent,
    norm_gains,
    w_qkv,
    w_out,
    w_shared_gu,
    w_shared_down,
    w_expert_gu,
    w_expert_down,
):
    tok_count, width = tokens.shape
    seq_count = lengths.shape[0]
    length = tok_count // seq_count
    local_experts = w_expert_gu.shape[0]
    owners = lax.axis_size("expert")
    experts = local_experts * owners
    top = routes.shape[1]
    capacity = tok_count * top * 9 // (8 * experts)
    head_dim = width // HEADS

    gains = lax.all_gather(norm_gains, GROUP, axis=1, tiled=True).astype(F32)
    qkv_weight = lax.all_gather(w_qkv, GROUP, axis=0, tiled=True)
    out_weight = lax.all_gather(w_out, GROUP, axis=0, tiled=True)
    sgu_weight = lax.all_gather(w_shared_gu, GROUP, axis=0, tiled=True)
    sdown_weight = lax.all_gather(w_shared_down, GROUP, axis=0, tiled=True)
    gain_one, gain_two = gains[0:1], gains[1:2]

    live_bool = lax.iota(jnp.int32, tok_count) % length < jnp.repeat(lengths, length)
    live = live_bool.astype(F32)[:, None]
    live_row = live_bool.astype(jnp.int32)[None, :]

    group = lax.axis_size("dp") * lax.axis_size("shard")

    dest_t = slots_of(routes.T, live_row, experts, capacity)
    dest = dest_t.T
    slots = owners * capacity

    def place(where):
        owner_of, part_of = where // (local_experts * capacity), (where // capacity) % local_experts
        return jnp.where(
            where < experts * capacity, part_of * slots + owner_of * capacity + where % capacity, experts * capacity
        )

    placed, placed_t = place(dest), place(dest_t)
    gates_t = route_gates.T
    grad_b = jnp.where(live_bool[:, None], cotangent, 0).astype(BF16)

    def exchange(rows):
        count = rows.shape[0] // owners
        return lax.all_to_all(
            rows.reshape(owners, count, width), "expert", split_axis=0, concat_axis=0, tiled=True
        ).reshape(rows.shape)

    send_grad = dispatch(dest_t, gates_t, grad_b, experts, capacity, True, 0)
    received_grad = exchange(send_grad).reshape(owners, local_experts * capacity, width)

    cosine, sine = rotary_tables(length, head_dim)
    normed_one = norm_one(tokens, gain_one)
    queries, keys, values, mixed, lse = attend_forward(normed_one, qkv_weight, cosine, sine, length, head_dim)
    first_sum, normed_two = norm_two(mixed, tokens, out_weight, gain_two)

    received = []
    for j in range(local_experts):
        rows = dispatch(placed_t, gates_t, normed_two, owners, capacity, False, j * owners)
        received.append(exchange(rows))
    shared_out, grad_shared, shared_pack = ffn_both(
        normed_two, grad_b, sgu_weight, sdown_weight, None, group, F32
    )
    back_rows, out_rows, expert_packs = [], [], []
    for j in range(local_experts):
        y, gx, pack = ffn_both(received[j], received_grad, w_expert_gu, w_expert_down, j, group, BF16)
        back_rows.append(exchange(gx))
        out_rows.append(y)
        expert_packs.append(pack)
    grad_first, grad_attn, grad_gain_two = norm_two_back(
        placed, live, cotangent, first_sum, grad_shared, gain_two, back_rows
    )

    grad_mixed = dot_nt(grad_attn, out_weight).astype(BF16)
    grads = attend_backward(queries, keys, values, mixed, grad_mixed, lse, cosine, sine, length, head_dim)
    input_grad, grad_gain_one = norm_one_back(grads, qkv_weight, tokens, grad_first, gain_one)
    own = width // group
    grad_gains = jnp.concatenate([grad_gain_one, grad_gain_two], axis=0).reshape(2, group, own).transpose(1, 0, 2)
    grad_gains = jnp.pad(grad_gains, ((0, 0), (0, 14), (0, LANES - own))).astype(BF16)
    attention_pack = attention_weights(normed_one, mixed, grads, grad_attn, grad_gains, group)

    returned = exchange_parts(out_rows, owners, "expert")
    layer_out = combine(placed, route_gates, live, first_sum, shared_out, returned)

    def spread(pack):
        return lax.psum_scatter(pack, GROUP, scatter_dimension=0, tiled=True)[0]

    shared_share = spread(shared_pack)
    expert_shares = [spread(pack) for pack in expert_packs]
    attention_share = spread(attention_pack)
    shared_share = lax.psum(shared_share, "expert").astype(F32)
    attention_share = lax.psum(attention_share, "expert").astype(F32)
    hidden = w_expert_down.shape[1]
    shared_hidden = sdown_weight.shape[0]
    gu_panels, d_panels = 2 * shared_hidden // LANES, width // LANES
    qkv_rows, out_rows_count = 3 * d_panels * own, 4 * d_panels * own
    columns = 2 * hidden // group
    gu_rows = columns // LANES * width
    return (
        layer_out,
        input_grad,
        attention_share[out_rows_count : out_rows_count + 2, :own],
        panels_to(attention_share[:qkv_rows], own, 3 * d_panels),
        panels_to(attention_share[qkv_rows:out_rows_count], own, d_panels),
        panels_to(shared_share[: gu_panels * own], own, gu_panels),
        panels_to(shared_share[gu_panels * own :], shared_hidden // group, d_panels),
        jnp.stack([panels_to(share[:gu_rows], width, columns // LANES) for share in expert_shares]).astype(F32),
        jnp.stack([panels_to(share[gu_rows:], hidden // group, d_panels) for share in expert_shares]).astype(F32),
    )


def exchange_parts(parts, owners, axis):
    width = parts[0].shape[1]
    count = parts[0].shape[0] // owners
    joined = jnp.concatenate([rows.reshape(owners, count, width) for rows in parts], axis=1)
    back = lax.all_to_all(joined, axis, split_axis=0, concat_axis=0, tiled=True)
    return [
        back[:, j * count : (j + 1) * count].reshape(owners * count, width) for j in range(len(parts))
    ]


def solution(mesh):
    rows = P(("dp", "expert", "shard"), None)
    split = P(GROUP, None)
    in_specs = (
        rows,
        P(("dp", "expert", "shard")),
        rows,
        rows,
        rows,
        P(None, GROUP),
        split,
        split,
        split,
        split,
        P("expert", None, None),
        P("expert", None, None),
    )
    out_specs = (
        rows,
        rows,
        P(None, GROUP),
        split,
        split,
        split,
        split,
        P("expert", None, GROUP),
        P("expert", GROUP, None),
    )

    return jax.shard_map(local, mesh=mesh, in_specs=in_specs, out_specs=out_specs, check_vma=False)
```

time: 1330 us -> 776 us (0.58)
  matrix products: 328 us -> 3.97 us
  waiting for transfers between devices: 680 us -> 395 us
  Pallas kernels: 0 us -> 270 us
  other arithmetic: 127 us -> 14.2 us
  local copies, waits for them, and re-layouts: 128 us -> 29.1 us
  blocking collectives: 22.7 us -> 8.95 us
    dot_general x30 -> x1, matrix products: 328 us -> 3.97 us  [dot_nt(): lax.dot_general(left, right, (((1,), (1,)), ((), ())), preferred_element_...]
    pallas_call x0 -> x15, Pallas kernels: none -> 270 us  [the longest x3 124 us: ffn_both(): call(functools.partial(ffn_kernel, out_type, layout, block), (steps,), [w...]
    all_to_all x4 -> x6, waiting for transfers between devices: 206 us -> 49.8 us  [the longest x5 49.8 us: exchange(): lax.all_to_all(rows.reshape(owners, count, width), 'expert', split_axis=0...]
    psum x1, waiting for transfers between devices: 136 us -> 72.2 us  [local(): attention_share = lax.psum(attention_share, 'expert').astype(F32)]
    reduce_sum x6 -> x0, other arithmetic: 60.5 us -> none  [the longest x1 29.7 us: local(): moe_out = jnp.sum(picked * route_gates[:, :, None], axis=1)]
    reduce_scatter x6 -> x4, waiting for transfers between devices: 327 us -> 268 us  [spread(): return lax.psum_scatter(pack, GROUP, scatter_dimension=0, tiled=True)[0]]
    gather x5 -> x0, local copies, waits for them, and re-layouts: 51.5 us -> none  [the longest x1 13.3 us: local(): jnp.take(padded_back, destination, axis=0).astype(jnp.float32)]
    convert_element_type x7 -> x5, other arithmetic: 36.1 us -> 4.59 us  [the longest x1 1.87 us: local(): jnp.stack([panels_to(share[:gu_rows], width, columns // LANES) for share...]
  transfers between devices with their start and end apart: 16 -> 15, of which waited for: 10 -> 8; matrix products, arithmetic and copies ran while one was open for 35% -> 3% of each run, Pallas kernels for 0% -> 26%
where the time goes in v1:
time: 776 us; the launch traced here: 766 us
  waiting for transfers between devices  395 us (51%)
  Pallas kernels  270 us (35%)
  starting transfers between devices  29.7 us (4%)
  local copies, waits for them, and re-layouts  29.1 us (4%)
  between operations  15.2 us (2%)
  other arithmetic  14.2 us (2%)
  blocking collectives  8.95 us (1%)
    reduce_scatter x4, waiting for transfers between devices, spread(): return lax.psum_scatter(pack, GROUP, scatter_dimension=0, tiled=True)[0]  268 us
    pallas_call x3, Pallas kernels, ffn_both(): call(functools.partial(ffn_kernel, out_type, layout, block), (steps,), [w...  124 us
    psum x1, waiting for transfers between devices, local(): attention_share = lax.psum(attention_share, 'expert').astype(F32)  72.2 us
    all_to_all x5, waiting for transfers between devices, exchange(): lax.all_to_all(rows.reshape(owners, count, width), 'expert', split_axis=0...  49.8 us
    pallas_call x1, Pallas kernels, attend_backward(): call(functools.partial(attend_backward_kernel, head_dim, block), (seqs, p...  34.4 us
    pallas_call x1, Pallas kernels, attend_forward(): call(functools.partial(attend_forward_kernel, head_dim, block), (seqs, pa...  33.1 us
    all_to_all x5, starting transfers between devices, exchange(): lax.all_to_all(rows.reshape(owners, count, width), 'expert', split_axis=0...  24.8 us
    pallas_call x3, Pallas kernels, dispatch(): call(functools.partial(dispatch_kernel, gated, first), (experts,), [whole...  18.8 us
  transfers between devices with their start and end apart: 15, of which 8 were waited for; matrix products, arithmetic and copies ran while one was open for 3% of the time, Pallas kernels for 26%

profile of v1, /device:TPU:0, one launch (start us, length us, event | category | flops | bytes accessed | tf_op | source)
XLA Modules:
  0.0 766.1 jit_solution(2994816656422617389)
XLA Ops:
  15.0 8.6 %shard_map.196 = bf16[2304,768]{1,0:T(8,128)(2,1)} custom-call(s32[2,1024]{1,0:T(2,128)} %shard_map.190.dest_ref, f32[2,1024]{1,0:T(2,128)} %bitcast.134, bf16[1024,768]{1,0:T(8,128)(2,1)} %broadcast_select_fusion.gy_ref.x_ref), custom_call_target="tpu_custom_call" | custom-call | flops 3623878656 | bytes 5111808 | tf_op jit(solution)/shard_map/pallas_call | solution.py:306
  23.6 6.5 all-to-all-start.1
  30.9 8.9 %all-gather = bf16[8,96,2]{1,2,0:T(2,128)(2,1)S(1)} all-gather(bf16[1,96,2]{1,2,0:T(2,128)(2,1)S(1)} %bitcast.137), channel_id=1, replica_groups=mesh['dp'=2,'expert'=4,'shard'=4] {'dp','shard'}, dimensions={0}, use_global_device_ids=true | all-gather | bytes 3456 | tf_op jit(solution)/shard_map/all_gather | solution.py:635
  48.9 33.1 %shard_map.192 = (bf16[1024,768]{1,0:T(8,128)(2,1)}, bf16[1024,768]{1,0:T(8,128)(2,1)}, bf16[1024,768]{1,0:T(8,128)(2,1)}, bf16[1024,768]{1,0:T(8,128)(2,1)}, f32[96,1024]{1,0:T(8,128)}) custom-call(bf16[1024,768]{1,0:T(8,128)(2,1)} %shard_map.191.x_ref.normed_ref, bf16[768,2304]{1,0:T(8,128)(2,1)} %all-gather.6.cloned.1.call-done.wq_ref.wk_ref.wv_ref, ...), custom_call_target="tpu_custom_call" | custom-call | flops 6845104128 | bytes 12582912 | tf_op jit(solution)/shard_map/pallas_call | solution.py:138
  82.0 5.8 shard_map.193
  87.9 5.1 shard_map.195
  93.0 16.4 %all-to-all-done.1.gy_ref = bf16[4,576,768]{2,1,0:T(8,128)(2,1)} async-done(((bf16[4,576,768]{2,1,0:T(8,128)(2,1)}), bf16[4,576,768]{2,1,0:T(8,128)(2,1)}, u32[]{:S(2)}, u32[]{:S(2)}) %all-to-all-start.1) | async-done | bytes 3538976 | tf_op jit(solution)/shard_map/all_to_all | solution.py:664
  115.6 5.1 shard_map.198
  120.8 32.8 %all-to-all-done = bf16[4,288,768]{2,1,0:T(8,128)(2,1)S(1)} async-done(((bf16[4,288,768]{2,1,0:T(8,128)(2,1)}), bf16[4,288,768]{2,1,0:T(8,128)(2,1)S(1)}, u32[]{:S(2)}, u32[]{:S(2)}) %all-to-all-start) | async-done | bytes 1769504 | tf_op jit(solution)/shard_map/all_to_all | solution.py:664
  159.4 42.8 %shard_map.197 = (bf16[1152,768]{1,0:T(8,128)(2,1)}, bf16[1152,768]{1,0:T(8,128)(2,1)}, bf16[8,4608,128]{2,1,0:T(8,128)(2,1)}) custom-call(bf16[1152,768]{1,0:T(8,128)(2,1)} %bitcast.119, bf16[4,576,768]{2,1,0:T(8,128)(2,1)} %all-to-all-done.1.gy_ref, bf16[2,768,4096]{2,1,0:T(8,128)(2,1)} %wu_ref.3, bf16[2,768,4096]{2,1,0:T(8,128)(2,1)} %wu_ref.3, ...), custom_call_target="tpu_custom_call" | custom-call | flops 32614907904 | bytes 33030144 | tf_op jit(solution)/shard_map/pallas_call | solution.py:545
  202.3 5.1 all-to-all-start.4
  207.3 42.7 %shard_map.199 = (bf16[1152,768]{1,0:T(8,128)(2,1)}, bf16[1152,768]{1,0:T(8,128)(2,1)}, bf16[8,4608,128]{2,1,0:T(8,128)(2,1)}) custom-call(bf16[1152,768]{1,0:T(8,128)(2,1)} %bitcast.19.x_ref, bf16[4,576,768]{2,1,0:T(8,128)(2,1)} %all-to-all-done.1.gy_ref, bf16[2,768,4096]{2,1,0:T(8,128)(2,1)} %wu_ref.3, bf16[2,768,4096]{2,1,0:T(8,128)(2,1)} %wu_ref.3, ...), custom_call_target="tpu_custom_call" | custom-call | flops 32614907904 | bytes 33030144 | tf_op jit(solution)/shard_map/pallas_call | solution.py:545
  251.2 5.1 all-to-all-start.5
  256.6 38.7 %shard_map.194 = (f32[1024,768]{1,0:T(8,128)}, f32[1024,768]{1,0:T(8,128)}, bf16[8,4608,128]{2,1,0:T(8,128)(2,1)}) custom-call(bf16[1024,768]{1,0:T(8,128)(2,1)} %get-tuple-element.35.x_ref, bf16[1024,768]{1,0:T(8,128)(2,1)} %broadcast_select_fusion.gy_ref.x_ref, bf16[768,4096]{1,0:T(8,128)(2,1)} %all-gather.10.cloned.1.call-done.wg_ref.wu_ref, ...), custom_call_target="tpu_custom_call" | custom-call | flops 28991029248 | bytes 31457280 | tf_op jit(solution)/shard_map/pallas_call | solution.py:545
  297.2 10.7 %shard_map.201 = (f32[1024,768]{1,0:T(8,128)}, bf16[1024,768]{1,0:T(8,128)(2,1)}, f32[1,768]{1,0:T(1,128)}) custom-call(s32[1024,2]{1,0:T(8,128)} %fusion.4.dest_ref, f32[1024,1]{1,0:T(8,128)} %fusion.16.live_ref, bf16[1024,768]{1,0:T(8,128)(2,1)} %cot_ref.1, f32[1024,768]{1,0:T(8,128)} %get-tuple-element.34.sum_ref, ...), custom_call_target="tpu_custom_call" | custom-call | flops 3623878656 | bytes 16121856 | tf_op jit(solution)/shard_map/pallas_call | solution.py:385
  312.5 34.4 %shard_map.202 = (bf16[1024,768]{1,0:T(8,128)(2,1)}, bf16[1024,768]{1,0:T(8,128)(2,1)}, bf16[1024,768]{1,0:T(8,128)(2,1)}) custom-call(bf16[1024,768]{1,0:T(8,128)(2,1)} %get-tuple-element.39.q_ref, bf16[1024,768]{1,0:T(8,128)(2,1)} %get-tuple-element.40.k_ref, bf16[1024,768]{1,0:T(8,128)(2,1)} %get-tuple-element.41.v_ref, ...), custom_call_target="tpu_custom_call" | custom-call | flops 8053063680 | bytes 12582912 | tf_op jit(solution)/shard_map/pallas_call | solution.py:209
  346.9 9.9 %shard_map.203 = (f32[1024,768]{1,0:T(8,128)}, f32[1,768]{1,0:T(1,128)}) custom-call(bf16[1024,768]{1,0:T(8,128)(2,1)} %get-tuple-element.47.gq_ref, bf16[1024,768]{1,0:T(8,128)(2,1)} %get-tuple-element.48.gk_ref, bf16[1024,768]{1,0:T(8,128)(2,1)} %get-tuple-element.49.gv_ref, bf16[768,2304]{1,0:T(8,128)(2,1)} %all-gather.6.cloned.1.call-done.wq_ref.wk_ref.wv_ref, ...), custom_call_target="tpu_custom_call" | custom-call | flops 3623878656 | bytes 17301504 | tf_op jit(solution)/shard_map/pallas_call | solution.py:421
  358.3 14.4 %shard_map.204 = bf16[8,2496,128]{2,1,0:T(8,128)(2,1)} custom-call(bf16[1024,768]{1,0:T(8,128)(2,1)} %shard_map.191.x_ref.normed_ref, bf16[1024,768]{1,0:T(8,128)(2,1)} %get-tuple-element.33.mixed_ref.o_ref, bf16[1024,768]{1,0:T(8,128)(2,1)} %get-tuple-element.47.gq_ref, bf16[1024,768]{1,0:T(8,128)(2,1)} %get-tuple-element.48.gk_ref, ...), custom_call_target="tpu_custom_call" | custom-call | flops 4831838208 | bytes 12582912 | tf_op jit(solution)/shard_map/pallas_call | solution.py:598
  382.7 46.8 %reduce-scatter.5.cloned.1.call-done = bf16[1,2496,128]{2,1,0:T(8,128)(2,1)} async-done(((bf16[8,2496,128]{2,1,0:T(8,128)(2,1)}), bf16[1,2496,128]{2,1,0:T(8,128)(2,1)}) %reduce-scatter.5.cloned.1.call-update) | async-done | bytes 638992 | tf_op jit(solution)/shard_map/reduce_scatter | solution.py:705
  429.5 80.2 %reduce-scatter.7.cloned.1.call-done = bf16[1,4608,128]{2,1,0:T(8,128)(2,1)} async-done(((bf16[8,4608,128]{2,1,0:T(8,128)(2,1)}), bf16[1,4608,128]{2,1,0:T(8,128)(2,1)}) %reduce-scatter.7.cloned.1.call-update) | async-done | bytes 1179664 | tf_op jit(solution)/shard_map/reduce_scatter | solution.py:705
  512.8 13.3 %shard_map.200 = bf16[1024,768]{1,0:T(8,128)(2,1)} custom-call(s32[1024,2]{1,0:T(8,128)} %fusion.4.dest_ref, f32[1024,2]{1,0:T(8,128)} %copy.100.gates_ref, f32[1024,1]{1,0:T(8,128)} %fusion.16.live_ref, f32[1024,768]{1,0:T(8,128)} %get-tuple-element.34.sum_ref, f32[1024,768]{1,0:T(8,128)} %get-tuple-element.36.shared_ref, bf16[1152,768]{1,0:T(8,128)(2,1)} %bitcast.115, ...), custom_call_target="tpu_custom_call" | custom-call | flops 7247757312 | bytes 11403264 | tf_op jit(solution)/shard_map/pallas_call | solution.py:342
  526.1 63.9 %reduce-scatter.9.cloned.1.call-done = bf16[1,4608,128]{2,1,0:T(8,128)(2,1)} async-done(((bf16[8,4608,128]{2,1,0:T(8,128)(2,1)}), bf16[1,4608,128]{2,1,0:T(8,128)(2,1)}) %reduce-scatter.9.cloned.1.call-update) | async-done | bytes 1179664 | tf_op jit(solution)/shard_map/reduce_scatter | solution.py:705
  593.1 77.3 %reduce-scatter.11.cloned.1.call-done = bf16[1,4608,128]{2,1,0:T(8,128)(2,1)} async-done(((bf16[8,4608,128]{2,1,0:T(8,128)(2,1)}), bf16[1,4608,128]{2,1,0:T(8,128)(2,1)}) %reduce-scatter.11.cloned.1.call-update) | async-done | bytes 1179664 | tf_op jit(solution)/shard_map/reduce_scatter | solution.py:705
  678.1 72.2 %all-reduce.4.cloned.1.call-done = (bf16[2496,128]{1,0:T(8,128)(2,1)}, bf16[4608,128]{1,0:T(8,128)(2,1)}) async-done(((bf16[2496,128]{1,0:T(8,128)(2,1)}, bf16[4608,128]{1,0:T(8,128)(2,1)}), (bf16[2496,128]{1,0:T(8,128)(2,1)}, bf16[4608,128]{1,0:T(8,128)(2,1)})) %all-reduce.4.cloned.1.call-update) | async-done | bytes 1818640 | tf_op jit(solution)/shard_map/psum | solution.py:711
  (108 shorter events, 71.1 us)
Async XLA Ops:
  7.2 41.8 %all-gather.6.cloned.1.call-start = ((), (), s32[]{:S(2)}) async-start(), calls=%async_computation.10 | async-start | bytes 3981312 | tf_op jit(solution)/shard_map/all_gather | solution.py:636
  7.9 74.1 %all-gather.8.cloned.1.call-start = ((), (), s32[]{:S(2)}) async-start(), calls=%async_computation.11 | async-start | bytes 1327104 | tf_op jit(solution)/shard_map/all_gather | solution.py:637
  8.7 247.9 %all-gather.12.cloned.1.call-start = ((), (), s32[]{:S(2)}) async-start(), calls=%async_computation.13 | async-start | bytes 3538944 | tf_op jit(solution)/shard_map/all_gather | solution.py:639
  23.6 7.0 copy-start.7
  23.6 7.3 copy-start.8
  23.6 85.8 %all-to-all-start.1 = ((bf16[4,576,768]{2,1,0:T(8,128)(2,1)}), bf16[4,576,768]{2,1,0:T(8,128)(2,1)}, u32[]{:S(2)}, u32[]{:S(2)}) async-start(bf16[4,576,768]{2,1,0:T(8,128)(2,1)} %bitcast.102), calls=%async_computation.1 | async-start | bytes 7077888 | tf_op jit(solution)/shard_map/all_to_all | solution.py:664
  30.1 226.5 %all-gather.10.cloned.1.call-start = ((), (), s32[]{:S(2)}) async-start(), calls=%async_computation.12 | async-start | bytes 7077888 | tf_op jit(solution)/shard_map/all_gather | solution.py:638
  109.4 44.2 %all-to-all-start = ((bf16[4,288,768]{2,1,0:T(8,128)(2,1)}), bf16[4,288,768]{2,1,0:T(8,128)(2,1)S(1)}, u32[]{:S(2)}, u32[]{:S(2)}) async-start(bf16[4,288,768]{2,1,0:T(8,128)(2,1)} %bitcast.121), calls=%async_computation | async-start | bytes 3538944 | tf_op jit(solution)/shard_map/all_to_all | solution.py:664
  153.6 1.3 copy-start.5
  154.9 47.4 %all-to-all-start.2 = ((bf16[4,288,768]{2,1,0:T(8,128)(2,1)}), bf16[4,288,768]{2,1,0:T(8,128)(2,1)}, u32[]{:S(2)}, u32[]{:S(2)}) async-start(bf16[4,288,768]{2,1,0:T(8,128)(2,1)} %bitcast.122), calls=%async_computation.2 | async-start | bytes 3538944 | tf_op jit(solution)/shard_map/all_to_all | solution.py:664
  202.3 47.8 %all-to-all-start.4 = ((bf16[4,288,768]{2,1,0:T(8,128)(2,1)}), bf16[4,288,768]{2,1,0:T(8,128)(2,1)S(1)}, u32[]{:S(2)}, u32[]{:S(2)}) async-start(bf16[4,288,768]{2,1,0:T(8,128)(2,1)} %bitcast.120), calls=%async_computation.4 | async-start | bytes 3538944 | tf_op jit(solution)/shard_map/all_to_all | solution.py:664
  251.2 44.7 %all-to-all-start.5 = ((bf16[4,288,768]{2,1,0:T(8,128)(2,1)}), bf16[4,288,768]{2,1,0:T(8,128)(2,1)S(1)}, u32[]{:S(2)}, u32[]{:S(2)}) async-start(bf16[4,288,768]{2,1,0:T(8,128)(2,1)} %bitcast.118), calls=%async_computation.5 | async-start | bytes 3538944 | tf_op jit(solution)/shard_map/all_to_all | solution.py:664
  256.3 173.1 %reduce-scatter.5.cloned.1.call-start = ((), (), s32[]{:S(2)}) async-start(), calls=%async_computation.14 | async-start | bytes 5750784 | tf_op jit(solution)/shard_map/reduce_scatter | solution.py:705
  295.9 1.2 copy-start.4
  297.2 11.4 %copy-start.9 = (bf16[768,768]{1,0:T(8,128)(2,1)S(1)}, bf16[768,768]{1,0:T(8,128)(2,1)}, u32[]{:S(2)}) copy-start(bf16[768,768]{1,0:T(8,128)(2,1)} %all-gather.8.cloned.1.call-done.weight_ref) | copy-start | bytes 3538948
  372.7 137.0 %reduce-scatter.7.cloned.1.call-start = ((), (), s32[]{:S(2)}) async-start(), calls=%async_computation.15 | async-start | bytes 10616832 | tf_op jit(solution)/shard_map/reduce_scatter | solution.py:705
  373.3 216.7 %reduce-scatter.9.cloned.1.call-start = ((), (), s32[]{:S(2)}) async-start(), calls=%async_computation.16 | async-start | bytes 10616832 | tf_op jit(solution)/shard_map/reduce_scatter | solution.py:705
  374.0 296.3 %reduce-scatter.11.cloned.1.call-start = ((), (), s32[]{:S(2)}) async-start(), calls=%async_computation.17 | async-start | bytes 10616832 | tf_op jit(solution)/shard_map/reduce_scatter | solution.py:705
  374.1 1.5 copy-start.1
  374.1 2.0 copy-start.2
  378.2 132.5 %all-to-all-start.3 = ((bf16[4,576,768]{2,1,0:T(8,128)(2,1)}), bf16[4,576,768]{2,1,0:T(8,128)(2,1)S(1)}, u32[]{:S(2)}, u32[]{:S(2)}) async-start(bf16[4,576,768]{2,1,0:T(8,128)(2,1)} %pad_maximum_fusion), calls=%async_computation.3 | async-start | bytes 7077888 | tf_op jit(solution)/shard_map/all_to_all | solution.py:735
  382.7 127.0 %copy-start.6 = (f32[1024,2]{0,1:T(2,128)S(1)}, f32[1024,2]{0,1:T(2,128)}, u32[]{:S(2)}) copy-start(f32[1024,2]{0,1:T(2,128)} %param.15) | copy-start | bytes 24580
  382.7 367.6 %all-reduce.4.cloned.1.call-start = ((), (), s32[]{:S(2)}) async-start(), calls=%async_computation.18 | async-start | bytes 3637248 | tf_op jit(solution)/shard_map/psum | solution.py:711
  750.3 3.3 copy-start
  (5 other events, 5.5 us)
Sparse Core Ops, SparseCore 0:
  9.9 36.6 all-gather.5
  48.4 23.9 all-gather.7
  74.3 32.1 all-gather.11
  108.2 45.3 all-gather.9
  372.8 56.6 reduce-scatter.4
  432.8 76.8 reduce-scatter.6
  513.1 76.8 reduce-scatter.8
  593.5 76.8 reduce-scatter.10
  672.8 77.4 all-reduce.3

commit v2 on v1

--- a/solution.py
+++ b/solution.py
@@ -17,7 +17,7 @@
 F32 = jnp.float32
 
 
-def call(kernel, grid, in_specs, out_specs, out_shape, scratch=(), flops=0, moved=0, trans=0):
+def call(kernel, grid, in_specs, out_specs, out_shape, scratch=(), flops=0, moved=0, trans=0, aliases=None):
     return pl.pallas_call(
         kernel,
         grid_spec=pltpu.PrefetchScalarGridSpec(
@@ -28,6 +28,7 @@
             scratch_shapes=list(scratch),
         ),
         out_shape=out_shape,
+        input_output_aliases=aliases or {},
         compiler_params=pltpu.CompilerParams(
             dimension_semantics=("arbitrary",) * len(grid), vmem_limit_bytes=VMEM_BYTES
         ),
@@ -219,6 +220,10 @@
     )(queries, keys, values, mixed, grad_mixed, lse, cosine, sine)
 
 
+def square(width, part):
+    return pl.BlockSpec((width, width), lambda i: (0, part), pipeline_mode=pl.Buffered(1))
+
+
 def norm_one_kernel(x_ref, gain_ref, out_ref):
     x = x_ref[...].astype(F32)
     scale = lax.rsqrt(jnp.mean(x * x, axis=1, keepdims=True) + EPSILON)
@@ -247,7 +252,7 @@
     block = min(256, rows)
     blocked = pl.BlockSpec((block, width), lambda i: (i, 0))
     return call(
-        norm_two_kernel, (rows // block,), [blocked, blocked, whole((width, width)), whole((1, width))],
+        norm_two_kernel, (rows // block,), [blocked, blocked, square(width, 3), whole((1, width))],
         [blocked, blocked], [shape_of((rows, width), F32), shape_of((rows, width), BF16)],
         flops=2 * rows * width * width, moved=10 * rows * width,
     )(mixed, tokens, weight, gain)
@@ -327,8 +332,8 @@
     out_ref[...] = (live_ref[...] * total).astype(BF16)
 
 
-def slot_numbers(block, slots, index):
-    return lax.broadcasted_iota(jnp.int32, (block, slots), 1) + index * slots
+def slot_numbers(block, slots, part):
+    return lax.broadcasted_iota(jnp.int32, (block, slots), 1) + part * slots
 
 
 def combine(dest, gates, live, first_sum, shared_out, returned):
@@ -348,16 +353,33 @@
     )(dest, gates, live, first_sum, shared_out, *returned)
 
 
-def norm_two_back_kernel(parts, dest_ref, live_ref, cot_ref, sum_ref, shared_ref, gain_ref, *rest):
-    y_refs = rest[:parts]
-    first_ref, attn_ref, gain_grad_ref = rest[parts:]
+def gathered(dest_ref, y_ref, part):
     block, top = dest_ref.shape
-    grad_normed = shared_ref[...]
     dest = dest_ref[...]
-    for index, y_ref in enumerate(y_refs):
-        slot = slot_numbers(block, y_ref.shape[0], index)
-        hit = functools.reduce(jnp.logical_or, [slot == dest[:, k : k + 1] for k in range(top)])
-        grad_normed = grad_normed + dot_nn(jnp.where(hit, 1.0, 0.0).astype(BF16), y_ref[...])
+    slot = slot_numbers(block, y_ref.shape[0], part)
+    hit = functools.reduce(jnp.logical_or, [slot == dest[:, k : k + 1] for k in range(top)])
+    return dot_nn(jnp.where(hit, 1.0, 0.0).astype(BF16), y_ref[...])
+
+
+def add_part_kernel(part, dest_ref, base_ref, y_ref, out_ref):
+    out_ref[...] = base_ref[...] + gathered(dest_ref, y_ref, part)
+
+
+def add_part(dest, base, rows_of, part):
+    rows, width = base.shape
+    block = min(256, rows)
+    blocked = pl.BlockSpec((block, width), lambda i: (i, 0))
+    return call(
+        functools.partial(add_part_kernel, part), (rows // block,),
+        [pl.BlockSpec((block, dest.shape[1]), lambda i: (i, 0)), blocked, whole(rows_of.shape)],
+        blocked, shape_of((rows, width), F32),
+        flops=2 * rows * rows_of.shape[0] * width, moved=8 * rows * width,
+    )(dest, base, rows_of)
+
+
+def norm_two_back_kernel(part, dest_ref, live_ref, cot_ref, sum_ref, base_ref, gain_ref, weight_ref, y_ref,
+                         first_ref, attn_ref, mixed_ref, gain_grad_ref):
+    grad_normed = base_ref[...] + gathered(dest_ref, y_ref, part)
     first_sum = sum_ref[...]
     scale = lax.rsqrt(jnp.mean(first_sum * first_sum, axis=1, keepdims=True) + EPSILON)
     weighted = grad_normed * gain_ref[...]
@@ -366,7 +388,9 @@
         cot_ref[...].astype(F32) * live_ref[...] + scale * weighted - first_sum * (scale * scale * scale * inner)
     )
     first_ref[...] = grad_first
-    attn_ref[...] = grad_first.astype(BF16)
+    grad_attn = grad_first.astype(BF16)
+    attn_ref[...] = grad_attn
+    mixed_ref[...] = dot_nt(grad_attn, weight_ref[...]).astype(BF16)
 
     @pl.when(pl.program_id(0) == 0)
     def _():
@@ -375,25 +399,23 @@
     gain_grad_ref[...] += jnp.sum(grad_normed * first_sum * scale, axis=0, keepdims=True)
 
 
-def norm_two_back(dest, live, cotangent, first_sum, grad_shared, gain, returned):
+def norm_two_back(dest, live, cotangent, first_sum, base, gain, weights, rows_of, part):
     rows, width = first_sum.shape
     top = dest.shape[1]
     block = min(256, rows)
-    parts = len(returned)
     blocked = pl.BlockSpec((block, width), lambda i: (i, 0))
-    slots = sum(y.shape[0] for y in returned)
-    return call(
-        functools.partial(norm_two_back_kernel, parts), (rows // block,),
+    return call(
+        functools.partial(norm_two_back_kernel, part), (rows // block,),
         [pl.BlockSpec((block, top), lambda i: (i, 0)), pl.BlockSpec((block, 1), lambda i: (i, 0)), blocked, blocked,
-         blocked, whole((1, width))]
-        + [whole(y.shape) for y in returned],
-        [blocked, blocked, pl.BlockSpec((1, width), lambda i: (0, 0))],
-        [shape_of((rows, width), F32), shape_of((rows, width), BF16), shape_of((1, width), F32)],
-        flops=2 * rows * slots * width, moved=16 * rows * width + 2 * slots * width,
-    )(dest, live, cotangent, first_sum, grad_shared, gain, *returned)
-
-
-def norm_one_back_kernel(gq_ref, gk_ref, gv_ref, wq_ref, wk_ref, wv_ref, tokens_ref, first_ref, gain_ref, out_ref, gain_grad_ref):
+         blocked, whole((1, width)), square(width, 3), whole(rows_of.shape)],
+        [blocked, blocked, blocked, pl.BlockSpec((1, width), lambda i: (0, 0))],
+        [shape_of((rows, width), F32), shape_of((rows, width), BF16), shape_of((rows, width), BF16),
+         shape_of((1, width), F32)],
+        flops=2 * rows * (rows_of.shape[0] + width) * width, moved=18 * rows * width,
+    )(dest, live, cotangent, first_sum, base, gain, weights, rows_of)
+
+
+def norm_one_back_kernel(gq_ref, gk_ref, gv_ref, wq_ref, wk_ref, wv_ref, tokens_ref, first_ref, gain_ref, out_ref):
     grad_normed = (
         dot_nt(gq_ref[...], wq_ref[...]) + dot_nt(gk_ref[...], wk_ref[...]) + dot_nt(gv_ref[...], wv_ref[...])
     )
@@ -403,32 +425,22 @@
     inner = jnp.mean(source * weighted, axis=1, keepdims=True)
     out_ref[...] = first_ref[...] + scale * weighted - source * (scale * scale * scale * inner)
 
-    @pl.when(pl.program_id(0) == 0)
-    def _():
-        gain_grad_ref[...] = jnp.zeros_like(gain_grad_ref)
-
-    gain_grad_ref[...] += jnp.sum(grad_normed * source * scale, axis=0, keepdims=True)
-
 
 def norm_one_back(grads, w_qkv, tokens, grad_first, gain):
     rows, width = tokens.shape
     block = min(256, rows)
     blocked = pl.BlockSpec((block, width), lambda i: (i, 0))
 
-    def weight(part):
-        return pl.BlockSpec((width, width), lambda i: (0, part), pipeline_mode=pl.Buffered(1))
-
     return call(
         norm_one_back_kernel, (rows // block,),
-        [blocked] * 3 + [weight(0), weight(1), weight(2), blocked, blocked, whole((1, width))],
-        [blocked, pl.BlockSpec((1, width), lambda i: (0, 0))],
-        [shape_of((rows, width), F32), shape_of((1, width), F32)],
+        [blocked] * 3 + [square(width, 0), square(width, 1), square(width, 2), blocked, blocked, whole((1, width))],
+        blocked, shape_of((rows, width), F32),
         flops=6 * rows * width * width, moved=22 * rows * width,
     )(*grads, w_qkv, w_qkv, w_qkv, tokens, grad_first, gain)
 
 
 def copies_of(layout, block, width, step, stage_g, stage_u, stage_d, slot, packed_ref, sems):
-    by_rows, owners, hidden = layout
+    by_rows, owners, hidden, base = layout
     panels = block // LANES
     rows_down = hidden // owners
     out = []
@@ -443,7 +455,7 @@
                 panel = half * (hidden // LANES) + step * panels + p
                 add(
                     stage.at[slot, :, :, pl.ds(p * LANES, LANES)],
-                    packed_ref.at[:, pl.ds(pl.multiple_of(panel * rows, 8), rows), :],
+                    packed_ref.at[:, pl.ds(pl.multiple_of(base + panel * rows, 8), rows), :],
                 )
         start = 2 * hidden // LANES * rows
     else:
@@ -454,7 +466,7 @@
                 owner, panel = column // columns, (column % columns) // LANES
                 add(
                     stage.at[slot, :, pl.ds(p * LANES, LANES)],
-                    packed_ref.at[owner, pl.ds(pl.multiple_of(panel * width, 8), width), :],
+                    packed_ref.at[owner, pl.ds(pl.multiple_of(base + panel * width, 8), width), :],
                 )
         start = columns // LANES * width
     for q in range(block // rows_down):
@@ -462,7 +474,7 @@
         for c in range(width // LANES):
             add(
                 stage_d.at[slot, pl.ds(q * rows_down, rows_down), pl.ds(c * LANES, LANES)],
-                packed_ref.at[owner, pl.ds(start + c * rows_down, rows_down), :],
+                packed_ref.at[owner, pl.ds(base + start + c * rows_down, rows_down), :],
             )
     return out
 
@@ -471,8 +483,8 @@
     return 3 * width * hidden // owners // LANES
 
 
-def ffn_kernel(out_type, layout, block, x_ref, gy_ref, wg_ref, wu_ref, wd_ref, y_ref, gx_ref, packed_ref, xt, y_acc, gx_acc,
-               stage_g, stage_u, stage_d, sems):
+def ffn_kernel(out_type, layout, block, x_ref, gy_ref, wg_ref, wu_ref, wd_ref, *rest):
+    y_ref, gx_ref, packed_ref, xt, y_acc, gx_acc, stage_g, stage_u, stage_d, sems = rest[-10:]
     step = pl.program_id(0)
     steps = layout[2] // block
     width = x_ref.shape[1]
@@ -491,7 +503,14 @@
             copy.wait()
 
     x, gy = x_ref[...], gy_ref[...].reshape(x_ref.shape)
-    wg, wu, wd = wg_ref[...], wu_ref[...], wd_ref[...]
+    if layout[0]:
+        wg, wu = wg_ref[...].reshape(width, block), wu_ref[...].reshape(width, block)
+        rows = wd_ref.shape[1] // (width // block)
+        wd = jnp.concatenate(
+            [wd_ref[:, pl.ds(c * rows, rows), :].reshape(block, block) for c in range(width // block)], axis=1
+        )
+    else:
+        wg, wu, wd = wg_ref[...], wu_ref[...], wd_ref[...]
     gate, up = dot_nn(x, wg), dot_nn(x, wu)
     grad_hidden = dot_nt(gy, wd)
     sigmoid = jax.nn.sigmoid(gate)
@@ -517,17 +536,21 @@
                     copy.wait()
 
 
-def ffn_both(x, gy, w_gu, w_down, expert, owners, out_type):
+BLOCK = 256
+
+
+def ffn_both(x, gy, w_gu, w_down, hidden, expert, owners, out_type, parts=1, pack=None):
     rows, width = x.shape
-    hidden = w_down.shape[-2]
-    block = min(256, hidden)
+    block = BLOCK
     steps = hidden // block
     by_rows = expert is None
     if by_rows:
-        gate = pl.BlockSpec((width, block), lambda f: (0, f))
-        up = pl.BlockSpec((width, block), lambda f: (0, steps + f))
-        down = pl.BlockSpec((block, width), lambda f: (f, 0))
-        stage = (2, owners, width // owners, block)
+        own, own_down, panels = width // owners, hidden // owners, width // block
+        ahead = 2 * steps * own // (panels * own_down)
+        gate = pl.BlockSpec((owners, own, block), lambda f: (0, f, 0))
+        up = pl.BlockSpec((owners, own, block), lambda f: (0, steps + f, 0))
+        down = pl.BlockSpec((block // own_down, panels * own_down, block), lambda f: (f, ahead, 0))
+        stage = (2, owners, own, block)
     else:
         gate = pl.BlockSpec((None, width, block), lambda f: (expert, 0, f))
         up = pl.BlockSpec((None, width, block), lambda f: (expert, 0, steps + f))
@@ -540,19 +563,27 @@
             (gy.shape[0], rows // gy.shape[0], width), lambda f: (0, expert, 0), pipeline_mode=pl.Buffered(1)
         )
     out_rows = whole((rows, width))
-    layout = (by_rows, owners, hidden)
+    count = packed_rows(width, hidden, owners)
+    layout = (by_rows, owners, hidden, (expert or 0) * count)
+    held = [] if pack is None else [pack]
     copies = 2 * (block // LANES) + block // (hidden // owners) * (width // LANES)
     return call(
         functools.partial(ffn_kernel, out_type, layout, block), (steps,),
-        [whole((rows, width)), grads, gate, up, down],
+        [whole((rows, width)), grads, gate, up, down] + [pl.BlockSpec(memory_space=pl.ANY)] * len(held),
         [out_rows, out_rows, pl.BlockSpec(memory_space=pl.ANY)],
         [shape_of((rows, width), out_type), shape_of((rows, width), out_type),
-         shape_of((owners, packed_rows(width, hidden, owners), LANES), BF16)],
+         shape_of((owners, parts * count, LANES), BF16)],
         scratch=[pltpu.VMEM((width, rows), BF16), pltpu.VMEM((rows, width), F32), pltpu.VMEM((rows, width), F32),
                  pltpu.VMEM(stage, BF16), pltpu.VMEM(stage, BF16), pltpu.VMEM((2, block, width), BF16),
                  pltpu.SemaphoreType.DMA((2, copies))],
         flops=18 * rows * width * hidden, moved=12 * width * hidden + 16 * rows * width, trans=rows * hidden,
-    )(x, gy, w_gu, w_gu, w_down)
+        aliases={5: 2} if held else None,
+    )(x, gy, w_gu, w_gu, w_down, *held)
+
+
+def to_panels(array):
+    rows, columns = array.shape
+    return jnp.transpose(array.reshape(rows, columns // BLOCK, BLOCK), (1, 0, 2)).reshape(-1, BLOCK)
 
 
 def panels_to(rows_array, rows, panels):
@@ -580,29 +611,83 @@
             for p in range(panels):
                 out_ref[:, pl.ds(p * rows, rows), :] = product[:, p * LANES : (p + 1) * LANES].reshape(owners, rows, LANES)
 
+    @pl.when(step >= 4 * per)
+    def _():
+        out_ref[...] = jnp.zeros_like(out_ref)
+
     @pl.when(step == 4 * per)
     def _():
-        out_ref[...] = jnp.zeros_like(out_ref)
         out_ref[:, pl.ds(0, gains_ref.shape[1]), :] = gains_ref[...]
 
 
-def attention_weights(normed, mixed, grads, grad_attn, gains, owners):
+def attention_weights(normed, mixed, grads, grad_attn, gains, owners, pieces):
     tokens, width = normed.shape
     rows = width // owners
-    block = 256
+    block = BLOCK
     panels, per = block // LANES, width // block
+    steps = 4 * per + 1
+    while steps * panels * rows % (16 * pieces):
+        steps += 1
 
     def columns(index):
         return pl.BlockSpec((tokens, block), lambda i: (0, jnp.clip(i - index * per, 0, per - 1)))
 
     return call(
-        functools.partial(attention_weights_kernel, per), (4 * per + 1,),
+        functools.partial(attention_weights_kernel, per), (steps,),
         [whole((tokens, width)), whole((tokens, width))] + [columns(index) for index in range(4)] + [whole(gains.shape)],
         pl.BlockSpec((owners, panels * rows, LANES), lambda i: (0, i, 0)),
-        shape_of((owners, (4 * per + 1) * panels * rows, LANES), BF16),
+        shape_of((owners, steps * panels * rows, LANES), BF16),
         scratch=[pltpu.VMEM((width, tokens), BF16)],
         flops=8 * tokens * width * width, moved=16 * tokens * width,
     )(normed, mixed, *grads, grad_attn, gains)
+
+
+def sum_over_kernel(axis, count, x_ref, out_ref, landed, own, send_sem, recv_sem):
+    me = lax.axis_index(axis)
+    peers = [lax.rem(me + step, count) for step in range(1, count)]
+    barrier = pltpu.get_barrier_semaphore()
+    for peer in peers:
+        pl.semaphore_signal(barrier, inc=1, device_id={axis: peer}, device_id_type=pl.DeviceIdType.MESH)
+    pl.semaphore_wait(barrier, count - 1)
+
+    def send(phase, step, source, target):
+        copy = pltpu.make_async_remote_copy(
+            src_ref=source, dst_ref=target, send_sem=send_sem.at[phase, step], recv_sem=recv_sem.at[phase, step],
+            device_id={axis: peers[step]}, device_id_type=pl.DeviceIdType.MESH,
+        )
+        copy.start()
+        return copy
+
+    first = [send(0, step, x_ref.at[peers[step]], landed.at[step]) for step in range(count - 1)]
+    total = x_ref[me].astype(F32)
+    for step, copy in enumerate(first):
+        copy.wait()
+        total = total + landed[step].astype(F32)
+    own[...] = total.astype(own.dtype)
+    second = [send(1, step, own, out_ref.at[me]) for step in range(count - 1)]
+    out_ref[me] = own[...]
+    for copy in second:
+        copy.wait()
+
+
+def sum_over(x, axis, count, collective_id):
+    rows = x.shape[0]
+    shape = (count, rows // count, LANES)
+    vmem = pl.BlockSpec(memory_space=pltpu.VMEM)
+    return pl.pallas_call(
+        functools.partial(sum_over_kernel, axis, count),
+        out_shape=shape_of(shape, x.dtype),
+        in_specs=[vmem],
+        out_specs=vmem,
+        scratch_shapes=[
+            pltpu.VMEM((count - 1,) + shape[1:], x.dtype),
+            pltpu.VMEM(shape[1:], x.dtype),
+            pltpu.SemaphoreType.DMA((2, count - 1)),
+            pltpu.SemaphoreType.DMA((2, count - 1)),
+        ],
+        compiler_params=pltpu.CompilerParams(collective_id=collective_id, has_side_effects=True),
+        cost_estimate=pl.CostEstimate(flops=rows * LANES * count, bytes_accessed=40 * rows * LANES, transcendentals=0),
+    )(x.reshape(shape)).reshape(rows, LANES)
 
 
 GROUP = ("dp", "shard")
@@ -631,12 +716,13 @@
     top = routes.shape[1]
     capacity = tok_count * top * 9 // (8 * experts)
     head_dim = width // HEADS
+    hidden = w_expert_down.shape[1]
 
     gains = lax.all_gather(norm_gains, GROUP, axis=1, tiled=True).astype(F32)
-    qkv_weight = lax.all_gather(w_qkv, GROUP, axis=0, tiled=True)
-    out_weight = lax.all_gather(w_out, GROUP, axis=0, tiled=True)
-    sgu_weight = lax.all_gather(w_shared_gu, GROUP, axis=0, tiled=True)
-    sdown_weight = lax.all_gather(w_shared_down, GROUP, axis=0, tiled=True)
+    attention_weight = lax.all_gather(jnp.concatenate([w_qkv, w_out], axis=1), GROUP, axis=0, tiled=True)
+    shared_weight = lax.all_gather(
+        jnp.concatenate([to_panels(w_shared_gu), to_panels(w_shared_down)], axis=0)[None], GROUP, axis=0, tiled=True
+    )
     gain_one, gain_two = gains[0:1], gains[1:2]
 
     live_bool = lax.iota(jnp.int32, tok_count) % length < jnp.repeat(lengths, length)
@@ -644,6 +730,7 @@
     live_row = live_bool.astype(jnp.int32)[None, :]
 
     group = lax.axis_size("dp") * lax.axis_size("shard")
+    shared_hidden = w_shared_down.shape[0] * group
 
     dest_t = slots_of(routes.T, live_row, experts, capacity)
     dest = dest_t.T
@@ -670,33 +757,36 @@
 
     cosine, sine = rotary_tables(length, head_dim)
     normed_one = norm_one(tokens, gain_one)
-    queries, keys, values, mixed, lse = attend_forward(normed_one, qkv_weight, cosine, sine, length, head_dim)
-    first_sum, normed_two = norm_two(mixed, tokens, out_weight, gain_two)
+    queries, keys, values, mixed, lse = attend_forward(normed_one, attention_weight, cosine, sine, length, head_dim)
+    first_sum, normed_two = norm_two(mixed, tokens, attention_weight, gain_two)
 
     received = []
     for j in range(local_experts):
         rows = dispatch(placed_t, gates_t, normed_two, owners, capacity, False, j * owners)
         received.append(exchange(rows))
     shared_out, grad_shared, shared_pack = ffn_both(
-        normed_two, grad_b, sgu_weight, sdown_weight, None, group, F32
-    )
-    back_rows, out_rows, expert_packs = [], [], []
+        normed_two, grad_b, shared_weight, shared_weight, shared_hidden, None, group, F32
+    )
+    back_rows, out_rows, pack = [], [], None
     for j in range(local_experts):
-        y, gx, pack = ffn_both(received[j], received_grad, w_expert_gu, w_expert_down, j, group, BF16)
+        y, gx, pack = ffn_both(
+            received[j], received_grad, w_expert_gu, w_expert_down, hidden, j, group, BF16, local_experts, pack
+        )
         back_rows.append(exchange(gx))
         out_rows.append(y)
-        expert_packs.append(pack)
-    grad_first, grad_attn, grad_gain_two = norm_two_back(
-        placed, live, cotangent, first_sum, grad_shared, gain_two, back_rows
-    )
-
-    grad_mixed = dot_nt(grad_attn, out_weight).astype(BF16)
+    base = grad_shared
+    for j, rows in enumerate(back_rows[:-1]):
+        base = add_part(placed, base, rows, j)
+    grad_first, grad_attn, grad_mixed, grad_gain_two = norm_two_back(
+        placed, live, cotangent, first_sum, base, gain_two, attention_weight, back_rows[-1], local_experts - 1
+    )
+
     grads = attend_backward(queries, keys, values, mixed, grad_mixed, lse, cosine, sine, length, head_dim)
-    input_grad, grad_gain_one = norm_one_back(grads, qkv_weight, tokens, grad_first, gain_one)
+    input_grad = norm_one_back(grads, attention_weight, tokens, grad_first, gain_one)
     own = width // group
-    grad_gains = jnp.concatenate([grad_gain_one, grad_gain_two], axis=0).reshape(2, group, own).transpose(1, 0, 2)
-    grad_gains = jnp.pad(grad_gains, ((0, 0), (0, 14), (0, LANES - own))).astype(BF16)
-    attention_pack = attention_weights(normed_one, mixed, grads, grad_attn, grad_gains, group)
+    grad_gains = grad_gain_two.reshape(group, 1, own)
+    grad_gains = jnp.pad(grad_gains, ((0, 0), (0, 15), (0, LANES - own))).astype(BF16)
+    attention_pack = attention_weights(normed_one, mixed, grads, grad_attn, grad_gains, group, owners)
 
     returned = exchange_parts(out_rows, owners, "expert")
     layer_out = combine(placed, route_gates, live, first_sum, shared_out, returned)
@@ -705,21 +795,21 @@
         return lax.psum_scatter(pack, GROUP, scatter_dimension=0, tiled=True)[0]
 
     shared_share = spread(shared_pack)
-    expert_shares = [spread(pack) for pack in expert_packs]
+    expert_shares = jnp.split(spread(pack), local_experts)
     attention_share = spread(attention_pack)
-    shared_share = lax.psum(shared_share, "expert").astype(F32)
-    attention_share = lax.psum(attention_share, "expert").astype(F32)
-    hidden = w_expert_down.shape[1]
-    shared_hidden = sdown_weight.shape[0]
+    shared_share = sum_over(shared_share, "expert", owners, 1).astype(F32)
+    attention_share = sum_over(attention_share, "expert", owners, 2).astype(F32)
     gu_panels, d_panels = 2 * shared_hidden // LANES, width // LANES
     qkv_rows, out_rows_count = 3 * d_panels * own, 4 * d_panels * own
     columns = 2 * hidden // group
     gu_rows = columns // LANES * width
+    qkv_grad = panels_to(attention_share[:qkv_rows], own, 3 * d_panels)
+    grad_gain_one = jnp.sum(w_qkv.astype(F32) * qkv_grad, axis=1) / norm_gains[0].astype(F32)
     return (
         layer_out,
         input_grad,
-        attention_share[out_rows_count : out_rows_count + 2, :own],
-        panels_to(attention_share[:qkv_rows], own, 3 * d_panels),
+        jnp.stack([grad_gain_one, attention_share[out_rows_count, :own]]),
+        qkv_grad,
         panels_to(attention_share[qkv_rows:out_rows_count], own, d_panels),
         panels_to(shared_share[: gu_panels * own], own, gu_panels),
         panels_to(shared_share[gu_panels * own :], shared_hidden // group, d_panels),

time: 776 us -> 658 us (0.85)
  waiting for transfers between devices: 395 us -> 190 us
  Pallas kernels: 270 us -> 360 us
    reduce_scatter x4 -> x3, waiting for transfers between devices: 268 us -> 62.6 us  [spread(): return lax.psum_scatter(pack, GROUP, scatter_dimension=0, tiled=True)[0]]
    pallas_call x4 -> x7, Pallas kernels: 40.8 us -> 130 us  [the longest x2 82.6 us: sum_over(): pl.pallas_call(functools.partial(sum_over_kernel, axis, count), out_shape...]
    all_to_all x1, waiting for transfers between devices: 0.01 us -> 75.9 us  [exchange_parts(): back = lax.all_to_all(joined, axis, split_axis=0, concat_axis=0, tiled=True)]
    psum x1 -> x0, waiting for transfers between devices: 72.2 us -> none  [local(): attention_share = lax.psum(attention_share, 'expert').astype(F32)]
  transfers between devices with their start and end apart: 15 -> 11, of which waited for: 8 -> 5; matrix products, arithmetic and copies ran while one was open for 3% -> 4% of each run, Pallas kernels for 26% -> 46%
where the time goes in v2:
time: 658 us; the launch traced here: 649 us
  Pallas kernels  360 us (55%)
  waiting for transfers between devices  190 us (29%)
  starting transfers between devices  31.1 us (5%)
  local copies, waits for them, and re-layouts  26.1 us (4%)
  other arithmetic  18.4 us (3%)
  between operations  15.4 us (2%)
  blocking collectives  8.93 us (1%)
    pallas_call x3, Pallas kernels, ffn_both(): call(functools.partial(ffn_kernel, out_type, layout, block), (steps,), [w...  124 us
    pallas_call x2, Pallas kernels, sum_over(): pl.pallas_call(functools.partial(sum_over_kernel, axis, count), out_shape...  82.6 us
    all_to_all x1, waiting for transfers between devices, exchange_parts(): back = lax.all_to_all(joined, axis, split_axis=0, concat_axis=0, tiled=True)  75.9 us
    reduce_scatter x3, waiting for transfers between devices, spread(): return lax.psum_scatter(pack, GROUP, scatter_dimension=0, tiled=True)[0]  62.6 us
    all_to_all x5, waiting for transfers between devices, exchange(): lax.all_to_all(rows.reshape(owners, count, width), 'expert', split_axis=0...  47.2 us
    pallas_call x1, Pallas kernels, attend_backward(): call(functools.partial(attend_backward_kernel, head_dim, block), (seqs, p...  34.3 us
    pallas_call x1, Pallas kernels, attend_forward(): call(functools.partial(attend_forward_kernel, head_dim, block), (seqs, pa...  33.1 us
    all_to_all x5, starting transfers between devices, exchange(): lax.all_to_all(rows.reshape(owners, count, width), 'expert', split_axis=0...  25.2 us
  transfers between devices with their start and end apart: 11, of which 5 were waited for; matrix products, arithmetic and copies ran while one was open for 4% of the time, Pallas kernels for 46%

profile of v2, /device:TPU:0, one launch (start us, length us, event | category | flops | bytes accessed | tf_op | source)
XLA Modules:
  0.0 649.1 jit_solution(6135127817221000397)
XLA Ops:
  16.0 8.6 %shard_map.196 = bf16[2304,768]{1,0:T(8,128)(2,1)} custom-call(s32[2,1024]{1,0:T(2,128)} %shard_map.190.dest_ref, f32[2,1024]{1,0:T(2,128)} %bitcast.150, bf16[1024,768]{1,0:T(8,128)(2,1)} %broadcast_select_fusion.gy_ref.x_ref), custom_call_target="tpu_custom_call" | custom-call | flops 3623878656 | bytes 5111808 | tf_op jit(solution)/shard_map/pallas_call | solution.py:311
  24.5 6.5 all-to-all-start.1
  34.0 8.9 %all-gather.1 = bf16[8,96,2]{1,2,0:T(2,128)(2,1)S(1)} all-gather(bf16[1,96,2]{1,2,0:T(2,128)(2,1)S(1)} %bitcast.153), channel_id=1, replica_groups=mesh['dp'=2,'expert'=4,'shard'=4] {'dp','shard'}, dimensions={0}, use_global_device_ids=true | all-gather | bytes 3456 | tf_op jit(solution)/shard_map/all_gather | solution.py:721
  52.0 33.1 %shard_map.192 = (bf16[1024,768]{1,0:T(8,128)(2,1)}, bf16[1024,768]{1,0:T(8,128)(2,1)}, bf16[1024,768]{1,0:T(8,128)(2,1)}, bf16[1024,768]{1,0:T(8,128)(2,1)}, f32[96,1024]{1,0:T(8,128)}) custom-call(bf16[1024,768]{1,0:T(8,128)(2,1)} %shard_map.191.x_ref.normed_ref, bf16[768,3072]{1,0:T(8,128)(2,1)} %all-gather.5.cloned.1.call-done.wq_ref.wk_ref.wv_ref.weight_ref, ...), custom_call_target="tpu_custom_call" | custom-call | flops 6845104128 | bytes 12582912 | tf_op jit(solution)/shard_map/pallas_call | solution.py:139
  85.1 5.8 shard_map.193
  90.9 5.1 shard_map.195
  96.0 14.3 %all-to-all-done.1.gy_ref = bf16[4,576,768]{2,1,0:T(8,128)(2,1)} async-done(((bf16[4,576,768]{2,1,0:T(8,128)(2,1)}), bf16[4,576,768]{2,1,0:T(8,128)(2,1)}, u32[]{:S(2)}, u32[]{:S(2)}) %all-to-all-start.1) | async-done | bytes 3538976 | tf_op jit(solution)/shard_map/all_to_all | solution.py:751
  122.1 32.9 %all-to-all-done = bf16[4,288,768]{2,1,0:T(8,128)(2,1)S(1)} async-done(((bf16[4,288,768]{2,1,0:T(8,128)(2,1)}), bf16[4,288,768]{2,1,0:T(8,128)(2,1)S(1)}, u32[]{:S(2)}, u32[]{:S(2)}) %all-to-all-start) | async-done | bytes 1769504 | tf_op jit(solution)/shard_map/all_to_all | solution.py:751
  160.6 42.8 %shard_map.197 = (bf16[1152,768]{1,0:T(8,128)(2,1)}, bf16[1152,768]{1,0:T(8,128)(2,1)}, bf16[8,9216,128]{2,1,0:T(8,128)(2,1)}) custom-call(bf16[1152,768]{1,0:T(8,128)(2,1)} %bitcast.132, bf16[4,576,768]{2,1,0:T(8,128)(2,1)} %all-to-all-done.1.gy_ref, bf16[2,768,4096]{2,1,0:T(8,128)(2,1)} %wu_ref.3, bf16[2,768,4096]{2,1,0:T(8,128)(2,1)} %wu_ref.3, ...), custom_call_target="tpu_custom_call" | custom-call | flops 32614907904 | bytes 33030144 | tf_op jit(solution)/shard_map/pallas_call | solution.py:570
  203.4 5.2 all-to-all-start.4
  208.6 42.8 %shard_map.199 = (bf16[1152,768]{1,0:T(8,128)(2,1)}, bf16[1152,768]{1,0:T(8,128)(2,1)}, bf16[8,9216,128]{2,1,0:T(8,128)(2,1)}) custom-call(bf16[1152,768]{1,0:T(8,128)(2,1)} %bitcast.25.x_ref, bf16[4,576,768]{2,1,0:T(8,128)(2,1)} %all-to-all-done.1.gy_ref, bf16[2,768,4096]{2,1,0:T(8,128)(2,1)} %wu_ref.3, ...), custom_call_target="tpu_custom_call", output_to_operand_aliasing={{2}: (5, {})} | custom-call | flops 32614907904 | bytes 33030144 | tf_op jit(solution)/shard_map/pallas_call | solution.py:570
  252.7 5.1 all-to-all-start.5
  258.0 38.7 %shard_map.194 = (f32[1024,768]{1,0:T(8,128)}, f32[1024,768]{1,0:T(8,128)}, bf16[8,4608,128]{2,1,0:T(8,128)(2,1)}) custom-call(bf16[1024,768]{1,0:T(8,128)(2,1)} %get-tuple-element.34.x_ref, bf16[1024,768]{1,0:T(8,128)(2,1)} %broadcast_select_fusion.gy_ref.x_ref, bf16[8,2304,256]{2,1,0:T(8,128)(2,1)} %bitcast.154, bf16[8,2304,256]{2,1,0:T(8,128)(2,1)} %bitcast.155, ...), custom_call_target="tpu_custom_call" | custom-call | flops 28991029248 | bytes 31457280 | tf_op jit(solution)/shard_map/pallas_call | solution.py:570
  296.7 6.6 %shard_map.201.base_ref = f32[1024,768]{1,0:T(8,128)} custom-call(s32[1024,2]{1,0:T(8,128)} %fusion.4.dest_ref, f32[1024,768]{1,0:T(8,128)} %get-tuple-element.42.base_ref, bf16[1152,768]{1,0:T(8,128)(2,1)} %bitcast.114), custom_call_target="tpu_custom_call" | custom-call | flops 1811939328 | bytes 6291456 | tf_op jit(solution)/shard_map/pallas_call | solution.py:372
  304.5 11.1 %shard_map.202 = (f32[1024,768]{1,0:T(8,128)}, bf16[1024,768]{1,0:T(8,128)(2,1)}, bf16[1024,768]{1,0:T(8,128)(2,1)}, f32[1,768]{1,0:T(1,128)}) custom-call(s32[1024,2]{1,0:T(8,128)} %fusion.4.dest_ref, f32[1024,1]{1,0:T(8,128)} %fusion.16.live_ref, bf16[1024,768]{1,0:T(8,128)(2,1)} %cot_ref.1, f32[1024,768]{1,0:T(8,128)} %get-tuple-element.33.sum_ref, ...), custom_call_target="tpu_custom_call" | custom-call | flops 3019898880 | bytes 14155776 | tf_op jit(solution)/shard_map/pallas_call | solution.py:407
  317.0 34.3 %shard_map.203 = (bf16[1024,768]{1,0:T(8,128)(2,1)}, bf16[1024,768]{1,0:T(8,128)(2,1)}, bf16[1024,768]{1,0:T(8,128)(2,1)}) custom-call(bf16[1024,768]{1,0:T(8,128)(2,1)} %get-tuple-element.39.q_ref, bf16[1024,768]{1,0:T(8,128)(2,1)} %get-tuple-element.40.k_ref, bf16[1024,768]{1,0:T(8,128)(2,1)} %get-tuple-element.41.v_ref, ...), custom_call_target="tpu_custom_call" | custom-call | flops 8053063680 | bytes 12582912 | tf_op jit(solution)/shard_map/pallas_call | solution.py:210
  351.3 14.5 %shard_map.205 = bf16[8,2496,128]{2,1,0:T(8,128)(2,1)} custom-call(bf16[1024,768]{1,0:T(8,128)(2,1)} %shard_map.191.x_ref.normed_ref, bf16[1024,768]{1,0:T(8,128)(2,1)} %get-tuple-element.32.mixed_ref.o_ref, bf16[1024,768]{1,0:T(8,128)(2,1)} %get-tuple-element.47.gq_ref, bf16[1024,768]{1,0:T(8,128)(2,1)} %get-tuple-element.48.gk_ref, ...), custom_call_target="tpu_custom_call" | custom-call | flops 4831838208 | bytes 12582912 | tf_op jit(solution)/shard_map/pallas_call | solution.py:635
  370.5 5.5 all-to-all-start.3
  377.1 75.9 %all-to-all-done.3 = bf16[4,576,768]{2,1,0:T(8,128)(2,1)S(1)} async-done(((bf16[4,576,768]{2,1,0:T(8,128)(2,1)}), bf16[4,576,768]{2,1,0:T(8,128)(2,1)S(1)}, u32[]{:S(2)}, u32[]{:S(2)}) %all-to-all-start.3) | async-done | bytes 3538976 | tf_op jit(solution)/shard_map/all_to_all | solution.py:825
  455.0 9.9 %shard_map.204 = f32[1024,768]{1,0:T(8,128)} custom-call(bf16[1024,768]{1,0:T(8,128)(2,1)} %get-tuple-element.47.gq_ref, bf16[1024,768]{1,0:T(8,128)(2,1)} %get-tuple-element.48.gk_ref, bf16[1024,768]{1,0:T(8,128)(2,1)} %get-tuple-element.49.gv_ref, bf16[768,3072]{1,0:T(8,128)(2,1)} %all-gather.5.cloned.1.call-done.wq_ref.wk_ref.wv_ref.weight_ref, ...), custom_call_target="tpu_custom_call" | custom-call | flops 3623878656 | bytes 17301504 | tf_op jit(solution)/shard_map/pallas_call | solution.py:434
  464.9 13.3 %shard_map.200 = bf16[1024,768]{1,0:T(8,128)(2,1)} custom-call(s32[1024,2]{1,0:T(8,128)} %fusion.4.dest_ref, f32[1024,2]{1,0:T(8,128)} %copy.138.gates_ref, f32[1024,1]{1,0:T(8,128)} %fusion.16.live_ref, f32[1024,768]{1,0:T(8,128)} %get-tuple-element.33.sum_ref, f32[1024,768]{1,0:T(8,128)} %get-tuple-element.35.shared_ref, bf16[1152,768]{1,0:T(8,128)(2,1)} %bitcast.130, ...), custom_call_target="tpu_custom_call" | custom-call | flops 7247757312 | bytes 11403264 | tf_op jit(solution)/shard_map/pallas_call | solution.py:347
  478.2 29.9 %shard_map.206 = bf16[4,624,128]{2,1,0:T(8,128)(2,1)} custom-call(bf16[4,624,128]{2,1,0:T(8,128)(2,1)} %bitcast.147), custom_call_target="tpu_custom_call" | custom-call | flops 1277952 | bytes 12779520 | tf_op jit(solution)/shard_map/pallas_call | solution.py:677
  512.7 52.6 %shard_map.207 = bf16[4,1152,128]{2,1,0:T(8,128)(2,1)} custom-call(bf16[4,1152,128]{2,1,0:T(8,128)(2,1)} %bitcast.144), custom_call_target="tpu_custom_call" | custom-call | flops 2359296 | bytes 23592960 | tf_op jit(solution)/shard_map/pallas_call | solution.py:677
  571.0 62.6 %reduce-scatter.8.cloned.1.call-done = bf16[1,9216,128]{2,1,0:T(8,128)(2,1)} async-done(((bf16[8,9216,128]{2,1,0:T(8,128)(2,1)}), bf16[1,9216,128]{2,1,0:T(8,128)(2,1)}) %reduce-scatter.8.cloned.1.call-update) | async-done | bytes 2359312 | tf_op jit(solution)/shard_map/reduce_scatter | solution.py:795
  (108 shorter events, 67.8 us)
Async XLA Ops:
  7.2 2.1 copy-start.8
  7.2 44.8 %all-gather.5.cloned.1.call-start = ((), (), s32[]{:S(2)}) async-start(), calls=%async_computation.9 | async-start | bytes 5308416 | tf_op jit(solution)/shard_map/all_gather | solution.py:722
  9.3 248.7 %all-gather.7.cloned.1.call-start = ((), (), s32[]{:S(2)}) async-start(), calls=%async_computation.13 | async-start | bytes 10616832 | tf_op jit(solution)/shard_map/all_gather | solution.py:723
  10.6 4.0 copy-start.3
  24.5 6.5 copy-start.11
  24.5 85.7 %all-to-all-start.1 = ((bf16[4,576,768]{2,1,0:T(8,128)(2,1)}), bf16[4,576,768]{2,1,0:T(8,128)(2,1)}, u32[]{:S(2)}, u32[]{:S(2)}) async-start(bf16[4,576,768]{2,1,0:T(8,128)(2,1)} %bitcast.118), calls=%async_computation.1 | async-start | bytes 7077888 | tf_op jit(solution)/shard_map/all_to_all | solution.py:751
  31.9 2.1 copy-start.12
  110.3 44.7 %all-to-all-start = ((bf16[4,288,768]{2,1,0:T(8,128)(2,1)}), bf16[4,288,768]{2,1,0:T(8,128)(2,1)S(1)}, u32[]{:S(2)}, u32[]{:S(2)}) async-start(bf16[4,288,768]{2,1,0:T(8,128)(2,1)} %bitcast.134), calls=%async_computation | async-start | bytes 3538944 | tf_op jit(solution)/shard_map/all_to_all | solution.py:751
  154.9 1.2 copy-start.6
  156.2 47.2 %all-to-all-start.2 = ((bf16[4,288,768]{2,1,0:T(8,128)(2,1)}), bf16[4,288,768]{2,1,0:T(8,128)(2,1)}, u32[]{:S(2)}, u32[]{:S(2)}) async-start(bf16[4,288,768]{2,1,0:T(8,128)(2,1)} %bitcast.135), calls=%async_computation.2 | async-start | bytes 3538944 | tf_op jit(solution)/shard_map/all_to_all | solution.py:751
  203.4 48.0 %all-to-all-start.4 = ((bf16[4,288,768]{2,1,0:T(8,128)(2,1)}), bf16[4,288,768]{2,1,0:T(8,128)(2,1)S(1)}, u32[]{:S(2)}, u32[]{:S(2)}) async-start(bf16[4,288,768]{2,1,0:T(8,128)(2,1)} %bitcast.133), calls=%async_computation.4 | async-start | bytes 3538944 | tf_op jit(solution)/shard_map/all_to_all | solution.py:751
  251.4 1.3 copy-start.1
  252.7 50.7 %all-to-all-start.5 = ((bf16[4,288,768]{2,1,0:T(8,128)(2,1)}), bf16[4,288,768]{2,1,0:T(8,128)(2,1)S(1)}, u32[]{:S(2)}, u32[]{:S(2)}) async-start(bf16[4,288,768]{2,1,0:T(8,128)(2,1)} %bitcast.131), calls=%async_computation.5 | async-start | bytes 3538944 | tf_op jit(solution)/shard_map/all_to_all | solution.py:751
  257.7 220.5 %reduce-scatter.4.cloned.1.call-start = ((), (), s32[]{:S(2)}) async-start(), calls=%async_computation.10 | async-start | bytes 5750784 | tf_op jit(solution)/shard_map/reduce_scatter | solution.py:795
  365.8 146.9 %reduce-scatter.6.cloned.1.call-start = ((), (), s32[]{:S(2)}) async-start(), calls=%async_computation.11 | async-start | bytes 10616832 | tf_op jit(solution)/shard_map/reduce_scatter | solution.py:795
  366.4 267.2 %reduce-scatter.8.cloned.1.call-start = ((), (), s32[]{:S(2)}) async-start(), calls=%async_computation.12 | async-start | bytes 21233664 | tf_op jit(solution)/shard_map/reduce_scatter | solution.py:795
  366.5 1.5 copy-start.4
  366.5 2.0 copy-start.5
  370.5 5.5 copy-start.10
  370.5 82.5 %all-to-all-start.3 = ((bf16[4,576,768]{2,1,0:T(8,128)(2,1)}), bf16[4,576,768]{2,1,0:T(8,128)(2,1)S(1)}, u32[]{:S(2)}, u32[]{:S(2)}) async-start(bf16[4,576,768]{2,1,0:T(8,128)(2,1)} %pad_maximum_fusion), calls=%async_computation.3 | async-start | bytes 7077888 | tf_op jit(solution)/shard_map/all_to_all | solution.py:825
  509.4 1.5 copy-start.7
  510.2 2.0 copy-start.13
  566.8 1.4 copy-start
  568.2 1.3 slice-start
  (2 other events, 2.2 us)
Sparse Core Ops, SparseCore 0:
  10.4 41.5 all-gather.4
  53.9 58.6 all-gather.6
  366.0 57.4 reduce-scatter.3
  426.8 76.8 reduce-scatter.5
  507.1 126.4 reduce-scatter.7

commit v3 on v2

--- a/solution.py
+++ b/solution.py
@@ -539,7 +539,7 @@
 BLOCK = 256
 
 
-def ffn_both(x, gy, w_gu, w_down, hidden, expert, owners, out_type, parts=1, pack=None):
+def ffn_both(x, gy, w_gu, w_down, hidden, expert, owners, out_type):
     rows, width = x.shape
     block = BLOCK
     steps = hidden // block
@@ -564,21 +564,19 @@
         )
     out_rows = whole((rows, width))
     count = packed_rows(width, hidden, owners)
-    layout = (by_rows, owners, hidden, (expert or 0) * count)
-    held = [] if pack is None else [pack]
+    layout = (by_rows, owners, hidden, 0)
     copies = 2 * (block // LANES) + block // (hidden // owners) * (width // LANES)
     return call(
         functools.partial(ffn_kernel, out_type, layout, block), (steps,),
-        [whole((rows, width)), grads, gate, up, down] + [pl.BlockSpec(memory_space=pl.ANY)] * len(held),
+        [whole((rows, width)), grads, gate, up, down],
         [out_rows, out_rows, pl.BlockSpec(memory_space=pl.ANY)],
         [shape_of((rows, width), out_type), shape_of((rows, width), out_type),
-         shape_of((owners, parts * count, LANES), BF16)],
+         shape_of((owners, count, LANES), BF16)],
         scratch=[pltpu.VMEM((width, rows), BF16), pltpu.VMEM((rows, width), F32), pltpu.VMEM((rows, width), F32),
                  pltpu.VMEM(stage, BF16), pltpu.VMEM(stage, BF16), pltpu.VMEM((2, block, width), BF16),
                  pltpu.SemaphoreType.DMA((2, copies))],
         flops=18 * rows * width * hidden, moved=12 * width * hidden + 16 * rows * width, trans=rows * hidden,
-        aliases={5: 2} if held else None,
-    )(x, gy, w_gu, w_gu, w_down, *held)
+    )(x, gy, w_gu, w_gu, w_down)
 
 
 def to_panels(array):
@@ -767,13 +765,14 @@
     shared_out, grad_shared, shared_pack = ffn_both(
         normed_two, grad_b, shared_weight, shared_weight, shared_hidden, None, group, F32
     )
-    back_rows, out_rows, pack = [], [], None
+    back_rows, out_rows, expert_packs = [], [], []
     for j in range(local_experts):
         y, gx, pack = ffn_both(
-            received[j], received_grad, w_expert_gu, w_expert_down, hidden, j, group, BF16, local_experts, pack
+            received[j], received_grad, w_expert_gu, w_expert_down, hidden, j, group, BF16
         )
         back_rows.append(exchange(gx))
         out_rows.append(y)
+        expert_packs.append(pack)
     base = grad_shared
     for j, rows in enumerate(back_rows[:-1]):
         base = add_part(placed, base, rows, j)
@@ -795,9 +794,17 @@
         return lax.psum_scatter(pack, GROUP, scatter_dimension=0, tiled=True)[0]
 
     shared_share = spread(shared_pack)
-    expert_shares = jnp.split(spread(pack), local_experts)
+    expert_shares = [spread(pack) for pack in expert_packs]
     attention_share = spread(attention_pack)
-    shared_share = sum_over(shared_share, "expert", owners, 1).astype(F32)
+    pieces = lax.all_to_all(shared_share.reshape(owners, -1, LANES), "expert", split_axis=0, concat_axis=0, tiled=True)
+    piece = jnp.sum(pieces.astype(F32), axis=0).astype(BF16)
+    shared_share = (
+        lax.all_to_all(
+            jnp.broadcast_to(piece[None], (owners,) + piece.shape), "expert", split_axis=0, concat_axis=0, tiled=True
+        )
+        .reshape(shared_share.shape)
+        .astype(F32)
+    )
     attention_share = sum_over(attention_share, "expert", owners, 2).astype(F32)
     gu_panels, d_panels = 2 * shared_hidden // LANES, width // LANES
     qkv_rows, out_rows_count = 3 * d_panels * own, 4 * d_panels * own

time: 658 us -> 652 us (level)
  blocking collectives: 8.93 us -> 90 us
  waiting for transfers between devices: 190 us -> 134 us
  Pallas kernels: 360 us -> 321 us
    all_to_all x0 -> x1, blocking collectives: none -> 81.2 us  [exchange_parts(): back = lax.all_to_all(joined, axis, split_axis=0, concat_axis=0, tiled=True)]
    all_to_all x1 -> x2, waiting for transfers between devices: 75.9 us -> 11.2 us  [the longest x1 11.2 us: local(): lax.all_to_all(shared_share.reshape(owners, -1, LANES), 'expert', split_a...]
    pallas_call x2 -> x1, Pallas kernels: 82.6 us -> 43.5 us  [sum_over(): pl.pallas_call(functools.partial(sum_over_kernel, axis, count), out_shape...]
    reduce_scatter x3 -> x4, waiting for transfers between devices: 62.6 us -> 30.2 us  [spread(): return lax.psum_scatter(pack, GROUP, scatter_dimension=0, tiled=True)[0]]
    all_gather x1, waiting for transfers between devices: 0.02 us -> 22.3 us  [local(): lax.all_gather(jnp.concatenate([to_panels(w_shared_gu), to_panels(w_share...]
    all_to_all x5, waiting for transfers between devices: 47.2 us -> 64.3 us  [exchange(): lax.all_to_all(rows.reshape(owners, count, width), 'expert', split_axis=0...]
    unnamed x34 -> x38, local copies, waits for them, and re-layouts: 11.9 us -> 13.4 us
  transfers between devices with their start and end apart: 11 -> 13, of which waited for: 5 -> 6; matrix products, arithmetic and copies ran while one was open for 4% -> 5% of each run, Pallas kernels for 46% -> 50%
where the time goes in v3:
time: 652 us; the launch traced here: 647 us
  Pallas kernels  321 us (49%)
  waiting for transfers between devices  134 us (21%)
  blocking collectives  90 us (14%)
  starting transfers between devices  33.6 us (5%)
  local copies, waits for them, and re-layouts  31.5 us (5%)
  other arithmetic  20.3 us (3%)
  between operations  15.4 us (2%)
    pallas_call x3, Pallas kernels, ffn_both(): call(functools.partial(ffn_kernel, out_type, layout, block), (steps,), [w...  125 us
    all_to_all x1, blocking collectives, exchange_parts(): back = lax.all_to_all(joined, axis, split_axis=0, concat_axis=0, tiled=True)  81.2 us
    all_to_all x5, waiting for transfers between devices, exchange(): lax.all_to_all(rows.reshape(owners, count, width), 'expert', split_axis=0...  64.3 us
    pallas_call x1, Pallas kernels, sum_over(): pl.pallas_call(functools.partial(sum_over_kernel, axis, count), out_shape...  43.5 us
    pallas_call x1, Pallas kernels, attend_backward(): call(functools.partial(attend_backward_kernel, head_dim, block), (seqs, p...  34.1 us
    pallas_call x1, Pallas kernels, attend_forward(): call(functools.partial(attend_forward_kernel, head_dim, block), (seqs, pa...  33.1 us
    reduce_scatter x4, waiting for transfers between devices, spread(): return lax.psum_scatter(pack, GROUP, scatter_dimension=0, tiled=True)[0]  30.2 us
    all_to_all x5, starting transfers between devices, exchange(): lax.all_to_all(rows.reshape(owners, count, width), 'expert', split_axis=0...  25 us
  transfers between devices with their start and end apart: 13, of which 6 were waited for; matrix products, arithmetic and copies ran while one was open for 5% of the time, Pallas kernels for 50%

profile of v3, /device:TPU:0, one launch (start us, length us, event | category | flops | bytes accessed | tf_op | source)
XLA Modules:
  0.0 646.6 jit_solution(7148127105513917939)
XLA Ops:
  15.5 8.6 %shard_map.196 = bf16[2304,768]{1,0:T(8,128)(2,1)} custom-call(s32[2,1024]{1,0:T(2,128)} %shard_map.190.dest_ref, f32[2,1024]{1,0:T(2,128)} %bitcast.151, bf16[1024,768]{1,0:T(8,128)(2,1)} %broadcast_select_fusion.gy_ref.x_ref), custom_call_target="tpu_custom_call" | custom-call | flops 3623878656 | bytes 5111808 | tf_op jit(solution)/shard_map/pallas_call | solution.py:311
  24.1 6.5 %all-to-all-start.1 = ((bf16[4,576,768]{2,1,0:T(8,128)(2,1)}), bf16[4,576,768]{2,1,0:T(8,128)(2,1)}, u32[]{:S(2)}, u32[]{:S(2)}) async-start(bf16[4,576,768]{2,1,0:T(8,128)(2,1)} %bitcast.118), calls=%async_computation.1 | async-start | bytes 7077888 | tf_op jit(solution)/shard_map/all_to_all | solution.py:749
  30.6 8.8 %all-gather.1 = bf16[8,96,2]{1,2,0:T(2,128)(2,1)S(1)} all-gather(bf16[1,96,2]{1,2,0:T(2,128)(2,1)S(1)} %bitcast.154), channel_id=1, replica_groups=mesh['dp'=2,'expert'=4,'shard'=4] {'dp','shard'}, dimensions={0}, use_global_device_ids=true | all-gather | bytes 3456 | tf_op jit(solution)/shard_map/all_gather | solution.py:719
  46.8 5.2 all-gather.5.cloned.1.call-done.wq_ref.wk_ref.wv_ref.weight_ref
  52.0 33.1 %shard_map.192 = (bf16[1024,768]{1,0:T(8,128)(2,1)}, bf16[1024,768]{1,0:T(8,128)(2,1)}, bf16[1024,768]{1,0:T(8,128)(2,1)}, bf16[1024,768]{1,0:T(8,128)(2,1)}, f32[96,1024]{1,0:T(8,128)}) custom-call(bf16[1024,768]{1,0:T(8,128)(2,1)} %shard_map.191.x_ref.normed_ref, bf16[768,3072]{1,0:T(8,128)(2,1)} %all-gather.5.cloned.1.call-done.wq_ref.wk_ref.wv_ref.weight_ref, ...), custom_call_target="tpu_custom_call" | custom-call | flops 6845104128 | bytes 12582912 | tf_op jit(solution)/shard_map/pallas_call | solution.py:139
  85.1 5.8 shard_map.193
  90.9 22.3 %all-gather.7.cloned.1.call-done = bf16[18432,256]{1,0:T(8,128)(2,1)} async-done(((bf16[2304,256]{1,0:T(8,128)(2,1)}), bf16[18432,256]{1,0:T(8,128)(2,1)}) %all-gather.7.cloned.1.call-update) | async-done | bytes 9437200 | tf_op jit(solution)/shard_map/all_gather | solution.py:721
  113.2 38.6 %shard_map.194 = (f32[1024,768]{1,0:T(8,128)}, f32[1024,768]{1,0:T(8,128)}, bf16[8,4608,128]{2,1,0:T(8,128)(2,1)}) custom-call(bf16[1024,768]{1,0:T(8,128)(2,1)} %get-tuple-element.34.x_ref, bf16[1024,768]{1,0:T(8,128)(2,1)} %broadcast_select_fusion.gy_ref.x_ref, bf16[8,2304,256]{2,1,0:T(8,128)(2,1)} %bitcast.155, bf16[8,2304,256]{2,1,0:T(8,128)(2,1)} %bitcast.156, ...), custom_call_target="tpu_custom_call" | custom-call | flops 28991029248 | bytes 31457280 | tf_op jit(solution)/shard_map/pallas_call | solution.py:569
  154.6 5.1 shard_map.195
  164.5 5.4 shard_map.198
  169.9 36.2 %all-to-all-done = bf16[4,288,768]{2,1,0:T(8,128)(2,1)S(1)} async-done(((bf16[4,288,768]{2,1,0:T(8,128)(2,1)}), bf16[4,288,768]{2,1,0:T(8,128)(2,1)S(1)}, u32[]{:S(2)}, u32[]{:S(2)}) %all-to-all-start) | async-done | bytes 1769504 | tf_op jit(solution)/shard_map/all_to_all | solution.py:749
  210.9 43.5 %shard_map.197 = (bf16[1152,768]{1,0:T(8,128)(2,1)}, bf16[1152,768]{1,0:T(8,128)(2,1)}, bf16[8,4608,128]{2,1,0:T(8,128)(2,1)}) custom-call(bf16[1152,768]{1,0:T(8,128)(2,1)} %bitcast.135, bf16[4,576,768]{2,1,0:T(8,128)(2,1)} %all-to-all-done.1.gy_ref, bf16[2,768,4096]{2,1,0:T(8,128)(2,1)} %wu_ref.3, bf16[2,768,4096]{2,1,0:T(8,128)(2,1)} %wu_ref.3, ...), custom_call_target="tpu_custom_call" | custom-call | flops 32614907904 | bytes 33030144 | tf_op jit(solution)/shard_map/pallas_call | solution.py:569
  260.8 42.8 %shard_map.199 = (bf16[1152,768]{1,0:T(8,128)(2,1)}, bf16[1152,768]{1,0:T(8,128)(2,1)}, bf16[8,4608,128]{2,1,0:T(8,128)(2,1)}) custom-call(bf16[1152,768]{1,0:T(8,128)(2,1)} %bitcast.133, bf16[4,576,768]{2,1,0:T(8,128)(2,1)} %all-to-all-done.1.gy_ref, bf16[2,768,4096]{2,1,0:T(8,128)(2,1)} %wu_ref.3, bf16[2,768,4096]{2,1,0:T(8,128)(2,1)} %wu_ref.3, ...), custom_call_target="tpu_custom_call" | custom-call | flops 32614907904 | bytes 33030144 | tf_op jit(solution)/shard_map/pallas_call | solution.py:569
  314.0 6.6 %shard_map.201.base_ref = f32[1024,768]{1,0:T(8,128)} custom-call(s32[1024,2]{1,0:T(8,128)} %fusion.4.dest_ref, f32[1024,768]{1,0:T(8,128)} %get-tuple-element.41.base_ref, bf16[1152,768]{1,0:T(8,128)(2,1)} %bitcast.114), custom_call_target="tpu_custom_call" | custom-call | flops 1811939328 | bytes 6291456 | tf_op jit(solution)/shard_map/pallas_call | solution.py:372
  320.6 28.2 %all-to-all-done.5 = bf16[4,288,768]{2,1,0:T(8,128)(2,1)S(1)} async-done(((bf16[4,288,768]{2,1,0:T(8,128)(2,1)}), bf16[4,288,768]{2,1,0:T(8,128)(2,1)S(1)}, u32[]{:S(2)}, u32[]{:S(2)}) %all-to-all-start.5) | async-done | bytes 1769504 | tf_op jit(solution)/shard_map/all_to_all | solution.py:749
  350.0 11.0 %shard_map.202 = (f32[1024,768]{1,0:T(8,128)}, bf16[1024,768]{1,0:T(8,128)(2,1)}, bf16[1024,768]{1,0:T(8,128)(2,1)}, f32[1,768]{1,0:T(1,128)}) custom-call(s32[1024,2]{1,0:T(8,128)} %fusion.4.dest_ref, f32[1024,1]{1,0:T(8,128)} %fusion.16.live_ref, bf16[1024,768]{1,0:T(8,128)(2,1)} %cot_ref.1, f32[1024,768]{1,0:T(8,128)} %get-tuple-element.33.sum_ref, ...), custom_call_target="tpu_custom_call" | custom-call | flops 3019898880 | bytes 14155776 | tf_op jit(solution)/shard_map/pallas_call | solution.py:407
  362.4 34.1 %shard_map.203 = (bf16[1024,768]{1,0:T(8,128)(2,1)}, bf16[1024,768]{1,0:T(8,128)(2,1)}, bf16[1024,768]{1,0:T(8,128)(2,1)}) custom-call(bf16[1024,768]{1,0:T(8,128)(2,1)} %get-tuple-element.38.q_ref, bf16[1024,768]{1,0:T(8,128)(2,1)} %get-tuple-element.39.k_ref, bf16[1024,768]{1,0:T(8,128)(2,1)} %get-tuple-element.40.v_ref, ...), custom_call_target="tpu_custom_call" | custom-call | flops 8053063680 | bytes 12582912 | tf_op jit(solution)/shard_map/pallas_call | solution.py:210
  396.5 14.5 %shard_map.205 = bf16[8,2496,128]{2,1,0:T(8,128)(2,1)} custom-call(bf16[1024,768]{1,0:T(8,128)(2,1)} %shard_map.191.x_ref.normed_ref, bf16[1024,768]{1,0:T(8,128)(2,1)} %get-tuple-element.32.mixed_ref.o_ref, bf16[1024,768]{1,0:T(8,128)(2,1)} %get-tuple-element.46.gq_ref, bf16[1024,768]{1,0:T(8,128)(2,1)} %get-tuple-element.47.gk_ref, ...), custom_call_target="tpu_custom_call" | custom-call | flops 4831838208 | bytes 12582912 | tf_op jit(solution)/shard_map/pallas_call | solution.py:633
  414.0 81.2 %all_to_all.40 = bf16[4,576,768]{2,1,0:T(8,128)(2,1)S(1)} all-to-all(bf16[4,576,768]{2,1,0:T(8,128)(2,1)S(1)} %pad_maximum_fusion), channel_id=1, replica_groups=mesh['dp'=2,'expert'=4,'shard'=4] {'expert'}, dimensions={0} | all-to-all | bytes 7077888 | tf_op jit(solution)/shard_map/all_to_all | solution.py:832
  502.8 13.3 %shard_map.200 = bf16[1024,768]{1,0:T(8,128)(2,1)} custom-call(s32[1024,2]{1,0:T(8,128)} %fusion.4.dest_ref, f32[1024,2]{1,0:T(8,128)} %copy.135.gates_ref, f32[1024,1]{1,0:T(8,128)} %fusion.16.live_ref, f32[1024,768]{1,0:T(8,128)} %get-tuple-element.33.sum_ref, f32[1024,768]{1,0:T(8,128)} %get-tuple-element.35.shared_ref, bf16[1152,768]{1,0:T(8,128)(2,1)} %bitcast.132, ...), custom_call_target="tpu_custom_call" | custom-call | flops 7247757312 | bytes 11403264 | tf_op jit(solution)/shard_map/pallas_call | solution.py:347
  516.1 11.2 %all-to-all-done.6 = bf16[4,1152,128]{2,1,0:T(8,128)(2,1)} async-done(((bf16[4,1152,128]{2,1,0:T(8,128)(2,1)}), bf16[4,1152,128]{2,1,0:T(8,128)(2,1)}, u32[]{:S(2)}, u32[]{:S(2)}) %all-to-all-start.6) | async-done | bytes 1179680 | tf_op jit(solution)/shard_map/all_to_all | solution.py:799
  533.6 9.9 %shard_map.204 = f32[1024,768]{1,0:T(8,128)} custom-call(bf16[1024,768]{1,0:T(8,128)(2,1)} %get-tuple-element.46.gq_ref, bf16[1024,768]{1,0:T(8,128)(2,1)} %get-tuple-element.47.gk_ref, bf16[1024,768]{1,0:T(8,128)(2,1)} %get-tuple-element.48.gv_ref, bf16[768,3072]{1,0:T(8,128)(2,1)} %all-gather.5.cloned.1.call-done.wq_ref.wk_ref.wv_ref.weight_ref, ...), custom_call_target="tpu_custom_call" | custom-call | flops 3623878656 | bytes 17301504 | tf_op jit(solution)/shard_map/pallas_call | solution.py:434
  543.5 43.5 %shard_map.206 = bf16[4,624,128]{2,1,0:T(8,128)(2,1)} custom-call(bf16[4,624,128]{2,1,0:T(8,128)(2,1)} %bitcast.148), custom_call_target="tpu_custom_call" | custom-call | flops 1277952 | bytes 12779520 | tf_op jit(solution)/shard_map/pallas_call | solution.py:675
  595.3 30.2 %reduce-scatter.11.cloned.1.call-done = bf16[1,4608,128]{2,1,0:T(8,128)(2,1)} async-done(((bf16[8,4608,128]{2,1,0:T(8,128)(2,1)}), bf16[1,4608,128]{2,1,0:T(8,128)(2,1)}) %reduce-scatter.11.cloned.1.call-update) | async-done | bytes 1179664 | tf_op jit(solution)/shard_map/reduce_scatter | solution.py:794
  (125 shorter events, 85.8 us)
Async XLA Ops:
  7.2 2.2 copy-start.11
  7.2 2.5 copy-start.10
  7.2 44.8 %all-gather.5.cloned.1.call-start = ((), (), s32[]{:S(2)}) async-start(), calls=%async_computation.12 | async-start | bytes 5308416 | tf_op jit(solution)/shard_map/all_gather | solution.py:720
  9.3 103.9 %all-gather.7.cloned.1.call-start = ((), (), s32[]{:S(2)}) async-start(), calls=%async_computation.17 | async-start | bytes 10616832 | tf_op jit(solution)/shard_map/all_gather | solution.py:721
  10.1 4.0 copy-start.3
  24.1 6.5 %copy-start.14 = (bf16[2,96]{1,0:T(2,128)(2,1)S(1)}, bf16[2,96]{1,0:T(2,128)(2,1)}, u32[]{:S(2)}) copy-start(bf16[2,96]{1,0:T(2,128)(2,1)} %param.17) | copy-start | bytes 1156
  24.1 135.6 %all-to-all-start.1 = ((bf16[4,576,768]{2,1,0:T(8,128)(2,1)}), bf16[4,576,768]{2,1,0:T(8,128)(2,1)}, u32[]{:S(2)}, u32[]{:S(2)}) async-start(bf16[4,576,768]{2,1,0:T(8,128)(2,1)} %bitcast.118), calls=%async_computation.1 | async-start | bytes 7077888 | tf_op jit(solution)/shard_map/all_to_all | solution.py:749
  30.6 464.5 %reduce-scatter.7.cloned.1.call-start = ((), (), s32[]{:S(2)}) async-start(), calls=%async_computation.14 | async-start | bytes 10616832 | tf_op jit(solution)/shard_map/reduce_scatter | solution.py:794
  152.8 6.9 %copy-start.4 = (s32[2,1024]{0,1:T(8,128)}, s32[2,1024]{0,1:T(8,128)S(1)}, u32[]{:S(2)}) copy-start(s32[2,1024]{0,1:T(8,128)S(1)} %copy.121) | copy-start | bytes 24580
  159.7 46.4 %all-to-all-start = ((bf16[4,288,768]{2,1,0:T(8,128)(2,1)}), bf16[4,288,768]{2,1,0:T(8,128)(2,1)S(1)}, u32[]{:S(2)}, u32[]{:S(2)}) async-start(bf16[4,288,768]{2,1,0:T(8,128)(2,1)} %bitcast.138), calls=%async_computation | async-start | bytes 3538944 | tf_op jit(solution)/shard_map/all_to_all | solution.py:749
  207.3 47.1 %all-to-all-start.2 = ((bf16[4,288,768]{2,1,0:T(8,128)(2,1)}), bf16[4,288,768]{2,1,0:T(8,128)(2,1)S(1)}, u32[]{:S(2)}, u32[]{:S(2)}) async-start(bf16[4,288,768]{2,1,0:T(8,128)(2,1)} %bitcast.137), calls=%async_computation.2 | async-start | bytes 3538944 | tf_op jit(solution)/shard_map/all_to_all | solution.py:749
  255.7 47.8 %all-to-all-start.4 = ((bf16[4,288,768]{2,1,0:T(8,128)(2,1)}), bf16[4,288,768]{2,1,0:T(8,128)(2,1)S(1)}, u32[]{:S(2)}, u32[]{:S(2)}) async-start(bf16[4,288,768]{2,1,0:T(8,128)(2,1)} %bitcast.136), calls=%async_computation.4 | async-start | bytes 3538944 | tf_op jit(solution)/shard_map/all_to_all | solution.py:749
  304.8 43.9 %all-to-all-start.5 = ((bf16[4,288,768]{2,1,0:T(8,128)(2,1)}), bf16[4,288,768]{2,1,0:T(8,128)(2,1)S(1)}, u32[]{:S(2)}, u32[]{:S(2)}) async-start(bf16[4,288,768]{2,1,0:T(8,128)(2,1)} %bitcast.134), calls=%async_computation.5 | async-start | bytes 3538944 | tf_op jit(solution)/shard_map/all_to_all | solution.py:749
  309.9 233.6 %reduce-scatter.5.cloned.1.call-start = ((), (), s32[]{:S(2)}) async-start(), calls=%async_computation.13 | async-start | bytes 5750784 | tf_op jit(solution)/shard_map/reduce_scatter | solution.py:794
  411.1 180.5 %reduce-scatter.9.cloned.1.call-start = ((), (), s32[]{:S(2)}) async-start(), calls=%async_computation.15 | async-start | bytes 10616832 | tf_op jit(solution)/shard_map/reduce_scatter | solution.py:794
  411.7 213.8 %reduce-scatter.11.cloned.1.call-start = ((), (), s32[]{:S(2)}) async-start(), calls=%async_computation.16 | async-start | bytes 10616832 | tf_op jit(solution)/shard_map/reduce_scatter | solution.py:794
  411.7 1.5 copy-start.5
  411.7 2.0 copy-start.6
  495.1 4.6 copy-start.12
  495.1 32.2 %all-to-all-start.6 = ((bf16[4,1152,128]{2,1,0:T(8,128)(2,1)}), bf16[4,1152,128]{2,1,0:T(8,128)(2,1)}, u32[]{:S(2)}, u32[]{:S(2)}) async-start(bf16[4,1152,128]{2,1,0:T(8,128)(2,1)} %bitcast.145), calls=%async_computation.8 | async-start | bytes 2359296 | tf_op jit(solution)/shard_map/all_to_all | solution.py:799
  530.0 105.1 %all-to-all-start.7 = ((bf16[4,1152,128]{2,1,0:T(8,128)(2,1)}), bf16[4,1152,128]{2,1,0:T(8,128)(2,1)S(1)}, u32[]{:S(2)}, u32[]{:S(2)}) async-start(bf16[4,1152,128]{2,1,0:T(8,128)(2,1)} %broadcast_in_dim.34), calls=%async_computation.9 | async-start | bytes 2359296 | tf_op jit(solution)/shard_map/all_to_all | solution.py:802
  588.3 1.5 copy-start.9
  635.4 1.4 copy-start
  636.8 1.3 slice-start
  (10 other events, 11.4 us)
Sparse Core Ops, SparseCore 0:
  10.5 41.4 all-gather.4
  54.5 58.6 all-gather.6
  152.0 76.8 reduce-scatter.6
  411.2 53.8 reduce-scatter.4
  468.4 76.8 reduce-scatter.8
  548.6 76.8 reduce-scatter.10

commit v4 on v3

--- a/solution.py
+++ b/solution.py
@@ -17,7 +17,7 @@
 F32 = jnp.float32
 
 
-def call(kernel, grid, in_specs, out_specs, out_shape, scratch=(), flops=0, moved=0, trans=0, aliases=None):
+def call(kernel, grid, in_specs, out_specs, out_shape, scratch=(), flops=0, moved=0, trans=0, collective_id=None):
     return pl.pallas_call(
         kernel,
         grid_spec=pltpu.PrefetchScalarGridSpec(
@@ -28,9 +28,9 @@
             scratch_shapes=list(scratch),
         ),
         out_shape=out_shape,
-        input_output_aliases=aliases or {},
         compiler_params=pltpu.CompilerParams(
-            dimension_semantics=("arbitrary",) * len(grid), vmem_limit_bytes=VMEM_BYTES
+            dimension_semantics=("arbitrary",) * len(grid), vmem_limit_bytes=VMEM_BYTES, collective_id=collective_id,
+            has_side_effects=collective_id is not None,
         ),
         cost_estimate=pl.CostEstimate(flops=flops, bytes_accessed=moved, transcendentals=trans),
     )
@@ -317,8 +317,36 @@
     )(dest_t, gates_t, x)
 
 
-def combine_kernel(parts, dest_ref, gates_ref, live_ref, sum_ref, shared_ref, *rest):
-    y_refs, out_ref = rest[:parts], rest[parts]
+def combine_kernel(parts, axis, count, dest_ref, gates_ref, live_ref, sum_ref, shared_ref, *rest):
+    y_refs, (x_ref, piece_ref, out_ref, total_ref, pieces_ref) = rest[:parts], rest[parts : parts + 5]
+    landed, own, gathered_x, gathered_p, send_sem, recv_sem = rest[parts + 5 :]
+    step = pl.program_id(0)
+    last = pl.num_programs(0) - 1
+    me = lax.axis_index(axis)
+
+    def scatter():
+        return peer_copies(
+            axis, count, lambda index, peer: x_ref.at[peer], lambda index, me: landed.at[index], send_sem.at[0], recv_sem.at[0]
+        )
+
+    def gather():
+        return peer_copies(
+            axis, count, lambda index, peer: own, lambda index, me: gathered_x.at[me], send_sem.at[1], recv_sem.at[1]
+        )
+
+    def gather_pieces():
+        return peer_copies(
+            axis, count, lambda index, peer: piece_ref, lambda index, me: gathered_p.at[me], send_sem.at[2], recv_sem.at[2]
+        )
+
+    @pl.when(step == 0)
+    def _():
+        barrier = pltpu.get_barrier_semaphore()
+        greet(barrier, axis, count)
+        pl.semaphore_wait(barrier, count - 1)
+        for copy in scatter() + gather_pieces():
+            copy.start()
+
     block, top = dest_ref.shape
     total = sum_ref[...] + shared_ref[...]
     dest = dest_ref[...]
@@ -331,12 +359,27 @@
             total = total + dot_nn(hit, y) * gates[:, k : k + 1]
     out_ref[...] = (live_ref[...] * total).astype(BF16)
 
-
-def slot_numbers(block, slots, part):
-    return lax.broadcasted_iota(jnp.int32, (block, slots), 1) + part * slots
-
-
-def combine(dest, gates, live, first_sum, shared_out, returned):
+    @pl.when(step == jnp.minimum(2, last))
+    def _():
+        piece = x_ref[me].astype(F32)
+        for index, copy in enumerate(scatter()):
+            copy.wait()
+            piece = piece + landed[index].astype(F32)
+        own[...] = piece.astype(own.dtype)
+        for copy in gather():
+            copy.start()
+
+    @pl.when(step == last)
+    def _():
+        gathered_x[me] = own[...]
+        gathered_p[me] = piece_ref[...]
+        for copy in gather_pieces() + gather():
+            copy.wait()
+        total_ref[...] = gathered_x[...]
+        pieces_ref[...] = gathered_p[...]
+
+
+def combine(dest, gates, live, first_sum, shared_out, returned, x, piece, axis, count):
     rows, width = first_sum.shape
     top = dest.shape[1]
     block = min(256, rows)
@@ -344,13 +387,23 @@
     blocked = pl.BlockSpec((block, width), lambda i: (i, 0))
     narrow = pl.BlockSpec((block, top), lambda i: (i, 0))
     slots = sum(y.shape[0] for y in returned)
-    return call(
-        functools.partial(combine_kernel, parts), (rows // block,),
+    shape = (count, x.shape[0] // count, LANES)
+    pieces = (count,) + piece.shape
+    out, total, total_pieces = call(
+        functools.partial(combine_kernel, parts, axis, count), (rows // block,),
         [narrow, narrow, pl.BlockSpec((block, 1), lambda i: (i, 0)), blocked, blocked]
-        + [whole(y.shape) for y in returned],
-        blocked, shape_of((rows, width), BF16),
-        flops=4 * rows * slots * width, moved=10 * rows * width + 2 * slots * width,
-    )(dest, gates, live, first_sum, shared_out, *returned)
+        + [whole(y.shape) for y in returned] + [whole(shape), whole(piece.shape)],
+        [blocked, whole(shape), whole(pieces)],
+        [shape_of((rows, width), BF16), shape_of(shape, BF16), shape_of(pieces, BF16)],
+        scratch=[pltpu.VMEM((count - 1,) + shape[1:], BF16), pltpu.VMEM(shape[1:], BF16), pltpu.VMEM(shape, BF16),
+                 pltpu.VMEM(pieces, BF16), pltpu.SemaphoreType.DMA((3, count - 1)), pltpu.SemaphoreType.DMA((3, count - 1))],
+        flops=4 * rows * slots * width, moved=10 * rows * width + 2 * slots * width, collective_id=2,
+    )(dest, gates, live, first_sum, shared_out, *returned, x.reshape(shape), piece)
+    return out, total.reshape(x.shape), total_pieces.reshape(-1, LANES)
+
+
+def slot_numbers(block, slots, part):
+    return lax.broadcasted_iota(jnp.int32, (block, slots), 1) + part * slots
 
 
 def gathered(dest_ref, y_ref, part):
@@ -415,7 +468,88 @@
     )(dest, live, cotangent, first_sum, base, gain, weights, rows_of)
 
 
-def norm_one_back_kernel(gq_ref, gk_ref, gv_ref, wq_ref, wk_ref, wv_ref, tokens_ref, first_ref, gain_ref, out_ref):
+def peer_copies(axis, count, source, target, send_sem, recv_sem):
+    me = lax.axis_index(axis)
+    out = []
+    for index in range(count - 1):
+        peer = lax.rem(me + index + 1, count)
+        out.append(
+            pltpu.make_async_remote_copy(
+                src_ref=source(index, peer), dst_ref=target(index, me), send_sem=send_sem.at[index],
+                recv_sem=recv_sem.at[index], device_id={axis: peer}, device_id_type=pl.DeviceIdType.MESH,
+            )
+        )
+    return out
+
+
+def greet(barrier, axis, count):
+    me = lax.axis_index(axis)
+    for index in range(count - 1):
+        pl.semaphore_signal(
+            barrier, inc=1, device_id={axis: lax.rem(me + index + 1, count)}, device_id_type=pl.DeviceIdType.MESH
+        )
+
+
+def settle_kernel(sizes, gq_ref, gk_ref, gv_ref, wq_ref, wk_ref, wv_ref, tokens_ref, first_ref, gain_ref, pack_ref,
+                  x_ref, out_ref, share_ref, piece_ref, own, landed, chosen, arrived, sem, pair_send, pair_recv, send_sem,
+                  recv_sem, x_landed, x_send, x_recv):
+    dp_size, shard_size, count = sizes
+    spread = shard_size // 2
+    halves = dp_size * spread
+    dp, shard = lax.axis_index("dp"), lax.axis_index("shard")
+    side = shard % 2
+    place = dp * spread + shard // 2
+    step = pl.program_id(0)
+    last = pl.num_programs(0) - 1
+
+    def target(piece, bit):
+        return {"dp": piece // spread, "shard": (piece % spread) * 2 + bit}
+
+    def x_copies():
+        return peer_copies(
+            "expert", count, lambda index, peer: x_ref.at[peer], lambda index, me: x_landed.at[index], x_send, x_recv
+        )
+
+    def pair_copy():
+        return pltpu.make_async_remote_copy(
+            src_ref=pack_ref.at[:, 1 - side], dst_ref=landed, send_sem=pair_send, recv_sem=pair_recv,
+            device_id=target(place, 1 - side), device_id_type=pl.DeviceIdType.MESH,
+        )
+
+    def own_copy():
+        return pltpu.make_async_copy(pack_ref.at[:, side], own, sem)
+
+    def send(index):
+        return pltpu.make_async_remote_copy(
+            src_ref=chosen.at[index], dst_ref=arrived.at[index], send_sem=send_sem.at[index], recv_sem=recv_sem.at[index],
+            device_id=target(lax.rem(place + index + 1, halves), side), device_id_type=pl.DeviceIdType.MESH,
+        )
+
+    @pl.when(step == 0)
+    def _():
+        barrier = pltpu.get_barrier_semaphore()
+        pl.semaphore_signal(barrier, inc=1, device_id=target(place, 1 - side), device_id_type=pl.DeviceIdType.MESH)
+        for index in range(halves - 1):
+            pl.semaphore_signal(
+                barrier, inc=1, device_id=target(lax.rem(place + index + 1, halves), side),
+                device_id_type=pl.DeviceIdType.MESH,
+            )
+        greet(barrier, "expert", count)
+        pl.semaphore_wait(barrier, halves + count - 1)
+        for copy in x_copies():
+            copy.start()
+        pair_copy().start()
+        own_copy().start()
+
+    @pl.when(step == 1)
+    def _():
+        own_copy().wait()
+        pair_copy().wait()
+        for index in range(halves - 1):
+            piece = lax.rem(place + index + 1, halves)
+            chosen[index] = (own[piece].astype(F32) + landed[piece].astype(F32)).astype(BF16)
+            send(index).start()
+
     grad_normed = (
         dot_nt(gq_ref[...], wq_ref[...]) + dot_nt(gk_ref[...], wk_ref[...]) + dot_nt(gv_ref[...], wv_ref[...])
     )
@@ -425,18 +559,41 @@
     inner = jnp.mean(source * weighted, axis=1, keepdims=True)
     out_ref[...] = first_ref[...] + scale * weighted - source * (scale * scale * scale * inner)
 
-
-def norm_one_back(grads, w_qkv, tokens, grad_first, gain):
+    @pl.when(step == last)
+    def _():
+        total = own[place].astype(F32) + landed[place].astype(F32)
+        for index in range(halves - 1):
+            send(index).wait()
+            total = total + arrived[index].astype(F32)
+        share_ref[...] = total.astype(BF16)
+        piece = x_ref[lax.axis_index("expert")].astype(F32)
+        for index, copy in enumerate(x_copies()):
+            copy.wait()
+            piece = piece + x_landed[index].astype(F32)
+        piece_ref[...] = piece.astype(BF16)
+
+
+def settle(grads, w_qkv, tokens, grad_first, gain, pack, x, sizes):
     rows, width = tokens.shape
     block = min(256, rows)
     blocked = pl.BlockSpec((block, width), lambda i: (i, 0))
-
-    return call(
-        norm_one_back_kernel, (rows // block,),
-        [blocked] * 3 + [square(width, 0), square(width, 1), square(width, 2), blocked, blocked, whole((1, width))],
-        blocked, shape_of((rows, width), F32),
-        flops=6 * rows * width * width, moved=22 * rows * width,
-    )(*grads, w_qkv, w_qkv, w_qkv, tokens, grad_first, gain)
+    halves, count = sizes[0] * sizes[1] // 2, pack.shape[1]
+    piece = (count, LANES)
+    x = x.reshape(sizes[2], -1, LANES)
+    return call(
+        functools.partial(settle_kernel, sizes), (rows // block,),
+        [blocked] * 3 + [square(width, 0), square(width, 1), square(width, 2), blocked, blocked, whole((1, width)),
+                         pl.BlockSpec(memory_space=pl.ANY), whole(x.shape)],
+        [blocked, whole(piece), whole(x.shape[1:])],
+        [shape_of((rows, width), F32), shape_of(piece, BF16), shape_of(x.shape[1:], BF16)],
+        scratch=[pltpu.VMEM((halves,) + piece, BF16), pltpu.VMEM((halves,) + piece, BF16),
+                 pltpu.VMEM((halves - 1,) + piece, BF16), pltpu.VMEM((halves - 1,) + piece, BF16),
+                 pltpu.SemaphoreType.DMA, pltpu.SemaphoreType.DMA, pltpu.SemaphoreType.DMA,
+                 pltpu.SemaphoreType.DMA((halves - 1,)), pltpu.SemaphoreType.DMA((halves - 1,)),
+                 pltpu.VMEM((sizes[2] - 1,) + x.shape[1:], BF16), pltpu.SemaphoreType.DMA((sizes[2] - 1,)),
+                 pltpu.SemaphoreType.DMA((sizes[2] - 1,))],
+        flops=6 * rows * width * width, moved=22 * rows * width, collective_id=1,
+    )(*grads, w_qkv, w_qkv, w_qkv, tokens, grad_first, gain, pack.reshape((halves, 2) + piece), x)
 
 
 def copies_of(layout, block, width, step, stage_g, stage_u, stage_d, slot, packed_ref, sems):
@@ -640,54 +797,6 @@
     )(normed, mixed, *grads, grad_attn, gains)
 
 
-def sum_over_kernel(axis, count, x_ref, out_ref, landed, own, send_sem, recv_sem):
-    me = lax.axis_index(axis)
-    peers = [lax.rem(me + step, count) for step in range(1, count)]
-    barrier = pltpu.get_barrier_semaphore()
-    for peer in peers:
-        pl.semaphore_signal(barrier, inc=1, device_id={axis: peer}, device_id_type=pl.DeviceIdType.MESH)
-    pl.semaphore_wait(barrier, count - 1)
-
-    def send(phase, step, source, target):
-        copy = pltpu.make_async_remote_copy(
-            src_ref=source, dst_ref=target, send_sem=send_sem.at[phase, step], recv_sem=recv_sem.at[phase, step],
-            device_id={axis: peers[step]}, device_id_type=pl.DeviceIdType.MESH,
-        )
-        copy.start()
-        return copy
-
-    first = [send(0, step, x_ref.at[peers[step]], landed.at[step]) for step in range(count - 1)]
-    total = x_ref[me].astype(F32)
-    for step, copy in enumerate(first):
-        copy.wait()
-        total = total + landed[step].astype(F32)
-    own[...] = total.astype(own.dtype)
-    second = [send(1, step, own, out_ref.at[me]) for step in range(count - 1)]
-    out_ref[me] = own[...]
-    for copy in second:
-        copy.wait()
-
-
-def sum_over(x, axis, count, collective_id):
-    rows = x.shape[0]
-    shape = (count, rows // count, LANES)
-    vmem = pl.BlockSpec(memory_space=pltpu.VMEM)
-    return pl.pallas_call(
-        functools.partial(sum_over_kernel, axis, count),
-        out_shape=shape_of(shape, x.dtype),
-        in_specs=[vmem],
-        out_specs=vmem,
-        scratch_shapes=[
-            pltpu.VMEM((count - 1,) + shape[1:], x.dtype),
-            pltpu.VMEM(shape[1:], x.dtype),
-            pltpu.SemaphoreType.DMA((2, count - 1)),
-            pltpu.SemaphoreType.DMA((2, count - 1)),
-        ],
-        compiler_params=pltpu.CompilerParams(collective_id=collective_id, has_side_effects=True),
-        cost_estimate=pl.CostEstimate(flops=rows * LANES * count, bytes_accessed=40 * rows * LANES, transcendentals=0),
-    )(x.reshape(shape)).reshape(rows, LANES)
-
-
 GROUP = ("dp", "shard")
 
 
@@ -781,31 +890,25 @@
     )
 
     grads = attend_backward(queries, keys, values, mixed, grad_mixed, lse, cosine, sine, length, head_dim)
-    input_grad = norm_one_back(grads, attention_weight, tokens, grad_first, gain_one)
     own = width // group
     grad_gains = grad_gain_two.reshape(group, 1, own)
     grad_gains = jnp.pad(grad_gains, ((0, 0), (0, 15), (0, LANES - own))).astype(BF16)
     attention_pack = attention_weights(normed_one, mixed, grads, grad_attn, grad_gains, group, owners)
 
-    returned = exchange_parts(out_rows, owners, "expert")
-    layer_out = combine(placed, route_gates, live, first_sum, shared_out, returned)
-
     def spread(pack):
         return lax.psum_scatter(pack, GROUP, scatter_dimension=0, tiled=True)[0]
 
     shared_share = spread(shared_pack)
     expert_shares = [spread(pack) for pack in expert_packs]
-    attention_share = spread(attention_pack)
-    pieces = lax.all_to_all(shared_share.reshape(owners, -1, LANES), "expert", split_axis=0, concat_axis=0, tiled=True)
-    piece = jnp.sum(pieces.astype(F32), axis=0).astype(BF16)
-    shared_share = (
-        lax.all_to_all(
-            jnp.broadcast_to(piece[None], (owners,) + piece.shape), "expert", split_axis=0, concat_axis=0, tiled=True
-        )
-        .reshape(shared_share.shape)
-        .astype(F32)
-    )
-    attention_share = sum_over(attention_share, "expert", owners, 2).astype(F32)
+    input_grad, attention_share, shared_piece = settle(
+        grads, attention_weight, tokens, grad_first, gain_one, attention_pack, shared_share,
+        (lax.axis_size("dp"), lax.axis_size("shard"), owners),
+    )
+    returned = exchange_parts(out_rows, owners, "expert")
+    layer_out, attention_share, shared_share = combine(
+        placed, route_gates, live, first_sum, shared_out, returned, attention_share, shared_piece, "expert", owners
+    )
+    attention_share, shared_share = attention_share.astype(F32), shared_share.astype(F32)
     gu_panels, d_panels = 2 * shared_hidden // LANES, width // LANES
     qkv_rows, out_rows_count = 3 * d_panels * own, 4 * d_panels * own
     columns = 2 * hidden // group

time: 652 us -> 718 us (1.10)
  blocking collectives: 90 us -> 182 us
  waiting for transfers between devices: 134 us -> 82.7 us
  Pallas kernels: 321 us -> 355 us
    all_to_all x0 -> x2, blocking collectives: none -> 90.4 us  [exchange(): lax.all_to_all(rows.reshape(owners, count, width), 'expert', split_axis=0...]
    pallas_call x3 -> x2, Pallas kernels: 66.7 us -> 100 us  [the longest x1 58.4 us: combine(): call(functools.partial(combine_kernel, parts, axis, count), (rows // bloc...]
    reduce_scatter x4 -> x3, waiting for transfers between devices: 30.2 us -> 0.02 us  [spread(): return lax.psum_scatter(pack, GROUP, scatter_dimension=0, tiled=True)[0]]
    all_gather x1, waiting for transfers between devices: 22.3 us -> 0.02 us  [local(): lax.all_gather(jnp.concatenate([to_panels(w_shared_gu), to_panels(w_share...]
    all_to_all x5 -> x3, waiting for transfers between devices: 64.3 us -> 79.2 us  [exchange(): lax.all_to_all(rows.reshape(owners, count, width), 'expert', split_axis=0...]
    reduce_scatter x4 -> x3, starting transfers between devices: 0.48 us -> 11.8 us  [spread(): return lax.psum_scatter(pack, GROUP, scatter_dimension=0, tiled=True)[0]]
    all_to_all x2 -> x0, waiting for transfers between devices: 11.2 us -> none  [the longest x1 11.2 us: local(): lax.all_to_all(shared_share.reshape(owners, -1, LANES), 'expert', split_a...]
    all_to_all x5 -> x3, starting transfers between devices: 25 us -> 15.7 us  [exchange(): lax.all_to_all(rows.reshape(owners, count, width), 'expert', split_axis=0...]
  transfers between devices with their start and end apart: 13 -> 8, of which waited for: 6 -> 4; matrix products, arithmetic and copies ran while one was open for 5% -> 4% of each run, Pallas kernels for 50% -> 36%
where the time goes in v4:
time: 718 us; the launch traced here: 709 us
  Pallas kernels  355 us (49%)
  blocking collectives  182 us (25%)
  waiting for transfers between devices  82.7 us (12%)
  starting transfers between devices  27.6 us (4%)
  local copies, waits for them, and re-layouts  27.5 us (4%)
  other arithmetic  19.4 us (3%)
  between operations  15.2 us (2%)
    pallas_call x3, Pallas kernels, ffn_both(): call(functools.partial(ffn_kernel, out_type, layout, block), (steps,), [w...  125 us
    all_to_all x2, blocking collectives, exchange(): lax.all_to_all(rows.reshape(owners, count, width), 'expert', split_axis=0...  90.4 us
    all_to_all x1, blocking collectives, exchange_parts(): back = lax.all_to_all(joined, axis, split_axis=0, concat_axis=0, tiled=True)  82.4 us
    all_to_all x3, waiting for transfers between devices, exchange(): lax.all_to_all(rows.reshape(owners, count, width), 'expert', split_axis=0...  79.2 us
    pallas_call x1, Pallas kernels, combine(): call(functools.partial(combine_kernel, parts, axis, count), (rows // bloc...  58.4 us
    pallas_call x1, Pallas kernels, settle(): call(functools.partial(settle_kernel, sizes), (rows // block,), [blocked]...  41.8 us
    pallas_call x1, Pallas kernels, attend_backward(): call(functools.partial(attend_backward_kernel, head_dim, block), (seqs, p...  34.1 us
    pallas_call x1, Pallas kernels, attend_forward(): call(functools.partial(attend_forward_kernel, head_dim, block), (seqs, pa...  33.1 us
  transfers between devices with their start and end apart: 8, of which 4 were waited for; matrix products, arithmetic and copies ran while one was open for 4% of the time, Pallas kernels for 36%

profile of v4, /device:TPU:0, one launch (start us, length us, event | category | flops | bytes accessed | tf_op | source)
XLA Modules:
  0.0 708.8 jit_solution(4534494047828069626)
XLA Ops:
  15.5 8.6 %shard_map.196 = bf16[2304,768]{1,0:T(8,128)(2,1)} custom-call(s32[2,1024]{1,0:T(2,128)} %shard_map.190.dest_ref, f32[2,1024]{1,0:T(2,128)} %bitcast.150, bf16[1024,768]{1,0:T(8,128)(2,1)} %broadcast_select_fusion.gy_ref.x_ref), custom_call_target="tpu_custom_call" | custom-call | flops 3623878656 | bytes 5111808 | tf_op jit(solution)/shard_map/pallas_call | solution.py:311
  24.1 6.5 all-to-all-start.1
  30.8 8.8 %all-gather.1 = bf16[8,96,2]{1,2,0:T(2,128)(2,1)S(1)} all-gather(bf16[1,96,2]{1,2,0:T(2,128)(2,1)S(1)} %bitcast.153), channel_id=1, replica_groups=mesh['dp'=2,'expert'=4,'shard'=4] {'dp','shard'}, dimensions={0}, use_global_device_ids=true | all-gather | bytes 3456 | tf_op jit(solution)/shard_map/all_gather | solution.py:828
  52.1 33.1 %shard_map.192 = (bf16[1024,768]{1,0:T(8,128)(2,1)}, bf16[1024,768]{1,0:T(8,128)(2,1)}, bf16[1024,768]{1,0:T(8,128)(2,1)}, bf16[1024,768]{1,0:T(8,128)(2,1)}, f32[96,1024]{1,0:T(8,128)}) custom-call(bf16[1024,768]{1,0:T(8,128)(2,1)} %shard_map.191.x_ref.normed_ref, bf16[768,3072]{1,0:T(8,128)(2,1)} %all-gather.5.cloned.1.call-done.wq_ref.wk_ref.wv_ref.weight_ref, ...), custom_call_target="tpu_custom_call" | custom-call | flops 6845104128 | bytes 12582912 | tf_op jit(solution)/shard_map/pallas_call | solution.py:139
  85.2 5.8 shard_map.193
  91.0 5.0 shard_map.195
  96.0 13.8 %all-to-all-done.1.gy_ref = bf16[4,576,768]{2,1,0:T(8,128)(2,1)} async-done(((bf16[4,576,768]{2,1,0:T(8,128)(2,1)}), bf16[4,576,768]{2,1,0:T(8,128)(2,1)}, u32[]{:S(2)}, u32[]{:S(2)}) %all-to-all-start.1) | async-done | bytes 3538976 | tf_op jit(solution)/shard_map/all_to_all | solution.py:858
  109.8 45.4 %all_to_all.30 = bf16[4,288,768]{2,1,0:T(8,128)(2,1)} all-to-all(bf16[4,288,768]{2,1,0:T(8,128)(2,1)} %bitcast.136), channel_id=1, replica_groups=mesh['dp'=2,'expert'=4,'shard'=4] {'expert'}, dimensions={0} | all-to-all | bytes 3538944 | tf_op jit(solution)/shard_map/all_to_all | solution.py:858
  155.2 42.7 %shard_map.197 = (bf16[1152,768]{1,0:T(8,128)(2,1)}, bf16[1152,768]{1,0:T(8,128)(2,1)}, bf16[8,4608,128]{2,1,0:T(8,128)(2,1)}) custom-call(bf16[1152,768]{1,0:T(8,128)(2,1)} %bitcast.138, bf16[4,576,768]{2,1,0:T(8,128)(2,1)} %all-to-all-done.1.gy_ref, bf16[2,768,4096]{2,1,0:T(8,128)(2,1)} %wu_ref.3, bf16[2,768,4096]{2,1,0:T(8,128)(2,1)} %wu_ref.3, ...), custom_call_target="tpu_custom_call" | custom-call | flops 32614907904 | bytes 33030144 | tf_op jit(solution)/shard_map/pallas_call | solution.py:726
  198.0 5.1 shard_map.198
  203.1 44.9 %all_to_all.31 = bf16[4,288,768]{2,1,0:T(8,128)(2,1)} all-to-all(bf16[4,288,768]{2,1,0:T(8,128)(2,1)} %bitcast.139), channel_id=1, replica_groups=mesh['dp'=2,'expert'=4,'shard'=4] {'expert'}, dimensions={0} | all-to-all | bytes 3538944 | tf_op jit(solution)/shard_map/all_to_all | solution.py:858
  248.0 42.8 %shard_map.199 = (bf16[1152,768]{1,0:T(8,128)(2,1)}, bf16[1152,768]{1,0:T(8,128)(2,1)}, bf16[8,4608,128]{2,1,0:T(8,128)(2,1)}) custom-call(bf16[1152,768]{1,0:T(8,128)(2,1)} %bitcast.137, bf16[4,576,768]{2,1,0:T(8,128)(2,1)} %all-to-all-done.1.gy_ref, bf16[2,768,4096]{2,1,0:T(8,128)(2,1)} %wu_ref.3, bf16[2,768,4096]{2,1,0:T(8,128)(2,1)} %wu_ref.3, ...), custom_call_target="tpu_custom_call" | custom-call | flops 32614907904 | bytes 33030144 | tf_op jit(solution)/shard_map/pallas_call | solution.py:726
  290.9 11.8 %reduce-scatter.4.cloned.1.call-start = ((), (), s32[]{:S(2)}) async-start(), calls=%async_computation.10 | async-start | bytes 10616832 | tf_op jit(solution)/shard_map/reduce_scatter | solution.py:899
  302.7 39.6 %shard_map.194 = (f32[1024,768]{1,0:T(8,128)}, f32[1024,768]{1,0:T(8,128)}, bf16[8,4608,128]{2,1,0:T(8,128)(2,1)}) custom-call(bf16[1024,768]{1,0:T(8,128)(2,1)} %get-tuple-element.40.x_ref, bf16[1024,768]{1,0:T(8,128)(2,1)} %broadcast_select_fusion.gy_ref.x_ref, bf16[8,2304,256]{2,1,0:T(8,128)(2,1)} %bitcast.154, bf16[8,2304,256]{2,1,0:T(8,128)(2,1)} %bitcast.155, ...), custom_call_target="tpu_custom_call" | custom-call | flops 28991029248 | bytes 31457280 | tf_op jit(solution)/shard_map/pallas_call | solution.py:726
  342.3 4.7 all-to-all-start.4
  349.1 38.4 %all-to-all-done.4 = bf16[4,288,768]{2,1,0:T(8,128)(2,1)} async-done(((bf16[4,288,768]{2,1,0:T(8,128)(2,1)}), bf16[4,288,768]{2,1,0:T(8,128)(2,1)}, u32[]{:S(2)}, u32[]{:S(2)}) %all-to-all-start.4) | async-done | bytes 1769504 | tf_op jit(solution)/shard_map/all_to_all | solution.py:858
  387.5 82.4 %all_to_all.32 = bf16[4,576,768]{2,1,0:T(8,128)(2,1)S(1)} all-to-all(bf16[4,576,768]{2,1,0:T(8,128)(2,1)} %pad_maximum_fusion), channel_id=1, replica_groups=mesh['dp'=2,'expert'=4,'shard'=4] {'expert'}, dimensions={0} | all-to-all | bytes 7077888 | tf_op jit(solution)/shard_map/all_to_all | solution.py:935
  481.1 6.6 shard_map.200.base_ref
  487.7 27.0 %all-to-all-done.5 = bf16[4,288,768]{2,1,0:T(8,128)(2,1)} async-done(((bf16[4,288,768]{2,1,0:T(8,128)(2,1)}), bf16[4,288,768]{2,1,0:T(8,128)(2,1)}, u32[]{:S(2)}, u32[]{:S(2)}) %all-to-all-start.5) | async-done | bytes 1769504 | tf_op jit(solution)/shard_map/all_to_all | solution.py:858
  514.7 11.0 %shard_map.201 = (f32[1024,768]{1,0:T(8,128)}, bf16[1024,768]{1,0:T(8,128)(2,1)}, bf16[1024,768]{1,0:T(8,128)(2,1)}, f32[1,768]{1,0:T(1,128)}) custom-call(s32[1024,2]{1,0:T(8,128)} %fusion.4.dest_ref, f32[1024,1]{1,0:T(8,128)} %fusion.16.live_ref, bf16[1024,768]{1,0:T(8,128)(2,1)} %cot_ref.1, f32[1024,768]{1,0:T(8,128)} %get-tuple-element.39.sum_ref, ...), custom_call_target="tpu_custom_call" | custom-call | flops 3019898880 | bytes 14155776 | tf_op jit(solution)/shard_map/pallas_call | solution.py:460
  527.1 34.1 %shard_map.202 = (bf16[1024,768]{1,0:T(8,128)(2,1)}, bf16[1024,768]{1,0:T(8,128)(2,1)}, bf16[1024,768]{1,0:T(8,128)(2,1)}) custom-call(bf16[1024,768]{1,0:T(8,128)(2,1)} %get-tuple-element.44.q_ref, bf16[1024,768]{1,0:T(8,128)(2,1)} %get-tuple-element.45.k_ref, bf16[1024,768]{1,0:T(8,128)(2,1)} %get-tuple-element.46.v_ref, ...), custom_call_target="tpu_custom_call" | custom-call | flops 8053063680 | bytes 12582912 | tf_op jit(solution)/shard_map/pallas_call | solution.py:210
  561.2 14.7 %shard_map.203 = bf16[8,2496,128]{2,1,0:T(8,128)(2,1)} custom-call(bf16[1024,768]{1,0:T(8,128)(2,1)} %shard_map.191.x_ref.normed_ref, bf16[1024,768]{1,0:T(8,128)(2,1)} %get-tuple-element.38.mixed_ref.o_ref, bf16[1024,768]{1,0:T(8,128)(2,1)} %get-tuple-element.52.gq_ref, bf16[1024,768]{1,0:T(8,128)(2,1)} %get-tuple-element.53.gk_ref, ...), custom_call_target="tpu_custom_call" | custom-call | flops 4831838208 | bytes 12582912 | tf_op jit(solution)/shard_map/pallas_call | solution.py:790
  586.8 41.8 %shard_map.204 = (f32[1024,768]{1,0:T(8,128)}, bf16[2496,128]{1,0:T(8,128)(2,1)}, bf16[1152,128]{1,0:T(8,128)(2,1)}) custom-call(bf16[1024,768]{1,0:T(8,128)(2,1)} %get-tuple-element.52.gq_ref, bf16[1024,768]{1,0:T(8,128)(2,1)} %get-tuple-element.53.gk_ref, bf16[1024,768]{1,0:T(8,128)(2,1)} %get-tuple-element.54.gv_ref, ...), custom_call_target="tpu_custom_call" | custom-call | flops 3623878656 | bytes 17301504 | tf_op jit(solution)/shard_map/pallas_call | solution.py:583
  628.6 58.4 %shard_map.205 = (bf16[1024,768]{1,0:T(8,128)(2,1)}, bf16[4,624,128]{2,1,0:T(8,128)(2,1)}, bf16[4,1152,128]{2,1,0:T(8,128)(2,1)}) custom-call(s32[1024,2]{1,0:T(8,128)} %fusion.4.dest_ref, f32[1024,2]{1,0:T(8,128)} %copy.140.gates_ref, f32[1024,1]{1,0:T(8,128)} %fusion.16.live_ref, f32[1024,768]{1,0:T(8,128)} %get-tuple-element.39.sum_ref, ...), custom_call_target="tpu_custom_call" | custom-call | flops 7247757312 | bytes 11403264 | tf_op jit(solution)/shard_map/pallas_call | solution.py:392
  (116 shorter events, 60.6 us)
Async XLA Ops:
  7.2 2.2 copy-start.10
  7.2 2.5 copy-start.9
  7.2 44.9 %all-gather.5.cloned.1.call-start = ((), (), s32[]{:S(2)}) async-start(), calls=%async_computation.9 | async-start | bytes 5308416 | tf_op jit(solution)/shard_map/all_gather | solution.py:829
  9.3 293.4 %all-gather.7.cloned.1.call-start = ((), (), s32[]{:S(2)}) async-start(), calls=%async_computation.13 | async-start | bytes 10616832 | tf_op jit(solution)/shard_map/all_gather | solution.py:830
  10.1 4.0 copy-start.1
  24.1 6.5 copy-start.12
  24.1 6.7 copy-start.13
  24.1 85.7 %all-to-all-start.1 = ((bf16[4,576,768]{2,1,0:T(8,128)(2,1)}), bf16[4,576,768]{2,1,0:T(8,128)(2,1)}, u32[]{:S(2)}, u32[]{:S(2)}) async-start(bf16[4,576,768]{2,1,0:T(8,128)(2,1)} %bitcast.120), calls=%async_computation.1 | async-start | bytes 7077888 | tf_op jit(solution)/shard_map/all_to_all | solution.py:858
  30.5 545.4 %reduce-scatter.6.cloned.1.call-start = ((), (), s32[]{:S(2)}) async-start(), calls=%async_computation.11 | async-start | bytes 10616832 | tf_op jit(solution)/shard_map/reduce_scatter | solution.py:899
  30.8 11.6 %copy-start.3 = (s32[2,1024]{0,1:T(8,128)}, s32[2,1024]{0,1:T(8,128)S(1)}, u32[]{:S(2)}) copy-start(s32[2,1024]{0,1:T(8,128)S(1)} %copy.123) | copy-start | bytes 24580
  198.0 381.0 %reduce-scatter.8.cloned.1.call-start = ((), (), s32[]{:S(2)}) async-start(), calls=%async_computation.12 | async-start | bytes 10616832 | tf_op jit(solution)/shard_map/reduce_scatter | solution.py:899
  290.9 295.9 %reduce-scatter.4.cloned.1.call-start = ((), (), s32[]{:S(2)}) async-start(), calls=%async_computation.10 | async-start | bytes 10616832 | tf_op jit(solution)/shard_map/reduce_scatter | solution.py:899
  342.3 4.7 copy-start.5
  342.3 4.7 copy-start.6
  342.3 45.2 %all-to-all-start.4 = ((bf16[4,288,768]{2,1,0:T(8,128)(2,1)}), bf16[4,288,768]{2,1,0:T(8,128)(2,1)}, u32[]{:S(2)}, u32[]{:S(2)}) async-start(bf16[4,288,768]{2,1,0:T(8,128)(2,1)} %bitcast.135), calls=%async_computation.4 | async-start | bytes 3538944 | tf_op jit(solution)/shard_map/all_to_all | solution.py:858
  469.9 4.5 copy-start.11
  469.9 44.8 %all-to-all-start.5 = ((bf16[4,288,768]{2,1,0:T(8,128)(2,1)}), bf16[4,288,768]{2,1,0:T(8,128)(2,1)}, u32[]{:S(2)}, u32[]{:S(2)}) async-start(bf16[4,288,768]{2,1,0:T(8,128)(2,1)} %bitcast.134), calls=%async_computation.5 | async-start | bytes 3538944 | tf_op jit(solution)/shard_map/all_to_all | solution.py:858
  687.0 1.5 copy-start.8
  689.3 1.4 slice-start.2
  689.3 2.4 slice-start.3
  690.7 1.5 copy-start.7
  692.2 1.7 slice-start.1
  693.5 1.8 slice-start
  696.7 3.5 copy-start.4
  (7 other events, 8.0 us)
Sparse Core Ops, SparseCore 0:
  10.5 41.6 all-gather.4
  54.0 58.6 all-gather.6
  198.1 75.8 reduce-scatter.5
  291.0 75.7 reduce-scatter.7
  370.2 76.8 reduce-scatter.3

commit v5 on v4

--- a/solution.py
+++ b/solution.py
@@ -17,7 +17,7 @@
 F32 = jnp.float32
 
 
-def call(kernel, grid, in_specs, out_specs, out_shape, scratch=(), flops=0, moved=0, trans=0, collective_id=None):
+def call(kernel, grid, in_specs, out_specs, out_shape, scratch=(), flops=0, moved=0, trans=0, collective_id=None, aliases=None):
     return pl.pallas_call(
         kernel,
         grid_spec=pltpu.PrefetchScalarGridSpec(
@@ -28,6 +28,7 @@
             scratch_shapes=list(scratch),
         ),
         out_shape=out_shape,
+        input_output_aliases=aliases or {},
         compiler_params=pltpu.CompilerParams(
             dimension_semantics=("arbitrary",) * len(grid), vmem_limit_bytes=VMEM_BYTES, collective_id=collective_id,
             has_side_effects=collective_id is not None,
@@ -317,35 +318,38 @@
     )(dest_t, gates_t, x)
 
 
-def combine_kernel(parts, axis, count, dest_ref, gates_ref, live_ref, sum_ref, shared_ref, *rest):
-    y_refs, (x_ref, piece_ref, out_ref, total_ref, pieces_ref) = rest[:parts], rest[parts : parts + 5]
-    landed, own, gathered_x, gathered_p, send_sem, recv_sem = rest[parts + 5 :]
+def unpack(source, start, rows, panels, target):
+    for p in range(panels):
+        target[:, pl.ds(p * LANES, LANES)] = source[pl.ds(start + p * rows, rows), :].astype(F32)
+
+
+def combine_kernel(parts, axis, count, own, gu_panels, experts, dest_ref, gates_ref, live_ref, sum_ref, shared_ref, *rest):
+    y_refs = rest[:parts]
+    x_ref, piece_ref, pack_ref, out_ref, egu_ref, ed_ref, qkv_ref, wo_ref, sgu_ref, sd_ref, gain_ref = rest[parts : parts + 11]
+    buffers, total_x, all_x, all_p, sum_send, sum_recv, x_send, x_recv, p_send, p_recv = rest[parts + 11 :]
     step = pl.program_id(0)
     last = pl.num_programs(0) - 1
-    me = lax.axis_index(axis)
-
-    def scatter():
-        return peer_copies(
-            axis, count, lambda index, peer: x_ref.at[peer], lambda index, me: landed.at[index], send_sem.at[0], recv_sem.at[0]
-        )
-
-    def gather():
-        return peer_copies(
-            axis, count, lambda index, peer: own, lambda index, me: gathered_x.at[me], send_sem.at[1], recv_sem.at[1]
-        )
-
-    def gather_pieces():
-        return peer_copies(
-            axis, count, lambda index, peer: piece_ref, lambda index, me: gathered_p.at[me], send_sem.at[2], recv_sem.at[2]
-        )
+    line = LineSum(axis, count, x_ref, buffers, sum_send, sum_recv)
+    gather_x = LineGather(axis, count, all_x, x_send, x_recv)
+    gather_p = LineGather(axis, count, all_p, p_send, p_recv)
+    width = out_ref.shape[1]
+    d_panels = width // LANES
+    packed = pack_ref.shape[0] // experts
+    e_panels, e_rows = egu_ref.shape[2] // LANES, egu_ref.shape[1]
 
     @pl.when(step == 0)
     def _():
         barrier = pltpu.get_barrier_semaphore()
-        greet(barrier, axis, count)
-        pl.semaphore_wait(barrier, count - 1)
-        for copy in scatter() + gather_pieces():
-            copy.start()
+        pl.semaphore_wait(barrier, greet_neighbours(barrier, axis, count))
+        line.start()
+        gather_p.start(piece_ref[...])
+        for e in range(experts):
+            unpack(pack_ref, e * packed + e_panels * width, ed_ref.shape[1], d_panels, ed_ref.at[e])
+
+    for e in range(experts):
+        for p in range(e_panels):
+            rows = pl.ds(pl.multiple_of(e * packed + p * width + step * e_rows, 16), e_rows)
+            egu_ref[e, :, pl.ds(p * LANES, LANES)] = pack_ref[rows, :].astype(F32)
 
     block, top = dest_ref.shape
     total = sum_ref[...] + shared_ref[...]
@@ -359,47 +363,56 @@
             total = total + dot_nn(hit, y) * gates[:, k : k + 1]
     out_ref[...] = (live_ref[...] * total).astype(BF16)
 
-    @pl.when(step == jnp.minimum(2, last))
-    def _():
-        piece = x_ref[me].astype(F32)
-        for index, copy in enumerate(scatter()):
-            copy.wait()
-            piece = piece + landed[index].astype(F32)
-        own[...] = piece.astype(own.dtype)
-        for copy in gather():
-            copy.start()
+    @pl.when(step == jnp.minimum(1, last))
+    def _():
+        line.relay()
+        gather_p.relay(1)
 
     @pl.when(step == last)
     def _():
-        gathered_x[me] = own[...]
-        gathered_p[me] = piece_ref[...]
-        for copy in gather_pieces() + gather():
-            copy.wait()
-        total_ref[...] = gathered_x[...]
-        pieces_ref[...] = gathered_p[...]
-
-
-def combine(dest, gates, live, first_sum, shared_out, returned, x, piece, axis, count):
+        line.finish(total_x)
+        gather_x.start(total_x[...].astype(BF16))
+        for k in range(1, count):
+            if k > 1:
+                gather_p.relay(k)
+            gather_x.relay(k)
+        gather_p.finish()
+        unpack(all_p, 0, own, gu_panels, sgu_ref)
+        unpack(all_p, gu_panels * own, sd_ref.shape[0], d_panels, sd_ref)
+        gather_x.finish()
+        unpack(all_x, 0, own, 3 * d_panels, qkv_ref)
+        unpack(all_x, 3 * d_panels * own, own, d_panels, wo_ref)
+        gain_ref[...] = all_x[pl.ds(4 * d_panels * own, gain_ref.shape[0]), :].astype(F32)
+
+
+def combine(dest, gates, live, first_sum, shared_out, returned, x, piece, pack, axis, count, own, shared_hidden, hidden):
     rows, width = first_sum.shape
     top = dest.shape[1]
     block = min(256, rows)
+    steps = rows // block
     parts = len(returned)
     blocked = pl.BlockSpec((block, width), lambda i: (i, 0))
     narrow = pl.BlockSpec((block, top), lambda i: (i, 0))
     slots = sum(y.shape[0] for y in returned)
-    shape = (count, x.shape[0] // count, LANES)
-    pieces = (count,) + piece.shape
-    out, total, total_pieces = call(
-        functools.partial(combine_kernel, parts, axis, count), (rows // block,),
+    group = width // own
+    columns = 2 * hidden // group
+    gu_panels = 2 * shared_hidden // LANES
+    x_piece, p_rows = (x.shape[0] // count, LANES), count * piece.shape[0]
+    outs = [
+        (parts, width, columns), (parts, hidden // group, width), (own, 3 * width), (own, width), (own, 2 * shared_hidden),
+        (shared_hidden // group, width), (8, LANES),
+    ]
+    sems = pltpu.SemaphoreType.DMA((2, count))
+    return call(
+        functools.partial(combine_kernel, parts, axis, count, own, gu_panels, parts), (steps,),
         [narrow, narrow, pl.BlockSpec((block, 1), lambda i: (i, 0)), blocked, blocked]
-        + [whole(y.shape) for y in returned] + [whole(shape), whole(piece.shape)],
-        [blocked, whole(shape), whole(pieces)],
-        [shape_of((rows, width), BF16), shape_of(shape, BF16), shape_of(pieces, BF16)],
-        scratch=[pltpu.VMEM((count - 1,) + shape[1:], BF16), pltpu.VMEM(shape[1:], BF16), pltpu.VMEM(shape, BF16),
-                 pltpu.VMEM(pieces, BF16), pltpu.SemaphoreType.DMA((3, count - 1)), pltpu.SemaphoreType.DMA((3, count - 1))],
+        + [whole(y.shape) for y in returned] + [whole(x.shape), whole(piece.shape), whole(pack.shape)],
+        [blocked, pl.BlockSpec((parts, width // steps, columns), lambda i: (0, i, 0))] + [whole(shape) for shape in outs[1:]],
+        [shape_of((rows, width), BF16)] + [shape_of(shape, F32) for shape in outs],
+        scratch=[pltpu.VMEM((2, 2, count) + x_piece, BF16), pltpu.VMEM(x_piece, F32), pltpu.VMEM(x.shape, BF16),
+                 pltpu.VMEM((p_rows, LANES), BF16)] + [sems] * 6,
         flops=4 * rows * slots * width, moved=10 * rows * width + 2 * slots * width, collective_id=2,
-    )(dest, gates, live, first_sum, shared_out, *returned, x.reshape(shape), piece)
-    return out, total.reshape(x.shape), total_pieces.reshape(-1, LANES)
+    )(dest, gates, live, first_sum, shared_out, *returned, x, piece, pack)
 
 
 def slot_numbers(block, slots, part):
@@ -468,31 +481,139 @@
     )(dest, live, cotangent, first_sum, base, gain, weights, rows_of)
 
 
-def peer_copies(axis, count, source, target, send_sem, recv_sem):
+def line_copy(axis, ahead, source, target, send_sem, recv_sem):
+    return pltpu.make_async_remote_copy(
+        src_ref=source, dst_ref=target, send_sem=send_sem, recv_sem=recv_sem,
+        device_id={axis: lax.axis_index(axis) + ahead}, device_id_type=pl.DeviceIdType.MESH,
+    )
+
+
+class LineSum:
+    def __init__(self, axis, count, x_ref, buffers, send_sem, recv_sem):
+        self.axis, self.count, self.x_ref, self.buffers = axis, count, x_ref, buffers
+        self.send_sem, self.recv_sem = send_sem, recv_sem
+        self.rows = buffers.shape[3]
+
+    def own(self, piece):
+        return self.x_ref[pl.ds(pl.multiple_of(piece * self.rows, 16), self.rows), :].astype(F32)
+
+    def copy(self, way, piece):
+        return line_copy(
+            self.axis, 1 - 2 * way, self.buffers.at[way, 1, piece], self.buffers.at[way, 0, piece],
+            self.send_sem.at[way, piece], self.recv_sem.at[way, piece],
+        )
+
+    def each(self, body):
+        me = lax.axis_index(self.axis)
+        for k in range(self.count - 1):
+            for way, piece in ((0, self.count - 1 - k), (1, k)):
+                before = me > 0 if way == 0 else me < self.count - 1
+                sends = me < piece if way == 0 else me > piece
+                body(way, piece, before, sends)
+
+    def start(self):
+        def body(way, piece, before, sends):
+            @pl.when(sends & jnp.logical_not(before))
+            def _():
+                self.buffers[way, 1, piece] = self.own(piece).astype(BF16)
+                self.copy(way, piece).start()
+
+        self.each(body)
+
+    def relay(self):
+        def body(way, piece, before, sends):
+            @pl.when(sends & before)
+            def _():
+                self.copy(way, piece).wait_recv()
+                self.buffers[way, 1, piece] = (self.own(piece) + self.buffers[way, 0, piece].astype(F32)).astype(BF16)
+                self.copy(way, piece).start()
+
+        self.each(body)
+
+    def finish(self, total_ref):
+        me = lax.axis_index(self.axis)
+        total_ref[...] = self.own(me)
+        for way, before in ((0, me > 0), (1, me < self.count - 1)):
+
+            @pl.when(before)
+            def _():
+                self.copy(way, me).wait_recv()
+                total_ref[...] += self.buffers[way, 0, me].astype(F32)
+
+        def body(way, piece, before, sends):
+            @pl.when(sends)
+            def _():
+                self.copy(way, piece).wait_send()
+
+        self.each(body)
+
+
+class LineGather:
+    def __init__(self, axis, count, out_ref, send_sem, recv_sem):
+        self.axis, self.count, self.out_ref = axis, count, out_ref
+        self.send_sem, self.recv_sem = send_sem, recv_sem
+        self.rows = out_ref.shape[0] // count
+
+    def place(self, piece):
+        return self.out_ref.at[pl.ds(pl.multiple_of(piece * self.rows, 16), self.rows), :]
+
+    def copy(self, way, piece):
+        return line_copy(
+            self.axis, 1 - 2 * way, self.place(piece), self.place(piece),
+            self.send_sem.at[way, piece], self.recv_sem.at[way, piece],
+        )
+
+    def start(self, value):
+        me = lax.axis_index(self.axis)
+        self.place(me)[...] = value
+        for way, more in ((0, me < self.count - 1), (1, me > 0)):
+
+            @pl.when(more)
+            def _():
+                self.copy(way, me).start()
+
+    def relay(self, k):
+        me = lax.axis_index(self.axis)
+        for way, piece, there, more in (
+            (0, me - k, me >= k, me < self.count - 1),
+            (1, me + k, me + k < self.count, me > 0),
+        ):
+
+            @pl.when(there)
+            def _():
+                self.copy(way, piece).wait_recv()
+
+            @pl.when(there & more)
+            def _():
+                self.copy(way, piece).start()
+
+    def finish(self):
+        me = lax.axis_index(self.axis)
+        for k in range(self.count):
+            for way, piece, sent in (
+                (0, me - k, (me >= k) & (me < self.count - 1)),
+                (1, me + k, (me + k < self.count) & (me > 0)),
+            ):
+
+                @pl.when(sent)
+                def _():
+                    self.copy(way, piece).wait_send()
+
+
+def greet_neighbours(barrier, axis, count):
     me = lax.axis_index(axis)
-    out = []
-    for index in range(count - 1):
-        peer = lax.rem(me + index + 1, count)
-        out.append(
-            pltpu.make_async_remote_copy(
-                src_ref=source(index, peer), dst_ref=target(index, me), send_sem=send_sem.at[index],
-                recv_sem=recv_sem.at[index], device_id={axis: peer}, device_id_type=pl.DeviceIdType.MESH,
-            )
-        )
-    return out
-
-
-def greet(barrier, axis, count):
-    me = lax.axis_index(axis)
-    for index in range(count - 1):
-        pl.semaphore_signal(
-            barrier, inc=1, device_id={axis: lax.rem(me + index + 1, count)}, device_id_type=pl.DeviceIdType.MESH
-        )
+    for ahead, there in ((1, me < count - 1), (-1, me > 0)):
+
+        @pl.when(there)
+        def _():
+            pl.semaphore_signal(barrier, inc=1, device_id={axis: me + ahead}, device_id_type=pl.DeviceIdType.MESH)
+
+    return (me < count - 1).astype(jnp.int32) + (me > 0).astype(jnp.int32)
 
 
 def settle_kernel(sizes, gq_ref, gk_ref, gv_ref, wq_ref, wk_ref, wv_ref, tokens_ref, first_ref, gain_ref, pack_ref,
                   x_ref, out_ref, share_ref, piece_ref, own, landed, chosen, arrived, sem, pair_send, pair_recv, send_sem,
-                  recv_sem, x_landed, x_send, x_recv):
+                  recv_sem, x_buffers, x_total, x_send, x_recv):
     dp_size, shard_size, count = sizes
     spread = shard_size // 2
     halves = dp_size * spread
@@ -505,10 +626,7 @@
     def target(piece, bit):
         return {"dp": piece // spread, "shard": (piece % spread) * 2 + bit}
 
-    def x_copies():
-        return peer_copies(
-            "expert", count, lambda index, peer: x_ref.at[peer], lambda index, me: x_landed.at[index], x_send, x_recv
-        )
+    line = LineSum("expert", count, x_ref, x_buffers, x_send, x_recv)
 
     def pair_copy():
         return pltpu.make_async_remote_copy(
@@ -534,12 +652,11 @@
                 barrier, inc=1, device_id=target(lax.rem(place + index + 1, halves), side),
                 device_id_type=pl.DeviceIdType.MESH,
             )
-        greet(barrier, "expert", count)
-        pl.semaphore_wait(barrier, halves + count - 1)
-        for copy in x_copies():
-            copy.start()
+        neighbours = greet_neighbours(barrier, "expert", count)
+        pl.semaphore_wait(barrier, halves + neighbours)
         pair_copy().start()
         own_copy().start()
+        line.start()
 
     @pl.when(step == 1)
     def _():
@@ -561,16 +678,14 @@
 
     @pl.when(step == last)
     def _():
+        line.relay()
         total = own[place].astype(F32) + landed[place].astype(F32)
         for index in range(halves - 1):
             send(index).wait()
             total = total + arrived[index].astype(F32)
         share_ref[...] = total.astype(BF16)
-        piece = x_ref[lax.axis_index("expert")].astype(F32)
-        for index, copy in enumerate(x_copies()):
-            copy.wait()
-            piece = piece + x_landed[index].astype(F32)
-        piece_ref[...] = piece.astype(BF16)
+        line.finish(x_total)
+        piece_ref[...] = x_total[...].astype(BF16)
 
 
 def settle(grads, w_qkv, tokens, grad_first, gain, pack, x, sizes):
@@ -579,19 +694,19 @@
     blocked = pl.BlockSpec((block, width), lambda i: (i, 0))
     halves, count = sizes[0] * sizes[1] // 2, pack.shape[1]
     piece = (count, LANES)
-    x = x.reshape(sizes[2], -1, LANES)
+    x_piece = (x.shape[0] // sizes[2], LANES)
     return call(
         functools.partial(settle_kernel, sizes), (rows // block,),
         [blocked] * 3 + [square(width, 0), square(width, 1), square(width, 2), blocked, blocked, whole((1, width)),
                          pl.BlockSpec(memory_space=pl.ANY), whole(x.shape)],
-        [blocked, whole(piece), whole(x.shape[1:])],
-        [shape_of((rows, width), F32), shape_of(piece, BF16), shape_of(x.shape[1:], BF16)],
+        [blocked, whole(piece), whole(x_piece)],
+        [shape_of((rows, width), F32), shape_of(piece, BF16), shape_of(x_piece, BF16)],
         scratch=[pltpu.VMEM((halves,) + piece, BF16), pltpu.VMEM((halves,) + piece, BF16),
                  pltpu.VMEM((halves - 1,) + piece, BF16), pltpu.VMEM((halves - 1,) + piece, BF16),
                  pltpu.SemaphoreType.DMA, pltpu.SemaphoreType.DMA, pltpu.SemaphoreType.DMA,
                  pltpu.SemaphoreType.DMA((halves - 1,)), pltpu.SemaphoreType.DMA((halves - 1,)),
-                 pltpu.VMEM((sizes[2] - 1,) + x.shape[1:], BF16), pltpu.SemaphoreType.DMA((sizes[2] - 1,)),
-                 pltpu.SemaphoreType.DMA((sizes[2] - 1,))],
+                 pltpu.VMEM((2, 2, sizes[2]) + x_piece, BF16), pltpu.VMEM(x_piece, F32),
+                 pltpu.SemaphoreType.DMA((2, sizes[2])), pltpu.SemaphoreType.DMA((2, sizes[2]))],
         flops=6 * rows * width * width, moved=22 * rows * width, collective_id=1,
     )(*grads, w_qkv, w_qkv, w_qkv, tokens, grad_first, gain, pack.reshape((halves, 2) + piece), x)
 
@@ -696,7 +811,7 @@
 BLOCK = 256
 
 
-def ffn_both(x, gy, w_gu, w_down, hidden, expert, owners, out_type):
+def ffn_both(x, gy, w_gu, w_down, hidden, expert, owners, out_type, parts=1, pack=None):
     rows, width = x.shape
     block = BLOCK
     steps = hidden // block
@@ -721,28 +836,26 @@
         )
     out_rows = whole((rows, width))
     count = packed_rows(width, hidden, owners)
-    layout = (by_rows, owners, hidden, 0)
+    layout = (by_rows, owners, hidden, (expert or 0) * count)
+    held = [] if pack is None else [pack]
     copies = 2 * (block // LANES) + block // (hidden // owners) * (width // LANES)
     return call(
         functools.partial(ffn_kernel, out_type, layout, block), (steps,),
-        [whole((rows, width)), grads, gate, up, down],
+        [whole((rows, width)), grads, gate, up, down] + [pl.BlockSpec(memory_space=pl.ANY)] * len(held),
         [out_rows, out_rows, pl.BlockSpec(memory_space=pl.ANY)],
         [shape_of((rows, width), out_type), shape_of((rows, width), out_type),
-         shape_of((owners, count, LANES), BF16)],
+         shape_of((owners, parts * count, LANES), BF16)],
         scratch=[pltpu.VMEM((width, rows), BF16), pltpu.VMEM((rows, width), F32), pltpu.VMEM((rows, width), F32),
                  pltpu.VMEM(stage, BF16), pltpu.VMEM(stage, BF16), pltpu.VMEM((2, block, width), BF16),
                  pltpu.SemaphoreType.DMA((2, copies))],
         flops=18 * rows * width * hidden, moved=12 * width * hidden + 16 * rows * width, trans=rows * hidden,
-    )(x, gy, w_gu, w_gu, w_down)
+        aliases={5: 2} if held else None,
+    )(x, gy, w_gu, w_gu, w_down, *held)
 
 
 def to_panels(array):
     rows, columns = array.shape
     return jnp.transpose(array.reshape(rows, columns // BLOCK, BLOCK), (1, 0, 2)).reshape(-1, BLOCK)
-
-
-def panels_to(rows_array, rows, panels):
-    return jnp.transpose(rows_array.reshape(panels, rows, LANES), (1, 0, 2)).reshape(rows, panels * LANES)
 
 
 def attention_weights_kernel(per, normed_ref, mixed_ref, gq_ref, gk_ref, gv_ref, ga_ref, gains_ref, out_ref, xt):
@@ -874,14 +987,13 @@
     shared_out, grad_shared, shared_pack = ffn_both(
         normed_two, grad_b, shared_weight, shared_weight, shared_hidden, None, group, F32
     )
-    back_rows, out_rows, expert_packs = [], [], []
+    back_rows, out_rows, pack = [], [], None
     for j in range(local_experts):
         y, gx, pack = ffn_both(
-            received[j], received_grad, w_expert_gu, w_expert_down, hidden, j, group, BF16
+            received[j], received_grad, w_expert_gu, w_expert_down, hidden, j, group, BF16, local_experts, pack
         )
         back_rows.append(exchange(gx))
         out_rows.append(y)
-        expert_packs.append(pack)
     base = grad_shared
     for j, rows in enumerate(back_rows[:-1]):
         base = add_part(placed, base, rows, j)
@@ -899,33 +1011,19 @@
         return lax.psum_scatter(pack, GROUP, scatter_dimension=0, tiled=True)[0]
 
     shared_share = spread(shared_pack)
-    expert_shares = [spread(pack) for pack in expert_packs]
+    expert_share = spread(pack)
     input_grad, attention_share, shared_piece = settle(
         grads, attention_weight, tokens, grad_first, gain_one, attention_pack, shared_share,
         (lax.axis_size("dp"), lax.axis_size("shard"), owners),
     )
     returned = exchange_parts(out_rows, owners, "expert")
-    layer_out, attention_share, shared_share = combine(
-        placed, route_gates, live, first_sum, shared_out, returned, attention_share, shared_piece, "expert", owners
-    )
-    attention_share, shared_share = attention_share.astype(F32), shared_share.astype(F32)
-    gu_panels, d_panels = 2 * shared_hidden // LANES, width // LANES
-    qkv_rows, out_rows_count = 3 * d_panels * own, 4 * d_panels * own
-    columns = 2 * hidden // group
-    gu_rows = columns // LANES * width
-    qkv_grad = panels_to(attention_share[:qkv_rows], own, 3 * d_panels)
+    layer_out, expert_gu, expert_down, qkv_grad, out_grad, shared_gu, shared_down, gain_rows = combine(
+        placed, route_gates, live, first_sum, shared_out, returned, attention_share, shared_piece, expert_share,
+        "expert", owners, own, shared_hidden, hidden,
+    )
     grad_gain_one = jnp.sum(w_qkv.astype(F32) * qkv_grad, axis=1) / norm_gains[0].astype(F32)
-    return (
-        layer_out,
-        input_grad,
-        jnp.stack([grad_gain_one, attention_share[out_rows_count, :own]]),
-        qkv_grad,
-        panels_to(attention_share[qkv_rows:out_rows_count], own, d_panels),
-        panels_to(shared_share[: gu_panels * own], own, gu_panels),
-        panels_to(shared_share[gu_panels * own :], shared_hidden // group, d_panels),
-        jnp.stack([panels_to(share[:gu_rows], width, columns // LANES) for share in expert_shares]).astype(F32),
-        jnp.stack([panels_to(share[gu_rows:], hidden // group, d_panels) for share in expert_shares]).astype(F32),
-    )
+    grad_gains = jnp.stack([grad_gain_one, gain_rows[0, :own]])
+    return layer_out, input_grad, grad_gains, qkv_grad, out_grad, shared_gu, shared_down, expert_gu, expert_down
 
 
 def exchange_parts(parts, owners, axis):

time: 718 us -> 742 us (1.033)
  waiting for transfers between devices: 82.7 us -> 214 us
  blocking collectives: 182 us -> 92.8 us
  Pallas kernels: 355 us -> 347 us
    all_to_all x3 -> x5, waiting for transfers between devices: 79.2 us -> 174 us  [exchange(): lax.all_to_all(rows.reshape(owners, count, width), 'expert', split_axis=0...]
    all_to_all x2 -> x0, blocking collectives: 90.4 us -> none  [exchange(): lax.all_to_all(rows.reshape(owners, count, width), 'expert', split_axis=0...]
    all_gather x1, waiting for transfers between devices: 0.02 us -> 22.3 us  [local(): lax.all_gather(jnp.concatenate([to_panels(w_shared_gu), to_panels(w_share...]
    all_gather x1, waiting for transfers between devices: 3.37 us -> 18.3 us  [local(): lax.all_gather(jnp.concatenate([w_qkv, w_out], axis=1), GROUP, axis=0, ti...]
    reduce_scatter x3 -> x2, starting transfers between devices: 11.8 us -> 0.08 us  [spread(): return lax.psum_scatter(pack, GROUP, scatter_dimension=0, tiled=True)[0]]
    all_to_all x3 -> x5, starting transfers between devices: 15.7 us -> 22.4 us  [exchange(): lax.all_to_all(rows.reshape(owners, count, width), 'expert', split_axis=0...]
    unnamed x38 -> x51, local copies, waits for them, and re-layouts: 11.8 us -> 16.9 us
  transfers between devices with their start and end apart: 8 -> 9, of which waited for: 4 -> 6; matrix products, arithmetic and copies ran while one was open for 4% -> 3% of each run, Pallas kernels for 36% -> 35%
where the time goes in v5:
time: 742 us; the launch traced here: 731 us
  Pallas kernels  347 us (47%)
  waiting for transfers between devices  214 us (29%)
  blocking collectives  92.8 us (13%)
  local copies, waits for them, and re-layouts  24.7 us (3%)
  starting transfers between devices  22.5 us (3%)
  between operations  15.2 us (2%)
  other arithmetic  15 us (2%)
    all_to_all x5, waiting for transfers between devices, exchange(): lax.all_to_all(rows.reshape(owners, count, width), 'expert', split_axis=0...  174 us
    pallas_call x3, Pallas kernels, ffn_both(): call(functools.partial(ffn_kernel, out_type, layout, block), (steps,), [w...  124 us
    all_to_all x1, blocking collectives, exchange_parts(): back = lax.all_to_all(joined, axis, split_axis=0, concat_axis=0, tiled=True)  82.4 us
    pallas_call x1, Pallas kernels, combine(): call(functools.partial(combine_kernel, parts, axis, count, own, gu_panels...  51.5 us
    pallas_call x1, Pallas kernels, settle(): call(functools.partial(settle_kernel, sizes), (rows // block,), [blocked]...  41.8 us
    pallas_call x1, Pallas kernels, attend_backward(): call(functools.partial(attend_backward_kernel, head_dim, block), (seqs, p...  34.1 us
    pallas_call x1, Pallas kernels, attend_forward(): call(functools.partial(attend_forward_kernel, head_dim, block), (seqs, pa...  33.1 us
    all_to_all x5, starting transfers between devices, exchange(): lax.all_to_all(rows.reshape(owners, count, width), 'expert', split_axis=0...  22.4 us
  transfers between devices with their start and end apart: 9, of which 6 were waited for; matrix products, arithmetic and copies ran while one was open for 3% of the time, Pallas kernels for 35%

profile of v5, /device:TPU:0, one launch (start us, length us, event | category | flops | bytes accessed | tf_op | source)
XLA Modules:
  0.0 731.3 jit_solution(7436758425083461969)
XLA Ops:
  14.5 10.4 %all-gather.1 = bf16[8,96,2]{1,2,0:T(2,128)(2,1)S(1)} all-gather(bf16[1,96,2]{1,2,0:T(2,128)(2,1)S(1)} %bitcast.95), channel_id=1, replica_groups=mesh['dp'=2,'expert'=4,'shard'=4] {'dp','shard'}, dimensions={0}, use_global_device_ids=true | all-gather | bytes 3456 | tf_op jit(solution)/shard_map/all_gather | solution.py:941
  33.7 18.3 %all-gather.5.cloned.1.call-done.wq_ref.wk_ref.wv_ref.weight_ref = bf16[768,3072]{1,0:T(8,128)(2,1)} async-done(((bf16[96,3072]{1,0:T(8,128)(2,1)}), bf16[768,3072]{1,0:T(8,128)(2,1)}) %all-gather.5.cloned.1.call-update) | async-done | bytes 4718608 | tf_op jit(solution)/shard_map/all_gather | solution.py:942
  52.0 33.1 %shard_map.192 = (bf16[1024,768]{1,0:T(8,128)(2,1)}, bf16[1024,768]{1,0:T(8,128)(2,1)}, bf16[1024,768]{1,0:T(8,128)(2,1)}, bf16[1024,768]{1,0:T(8,128)(2,1)}, f32[96,1024]{1,0:T(8,128)}) custom-call(bf16[1024,768]{1,0:T(8,128)(2,1)} %shard_map.191.x_ref.normed_ref, bf16[768,3072]{1,0:T(8,128)(2,1)} %all-gather.5.cloned.1.call-done.wq_ref.wk_ref.wv_ref.weight_ref, ...), custom_call_target="tpu_custom_call" | custom-call | flops 6845104128 | bytes 12582912 | tf_op jit(solution)/shard_map/pallas_call | solution.py:140
  85.1 5.8 shard_map.193
  90.8 22.3 %all-gather.7.cloned.1.call-done = bf16[18432,256]{1,0:T(8,128)(2,1)} async-done(((bf16[2304,256]{1,0:T(8,128)(2,1)}), bf16[18432,256]{1,0:T(8,128)(2,1)}) %all-gather.7.cloned.1.call-update) | async-done | bytes 9437200 | tf_op jit(solution)/shard_map/all_gather | solution.py:943
  113.2 38.7 %shard_map.194 = (f32[1024,768]{1,0:T(8,128)}, f32[1024,768]{1,0:T(8,128)}, bf16[8,4608,128]{2,1,0:T(8,128)(2,1)}) custom-call(bf16[1024,768]{1,0:T(8,128)(2,1)} %get-tuple-element.45.x_ref, bf16[1024,768]{1,0:T(8,128)(2,1)} %broadcast_select_fusion.gy_ref.x_ref, bf16[8,2304,256]{2,1,0:T(8,128)(2,1)} %bitcast.96, bf16[8,2304,256]{2,1,0:T(8,128)(2,1)} %bitcast.97, ...), custom_call_target="tpu_custom_call" | custom-call | flops 28991029248 | bytes 31457280 | tf_op jit(solution)/shard_map/pallas_call | solution.py:842
  151.9 8.6 %shard_map.196 = bf16[2304,768]{1,0:T(8,128)(2,1)} custom-call(s32[2,1024]{1,0:T(2,128)} %shard_map.190.dest_ref, f32[2,1024]{1,0:T(2,128)} %bitcast.92, bf16[1024,768]{1,0:T(8,128)(2,1)} %broadcast_select_fusion.gy_ref.x_ref), custom_call_target="tpu_custom_call" | custom-call | flops 3623878656 | bytes 5111808 | tf_op jit(solution)/shard_map/pallas_call | solution.py:312
  160.5 5.2 all-to-all-start.1
  167.7 5.2 shard_map.195
  172.9 72.6 %all-to-all-done.1.gy_ref = bf16[4,576,768]{2,1,0:T(8,128)(2,1)} async-done(((bf16[4,576,768]{2,1,0:T(8,128)(2,1)}), bf16[4,576,768]{2,1,0:T(8,128)(2,1)}, u32[]{:S(2)}, u32[]{:S(2)}) %all-to-all-start.1) | async-done | bytes 3538976 | tf_op jit(solution)/shard_map/all_to_all | solution.py:971
  249.0 5.1 shard_map.198
  254.2 35.8 %all-to-all-done = bf16[4,288,768]{2,1,0:T(8,128)(2,1)S(1)} async-done(((bf16[4,288,768]{2,1,0:T(8,128)(2,1)}), bf16[4,288,768]{2,1,0:T(8,128)(2,1)S(1)}, u32[]{:S(2)}, u32[]{:S(2)}) %all-to-all-start) | async-done | bytes 1769504 | tf_op jit(solution)/shard_map/all_to_all | solution.py:971
  294.8 42.8 %shard_map.197 = (bf16[1152,768]{1,0:T(8,128)(2,1)}, bf16[1152,768]{1,0:T(8,128)(2,1)}, bf16[8,9216,128]{2,1,0:T(8,128)(2,1)}) custom-call(bf16[1152,768]{1,0:T(8,128)(2,1)} %bitcast.83, bf16[4,576,768]{2,1,0:T(8,128)(2,1)} %all-to-all-done.1.gy_ref, bf16[2,768,4096]{2,1,0:T(8,128)(2,1)} %wu_ref.3, bf16[2,768,4096]{2,1,0:T(8,128)(2,1)} %wu_ref.3, ...), custom_call_target="tpu_custom_call" | custom-call | flops 32614907904 | bytes 33030144 | tf_op jit(solution)/shard_map/pallas_call | solution.py:842
  338.8 42.7 %shard_map.199 = (bf16[1152,768]{1,0:T(8,128)(2,1)}, bf16[1152,768]{1,0:T(8,128)(2,1)}, bf16[8,9216,128]{2,1,0:T(8,128)(2,1)}) custom-call(bf16[1152,768]{1,0:T(8,128)(2,1)} %bitcast.84, bf16[4,576,768]{2,1,0:T(8,128)(2,1)} %all-to-all-done.1.gy_ref, bf16[2,768,4096]{2,1,0:T(8,128)(2,1)} %wu_ref.3, ...), custom_call_target="tpu_custom_call", output_to_operand_aliasing={{2}: (5, {})} | custom-call | flops 32614907904 | bytes 33030144 | tf_op jit(solution)/shard_map/pallas_call | solution.py:842
  381.6 5.3 all-to-all-start.4
  388.9 38.3 %all-to-all-done.4 = bf16[4,288,768]{2,1,0:T(8,128)(2,1)} async-done(((bf16[4,288,768]{2,1,0:T(8,128)(2,1)}), bf16[4,288,768]{2,1,0:T(8,128)(2,1)}, u32[]{:S(2)}, u32[]{:S(2)}) %all-to-all-start.4) | async-done | bytes 1769504 | tf_op jit(solution)/shard_map/all_to_all | solution.py:971
  427.1 82.4 %all_to_all.30 = bf16[4,576,768]{2,1,0:T(8,128)(2,1)S(1)} all-to-all(bf16[4,576,768]{2,1,0:T(8,128)(2,1)} %pad_maximum_fusion), channel_id=1, replica_groups=mesh['dp'=2,'expert'=4,'shard'=4] {'expert'}, dimensions={0} | all-to-all | bytes 7077888 | tf_op jit(solution)/shard_map/all_to_all | solution.py:1033
  521.0 6.6 shard_map.200.base_ref
  527.6 26.9 %all-to-all-done.5 = bf16[4,288,768]{2,1,0:T(8,128)(2,1)} async-done(((bf16[4,288,768]{2,1,0:T(8,128)(2,1)}), bf16[4,288,768]{2,1,0:T(8,128)(2,1)}, u32[]{:S(2)}, u32[]{:S(2)}) %all-to-all-start.5) | async-done | bytes 1769504 | tf_op jit(solution)/shard_map/all_to_all | solution.py:971
  554.5 11.0 %shard_map.201 = (f32[1024,768]{1,0:T(8,128)}, bf16[1024,768]{1,0:T(8,128)(2,1)}, bf16[1024,768]{1,0:T(8,128)(2,1)}, f32[1,768]{1,0:T(1,128)}) custom-call(s32[1024,2]{1,0:T(8,128)} %fusion.4.dest_ref, f32[1024,1]{1,0:T(8,128)} %fusion.16.live_ref, bf16[1024,768]{1,0:T(8,128)(2,1)} %cot_ref.1, f32[1024,768]{1,0:T(8,128)} %get-tuple-element.44.sum_ref, ...), custom_call_target="tpu_custom_call" | custom-call | flops 3019898880 | bytes 14155776 | tf_op jit(solution)/shard_map/pallas_call | solution.py:473
  566.9 34.1 %shard_map.202 = (bf16[1024,768]{1,0:T(8,128)(2,1)}, bf16[1024,768]{1,0:T(8,128)(2,1)}, bf16[1024,768]{1,0:T(8,128)(2,1)}) custom-call(bf16[1024,768]{1,0:T(8,128)(2,1)} %get-tuple-element.50.q_ref, bf16[1024,768]{1,0:T(8,128)(2,1)} %get-tuple-element.51.k_ref, bf16[1024,768]{1,0:T(8,128)(2,1)} %get-tuple-element.52.v_ref, ...), custom_call_target="tpu_custom_call" | custom-call | flops 8053063680 | bytes 12582912 | tf_op jit(solution)/shard_map/pallas_call | solution.py:211
  601.0 14.5 %shard_map.203 = bf16[8,2496,128]{2,1,0:T(8,128)(2,1)} custom-call(bf16[1024,768]{1,0:T(8,128)(2,1)} %shard_map.191.x_ref.normed_ref, bf16[1024,768]{1,0:T(8,128)(2,1)} %get-tuple-element.43.mixed_ref.o_ref, bf16[1024,768]{1,0:T(8,128)(2,1)} %get-tuple-element.58.gq_ref, bf16[1024,768]{1,0:T(8,128)(2,1)} %get-tuple-element.59.gk_ref, ...), custom_call_target="tpu_custom_call" | custom-call | flops 4831838208 | bytes 12582912 | tf_op jit(solution)/shard_map/pallas_call | solution.py:903
  615.5 41.8 %shard_map.204 = (f32[1024,768]{1,0:T(8,128)}, bf16[2496,128]{1,0:T(8,128)(2,1)}, bf16[1152,128]{1,0:T(8,128)(2,1)}) custom-call(bf16[1024,768]{1,0:T(8,128)(2,1)} %get-tuple-element.58.gq_ref, bf16[1024,768]{1,0:T(8,128)(2,1)} %get-tuple-element.59.gk_ref, bf16[1024,768]{1,0:T(8,128)(2,1)} %get-tuple-element.60.gv_ref, ...), custom_call_target="tpu_custom_call" | custom-call | flops 3623878656 | bytes 17301504 | tf_op jit(solution)/shard_map/pallas_call | solution.py:698
  657.3 51.5 %shard_map.205 = (bf16[1024,768]{1,0:T(8,128)(2,1)}, f32[2,768,512]{2,1,0:T(8,128)}, f32[2,256,768]{2,1,0:T(8,128)}, f32[96,2304]{1,0:T(8,128)}, f32[96,768]{1,0...) custom-call(s32[1024,2]{1,0:T(8,128)} %fusion.4.dest_ref, f32[1024,2]{1,0:T(8,128)} %copy.104.gates_ref, ...), custom_call_target="tpu_custom_call" | custom-call | flops 7247757312 | bytes 11403264 | tf_op jit(solution)/shard_map/pallas_call | solution.py:406
  (98 shorter events, 57.4 us)
Async XLA Ops:
  7.2 2.1 copy-start.12
  7.2 44.8 %all-gather.5.cloned.1.call-start = ((), (), s32[]{:S(2)}) async-start(), calls=%async_computation.8 | async-start | bytes 5308416 | tf_op jit(solution)/shard_map/all_gather | solution.py:942
  9.3 103.9 %all-gather.7.cloned.1.call-start = ((), (), s32[]{:S(2)}) async-start(), calls=%async_computation.11 | async-start | bytes 10616832 | tf_op jit(solution)/shard_map/all_gather | solution.py:943
  11.7 603.8 %reduce-scatter.3.cloned.1.call-start = ((), (), s32[]{:S(2)}) async-start(), calls=%async_computation.9 | async-start | bytes 10616832 | tf_op jit(solution)/shard_map/reduce_scatter | solution.py:1011
  12.4 2.1 copy-start.18
  14.5 17.9 %copy-start = (bf16[1024,768]{1,0:T(8,128)(2,1)S(1)}, bf16[1024,768]{1,0:T(8,128)(2,1)}, u32[]{:S(2)}) copy-start(bf16[1024,768]{1,0:T(8,128)(2,1)} %cot_ref.1) | copy-start | bytes 4718596
  160.5 5.2 copy-start.17
  160.5 85.0 %all-to-all-start.1 = ((bf16[4,576,768]{2,1,0:T(8,128)(2,1)}), bf16[4,576,768]{2,1,0:T(8,128)(2,1)}, u32[]{:S(2)}, u32[]{:S(2)}) async-start(bf16[4,576,768]{2,1,0:T(8,128)(2,1)} %bitcast.72), calls=%async_computation.1 | async-start | bytes 7077888 | tf_op jit(solution)/shard_map/all_to_all | solution.py:971
  165.9 7.0 copy-start.1
  245.5 44.5 %all-to-all-start = ((bf16[4,288,768]{2,1,0:T(8,128)(2,1)}), bf16[4,288,768]{2,1,0:T(8,128)(2,1)S(1)}, u32[]{:S(2)}, u32[]{:S(2)}) async-start(bf16[4,288,768]{2,1,0:T(8,128)(2,1)} %bitcast.86), calls=%async_computation | async-start | bytes 3538944 | tf_op jit(solution)/shard_map/all_to_all | solution.py:971
  291.2 46.5 %all-to-all-start.2 = ((bf16[4,288,768]{2,1,0:T(8,128)(2,1)}), bf16[4,288,768]{2,1,0:T(8,128)(2,1)S(1)}, u32[]{:S(2)}, u32[]{:S(2)}) async-start(bf16[4,288,768]{2,1,0:T(8,128)(2,1)} %bitcast.85), calls=%async_computation.2 | async-start | bytes 3538944 | tf_op jit(solution)/shard_map/all_to_all | solution.py:971
  294.8 362.5 %reduce-scatter.5.cloned.1.call-start = ((), (), s32[]{:S(2)}) async-start(), calls=%async_computation.10 | async-start | bytes 21233664 | tf_op jit(solution)/shard_map/reduce_scatter | solution.py:1011
  381.6 5.3 copy-start.5
  381.6 5.3 copy-start.6
  381.6 45.5 %all-to-all-start.4 = ((bf16[4,288,768]{2,1,0:T(8,128)(2,1)}), bf16[4,288,768]{2,1,0:T(8,128)(2,1)}, u32[]{:S(2)}, u32[]{:S(2)}) async-start(bf16[4,288,768]{2,1,0:T(8,128)(2,1)} %bitcast.82), calls=%async_computation.4 | async-start | bytes 3538944 | tf_op jit(solution)/shard_map/all_to_all | solution.py:971
  509.5 4.8 copy-start.16
  509.5 45.0 %all-to-all-start.5 = ((bf16[4,288,768]{2,1,0:T(8,128)(2,1)}), bf16[4,288,768]{2,1,0:T(8,128)(2,1)}, u32[]{:S(2)}, u32[]{:S(2)}) async-start(bf16[4,288,768]{2,1,0:T(8,128)(2,1)} %bitcast.81), calls=%async_computation.5 | async-start | bytes 3538944 | tf_op jit(solution)/shard_map/all_to_all | solution.py:971
  657.3 51.5 %copy-start.9 = (bf16[96,2304]{1,0:T(8,128)(2,1)S(1)}, bf16[96,2304]{1,0:T(8,128)(2,1)}, u32[]{:S(2)}) copy-start(bf16[96,2304]{1,0:T(8,128)(2,1)} %param.18) | copy-start | bytes 1327108
  657.3 52.9 %copy-start.19 = (bf16[2,96]{1,0:T(2,128)(2,1)S(1)}, bf16[2,96]{1,0:T(2,128)(2,1)}, u32[]{:S(2)}) copy-start(bf16[2,96]{1,0:T(2,128)(2,1)} %param.17) | copy-start | bytes 1156
  710.2 4.1 copy-start.3
  714.3 2.7 copy-start.15
  717.0 2.0 copy-start.13
  717.8 2.8 copy-start.4
  720.6 2.5 copy-start.10
  (5 other events, 6.9 us)
Sparse Core Ops, SparseCore 0:
  10.4 41.4 all-gather.4
  54.4 58.6 all-gather.6
  152.0 76.8 reduce-scatter.2
  381.7 126.9 reduce-scatter.4

commit v6 on v5

--- a/solution.py
+++ b/solution.py
@@ -259,7 +259,7 @@
     )(mixed, tokens, weight, gain)
 
 
-def slots_kernel(experts, capacity, routes_ref, live_ref, dest_ref):
+def slots_kernel(experts, parts, capacity, routes_ref, live_ref, rows_ref, columns_ref):
     top, tokens = routes_ref.shape
     live = live_ref[...]
     number = lax.broadcasted_iota(jnp.int32, (experts, tokens), 0)
@@ -274,28 +274,35 @@
     ).astype(BF16)
     ranks = dot_nn(jnp.concatenate(hits, axis=0).astype(BF16), earlier)
     before = jnp.zeros((experts, 1), F32)
+    expert = lax.broadcasted_iota(jnp.int32, (experts, tokens), 0)
+    start = ((expert % parts) * (experts // parts) + expert // parts) * capacity
+    found = []
     for k in range(top):
-        rank = ranks[k * experts : (k + 1) * experts, :]
-        place = number.astype(F32) * capacity + before + rank - 1.0
-        slot = jnp.sum(hits[k] * place, axis=0, keepdims=True).astype(jnp.int32)
-        dest_ref[pl.ds(k, 1), :] = jnp.where(live > 0, slot, experts * capacity)
+        rank = ranks[k * experts : (k + 1) * experts, :] + before - 1.0
+        for first in (number * capacity, start):
+            slot = jnp.sum(hits[k] * (first.astype(F32) + rank), axis=0, keepdims=True).astype(jnp.int32)
+            found.append(jnp.where(live > 0, slot, experts * capacity))
         before = before + jnp.sum(hits[k], axis=1, keepdims=True)
-
-
-def slots_of(routes_t, live_row, experts, capacity):
+    table = jnp.concatenate(found[0::2] + found[1::2] + [jnp.zeros((8 - 2 * top, tokens), jnp.int32)], axis=0)
+    rows_ref[...] = table
+    columns_ref[...] = table.T
+
+
+def slots_of(routes_t, live_row, experts, parts, capacity):
     top, tokens = routes_t.shape
     return call(
-        functools.partial(slots_kernel, experts, capacity), (1,),
-        [whole((top, tokens)), whole((1, tokens))], whole((top, tokens)), shape_of((top, tokens), jnp.int32),
+        functools.partial(slots_kernel, experts, parts, capacity), (1,),
+        [whole((top, tokens)), whole((1, tokens))], [whole((8, tokens)), whole((tokens, 8))],
+        [shape_of((8, tokens), jnp.int32), shape_of((tokens, 8), jnp.int32)],
         flops=2 * top * experts * tokens * tokens, moved=16 * tokens,
     )(routes_t, live_row)
 
 
-def dispatch_kernel(gated, first, dest_ref, gates_ref, x_ref, out_ref):
-    top, tokens = dest_ref.shape
+def dispatch_kernel(gated, first, base, dest_ref, gates_ref, x_ref, out_ref):
+    top, tokens = gates_ref.shape
     capacity = out_ref.shape[0]
     slot = lax.broadcasted_iota(jnp.int32, (capacity, tokens), 0) + (first + pl.program_id(0)) * capacity
-    hits = [slot == dest_ref[pl.ds(k, 1), :] for k in range(top)]
+    hits = [slot == dest_ref[pl.ds(base + k, 1), :] for k in range(top)]
     chosen = functools.reduce(jnp.logical_or, hits)
     rows = dot_nn(jnp.where(chosen, 1.0, 0.0).astype(BF16), x_ref[...])
     if gated:
@@ -306,12 +313,12 @@
     out_ref[...] = rows.astype(BF16)
 
 
-def dispatch(dest_t, gates_t, x, experts, capacity, gated, first):
-    top, tokens = dest_t.shape
+def dispatch(dest_t, gates_t, x, experts, capacity, gated, first, base):
+    top, tokens = gates_t.shape
     width = x.shape[1]
     return call(
-        functools.partial(dispatch_kernel, gated, first), (experts,),
-        [whole((top, tokens)), whole((top, tokens)), whole((tokens, width))],
+        functools.partial(dispatch_kernel, gated, first, base), (experts,),
+        [whole(dest_t.shape), whole((top, tokens)), whole((tokens, width))],
         pl.BlockSpec((capacity, width), lambda e: (e, 0)),
         shape_of((experts * capacity, width), BF16),
         flops=2 * experts * capacity * tokens * width, moved=2 * (experts * capacity + tokens) * width,
@@ -323,15 +330,13 @@
         target[:, pl.ds(p * LANES, LANES)] = source[pl.ds(start + p * rows, rows), :].astype(F32)
 
 
-def combine_kernel(parts, axis, count, own, gu_panels, experts, dest_ref, gates_ref, live_ref, sum_ref, shared_ref, *rest):
-    y_refs = rest[:parts]
-    x_ref, piece_ref, pack_ref, out_ref, egu_ref, ed_ref, qkv_ref, wo_ref, sgu_ref, sd_ref, gain_ref = rest[parts : parts + 11]
-    buffers, total_x, all_x, all_p, sum_send, sum_recv, x_send, x_recv, p_send, p_recv = rest[parts + 11 :]
+def combine_kernel(axis, count, own, gu_panels, experts, dest_ref, gates_ref, live_ref, sum_ref, shared_ref, y_ref, *rest):
+    x_ref, p_ref, pack_ref, out_ref, egu_ref, ed_ref, qkv_ref, wo_ref, sgu_ref, sd_ref, gain_ref = rest[:11]
+    buffers, total_x, all_x, sum_send, sum_recv, x_send, x_recv = rest[11:]
     step = pl.program_id(0)
     last = pl.num_programs(0) - 1
     line = LineSum(axis, count, x_ref, buffers, sum_send, sum_recv)
     gather_x = LineGather(axis, count, all_x, x_send, x_recv)
-    gather_p = LineGather(axis, count, all_p, p_send, p_recv)
     width = out_ref.shape[1]
     d_panels = width // LANES
     packed = pack_ref.shape[0] // experts
@@ -342,7 +347,8 @@
         barrier = pltpu.get_barrier_semaphore()
         pl.semaphore_wait(barrier, greet_neighbours(barrier, axis, count))
         line.start()
-        gather_p.start(piece_ref[...])
+        unpack(p_ref, 0, own, gu_panels, sgu_ref)
+        unpack(p_ref, gu_panels * own, sd_ref.shape[0], d_panels, sd_ref)
         for e in range(experts):
             unpack(pack_ref, e * packed + e_panels * width, ed_ref.shape[1], d_panels, ed_ref.at[e])
 
@@ -351,101 +357,145 @@
             rows = pl.ds(pl.multiple_of(e * packed + p * width + step * e_rows, 16), e_rows)
             egu_ref[e, :, pl.ds(p * LANES, LANES)] = pack_ref[rows, :].astype(F32)
 
-    block, top = dest_ref.shape
+    block, top = gates_ref.shape
     total = sum_ref[...] + shared_ref[...]
     dest = dest_ref[...]
     gates = gates_ref[...]
-    for index, y_ref in enumerate(y_refs):
-        y = y_ref[...]
-        slot = slot_numbers(block, y_ref.shape[0], index)
-        for k in range(top):
-            hit = jnp.where(slot == dest[:, k : k + 1], 1.0, 0.0).astype(BF16)
-            total = total + dot_nn(hit, y) * gates[:, k : k + 1]
+    slot = slot_numbers(block, y_ref.shape[0], 0)
+    for k in range(top):
+        hit = jnp.where(slot == dest[:, k : k + 1], 1.0, 0.0).astype(BF16)
+        total = total + dot_nn(hit, y_ref[...]) * gates[:, k : k + 1]
     out_ref[...] = (live_ref[...] * total).astype(BF16)
 
     @pl.when(step == jnp.minimum(1, last))
     def _():
         line.relay()
-        gather_p.relay(1)
-
-    @pl.when(step == last)
+
+    @pl.when(step == jnp.minimum(2, last))
     def _():
         line.finish(total_x)
         gather_x.start(total_x[...].astype(BF16))
+
+    @pl.when(step == last)
+    def _():
         for k in range(1, count):
-            if k > 1:
-                gather_p.relay(k)
             gather_x.relay(k)
-        gather_p.finish()
-        unpack(all_p, 0, own, gu_panels, sgu_ref)
-        unpack(all_p, gu_panels * own, sd_ref.shape[0], d_panels, sd_ref)
         gather_x.finish()
         unpack(all_x, 0, own, 3 * d_panels, qkv_ref)
         unpack(all_x, 3 * d_panels * own, own, d_panels, wo_ref)
         gain_ref[...] = all_x[pl.ds(4 * d_panels * own, gain_ref.shape[0]), :].astype(F32)
 
 
-def combine(dest, gates, live, first_sum, shared_out, returned, x, piece, pack, axis, count, own, shared_hidden, hidden):
+def combine(dest, gates, live, first_sum, shared_out, returned, x, piece, pack, parts, axis, count, own, shared_hidden, hidden):
     rows, width = first_sum.shape
-    top = dest.shape[1]
+    top = gates.shape[1]
     block = min(256, rows)
     steps = rows // block
-    parts = len(returned)
     blocked = pl.BlockSpec((block, width), lambda i: (i, 0))
-    narrow = pl.BlockSpec((block, top), lambda i: (i, 0))
-    slots = sum(y.shape[0] for y in returned)
+    slots = returned.shape[0]
     group = width // own
     columns = 2 * hidden // group
     gu_panels = 2 * shared_hidden // LANES
-    x_piece, p_rows = (x.shape[0] // count, LANES), count * piece.shape[0]
+    x_piece = (x.shape[0] // count, LANES)
     outs = [
         (parts, width, columns), (parts, hidden // group, width), (own, 3 * width), (own, width), (own, 2 * shared_hidden),
         (shared_hidden // group, width), (8, LANES),
     ]
     sems = pltpu.SemaphoreType.DMA((2, count))
     return call(
-        functools.partial(combine_kernel, parts, axis, count, own, gu_panels, parts), (steps,),
-        [narrow, narrow, pl.BlockSpec((block, 1), lambda i: (i, 0)), blocked, blocked]
-        + [whole(y.shape) for y in returned] + [whole(x.shape), whole(piece.shape), whole(pack.shape)],
+        functools.partial(combine_kernel, axis, count, own, gu_panels, parts), (steps,),
+        [pl.BlockSpec((block, dest.shape[1]), lambda i: (i, 0)), pl.BlockSpec((block, top), lambda i: (i, 0)), pl.BlockSpec((block, 1), lambda i: (i, 0)), blocked, blocked]
+        + [whole(returned.shape), whole(x.shape), whole(piece.shape), whole(pack.shape)],
         [blocked, pl.BlockSpec((parts, width // steps, columns), lambda i: (0, i, 0))] + [whole(shape) for shape in outs[1:]],
         [shape_of((rows, width), BF16)] + [shape_of(shape, F32) for shape in outs],
-        scratch=[pltpu.VMEM((2, 2, count) + x_piece, BF16), pltpu.VMEM(x_piece, F32), pltpu.VMEM(x.shape, BF16),
-                 pltpu.VMEM((p_rows, LANES), BF16)] + [sems] * 6,
+        scratch=[pltpu.VMEM((2, 2, count) + x_piece, BF16), pltpu.VMEM(x_piece, F32), pltpu.VMEM(x.shape, BF16)] + [sems] * 4,
         flops=4 * rows * slots * width, moved=10 * rows * width + 2 * slots * width, collective_id=2,
-    )(dest, gates, live, first_sum, shared_out, *returned, x, piece, pack)
+    )(dest, gates, live, first_sum, shared_out, returned, x, piece, pack)
 
 
 def slot_numbers(block, slots, part):
     return lax.broadcasted_iota(jnp.int32, (block, slots), 1) + part * slots
 
 
-def gathered(dest_ref, y_ref, part):
-    block, top = dest_ref.shape
-    dest = dest_ref[...]
+def gathered(top, dest_ref, y_ref, part):
+    block = dest_ref.shape[0]
+    dest = dest_ref[:, top : 2 * top]
     slot = slot_numbers(block, y_ref.shape[0], part)
     hit = functools.reduce(jnp.logical_or, [slot == dest[:, k : k + 1] for k in range(top)])
     return dot_nn(jnp.where(hit, 1.0, 0.0).astype(BF16), y_ref[...])
 
 
-def add_part_kernel(part, dest_ref, base_ref, y_ref, out_ref):
-    out_ref[...] = base_ref[...] + gathered(dest_ref, y_ref, part)
-
-
-def add_part(dest, base, rows_of, part):
+class Exchange:
+    def __init__(self, axis, count, sent_ref, kept_ref, own_sem, send_sem, recv_sem):
+        self.axis, self.count = axis, count
+        me = lax.axis_index(axis)
+        self.peers = [lax.rem(me + ahead, count) for ahead in range(1, count)]
+        self.me, self.sent_ref, self.kept_ref = me, sent_ref, kept_ref
+        self.own_sem, self.send_sem, self.recv_sem = own_sem, send_sem, recv_sem
+
+    def copies(self):
+        out = [pltpu.make_async_copy(self.sent_ref.at[self.me], self.kept_ref.at[self.me], self.own_sem)]
+        for index, peer in enumerate(self.peers):
+            out.append(
+                pltpu.make_async_remote_copy(
+                    src_ref=self.sent_ref.at[peer], dst_ref=self.kept_ref.at[self.me],
+                    send_sem=self.send_sem.at[index], recv_sem=self.recv_sem.at[index],
+                    device_id={self.axis: peer}, device_id_type=pl.DeviceIdType.MESH,
+                )
+            )
+        return out
+
+    def start(self):
+        barrier = pltpu.get_barrier_semaphore()
+        for peer in self.peers:
+            pl.semaphore_signal(barrier, inc=1, device_id={self.axis: peer}, device_id_type=pl.DeviceIdType.MESH)
+        pl.semaphore_wait(barrier, self.count - 1)
+        for copy in self.copies():
+            copy.start()
+
+    def wait(self):
+        for copy in self.copies():
+            copy.wait()
+
+    @staticmethod
+    def scratch(count):
+        sems = pltpu.SemaphoreType.DMA((count - 1,))
+        return [pltpu.SemaphoreType.DMA, sems, sems]
+
+
+def add_part_kernel(part, top, axis, count, dest_ref, base_ref, y_ref, sent_ref, out_ref, kept_ref, *sems):
+    exchange = Exchange(axis, count, sent_ref, kept_ref, *sems)
+
+    @pl.when(pl.program_id(0) == 0)
+    def _():
+        exchange.start()
+
+    out_ref[...] = base_ref[...] + gathered(top, dest_ref, y_ref, part)
+
+    @pl.when(pl.program_id(0) == pl.num_programs(0) - 1)
+    def _():
+        exchange.wait()
+
+
+def add_part(top, dest, base, rows_of, part, sent, axis, count, collective_id):
     rows, width = base.shape
     block = min(256, rows)
     blocked = pl.BlockSpec((block, width), lambda i: (i, 0))
-    return call(
-        functools.partial(add_part_kernel, part), (rows // block,),
-        [pl.BlockSpec((block, dest.shape[1]), lambda i: (i, 0)), blocked, whole(rows_of.shape)],
-        blocked, shape_of((rows, width), F32),
-        flops=2 * rows * rows_of.shape[0] * width, moved=8 * rows * width,
-    )(dest, base, rows_of)
-
-
-def norm_two_back_kernel(part, dest_ref, live_ref, cot_ref, sum_ref, base_ref, gain_ref, weight_ref, y_ref,
+    hbm = pl.BlockSpec(memory_space=pl.ANY)
+    sent = sent.reshape(count, -1, width)
+    out, kept = call(
+        functools.partial(add_part_kernel, part, top, axis, count), (rows // block,),
+        [pl.BlockSpec((block, dest.shape[1]), lambda i: (i, 0)), blocked, whole(rows_of.shape), hbm],
+        [blocked, hbm], [shape_of((rows, width), F32), shape_of(sent.shape, BF16)],
+        scratch=Exchange.scratch(count),
+        flops=2 * rows * rows_of.shape[0] * width, moved=8 * rows * width, collective_id=collective_id,
+    )(dest, base, rows_of, sent)
+    return out, kept.reshape(-1, width)
+
+
+def norm_two_back_kernel(part, top, dest_ref, live_ref, cot_ref, sum_ref, base_ref, gain_ref, weight_ref, y_ref,
                          first_ref, attn_ref, mixed_ref, gain_grad_ref):
-    grad_normed = base_ref[...] + gathered(dest_ref, y_ref, part)
+    grad_normed = base_ref[...] + gathered(top, dest_ref, y_ref, part)
     first_sum = sum_ref[...]
     scale = lax.rsqrt(jnp.mean(first_sum * first_sum, axis=1, keepdims=True) + EPSILON)
     weighted = grad_normed * gain_ref[...]
@@ -465,14 +515,13 @@
     gain_grad_ref[...] += jnp.sum(grad_normed * first_sum * scale, axis=0, keepdims=True)
 
 
-def norm_two_back(dest, live, cotangent, first_sum, base, gain, weights, rows_of, part):
+def norm_two_back(top, dest, live, cotangent, first_sum, base, gain, weights, rows_of, part):
     rows, width = first_sum.shape
-    top = dest.shape[1]
     block = min(256, rows)
     blocked = pl.BlockSpec((block, width), lambda i: (i, 0))
     return call(
-        functools.partial(norm_two_back_kernel, part), (rows // block,),
-        [pl.BlockSpec((block, top), lambda i: (i, 0)), pl.BlockSpec((block, 1), lambda i: (i, 0)), blocked, blocked,
+        functools.partial(norm_two_back_kernel, part, top), (rows // block,),
+        [pl.BlockSpec((block, dest.shape[1]), lambda i: (i, 0)), pl.BlockSpec((block, 1), lambda i: (i, 0)), blocked, blocked,
          blocked, whole((1, width)), square(width, 3), whole(rows_of.shape)],
         [blocked, blocked, blocked, pl.BlockSpec((1, width), lambda i: (0, 0))],
         [shape_of((rows, width), F32), shape_of((rows, width), BF16), shape_of((rows, width), BF16),
@@ -612,8 +661,8 @@
 
 
 def settle_kernel(sizes, gq_ref, gk_ref, gv_ref, wq_ref, wk_ref, wv_ref, tokens_ref, first_ref, gain_ref, pack_ref,
-                  x_ref, out_ref, share_ref, piece_ref, own, landed, chosen, arrived, sem, pair_send, pair_recv, send_sem,
-                  recv_sem, x_buffers, x_total, x_send, x_recv):
+                  x_ref, out_ref, share_ref, all_ref, own, landed, chosen, arrived, sem, pair_send, pair_recv, send_sem,
+                  recv_sem, x_buffers, x_total, x_all, x_send, x_recv, g_send, g_recv):
     dp_size, shard_size, count = sizes
     spread = shard_size // 2
     halves = dp_size * spread
@@ -627,6 +676,7 @@
         return {"dp": piece // spread, "shard": (piece % spread) * 2 + bit}
 
     line = LineSum("expert", count, x_ref, x_buffers, x_send, x_recv)
+    gather = LineGather("expert", count, x_all, g_send, g_recv)
 
     def pair_copy():
         return pltpu.make_async_remote_copy(
@@ -679,13 +729,17 @@
     @pl.when(step == last)
     def _():
         line.relay()
+        line.finish(x_total)
+        gather.start(x_total[...].astype(BF16))
         total = own[place].astype(F32) + landed[place].astype(F32)
         for index in range(halves - 1):
             send(index).wait()
             total = total + arrived[index].astype(F32)
         share_ref[...] = total.astype(BF16)
-        line.finish(x_total)
-        piece_ref[...] = x_total[...].astype(BF16)
+        for k in range(1, count):
+            gather.relay(k)
+        gather.finish()
+        all_ref[...] = x_all[...]
 
 
 def settle(grads, w_qkv, tokens, grad_first, gain, pack, x, sizes):
@@ -699,14 +753,14 @@
         functools.partial(settle_kernel, sizes), (rows // block,),
         [blocked] * 3 + [square(width, 0), square(width, 1), square(width, 2), blocked, blocked, whole((1, width)),
                          pl.BlockSpec(memory_space=pl.ANY), whole(x.shape)],
-        [blocked, whole(piece), whole(x_piece)],
-        [shape_of((rows, width), F32), shape_of(piece, BF16), shape_of(x_piece, BF16)],
+        [blocked, whole(piece), whole(x.shape)],
+        [shape_of((rows, width), F32), shape_of(piece, BF16), shape_of(x.shape, BF16)],
         scratch=[pltpu.VMEM((halves,) + piece, BF16), pltpu.VMEM((halves,) + piece, BF16),
                  pltpu.VMEM((halves - 1,) + piece, BF16), pltpu.VMEM((halves - 1,) + piece, BF16),
                  pltpu.SemaphoreType.DMA, pltpu.SemaphoreType.DMA, pltpu.SemaphoreType.DMA,
                  pltpu.SemaphoreType.DMA((halves - 1,)), pltpu.SemaphoreType.DMA((halves - 1,)),
-                 pltpu.VMEM((2, 2, sizes[2]) + x_piece, BF16), pltpu.VMEM(x_piece, F32),
-                 pltpu.SemaphoreType.DMA((2, sizes[2])), pltpu.SemaphoreType.DMA((2, sizes[2]))],
+                 pltpu.VMEM((2, 2, sizes[2]) + x_piece, BF16), pltpu.VMEM(x_piece, F32), pltpu.VMEM(x.shape, BF16)]
+        + [pltpu.SemaphoreType.DMA((2, sizes[2]))] * 4,
         flops=6 * rows * width * width, moved=22 * rows * width, collective_id=1,
     )(*grads, w_qkv, w_qkv, w_qkv, tokens, grad_first, gain, pack.reshape((halves, 2) + piece), x)
 
@@ -755,8 +809,9 @@
     return 3 * width * hidden // owners // LANES
 
 
-def ffn_kernel(out_type, layout, block, x_ref, gy_ref, wg_ref, wu_ref, wd_ref, *rest):
-    y_ref, gx_ref, packed_ref, xt, y_acc, gx_acc, stage_g, stage_u, stage_d, sems = rest[-10:]
+def ffn_kernel(out_type, layout, block, axis, count, x_ref, gy_ref, wg_ref, wu_ref, wd_ref, sent_ref, *rest):
+    y_ref, gx_ref, packed_ref, kept_ref, xt, y_acc, gx_acc, stage_g, stage_u, stage_d, sems, *exchange_sems = rest[-14:]
+    exchange = Exchange(axis, count, sent_ref, kept_ref, *exchange_sems)
     step = pl.program_id(0)
     steps = layout[2] // block
     width = x_ref.shape[1]
@@ -765,6 +820,7 @@
 
     @pl.when(step == 0)
     def _():
+        exchange.start()
         xt[...] = x_ref[...].T
         y_acc[...] = jnp.zeros_like(y_acc)
         gx_acc[...] = jnp.zeros_like(gx_acc)
@@ -800,7 +856,8 @@
 
     @pl.when(step == steps - 1)
     def _():
-        y_ref[...] = y_acc[...].astype(out_type)
+        exchange.wait()
+        y_ref[...] = y_acc[...].astype(out_type).reshape(y_ref.shape)
         gx_ref[...] = gx_acc[...].astype(out_type)
         for back in (1, 0):
             if steps > back:
@@ -811,7 +868,7 @@
 BLOCK = 256
 
 
-def ffn_both(x, gy, w_gu, w_down, hidden, expert, owners, out_type, parts=1, pack=None):
+def ffn_both(x, gy, w_gu, w_down, hidden, expert, owners, out_type, sent, axis, count, collective_id, parts=1, held=()):
     rows, width = x.shape
     block = BLOCK
     steps = hidden // block
@@ -830,27 +887,34 @@
         stage = (2, width, block)
     if by_rows:
         grads = whole((rows, width))
+        y_block, y_shape = whole((rows, width)), (rows, width)
     else:
+        y_shape = (gy.shape[0], parts * (rows // gy.shape[0]), width)
+        y_block = pl.BlockSpec(
+            (gy.shape[0], rows // gy.shape[0], width), lambda f: (0, expert, 0), pipeline_mode=pl.Buffered(1)
+        )
         grads = pl.BlockSpec(
             (gy.shape[0], rows // gy.shape[0], width), lambda f: (0, expert, 0), pipeline_mode=pl.Buffered(1)
         )
     out_rows = whole((rows, width))
-    count = packed_rows(width, hidden, owners)
-    layout = (by_rows, owners, hidden, (expert or 0) * count)
-    held = [] if pack is None else [pack]
+    pack_rows = packed_rows(width, hidden, owners)
+    layout = (by_rows, owners, hidden, (expert or 0) * pack_rows)
+    hbm = pl.BlockSpec(memory_space=pl.ANY)
+    sent = sent.reshape(count, -1, width)
     copies = 2 * (block // LANES) + block // (hidden // owners) * (width // LANES)
-    return call(
-        functools.partial(ffn_kernel, out_type, layout, block), (steps,),
-        [whole((rows, width)), grads, gate, up, down] + [pl.BlockSpec(memory_space=pl.ANY)] * len(held),
-        [out_rows, out_rows, pl.BlockSpec(memory_space=pl.ANY)],
-        [shape_of((rows, width), out_type), shape_of((rows, width), out_type),
-         shape_of((owners, parts * count, LANES), BF16)],
+    y, gx, pack, kept = call(
+        functools.partial(ffn_kernel, out_type, layout, block, axis, count), (steps,),
+        [whole((rows, width)), grads, gate, up, down, hbm] + [hbm] * len(held),
+        [y_block, out_rows, hbm, hbm],
+        [shape_of(y_shape, out_type), shape_of((rows, width), out_type),
+         shape_of((owners, parts * pack_rows, LANES), BF16), shape_of(sent.shape, BF16)],
         scratch=[pltpu.VMEM((width, rows), BF16), pltpu.VMEM((rows, width), F32), pltpu.VMEM((rows, width), F32),
                  pltpu.VMEM(stage, BF16), pltpu.VMEM(stage, BF16), pltpu.VMEM((2, block, width), BF16),
-                 pltpu.SemaphoreType.DMA((2, copies))],
+                 pltpu.SemaphoreType.DMA((2, copies))] + Exchange.scratch(count),
         flops=18 * rows * width * hidden, moved=12 * width * hidden + 16 * rows * width, trans=rows * hidden,
-        aliases={5: 2} if held else None,
-    )(x, gy, w_gu, w_gu, w_down, *held)
+        aliases={6: 0, 7: 2} if held else None, collective_id=collective_id,
+    )(x, gy, w_gu, w_gu, w_down, sent, *held)
+    return y, gx, pack, kept.reshape(-1, width)
 
 
 def to_panels(array):
@@ -952,27 +1016,16 @@
     group = lax.axis_size("dp") * lax.axis_size("shard")
     shared_hidden = w_shared_down.shape[0] * group
 
-    dest_t = slots_of(routes.T, live_row, experts, capacity)
-    dest = dest_t.T
-    slots = owners * capacity
-
-    def place(where):
-        owner_of, part_of = where // (local_experts * capacity), (where // capacity) % local_experts
-        return jnp.where(
-            where < experts * capacity, part_of * slots + owner_of * capacity + where % capacity, experts * capacity
-        )
-
-    placed, placed_t = place(dest), place(dest_t)
+    table_t, table = slots_of(routes.T, live_row, experts, local_experts, capacity)
     gates_t = route_gates.T
     grad_b = jnp.where(live_bool[:, None], cotangent, 0).astype(BF16)
 
     def exchange(rows):
-        count = rows.shape[0] // owners
         return lax.all_to_all(
-            rows.reshape(owners, count, width), "expert", split_axis=0, concat_axis=0, tiled=True
+            rows.reshape(owners, -1, width), "expert", split_axis=0, concat_axis=0, tiled=True
         ).reshape(rows.shape)
 
-    send_grad = dispatch(dest_t, gates_t, grad_b, experts, capacity, True, 0)
+    send_grad = dispatch(table_t, gates_t, grad_b, experts, capacity, True, 0, 0)
     received_grad = exchange(send_grad).reshape(owners, local_experts * capacity, width)
 
     cosine, sine = rotary_tables(length, head_dim)
@@ -980,25 +1033,34 @@
     queries, keys, values, mixed, lse = attend_forward(normed_one, attention_weight, cosine, sine, length, head_dim)
     first_sum, normed_two = norm_two(mixed, tokens, attention_weight, gain_two)
 
-    received = []
+    send_rows = []
     for j in range(local_experts):
-        rows = dispatch(placed_t, gates_t, normed_two, owners, capacity, False, j * owners)
-        received.append(exchange(rows))
-    shared_out, grad_shared, shared_pack = ffn_both(
-        normed_two, grad_b, shared_weight, shared_weight, shared_hidden, None, group, F32
-    )
-    back_rows, out_rows, pack = [], [], None
+        send_rows.append(dispatch(table_t, gates_t, normed_two, owners, capacity, False, j * owners, top))
+    shared_out, grad_shared, shared_pack, received = ffn_both(
+        normed_two, grad_b, shared_weight, shared_weight, shared_hidden, None, group, F32,
+        send_rows[0], "expert", owners, 3,
+    )
+    waiting = send_rows[1:]
+    back_rows, base, held = [], grad_shared, ()
     for j in range(local_experts):
-        y, gx, pack = ffn_both(
-            received[j], received_grad, w_expert_gu, w_expert_down, hidden, j, group, BF16, local_experts, pack
+        y, gx, pack, arrived = ffn_both(
+            received, received_grad, w_expert_gu, w_expert_down, hidden, j, group, BF16,
+            waiting.pop(0), "expert", owners, 4 + j, local_experts, held,
         )
-        back_rows.append(exchange(gx))
-        out_rows.append(y)
-    base = grad_shared
-    for j, rows in enumerate(back_rows[:-1]):
-        base = add_part(placed, base, rows, j)
+        held = (y, pack)
+        waiting.append(gx)
+        if j < local_experts - 1:
+            received = arrived
+        else:
+            back_rows.append(arrived)
+    for j, sent in enumerate(waiting):
+        base, arrived = add_part(
+            top, table, base, back_rows[j], j, sent, "expert", owners, 4 + local_experts + j
+        )
+        back_rows.append(arrived)
+    y, base = lax.optimization_barrier((y, base))
     grad_first, grad_attn, grad_mixed, grad_gain_two = norm_two_back(
-        placed, live, cotangent, first_sum, base, gain_two, attention_weight, back_rows[-1], local_experts - 1
+        top, table, live, cotangent, first_sum, base, gain_two, attention_weight, back_rows[-1], local_experts - 1
     )
 
     grads = attend_backward(queries, keys, values, mixed, grad_mixed, lse, cosine, sine, length, head_dim)
@@ -1012,28 +1074,18 @@
 
     shared_share = spread(shared_pack)
     expert_share = spread(pack)
-    input_grad, attention_share, shared_piece = settle(
+    input_grad, attention_share, shared_share = settle(
         grads, attention_weight, tokens, grad_first, gain_one, attention_pack, shared_share,
         (lax.axis_size("dp"), lax.axis_size("shard"), owners),
     )
-    returned = exchange_parts(out_rows, owners, "expert")
+    returned = exchange(y)
     layer_out, expert_gu, expert_down, qkv_grad, out_grad, shared_gu, shared_down, gain_rows = combine(
-        placed, route_gates, live, first_sum, shared_out, returned, attention_share, shared_piece, expert_share,
-        "expert", owners, own, shared_hidden, hidden,
+        table, route_gates, live, first_sum, shared_out, returned.reshape(-1, width), attention_share, shared_share,
+        expert_share, local_experts, "expert", owners, own, shared_hidden, hidden,
     )
     grad_gain_one = jnp.sum(w_qkv.astype(F32) * qkv_grad, axis=1) / norm_gains[0].astype(F32)
     grad_gains = jnp.stack([grad_gain_one, gain_rows[0, :own]])
     return layer_out, input_grad, grad_gains, qkv_grad, out_grad, shared_gu, shared_down, expert_gu, expert_down
-
-
-def exchange_parts(parts, owners, axis):
-    width = parts[0].shape[1]
-    count = parts[0].shape[0] // owners
-    joined = jnp.concatenate([rows.reshape(owners, count, width) for rows in parts], axis=1)
-    back = lax.all_to_all(joined, axis, split_axis=0, concat_axis=0, tiled=True)
-    return [
-        back[:, j * count : (j + 1) * count].reshape(owners * count, width) for j in range(len(parts))
-    ]
 
 
 def solution(mesh):

time: 742 us -> 589 us (0.79)
  waiting for transfers between devices: 214 us -> 108 us
  blocking collectives: 92.8 us -> 10.3 us
  Pallas kernels: 347 us -> 392 us
    all_to_all x5 -> x2, waiting for transfers between devices: 174 us -> 72.8 us  [exchange(): lax.all_to_all(rows.reshape(owners, -1, width), 'expert', split_axis=0, c...]
    all_to_all x1 -> x0, blocking collectives: 82.4 us -> none  [exchange_parts(): back = lax.all_to_all(joined, axis, split_axis=0, concat_axis=0, tiled=True)]
    pallas_call x10, Pallas kernels: 214 us -> 238 us  [the longest x3 132 us: ffn_both(): call(functools.partial(ffn_kernel, out_type, layout, block, axis, count),...]
    pallas_call x1, Pallas kernels: 41.8 us -> 62.2 us  [settle(): call(functools.partial(settle_kernel, sizes), (rows // block,), [blocked]...]
    all_to_all x5 -> x2, starting transfers between devices: 22.4 us -> 21.4 us  [exchange(): lax.all_to_all(rows.reshape(owners, -1, width), 'expert', split_axis=0, c...]
    unnamed x51 -> x43, local copies, waits for them, and re-layouts: 16.9 us -> 17.5 us
  transfers between devices with their start and end apart: 9 -> 6, of which waited for: 6 -> 3; matrix products, arithmetic and copies ran while one was open for 3% -> 2% of each run, Pallas kernels for 35% -> 54%
where the time goes in v6:
time: 589 us; the launch traced here: 578 us
  Pallas kernels  392 us (67%)
  waiting for transfers between devices  108 us (18%)
  local copies, waits for them, and re-layouts  22.3 us (4%)
  starting transfers between devices  21.6 us (4%)
  between operations  14.9 us (3%)
  blocking collectives  10.3 us (2%)
  other arithmetic  9.23 us (2%)
    pallas_call x3, Pallas kernels, ffn_both(): call(functools.partial(ffn_kernel, out_type, layout, block, axis, count),...  132 us
    all_to_all x2, waiting for transfers between devices, exchange(): lax.all_to_all(rows.reshape(owners, -1, width), 'expert', split_axis=0, c...  72.8 us
    pallas_call x1, Pallas kernels, settle(): call(functools.partial(settle_kernel, sizes), (rows // block,), [blocked]...  62.2 us
    pallas_call x1, Pallas kernels, combine(): call(functools.partial(combine_kernel, axis, count, own, gu_panels, parts...  37.9 us
    pallas_call x1, Pallas kernels, add_part(): call(functools.partial(add_part_kernel, part, top, axis, count), (rows //...  35 us
    pallas_call x1, Pallas kernels, attend_backward(): call(functools.partial(attend_backward_kernel, head_dim, block), (seqs, p...  34.1 us
    pallas_call x1, Pallas kernels, attend_forward(): call(functools.partial(attend_forward_kernel, head_dim, block), (seqs, pa...  33.1 us
    all_to_all x2, starting transfers between devices, exchange(): lax.all_to_all(rows.reshape(owners, -1, width), 'expert', split_axis=0, c...  21.4 us
  transfers between devices with their start and end apart: 6, of which 3 were waited for; matrix products, arithmetic and copies ran while one was open for 2% of the time, Pallas kernels for 54%

profile of v6, /device:TPU:0, one launch (start us, length us, event | category | flops | bytes accessed | tf_op | source)
XLA Modules:
  0.0 578.4 jit_solution(2617458087712050414)
XLA Ops:
  7.2 2.0 pad_maximum_fusion.1
  12.0 10.3 %all-gather.1 = bf16[8,96,2]{1,2,0:T(2,128)(2,1)S(1)} all-gather(bf16[1,96,2]{1,2,0:T(2,128)(2,1)S(1)} %bitcast.57), channel_id=1, replica_groups=mesh['dp'=2,'expert'=4,'shard'=4] {'dp','shard'}, dimensions={0}, use_global_device_ids=true | all-gather | bytes 3456 | tf_op jit(solution)/shard_map/all_gather | solution.py:1005
  25.8 3.9 shard_map.191.x_ref.normed_ref
  30.2 2.1 shard_map.190
  33.7 18.3 %all-gather.5.cloned.1.call-done.wq_ref.wk_ref.wv_ref.weight_ref = bf16[768,3072]{1,0:T(8,128)(2,1)} async-done(((bf16[96,3072]{1,0:T(8,128)(2,1)}), bf16[768,3072]{1,0:T(8,128)(2,1)}) %all-gather.5.cloned.1.call-update) | async-done | bytes 4718608 | tf_op jit(solution)/shard_map/all_gather | solution.py:1006
  52.0 33.1 %shard_map.192 = (bf16[1024,768]{1,0:T(8,128)(2,1)}, bf16[1024,768]{1,0:T(8,128)(2,1)}, bf16[1024,768]{1,0:T(8,128)(2,1)}, bf16[1024,768]{1,0:T(8,128)(2,1)}, f32[96,1024]{1,0:T(8,128)}) custom-call(bf16[1024,768]{1,0:T(8,128)(2,1)} %shard_map.191.x_ref.normed_ref, bf16[768,3072]{1,0:T(8,128)(2,1)} %all-gather.5.cloned.1.call-done.wq_ref.wk_ref.wv_ref.weight_ref, ...), custom_call_target="tpu_custom_call" | custom-call | flops 6845104128 | bytes 12582912 | tf_op jit(solution)/shard_map/pallas_call | solution.py:140
  85.1 5.8 shard_map.193
  90.8 5.1 shard_map.194
  95.9 16.7 %all-gather.7.cloned.1.call-done = bf16[18432,256]{1,0:T(8,128)(2,1)} async-done(((bf16[2304,256]{1,0:T(8,128)(2,1)}), bf16[18432,256]{1,0:T(8,128)(2,1)}) %all-gather.7.cloned.1.call-update) | async-done | bytes 9437200 | tf_op jit(solution)/shard_map/all_gather | solution.py:1007
  112.6 42.0 %shard_map.195 = (f32[1024,768]{1,0:T(8,128)}, f32[1024,768]{1,0:T(8,128)}, bf16[8,4608,128]{2,1,0:T(8,128)(2,1)}, bf16[4,288,768]{2,1,0:T(8,128)(2,1)}) custom-call(bf16[1024,768]{1,0:T(8,128)(2,1)} %get-tuple-element.55.x_ref, bf16[1024,768]{1,0:T(8,128)(2,1)} %broadcast_select_fusion.gy_ref.x_ref, bf16[8,2304,256]{2,1,0:T(8,128)(2,1)} %bitcast.58, ...), custom_call_target="tpu_custom_call" | custom-call | flops 28991029248 | bytes 31457280 | tf_op jit(solution)/shard_map/pallas_call | solution.py:905
  154.7 8.6 %shard_map.196 = bf16[2304,768]{1,0:T(8,128)(2,1)} custom-call(s32[8,1024]{1,0:T(8,128)} %get-tuple-element.56.dest_ref, f32[2,1024]{1,0:T(2,128)} %bitcast.55, bf16[1024,768]{1,0:T(8,128)(2,1)} %broadcast_select_fusion.gy_ref.x_ref), custom_call_target="tpu_custom_call" | custom-call | flops 3623878656 | bytes 5111808 | tf_op jit(solution)/shard_map/pallas_call | solution.py:319
  163.3 10.1 %all-to-all-start = ((bf16[4,576,768]{2,1,0:T(8,128)(2,1)}), bf16[4,576,768]{2,1,0:T(8,128)(2,1)S(1)}, u32[]{:S(2)}, u32[]{:S(2)}) async-start(bf16[4,576,768]{2,1,0:T(8,128)(2,1)} %bitcast.41), calls=%async_computation | async-start | bytes 7077888 | tf_op jit(solution)/shard_map/all_to_all | solution.py:1024
  173.4 5.9 %shard_map.197 = bf16[1152,768]{1,0:T(8,128)(2,1)} custom-call(s32[8,1024]{1,0:T(8,128)} %get-tuple-element.56.dest_ref, f32[2,1024]{1,0:T(2,128)} %bitcast.56, bf16[1024,768]{1,0:T(8,128)(2,1)} %get-tuple-element.55.x_ref), custom_call_target="tpu_custom_call" | custom-call | flops 1811939328 | bytes 3342336 | tf_op jit(solution)/shard_map/pallas_call | solution.py:319
  179.3 72.8 %all-to-all-done.gy_ref = bf16[4,576,768]{2,1,0:T(8,128)(2,1)S(1)} async-done(((bf16[4,576,768]{2,1,0:T(8,128)(2,1)}), bf16[4,576,768]{2,1,0:T(8,128)(2,1)S(1)}, u32[]{:S(2)}, u32[]{:S(2)}) %all-to-all-start) | async-done | bytes 3538976 | tf_op jit(solution)/shard_map/all_to_all | solution.py:1024
  253.8 44.4 %shard_map.198 = (bf16[4,576,768]{2,1,0:T(8,128)(2,1)}, bf16[1152,768]{1,0:T(8,128)(2,1)}, bf16[8,9216,128]{2,1,0:T(8,128)(2,1)}, bf16[4,288,768]{2,1,0:T(8,128)(2,1)}) custom-call(bf16[1152,768]{1,0:T(8,128)(2,1)} %bitcast.63, bf16[4,576,768]{2,1,0:T(8,128)(2,1)} %copy-done.2, bf16[2,768,4096]{2,1,0:T(8,128)(2,1)} %wu_ref.3, bf16[2,768,4096]{2,1,0:T(8,128)(2,1)} %wu_ref.3, ...), custom_call_target="tpu_custom_call" | custom-call | flops 32614907904 | bytes 33030144 | tf_op jit(solution)/shard_map/pallas_call | solution.py:905
  298.2 45.6 %shard_map.199 = (bf16[4,576,768]{2,1,0:T(8,128)(2,1)}, bf16[1152,768]{1,0:T(8,128)(2,1)}, bf16[8,9216,128]{2,1,0:T(8,128)(2,1)}, bf16[4,288,768]{2,1,0:T(8,128)(2,1)}) custom-call(bf16[1152,768]{1,0:T(8,128)(2,1)} %bitcast.66, bf16[4,576,768]{2,1,0:T(8,128)(2,1)} %copy-done.2, ...), custom_call_target="tpu_custom_call", output_to_operand_aliasing={{0}: (6, {}), {2}: (7, {})} | custom-call | flops 32614907904 | bytes 33030144 | tf_op jit(solution)/shard_map/pallas_call | solution.py:905
  343.9 35.0 %shard_map.200 = (f32[1024,768]{1,0:T(8,128)}, bf16[4,288,768]{2,1,0:T(8,128)(2,1)}) custom-call(s32[1024,8]{1,0:T(8,128)} %get-tuple-element.52.dest_ref, f32[1024,768]{1,0:T(8,128)} %get-tuple-element.64.base_ref, bf16[1152,768]{1,0:T(8,128)(2,1)} %bitcast.47, bf16[4,288,768]{2,1,0:T(8,128)(2,1)} %bitcast.46), custom_call_target="tpu_custom_call" | custom-call | flops 1811939328 | bytes 6291456 | tf_op jit(solution)/shard_map/pallas_call | solution.py:486
  378.9 11.4 %all-to-all-start.1 = ((bf16[4,576,768]{2,1,0:T(8,128)(2,1)}), bf16[4,576,768]{2,1,0:T(8,128)(2,1)S(1)}, u32[]{:S(2)}, u32[]{:S(2)}) async-start(bf16[4,576,768]{2,1,0:T(8,128)(2,1)} %get-tuple-element.68), calls=%async_computation.1 | async-start | bytes 7077888 | tf_op jit(solution)/shard_map/all_to_all | solution.py:1024
  392.1 11.4 %shard_map.201 = (f32[1024,768]{1,0:T(8,128)}, bf16[1024,768]{1,0:T(8,128)(2,1)}, bf16[1024,768]{1,0:T(8,128)(2,1)}, f32[1,768]{1,0:T(1,128)}) custom-call(s32[1024,8]{1,0:T(8,128)} %get-tuple-element.52.dest_ref, f32[1024,1]{1,0:T(8,128)} %fusion.4.live_ref, bf16[1024,768]{1,0:T(8,128)(2,1)} %cot_ref.1, f32[1024,768]{1,0:T(8,128)} %get-tuple-element.54.sum_ref, ...), custom_call_target="tpu_custom_call" | custom-call | flops 3019898880 | bytes 14155776 | tf_op jit(solution)/shard_map/pallas_call | solution.py:522
  405.0 34.1 %shard_map.202 = (bf16[1024,768]{1,0:T(8,128)(2,1)}, bf16[1024,768]{1,0:T(8,128)(2,1)}, bf16[1024,768]{1,0:T(8,128)(2,1)}) custom-call(bf16[1024,768]{1,0:T(8,128)(2,1)} %get-tuple-element.69.q_ref, bf16[1024,768]{1,0:T(8,128)(2,1)} %get-tuple-element.70.k_ref, bf16[1024,768]{1,0:T(8,128)(2,1)} %get-tuple-element.71.v_ref, ...), custom_call_target="tpu_custom_call" | custom-call | flops 8053063680 | bytes 12582912 | tf_op jit(solution)/shard_map/pallas_call | solution.py:211
  439.0 15.3 %shard_map.203 = bf16[8,2496,128]{2,1,0:T(8,128)(2,1)} custom-call(bf16[1024,768]{1,0:T(8,128)(2,1)} %shard_map.191.x_ref.normed_ref, bf16[1024,768]{1,0:T(8,128)(2,1)} %get-tuple-element.53.mixed_ref.o_ref, bf16[1024,768]{1,0:T(8,128)(2,1)} %get-tuple-element.76.gq_ref, bf16[1024,768]{1,0:T(8,128)(2,1)} %get-tuple-element.77.gk_ref, ...), custom_call_target="tpu_custom_call" | custom-call | flops 4831838208 | bytes 12582912 | tf_op jit(solution)/shard_map/pallas_call | solution.py:967
  454.3 62.2 %shard_map.204 = (f32[1024,768]{1,0:T(8,128)}, bf16[2496,128]{1,0:T(8,128)(2,1)}, bf16[4608,128]{1,0:T(8,128)(2,1)}) custom-call(bf16[1024,768]{1,0:T(8,128)(2,1)} %get-tuple-element.76.gq_ref, bf16[1024,768]{1,0:T(8,128)(2,1)} %get-tuple-element.77.gk_ref, bf16[1024,768]{1,0:T(8,128)(2,1)} %get-tuple-element.78.gv_ref, ...), custom_call_target="tpu_custom_call" | custom-call | flops 3623878656 | bytes 17301504 | tf_op jit(solution)/shard_map/pallas_call | solution.py:752
  518.3 37.9 %shard_map.205 = (bf16[1024,768]{1,0:T(8,128)(2,1)}, f32[2,768,512]{2,1,0:T(8,128)}, f32[2,256,768]{2,1,0:T(8,128)}, f32[96,2304]{1,0:T(8,128)}, f32[96,768]{1,0...) custom-call(s32[1024,8]{1,0:T(8,128)} %get-tuple-element.52.dest_ref, ...), custom_call_target="tpu_custom_call" | custom-call | flops 7247757312 | bytes 11403264 | tf_op jit(solution)/shard_map/pallas_call | solution.py:405
  558.9 2.7 copy.79
  (77 shorter events, 27.1 us)
Async XLA Ops:
  7.2 2.2 copy-start.11
  7.2 2.5 copy-start.9
  7.2 44.8 %all-gather.5.cloned.1.call-start = ((), (), s32[]{:S(2)}) async-start(), calls=%async_computation.4 | async-start | bytes 5308416 | tf_op jit(solution)/shard_map/all_gather | solution.py:1006
  9.3 103.3 %all-gather.7.cloned.1.call-start = ((), (), s32[]{:S(2)}) async-start(), calls=%async_computation.7 | async-start | bytes 10616832 | tf_op jit(solution)/shard_map/all_gather | solution.py:1007
  10.1 1.8 copy-start.14
  11.3 443.0 %reduce-scatter.3.cloned.1.call-start = ((), (), s32[]{:S(2)}) async-start(), calls=%async_computation.5 | async-start | bytes 10616832 | tf_op jit(solution)/shard_map/reduce_scatter | solution.py:1073
  25.2 7.1 %copy-start = (bf16[1024,768]{1,0:T(8,128)(2,1)S(1)}, bf16[1024,768]{1,0:T(8,128)(2,1)}, u32[]{:S(2)}) copy-start(bf16[1024,768]{1,0:T(8,128)(2,1)} %cot_ref.1) | copy-start | bytes 4718596
  163.3 88.7 %all-to-all-start = ((bf16[4,576,768]{2,1,0:T(8,128)(2,1)}), bf16[4,576,768]{2,1,0:T(8,128)(2,1)S(1)}, u32[]{:S(2)}, u32[]{:S(2)}) async-start(bf16[4,576,768]{2,1,0:T(8,128)(2,1)} %bitcast.41), calls=%async_computation | async-start | bytes 7077888 | tf_op jit(solution)/shard_map/all_to_all | solution.py:1024
  173.4 343.1 %reduce-scatter.5.cloned.1.call-start = ((), (), s32[]{:S(2)}) async-start(), calls=%async_computation.6 | async-start | bytes 21233664 | tf_op jit(solution)/shard_map/reduce_scatter | solution.py:1073
  252.1 1.8 copy-start.2
  378.9 11.4 %copy-start.13 = (f32[1024,2]{0,1:T(2,128)S(1)}, f32[1024,2]{0,1:T(2,128)}, u32[]{:S(2)}) copy-start(f32[1024,2]{0,1:T(2,128)} %param.15) | copy-start | bytes 24580
  378.9 137.6 %all-to-all-start.1 = ((bf16[4,576,768]{2,1,0:T(8,128)(2,1)}), bf16[4,576,768]{2,1,0:T(8,128)(2,1)S(1)}, u32[]{:S(2)}, u32[]{:S(2)}) async-start(bf16[4,576,768]{2,1,0:T(8,128)(2,1)} %get-tuple-element.68), calls=%async_computation.1 | async-start | bytes 7077888 | tf_op jit(solution)/shard_map/all_to_all | solution.py:1024
  516.5 1.8 copy-start.1
  518.3 37.9 %copy-start.6 = (bf16[96,2304]{1,0:T(8,128)(2,1)S(1)}, bf16[96,2304]{1,0:T(8,128)(2,1)}, u32[]{:S(2)}) copy-start(bf16[96,2304]{1,0:T(8,128)(2,1)} %param.18) | copy-start | bytes 1327108
  518.3 40.1 %copy-start.15 = (bf16[2,96]{1,0:T(2,128)(2,1)S(1)}, bf16[2,96]{1,0:T(2,128)(2,1)}, u32[]{:S(2)}) copy-start(bf16[2,96]{1,0:T(2,128)(2,1)} %param.17) | copy-start | bytes 1156
  557.5 4.1 copy-start.4
  561.6 1.8 copy-start.3
  561.6 2.7 copy-start.12
  563.4 1.8 copy-start.8
  564.3 2.0 copy-start.10
  565.1 2.8 copy-start.5
  567.9 2.5 copy-start.7
Sparse Core Ops, SparseCore 0:
  10.5 41.4 all-gather.4
  53.9 58.6 all-gather.6
  154.8 82.2 reduce-scatter.2
  344.0 125.1 reduce-scatter.4

commit v7 on v6

--- a/solution.py
+++ b/solution.py
@@ -330,33 +330,7 @@
         target[:, pl.ds(p * LANES, LANES)] = source[pl.ds(start + p * rows, rows), :].astype(F32)
 
 
-def combine_kernel(axis, count, own, gu_panels, experts, dest_ref, gates_ref, live_ref, sum_ref, shared_ref, y_ref, *rest):
-    x_ref, p_ref, pack_ref, out_ref, egu_ref, ed_ref, qkv_ref, wo_ref, sgu_ref, sd_ref, gain_ref = rest[:11]
-    buffers, total_x, all_x, sum_send, sum_recv, x_send, x_recv = rest[11:]
-    step = pl.program_id(0)
-    last = pl.num_programs(0) - 1
-    line = LineSum(axis, count, x_ref, buffers, sum_send, sum_recv)
-    gather_x = LineGather(axis, count, all_x, x_send, x_recv)
-    width = out_ref.shape[1]
-    d_panels = width // LANES
-    packed = pack_ref.shape[0] // experts
-    e_panels, e_rows = egu_ref.shape[2] // LANES, egu_ref.shape[1]
-
-    @pl.when(step == 0)
-    def _():
-        barrier = pltpu.get_barrier_semaphore()
-        pl.semaphore_wait(barrier, greet_neighbours(barrier, axis, count))
-        line.start()
-        unpack(p_ref, 0, own, gu_panels, sgu_ref)
-        unpack(p_ref, gu_panels * own, sd_ref.shape[0], d_panels, sd_ref)
-        for e in range(experts):
-            unpack(pack_ref, e * packed + e_panels * width, ed_ref.shape[1], d_panels, ed_ref.at[e])
-
-    for e in range(experts):
-        for p in range(e_panels):
-            rows = pl.ds(pl.multiple_of(e * packed + p * width + step * e_rows, 16), e_rows)
-            egu_ref[e, :, pl.ds(p * LANES, LANES)] = pack_ref[rows, :].astype(F32)
-
+def combine_kernel(dest_ref, gates_ref, live_ref, sum_ref, shared_ref, y_ref, out_ref):
     block, top = gates_ref.shape
     total = sum_ref[...] + shared_ref[...]
     dest = dest_ref[...]
@@ -367,50 +341,76 @@
         total = total + dot_nn(hit, y_ref[...]) * gates[:, k : k + 1]
     out_ref[...] = (live_ref[...] * total).astype(BF16)
 
-    @pl.when(step == jnp.minimum(1, last))
-    def _():
-        line.relay()
-
-    @pl.when(step == jnp.minimum(2, last))
-    def _():
-        line.finish(total_x)
-        gather_x.start(total_x[...].astype(BF16))
-
-    @pl.when(step == last)
-    def _():
-        for k in range(1, count):
-            gather_x.relay(k)
-        gather_x.finish()
-        unpack(all_x, 0, own, 3 * d_panels, qkv_ref)
-        unpack(all_x, 3 * d_panels * own, own, d_panels, wo_ref)
-        gain_ref[...] = all_x[pl.ds(4 * d_panels * own, gain_ref.shape[0]), :].astype(F32)
-
-
-def combine(dest, gates, live, first_sum, shared_out, returned, x, piece, pack, parts, axis, count, own, shared_hidden, hidden):
+
+def combine(dest, gates, live, first_sum, shared_out, returned):
     rows, width = first_sum.shape
     top = gates.shape[1]
     block = min(256, rows)
-    steps = rows // block
     blocked = pl.BlockSpec((block, width), lambda i: (i, 0))
     slots = returned.shape[0]
-    group = width // own
+    return call(
+        combine_kernel, (rows // block,),
+        [pl.BlockSpec((block, dest.shape[1]), lambda i: (i, 0)), pl.BlockSpec((block, top), lambda i: (i, 0)),
+         pl.BlockSpec((block, 1), lambda i: (i, 0)), blocked, blocked, whole(returned.shape)],
+        blocked, shape_of((rows, width), BF16),
+        flops=4 * rows * slots * width, moved=10 * rows * width + 2 * slots * width,
+    )(dest, gates, live, first_sum, shared_out, returned)
+
+
+def unpack(source, start, rows, panels, target):
+    for p in range(panels):
+        target[:, pl.ds(p * LANES, LANES)] = source[pl.ds(start + p * rows, rows), :].astype(F32)
+
+
+def lay_out_kernel(parts, own, gu_panels, shared_ref, pack_ref, egu_ref, ed_ref, sgu_ref, sd_ref):
+    step = pl.program_id(0)
+    width = ed_ref.shape[2]
+    packed = pack_ref.shape[0] // parts
+    e_panels, e_rows = egu_ref.shape[2] // LANES, egu_ref.shape[1]
+    for e in range(parts):
+        for p in range(e_panels):
+            rows = pl.ds(pl.multiple_of(e * packed + p * width + step * e_rows, 16), e_rows)
+            egu_ref[e, :, pl.ds(p * LANES, LANES)] = pack_ref[rows, :].astype(F32)
+
+    @pl.when(step == 0)
+    def _():
+        for e in range(parts):
+            unpack(pack_ref, e * packed + e_panels * width, ed_ref.shape[1], width // LANES, ed_ref.at[e])
+
+    @pl.when(step == pl.num_programs(0) - 1)
+    def _():
+        unpack(shared_ref, 0, own, gu_panels, sgu_ref)
+        unpack(shared_ref, gu_panels * own, sd_ref.shape[0], width // LANES, sd_ref)
+
+
+def lay_out(shared, pack, parts, own, width, shared_hidden, hidden):
+    group, steps = width // own, 4
     columns = 2 * hidden // group
-    gu_panels = 2 * shared_hidden // LANES
-    x_piece = (x.shape[0] // count, LANES)
     outs = [
-        (parts, width, columns), (parts, hidden // group, width), (own, 3 * width), (own, width), (own, 2 * shared_hidden),
-        (shared_hidden // group, width), (8, LANES),
+        (parts, width, columns), (parts, hidden // group, width), (own, 2 * shared_hidden), (shared_hidden // group, width)
     ]
-    sems = pltpu.SemaphoreType.DMA((2, count))
     return call(
-        functools.partial(combine_kernel, axis, count, own, gu_panels, parts), (steps,),
-        [pl.BlockSpec((block, dest.shape[1]), lambda i: (i, 0)), pl.BlockSpec((block, top), lambda i: (i, 0)), pl.BlockSpec((block, 1), lambda i: (i, 0)), blocked, blocked]
-        + [whole(returned.shape), whole(x.shape), whole(piece.shape), whole(pack.shape)],
-        [blocked, pl.BlockSpec((parts, width // steps, columns), lambda i: (0, i, 0))] + [whole(shape) for shape in outs[1:]],
-        [shape_of((rows, width), BF16)] + [shape_of(shape, F32) for shape in outs],
-        scratch=[pltpu.VMEM((2, 2, count) + x_piece, BF16), pltpu.VMEM(x_piece, F32), pltpu.VMEM(x.shape, BF16)] + [sems] * 4,
-        flops=4 * rows * slots * width, moved=10 * rows * width + 2 * slots * width, collective_id=2,
-    )(dest, gates, live, first_sum, shared_out, returned, x, piece, pack)
+        functools.partial(lay_out_kernel, parts, own, 2 * shared_hidden // LANES), (steps,),
+        [whole(shared.shape), whole(pack.shape)],
+        [pl.BlockSpec((parts, width // steps, columns), lambda i: (0, i, 0))] + [whole(shape) for shape in outs[1:]],
+        [shape_of(shape, F32) for shape in outs],
+        flops=shared.size + pack.size, moved=6 * (shared.size + pack.size),
+    )(shared, pack)
+
+
+def lay_out_attention_kernel(own, x_ref, qkv_ref, wo_ref, gain_ref):
+    panels = wo_ref.shape[1] // LANES
+    unpack(x_ref, 0, own, 3 * panels, qkv_ref)
+    unpack(x_ref, 3 * panels * own, own, panels, wo_ref)
+    gain_ref[...] = x_ref[pl.ds(4 * panels * own, gain_ref.shape[0]), :].astype(F32)
+
+
+def lay_out_attention(x, own, width):
+    outs = [(own, 3 * width), (own, width), (8, LANES)]
+    return call(
+        functools.partial(lay_out_attention_kernel, own), (1,), [whole(x.shape)], [whole(shape) for shape in outs],
+        [shape_of(shape, F32) for shape in outs], flops=x.size, moved=6 * x.size,
+    )(x)
 
 
 def slot_numbers(block, slots, part):
@@ -538,13 +538,14 @@
 
 
 class LineSum:
-    def __init__(self, axis, count, x_ref, buffers, send_sem, recv_sem):
+    def __init__(self, axis, count, x_ref, buffers, send_sem, recv_sem, turn, turns):
         self.axis, self.count, self.x_ref, self.buffers = axis, count, x_ref, buffers
         self.send_sem, self.recv_sem = send_sem, recv_sem
-        self.rows = buffers.shape[3]
+        self.rows, self.turn, self.turns = buffers.shape[3], turn, turns
 
     def own(self, piece):
-        return self.x_ref[pl.ds(pl.multiple_of(piece * self.rows, 16), self.rows), :].astype(F32)
+        first = (piece * self.turns + self.turn) * self.rows
+        return self.x_ref[pl.ds(pl.multiple_of(first, 16), self.rows), :].astype(F32)
 
     def copy(self, way, piece):
         return line_copy(
@@ -598,13 +599,14 @@
 
 
 class LineGather:
-    def __init__(self, axis, count, out_ref, send_sem, recv_sem):
+    def __init__(self, axis, count, out_ref, send_sem, recv_sem, turn, turns):
         self.axis, self.count, self.out_ref = axis, count, out_ref
         self.send_sem, self.recv_sem = send_sem, recv_sem
-        self.rows = out_ref.shape[0] // count
+        self.rows, self.turn, self.turns = out_ref.shape[0] // count // turns, turn, turns
 
     def place(self, piece):
-        return self.out_ref.at[pl.ds(pl.multiple_of(piece * self.rows, 16), self.rows), :]
+        first = (piece * self.turns + self.turn) * self.rows
+        return self.out_ref.at[pl.ds(pl.multiple_of(first, 16), self.rows), :]
 
     def copy(self, way, piece):
         return line_copy(
@@ -675,8 +677,11 @@
     def target(piece, bit):
         return {"dp": piece // spread, "shard": (piece % spread) * 2 + bit}
 
-    line = LineSum("expert", count, x_ref, x_buffers, x_send, x_recv)
-    gather = LineGather("expert", count, x_all, g_send, g_recv)
+    turns = x_buffers.shape[0]
+    lines = [
+        LineSum("expert", count, x_ref, x_buffers.at[t], x_send.at[t], x_recv.at[t], t, turns) for t in range(turns)
+    ]
+    gathers = [LineGather("expert", count, x_all, g_send.at[t], g_recv.at[t], t, turns) for t in range(turns)]
 
     def pair_copy():
         return pltpu.make_async_remote_copy(
@@ -706,7 +711,7 @@
         pl.semaphore_wait(barrier, halves + neighbours)
         pair_copy().start()
         own_copy().start()
-        line.start()
+        lines[0].start()
 
     @pl.when(step == 1)
     def _():
@@ -728,17 +733,25 @@
 
     @pl.when(step == last)
     def _():
-        line.relay()
-        line.finish(x_total)
-        gather.start(x_total[...].astype(BF16))
+        for t in range(turns):
+            if t:
+                lines[t].start()
+            lines[t].relay()
+            if t:
+                gathers[t - 1].relay(1)
+            lines[t].finish(x_total)
+            gathers[t].start(x_total[...].astype(BF16))
         total = own[place].astype(F32) + landed[place].astype(F32)
         for index in range(halves - 1):
             send(index).wait()
             total = total + arrived[index].astype(F32)
         share_ref[...] = total.astype(BF16)
         for k in range(1, count):
-            gather.relay(k)
-        gather.finish()
+            for t in range(turns):
+                if k > 1 or t == turns - 1:
+                    gathers[t].relay(k)
+        for gather in gathers:
+            gather.finish()
         all_ref[...] = x_all[...]
 
 
@@ -748,7 +761,8 @@
     blocked = pl.BlockSpec((block, width), lambda i: (i, 0))
     halves, count = sizes[0] * sizes[1] // 2, pack.shape[1]
     piece = (count, LANES)
-    x_piece = (x.shape[0] // sizes[2], LANES)
+    turns = 2 if x.shape[0] // sizes[2] % 32 == 0 else 1
+    x_piece = (x.shape[0] // sizes[2] // turns, LANES)
     return call(
         functools.partial(settle_kernel, sizes), (rows // block,),
         [blocked] * 3 + [square(width, 0), square(width, 1), square(width, 2), blocked, blocked, whole((1, width)),
@@ -759,8 +773,8 @@
                  pltpu.VMEM((halves - 1,) + piece, BF16), pltpu.VMEM((halves - 1,) + piece, BF16),
                  pltpu.SemaphoreType.DMA, pltpu.SemaphoreType.DMA, pltpu.SemaphoreType.DMA,
                  pltpu.SemaphoreType.DMA((halves - 1,)), pltpu.SemaphoreType.DMA((halves - 1,)),
-                 pltpu.VMEM((2, 2, sizes[2]) + x_piece, BF16), pltpu.VMEM(x_piece, F32), pltpu.VMEM(x.shape, BF16)]
-        + [pltpu.SemaphoreType.DMA((2, sizes[2]))] * 4,
+                 pltpu.VMEM((turns, 2, 2, sizes[2]) + x_piece, BF16), pltpu.VMEM(x_piece, F32), pltpu.VMEM(x.shape, BF16)]
+        + [pltpu.SemaphoreType.DMA((turns, 2, sizes[2]))] * 4,
         flops=6 * rows * width * width, moved=22 * rows * width, collective_id=1,
     )(*grads, w_qkv, w_qkv, w_qkv, tokens, grad_first, gain, pack.reshape((halves, 2) + piece), x)
 
@@ -1079,10 +1093,18 @@
         (lax.axis_size("dp"), lax.axis_size("shard"), owners),
     )
     returned = exchange(y)
-    layer_out, expert_gu, expert_down, qkv_grad, out_grad, shared_gu, shared_down, gain_rows = combine(
-        table, route_gates, live, first_sum, shared_out, returned.reshape(-1, width), attention_share, shared_share,
-        expert_share, local_experts, "expert", owners, own, shared_hidden, hidden,
-    )
+    pieces = lax.all_to_all(
+        attention_share.reshape(owners, -1, LANES), "expert", split_axis=0, concat_axis=0, tiled=True
+    )
+    piece = jnp.sum(pieces.astype(F32), axis=0).astype(BF16)
+    attention_share = lax.all_to_all(
+        jnp.broadcast_to(piece[None], pieces.shape), "expert", split_axis=0, concat_axis=0, tiled=True
+    ).reshape(attention_share.shape)
+    layer_out = combine(table, route_gates, live, first_sum, shared_out, returned.reshape(-1, width))
+    expert_gu, expert_down, shared_gu, shared_down = lay_out(
+        shared_share, expert_share, local_experts, own, width, shared_hidden, hidden
+    )
+    qkv_grad, out_grad, gain_rows = lay_out_attention(attention_share, own, width)
     grad_gain_one = jnp.sum(w_qkv.astype(F32) * qkv_grad, axis=1) / norm_gains[0].astype(F32)
     grad_gains = jnp.stack([grad_gain_one, gain_rows[0, :own]])
     return layer_out, input_grad, grad_gains, qkv_grad, out_grad, shared_gu, shared_down, expert_gu, expert_down

time: 589 us -> 666 us (1.13)
  waiting for transfers between devices: 108 us -> 185 us
  blocking collectives: 10.3 us -> 26.8 us
  local copies, waits for them, and re-layouts: 22.3 us -> 11.5 us
    all_to_all x2, waiting for transfers between devices: 72.8 us -> 146 us  [exchange(): lax.all_to_all(rows.reshape(owners, -1, width), 'expert', split_axis=0, c...]
    pallas_call x1 -> x3, Pallas kernels: 37.9 us -> 20.1 us  [the longest x1 12.1 us: combine(): call(combine_kernel, (rows // block,), [pl.BlockSpec((block, dest.shape[1...]
    all_to_all x0 -> x1, blocking collectives: none -> 16.5 us  [local(): lax.all_to_all(attention_share.reshape(owners, -1, LANES), 'expert', spli...]
    unnamed x43 -> x22, local copies, waits for them, and re-layouts: 17.5 us -> 4.81 us
    pallas_call x1, Pallas kernels: 62.2 us -> 74.9 us  [settle(): call(functools.partial(settle_kernel, sizes), (rows // block,), [blocked]...]
    all_to_all x2, starting transfers between devices: 21.4 us -> 13.8 us  [exchange(): lax.all_to_all(rows.reshape(owners, -1, width), 'expert', split_axis=0, c...]
  transfers between devices with their start and end apart: 6 -> 7, of which waited for: 3 -> 5; matrix products, arithmetic and copies ran while one was open for 2% -> 3% of each run, Pallas kernels for 54% -> 52%
where the time goes in v7:
time: 666 us; the launch traced here: 655 us
  Pallas kernels  388 us (58%)
  waiting for transfers between devices  185 us (28%)
  blocking collectives  26.8 us (4%)
  starting transfers between devices  18.1 us (3%)
  between operations  14.9 us (2%)
  local copies, waits for them, and re-layouts  11.5 us (2%)
  other arithmetic  11.2 us (2%)
    all_to_all x2, waiting for transfers between devices, exchange(): lax.all_to_all(rows.reshape(owners, -1, width), 'expert', split_axis=0, c...  146 us
    pallas_call x3, Pallas kernels, ffn_both(): call(functools.partial(ffn_kernel, out_type, layout, block, axis, count),...  132 us
    pallas_call x1, Pallas kernels, settle(): call(functools.partial(settle_kernel, sizes), (rows // block,), [blocked]...  74.9 us
    pallas_call x1, Pallas kernels, add_part(): call(functools.partial(add_part_kernel, part, top, axis, count), (rows //...  34.9 us
    pallas_call x1, Pallas kernels, attend_backward(): call(functools.partial(attend_backward_kernel, head_dim, block), (seqs, p...  34.5 us
    pallas_call x1, Pallas kernels, attend_forward(): call(functools.partial(attend_forward_kernel, head_dim, block), (seqs, pa...  33.1 us
    pallas_call x3, Pallas kernels, dispatch(): call(functools.partial(dispatch_kernel, gated, first, base), (experts,),...  19.6 us
    all_gather x1, waiting for transfers between devices, local(): lax.all_gather(jnp.concatenate([w_qkv, w_out], axis=1), GROUP, axis=0, ti...  18.4 us
  transfers between devices with their start and end apart: 7, of which 5 were waited for; matrix products, arithmetic and copies ran while one was open for 3% of the time, Pallas kernels for 52%

profile of v7, /device:TPU:0, one launch (start us, length us, event | category | flops | bytes accessed | tf_op | source)
XLA Modules:
  0.0 655.1 jit_solution(402908598626415035)
XLA Ops:
  12.0 10.3 %all-gather.1 = bf16[8,96,2]{1,2,0:T(2,128)(2,1)S(1)} all-gather(bf16[1,96,2]{1,2,0:T(2,128)(2,1)S(1)} %bitcast.61), channel_id=1, replica_groups=mesh['dp'=2,'expert'=4,'shard'=4] {'dp','shard'}, dimensions={0}, use_global_device_ids=true | all-gather | bytes 3456 | tf_op jit(solution)/shard_map/all_gather | solution.py:1019
  25.7 3.9 shard_map.191.x_ref.normed_ref
  33.6 18.4 %all-gather.5.cloned.1.call-done.wq_ref.wk_ref.wv_ref.weight_ref = bf16[768,3072]{1,0:T(8,128)(2,1)} async-done(((bf16[96,3072]{1,0:T(8,128)(2,1)}), bf16[768,3072]{1,0:T(8,128)(2,1)}) %all-gather.5.cloned.1.call-update) | async-done | bytes 4718608 | tf_op jit(solution)/shard_map/all_gather | solution.py:1020
  52.0 33.1 %shard_map.192 = (bf16[1024,768]{1,0:T(8,128)(2,1)}, bf16[1024,768]{1,0:T(8,128)(2,1)}, bf16[1024,768]{1,0:T(8,128)(2,1)}, bf16[1024,768]{1,0:T(8,128)(2,1)}, f32[96,1024]{1,0:T(8,128)}) custom-call(bf16[1024,768]{1,0:T(8,128)(2,1)} %shard_map.191.x_ref.normed_ref, bf16[768,3072]{1,0:T(8,128)(2,1)} %all-gather.5.cloned.1.call-done.wq_ref.wk_ref.wv_ref.weight_ref, ...), custom_call_target="tpu_custom_call" | custom-call | flops 6845104128 | bytes 12582912 | tf_op jit(solution)/shard_map/pallas_call | solution.py:140
  85.1 5.8 shard_map.193
  90.9 5.1 shard_map.194
  95.9 16.7 %all-gather.7.cloned.1.call-done = bf16[18432,256]{1,0:T(8,128)(2,1)} async-done(((bf16[2304,256]{1,0:T(8,128)(2,1)}), bf16[18432,256]{1,0:T(8,128)(2,1)}) %all-gather.7.cloned.1.call-update) | async-done | bytes 9437200 | tf_op jit(solution)/shard_map/all_gather | solution.py:1021
  112.6 42.1 %shard_map.195 = (f32[1024,768]{1,0:T(8,128)}, f32[1024,768]{1,0:T(8,128)}, bf16[8,4608,128]{2,1,0:T(8,128)(2,1)}, bf16[4,288,768]{2,1,0:T(8,128)(2,1)}) custom-call(bf16[1024,768]{1,0:T(8,128)(2,1)} %get-tuple-element.54.x_ref, bf16[1024,768]{1,0:T(8,128)(2,1)} %broadcast_select_fusion.gy_ref.x_ref, bf16[8,2304,256]{2,1,0:T(8,128)(2,1)} %bitcast.62, ...), custom_call_target="tpu_custom_call" | custom-call | flops 28991029248 | bytes 31457280 | tf_op jit(solution)/shard_map/pallas_call | solution.py:919
  154.7 8.6 %shard_map.196 = bf16[2304,768]{1,0:T(8,128)(2,1)} custom-call(s32[8,1024]{1,0:T(8,128)} %get-tuple-element.55.dest_ref, f32[2,1024]{1,0:T(2,128)} %bitcast.59, bf16[1024,768]{1,0:T(8,128)(2,1)} %broadcast_select_fusion.gy_ref.x_ref), custom_call_target="tpu_custom_call" | custom-call | flops 3623878656 | bytes 5111808 | tf_op jit(solution)/shard_map/pallas_call | solution.py:319
  163.3 10.1 %all-to-all-start = ((bf16[4,576,768]{2,1,0:T(8,128)(2,1)}), bf16[4,576,768]{2,1,0:T(8,128)(2,1)S(1)}, u32[]{:S(2)}, u32[]{:S(2)}) async-start(bf16[4,576,768]{2,1,0:T(8,128)(2,1)} %bitcast.43), calls=%async_computation | async-start | bytes 7077888 | tf_op jit(solution)/shard_map/all_to_all | solution.py:1038
  173.4 5.9 shard_map.197
  179.3 72.8 %all-to-all-done.gy_ref = bf16[4,576,768]{2,1,0:T(8,128)(2,1)S(1)} async-done(((bf16[4,576,768]{2,1,0:T(8,128)(2,1)}), bf16[4,576,768]{2,1,0:T(8,128)(2,1)S(1)}, u32[]{:S(2)}, u32[]{:S(2)}) %all-to-all-start) | async-done | bytes 3538976 | tf_op jit(solution)/shard_map/all_to_all | solution.py:1038
  253.8 44.5 %shard_map.198 = (bf16[4,576,768]{2,1,0:T(8,128)(2,1)}, bf16[1152,768]{1,0:T(8,128)(2,1)}, bf16[8,9216,128]{2,1,0:T(8,128)(2,1)}, bf16[4,288,768]{2,1,0:T(8,128)(2,1)}) custom-call(bf16[1152,768]{1,0:T(8,128)(2,1)} %bitcast.66, bf16[4,576,768]{2,1,0:T(8,128)(2,1)} %copy-done.1, bf16[2,768,4096]{2,1,0:T(8,128)(2,1)} %wu_ref.3, bf16[2,768,4096]{2,1,0:T(8,128)(2,1)} %wu_ref.3, ...), custom_call_target="tpu_custom_call" | custom-call | flops 32614907904 | bytes 33030144 | tf_op jit(solution)/shard_map/pallas_call | solution.py:919
  298.3 45.6 %shard_map.199 = (bf16[4,576,768]{2,1,0:T(8,128)(2,1)}, bf16[1152,768]{1,0:T(8,128)(2,1)}, bf16[8,9216,128]{2,1,0:T(8,128)(2,1)}, bf16[4,288,768]{2,1,0:T(8,128)(2,1)}) custom-call(bf16[1152,768]{1,0:T(8,128)(2,1)} %bitcast.69, bf16[4,576,768]{2,1,0:T(8,128)(2,1)} %copy-done.1, ...), custom_call_target="tpu_custom_call", output_to_operand_aliasing={{0}: (6, {}), {2}: (7, {})} | custom-call | flops 32614907904 | bytes 33030144 | tf_op jit(solution)/shard_map/pallas_call | solution.py:919
  344.8 34.9 %shard_map.200 = (f32[1024,768]{1,0:T(8,128)}, bf16[4,288,768]{2,1,0:T(8,128)(2,1)}) custom-call(s32[1024,8]{1,0:T(8,128)} %get-tuple-element.51.dest_ref, f32[1024,768]{1,0:T(8,128)} %get-tuple-element.63.base_ref, bf16[1152,768]{1,0:T(8,128)(2,1)} %bitcast.50, bf16[4,288,768]{2,1,0:T(8,128)(2,1)} %bitcast.49), custom_call_target="tpu_custom_call" | custom-call | flops 1811939328 | bytes 6291456 | tf_op jit(solution)/shard_map/pallas_call | solution.py:486
  379.7 12.1 %shard_map.202 = (f32[1024,768]{1,0:T(8,128)}, bf16[1024,768]{1,0:T(8,128)(2,1)}, bf16[1024,768]{1,0:T(8,128)(2,1)}, f32[1,768]{1,0:T(1,128)}) custom-call(s32[1024,8]{1,0:T(8,128)} %get-tuple-element.51.dest_ref, f32[1024,1]{1,0:T(8,128)} %fusion.4.live_ref, bf16[1024,768]{1,0:T(8,128)(2,1)} %cot_ref.1, f32[1024,768]{1,0:T(8,128)} %get-tuple-element.53.sum_ref, ...), custom_call_target="tpu_custom_call" | custom-call | flops 3019898880 | bytes 14155776 | tf_op jit(solution)/shard_map/pallas_call | solution.py:522
  393.2 34.5 %shard_map.203 = (bf16[1024,768]{1,0:T(8,128)(2,1)}, bf16[1024,768]{1,0:T(8,128)(2,1)}, bf16[1024,768]{1,0:T(8,128)(2,1)}) custom-call(bf16[1024,768]{1,0:T(8,128)(2,1)} %get-tuple-element.68.q_ref, bf16[1024,768]{1,0:T(8,128)(2,1)} %get-tuple-element.69.k_ref, bf16[1024,768]{1,0:T(8,128)(2,1)} %get-tuple-element.70.v_ref, ...), custom_call_target="tpu_custom_call" | custom-call | flops 8053063680 | bytes 12582912 | tf_op jit(solution)/shard_map/pallas_call | solution.py:211
  427.7 14.8 %shard_map.204 = bf16[8,2496,128]{2,1,0:T(8,128)(2,1)} custom-call(bf16[1024,768]{1,0:T(8,128)(2,1)} %shard_map.191.x_ref.normed_ref, bf16[1024,768]{1,0:T(8,128)(2,1)} %get-tuple-element.52.mixed_ref.o_ref, bf16[1024,768]{1,0:T(8,128)(2,1)} %get-tuple-element.75.gq_ref, bf16[1024,768]{1,0:T(8,128)(2,1)} %get-tuple-element.76.gk_ref, ...), custom_call_target="tpu_custom_call" | custom-call | flops 4831838208 | bytes 12582912 | tf_op jit(solution)/shard_map/pallas_call | solution.py:981
  442.5 74.9 %shard_map.205 = (f32[1024,768]{1,0:T(8,128)}, bf16[2496,128]{1,0:T(8,128)(2,1)}, bf16[4608,128]{1,0:T(8,128)(2,1)}) custom-call(bf16[1024,768]{1,0:T(8,128)(2,1)} %get-tuple-element.75.gq_ref, bf16[1024,768]{1,0:T(8,128)(2,1)} %get-tuple-element.76.gk_ref, bf16[1024,768]{1,0:T(8,128)(2,1)} %get-tuple-element.77.gv_ref, ...), custom_call_target="tpu_custom_call" | custom-call | flops 3623878656 | bytes 17301504 | tf_op jit(solution)/shard_map/pallas_call | solution.py:766
  517.3 16.5 %all_to_all.20 = bf16[4,624,128]{2,1,0:T(8,128)(2,1)} all-to-all(bf16[4,624,128]{2,1,0:T(8,128)(2,1)} %bitcast.56), channel_id=1, replica_groups=mesh['dp'=2,'expert'=4,'shard'=4] {'expert'}, dimensions={0} | all-to-all | bytes 1277952 | tf_op jit(solution)/shard_map/all_to_all | solution.py:1096
  539.5 73.6 %all-to-all-done.1 = bf16[4,576,768]{2,1,0:T(8,128)(2,1)S(1)} async-done(((bf16[4,576,768]{2,1,0:T(8,128)(2,1)}), bf16[4,576,768]{2,1,0:T(8,128)(2,1)S(1)}, u32[]{:S(2)}, u32[]{:S(2)}) %all-to-all-start.1) | async-done | bytes 3538976 | tf_op jit(solution)/shard_map/all_to_all | solution.py:1038
  615.1 4.2 all-to-all-start.3
  620.3 12.1 %shard_map.201 = bf16[1024,768]{1,0:T(8,128)(2,1)} custom-call(s32[1024,8]{1,0:T(8,128)} %get-tuple-element.51.dest_ref, f32[1024,2]{1,0:T(8,128)} %copy.62.gates_ref, f32[1024,1]{1,0:T(8,128)} %fusion.4.live_ref, f32[1024,768]{1,0:T(8,128)} %get-tuple-element.53.sum_ref, f32[1024,768]{1,0:T(8,128)} %get-tuple-element.56.shared_ref, bf16[2304,768]{1,0:T(8,128)(2,1)} %bitcast.42), custom_call_target="tpu_custom_call" | custom-call | flops 7247757312 | bytes 11403264 | tf_op jit(solution)/shard_map/pallas_call | solution.py:351
  640.7 5.9 shard_map.207
  (63 shorter events, 34.2 us)
Async XLA Ops:
  7.2 2.2 copy-start.5
  7.2 2.5 copy-start.4
  7.2 44.8 %all-gather.5.cloned.1.call-start = ((), (), s32[]{:S(2)}) async-start(), calls=%async_computation.6 | async-start | bytes 5308416 | tf_op jit(solution)/shard_map/all_gather | solution.py:1020
  9.3 103.3 %all-gather.7.cloned.1.call-start = ((), (), s32[]{:S(2)}) async-start(), calls=%async_computation.9 | async-start | bytes 10616832 | tf_op jit(solution)/shard_map/all_gather | solution.py:1021
  10.1 1.8 copy-start.7
  11.3 431.2 %reduce-scatter.3.cloned.1.call-start = ((), (), s32[]{:S(2)}) async-start(), calls=%async_computation.7 | async-start | bytes 10616832 | tf_op jit(solution)/shard_map/reduce_scatter | solution.py:1087
  25.1 7.1 %copy-start = (bf16[1024,768]{1,0:T(8,128)(2,1)S(1)}, bf16[1024,768]{1,0:T(8,128)(2,1)}, u32[]{:S(2)}) copy-start(bf16[1024,768]{1,0:T(8,128)(2,1)} %cot_ref.1) | copy-start | bytes 4718596
  163.3 88.7 %all-to-all-start = ((bf16[4,576,768]{2,1,0:T(8,128)(2,1)}), bf16[4,576,768]{2,1,0:T(8,128)(2,1)S(1)}, u32[]{:S(2)}, u32[]{:S(2)}) async-start(bf16[4,576,768]{2,1,0:T(8,128)(2,1)} %bitcast.43), calls=%async_computation | async-start | bytes 7077888 | tf_op jit(solution)/shard_map/all_to_all | solution.py:1038
  173.4 467.3 %reduce-scatter.5.cloned.1.call-start = ((), (), s32[]{:S(2)}) async-start(), calls=%async_computation.8 | async-start | bytes 21233664 | tf_op jit(solution)/shard_map/reduce_scatter | solution.py:1087
  252.1 1.7 copy-start.1
  533.8 79.2 %all-to-all-start.1 = ((bf16[4,576,768]{2,1,0:T(8,128)(2,1)}), bf16[4,576,768]{2,1,0:T(8,128)(2,1)S(1)}, u32[]{:S(2)}, u32[]{:S(2)}) async-start(bf16[4,576,768]{2,1,0:T(8,128)(2,1)} %get-tuple-element.67), calls=%async_computation.1 | async-start | bytes 7077888 | tf_op jit(solution)/shard_map/all_to_all | solution.py:1038
  537.6 81.7 %copy-start.6 = (f32[1024,2]{0,1:T(2,128)S(1)}, f32[1024,2]{0,1:T(2,128)}, u32[]{:S(2)}) copy-start(f32[1024,2]{0,1:T(2,128)} %param.15) | copy-start | bytes 24580
  613.1 7.3 %copy-start.2 = (bf16[4,576,768]{2,1,0:T(8,128)(2,1)}, bf16[4,576,768]{2,1,0:T(8,128)(2,1)S(1)}, u32[]{:S(2)}) copy-start(bf16[4,576,768]{2,1,0:T(8,128)(2,1)S(1)} %all-to-all-done.1) | copy-start | bytes 10616836
  615.1 20.7 %all-to-all-start.3 = ((bf16[4,624,128]{2,1,0:T(8,128)(2,1)}), bf16[4,624,128]{2,1,0:T(8,128)(2,1)}, u32[]{:S(2)}, u32[]{:S(2)}) async-start(bf16[4,624,128]{2,1,0:T(8,128)(2,1)} %broadcast_in_dim.30), calls=%async_computation.4 | async-start | bytes 1277952 | tf_op jit(solution)/shard_map/all_to_all | solution.py:1100
  632.5 7.7 %copy-start.8 = (bf16[2,96]{1,0:T(2,128)(2,1)S(1)}, bf16[2,96]{1,0:T(2,128)(2,1)}, u32[]{:S(2)}) copy-start(bf16[2,96]{1,0:T(2,128)(2,1)} %param.17) | copy-start | bytes 1156
  640.7 5.9 copy-start.3
Sparse Core Ops, SparseCore 0:
  10.5 41.4 all-gather.4
  53.9 58.6 all-gather.6
  154.8 82.2 reduce-scatter.2
  344.1 144.9 reduce-scatter.4

commit v8 on v7

--- a/solution.py
+++ b/solution.py
@@ -362,7 +362,7 @@
         target[:, pl.ds(p * LANES, LANES)] = source[pl.ds(start + p * rows, rows), :].astype(F32)
 
 
-def lay_out_kernel(parts, own, gu_panels, shared_ref, pack_ref, egu_ref, ed_ref, sgu_ref, sd_ref):
+def lay_out_kernel(parts, pack_ref, egu_ref, ed_ref):
     step = pl.program_id(0)
     width = ed_ref.shape[2]
     packed = pack_ref.shape[0] // parts
@@ -377,25 +377,30 @@
         for e in range(parts):
             unpack(pack_ref, e * packed + e_panels * width, ed_ref.shape[1], width // LANES, ed_ref.at[e])
 
-    @pl.when(step == pl.num_programs(0) - 1)
-    def _():
-        unpack(shared_ref, 0, own, gu_panels, sgu_ref)
-        unpack(shared_ref, gu_panels * own, sd_ref.shape[0], width // LANES, sd_ref)
-
-
-def lay_out(shared, pack, parts, own, width, shared_hidden, hidden):
+
+def lay_out(pack, parts, own, width, hidden):
     group, steps = width // own, 4
     columns = 2 * hidden // group
-    outs = [
-        (parts, width, columns), (parts, hidden // group, width), (own, 2 * shared_hidden), (shared_hidden // group, width)
-    ]
-    return call(
-        functools.partial(lay_out_kernel, parts, own, 2 * shared_hidden // LANES), (steps,),
-        [whole(shared.shape), whole(pack.shape)],
-        [pl.BlockSpec((parts, width // steps, columns), lambda i: (0, i, 0))] + [whole(shape) for shape in outs[1:]],
+    outs = [(parts, width, columns), (parts, hidden // group, width)]
+    return call(
+        functools.partial(lay_out_kernel, parts), (steps,), [whole(pack.shape)],
+        [pl.BlockSpec((parts, width // steps, columns), lambda i: (0, i, 0)), whole(outs[1])],
         [shape_of(shape, F32) for shape in outs],
-        flops=shared.size + pack.size, moved=6 * (shared.size + pack.size),
-    )(shared, pack)
+        flops=pack.size, moved=6 * pack.size,
+    )(pack)
+
+
+def lay_out_shared_kernel(own, gu_panels, x_ref, sgu_ref, sd_ref):
+    unpack(x_ref, 0, own, gu_panels, sgu_ref)
+    unpack(x_ref, gu_panels * own, sd_ref.shape[0], sd_ref.shape[1] // LANES, sd_ref)
+
+
+def lay_out_shared(x, own, width, hidden):
+    outs = [(own, 2 * hidden), (hidden // (width // own), width)]
+    return call(
+        functools.partial(lay_out_shared_kernel, own, 2 * hidden // LANES), (1,), [whole(x.shape)],
+        [whole(shape) for shape in outs], [shape_of(shape, F32) for shape in outs], flops=x.size, moved=6 * x.size,
+    )(x)
 
 
 def lay_out_attention_kernel(own, x_ref, qkv_ref, wo_ref, gain_ref):
@@ -530,142 +535,9 @@
     )(dest, live, cotangent, first_sum, base, gain, weights, rows_of)
 
 
-def line_copy(axis, ahead, source, target, send_sem, recv_sem):
-    return pltpu.make_async_remote_copy(
-        src_ref=source, dst_ref=target, send_sem=send_sem, recv_sem=recv_sem,
-        device_id={axis: lax.axis_index(axis) + ahead}, device_id_type=pl.DeviceIdType.MESH,
-    )
-
-
-class LineSum:
-    def __init__(self, axis, count, x_ref, buffers, send_sem, recv_sem, turn, turns):
-        self.axis, self.count, self.x_ref, self.buffers = axis, count, x_ref, buffers
-        self.send_sem, self.recv_sem = send_sem, recv_sem
-        self.rows, self.turn, self.turns = buffers.shape[3], turn, turns
-
-    def own(self, piece):
-        first = (piece * self.turns + self.turn) * self.rows
-        return self.x_ref[pl.ds(pl.multiple_of(first, 16), self.rows), :].astype(F32)
-
-    def copy(self, way, piece):
-        return line_copy(
-            self.axis, 1 - 2 * way, self.buffers.at[way, 1, piece], self.buffers.at[way, 0, piece],
-            self.send_sem.at[way, piece], self.recv_sem.at[way, piece],
-        )
-
-    def each(self, body):
-        me = lax.axis_index(self.axis)
-        for k in range(self.count - 1):
-            for way, piece in ((0, self.count - 1 - k), (1, k)):
-                before = me > 0 if way == 0 else me < self.count - 1
-                sends = me < piece if way == 0 else me > piece
-                body(way, piece, before, sends)
-
-    def start(self):
-        def body(way, piece, before, sends):
-            @pl.when(sends & jnp.logical_not(before))
-            def _():
-                self.buffers[way, 1, piece] = self.own(piece).astype(BF16)
-                self.copy(way, piece).start()
-
-        self.each(body)
-
-    def relay(self):
-        def body(way, piece, before, sends):
-            @pl.when(sends & before)
-            def _():
-                self.copy(way, piece).wait_recv()
-                self.buffers[way, 1, piece] = (self.own(piece) + self.buffers[way, 0, piece].astype(F32)).astype(BF16)
-                self.copy(way, piece).start()
-
-        self.each(body)
-
-    def finish(self, total_ref):
-        me = lax.axis_index(self.axis)
-        total_ref[...] = self.own(me)
-        for way, before in ((0, me > 0), (1, me < self.count - 1)):
-
-            @pl.when(before)
-            def _():
-                self.copy(way, me).wait_recv()
-                total_ref[...] += self.buffers[way, 0, me].astype(F32)
-
-        def body(way, piece, before, sends):
-            @pl.when(sends)
-            def _():
-                self.copy(way, piece).wait_send()
-
-        self.each(body)
-
-
-class LineGather:
-    def __init__(self, axis, count, out_ref, send_sem, recv_sem, turn, turns):
-        self.axis, self.count, self.out_ref = axis, count, out_ref
-        self.send_sem, self.recv_sem = send_sem, recv_sem
-        self.rows, self.turn, self.turns = out_ref.shape[0] // count // turns, turn, turns
-
-    def place(self, piece):
-        first = (piece * self.turns + self.turn) * self.rows
-        return self.out_ref.at[pl.ds(pl.multiple_of(first, 16), self.rows), :]
-
-    def copy(self, way, piece):
-        return line_copy(
-            self.axis, 1 - 2 * way, self.place(piece), self.place(piece),
-            self.send_sem.at[way, piece], self.recv_sem.at[way, piece],
-        )
-
-    def start(self, value):
-        me = lax.axis_index(self.axis)
-        self.place(me)[...] = value
-        for way, more in ((0, me < self.count - 1), (1, me > 0)):
-
-            @pl.when(more)
-            def _():
-                self.copy(way, me).start()
-
-    def relay(self, k):
-        me = lax.axis_index(self.axis)
-        for way, piece, there, more in (
-            (0, me - k, me >= k, me < self.count - 1),
-            (1, me + k, me + k < self.count, me > 0),
-        ):
-
-            @pl.when(there)
-            def _():
-                self.copy(way, piece).wait_recv()
-
-            @pl.when(there & more)
-            def _():
-                self.copy(way, piece).start()
-
-    def finish(self):
-        me = lax.axis_index(self.axis)
-        for k in range(self.count):
-            for way, piece, sent in (
-                (0, me - k, (me >= k) & (me < self.count - 1)),
-                (1, me + k, (me + k < self.count) & (me > 0)),
-            ):
-
-                @pl.when(sent)
-                def _():
-                    self.copy(way, piece).wait_send()
-
-
-def greet_neighbours(barrier, axis, count):
-    me = lax.axis_index(axis)
-    for ahead, there in ((1, me < count - 1), (-1, me > 0)):
-
-        @pl.when(there)
-        def _():
-            pl.semaphore_signal(barrier, inc=1, device_id={axis: me + ahead}, device_id_type=pl.DeviceIdType.MESH)
-
-    return (me < count - 1).astype(jnp.int32) + (me > 0).astype(jnp.int32)
-
-
 def settle_kernel(sizes, gq_ref, gk_ref, gv_ref, wq_ref, wk_ref, wv_ref, tokens_ref, first_ref, gain_ref, pack_ref,
-                  x_ref, out_ref, share_ref, all_ref, own, landed, chosen, arrived, sem, pair_send, pair_recv, send_sem,
-                  recv_sem, x_buffers, x_total, x_all, x_send, x_recv, g_send, g_recv):
-    dp_size, shard_size, count = sizes
+                  out_ref, share_ref, own, landed, chosen, arrived, sem, pair_send, pair_recv, send_sem, recv_sem):
+    dp_size, shard_size = sizes
     spread = shard_size // 2
     halves = dp_size * spread
     dp, shard = lax.axis_index("dp"), lax.axis_index("shard")
@@ -677,12 +549,6 @@
     def target(piece, bit):
         return {"dp": piece // spread, "shard": (piece % spread) * 2 + bit}
 
-    turns = x_buffers.shape[0]
-    lines = [
-        LineSum("expert", count, x_ref, x_buffers.at[t], x_send.at[t], x_recv.at[t], t, turns) for t in range(turns)
-    ]
-    gathers = [LineGather("expert", count, x_all, g_send.at[t], g_recv.at[t], t, turns) for t in range(turns)]
-
     def pair_copy():
         return pltpu.make_async_remote_copy(
             src_ref=pack_ref.at[:, 1 - side], dst_ref=landed, send_sem=pair_send, recv_sem=pair_recv,
@@ -707,11 +573,9 @@
                 barrier, inc=1, device_id=target(lax.rem(place + index + 1, halves), side),
                 device_id_type=pl.DeviceIdType.MESH,
             )
-        neighbours = greet_neighbours(barrier, "expert", count)
-        pl.semaphore_wait(barrier, halves + neighbours)
+        pl.semaphore_wait(barrier, halves)
         pair_copy().start()
         own_copy().start()
-        lines[0].start()
 
     @pl.when(step == 1)
     def _():
@@ -733,50 +597,30 @@
 
     @pl.when(step == last)
     def _():
-        for t in range(turns):
-            if t:
-                lines[t].start()
-            lines[t].relay()
-            if t:
-                gathers[t - 1].relay(1)
-            lines[t].finish(x_total)
-            gathers[t].start(x_total[...].astype(BF16))
         total = own[place].astype(F32) + landed[place].astype(F32)
         for index in range(halves - 1):
             send(index).wait()
             total = total + arrived[index].astype(F32)
         share_ref[...] = total.astype(BF16)
-        for k in range(1, count):
-            for t in range(turns):
-                if k > 1 or t == turns - 1:
-                    gathers[t].relay(k)
-        for gather in gathers:
-            gather.finish()
-        all_ref[...] = x_all[...]
-
-
-def settle(grads, w_qkv, tokens, grad_first, gain, pack, x, sizes):
+
+
+def settle(grads, w_qkv, tokens, grad_first, gain, pack, sizes):
     rows, width = tokens.shape
     block = min(256, rows)
     blocked = pl.BlockSpec((block, width), lambda i: (i, 0))
     halves, count = sizes[0] * sizes[1] // 2, pack.shape[1]
     piece = (count, LANES)
-    turns = 2 if x.shape[0] // sizes[2] % 32 == 0 else 1
-    x_piece = (x.shape[0] // sizes[2] // turns, LANES)
     return call(
         functools.partial(settle_kernel, sizes), (rows // block,),
         [blocked] * 3 + [square(width, 0), square(width, 1), square(width, 2), blocked, blocked, whole((1, width)),
-                         pl.BlockSpec(memory_space=pl.ANY), whole(x.shape)],
-        [blocked, whole(piece), whole(x.shape)],
-        [shape_of((rows, width), F32), shape_of(piece, BF16), shape_of(x.shape, BF16)],
+                         pl.BlockSpec(memory_space=pl.ANY)],
+        [blocked, whole(piece)], [shape_of((rows, width), F32), shape_of(piece, BF16)],
         scratch=[pltpu.VMEM((halves,) + piece, BF16), pltpu.VMEM((halves,) + piece, BF16),
                  pltpu.VMEM((halves - 1,) + piece, BF16), pltpu.VMEM((halves - 1,) + piece, BF16),
                  pltpu.SemaphoreType.DMA, pltpu.SemaphoreType.DMA, pltpu.SemaphoreType.DMA,
-                 pltpu.SemaphoreType.DMA((halves - 1,)), pltpu.SemaphoreType.DMA((halves - 1,)),
-                 pltpu.VMEM((turns, 2, 2, sizes[2]) + x_piece, BF16), pltpu.VMEM(x_piece, F32), pltpu.VMEM(x.shape, BF16)]
-        + [pltpu.SemaphoreType.DMA((turns, 2, sizes[2]))] * 4,
+                 pltpu.SemaphoreType.DMA((halves - 1,)), pltpu.SemaphoreType.DMA((halves - 1,))],
         flops=6 * rows * width * width, moved=22 * rows * width, collective_id=1,
-    )(*grads, w_qkv, w_qkv, w_qkv, tokens, grad_first, gain, pack.reshape((halves, 2) + piece), x)
+    )(*grads, w_qkv, w_qkv, w_qkv, tokens, grad_first, gain, pack.reshape((halves, 2) + piece))
 
 
 def copies_of(layout, block, width, step, stage_g, stage_u, stage_d, slot, packed_ref, sems):
@@ -1039,7 +883,7 @@
             rows.reshape(owners, -1, width), "expert", split_axis=0, concat_axis=0, tiled=True
         ).reshape(rows.shape)
 
-    send_grad = dispatch(table_t, gates_t, grad_b, experts, capacity, True, 0, 0)
+    send_grad = dispatch(table_t, gates_t, cotangent, experts, capacity, True, 0, 0)
     received_grad = exchange(send_grad).reshape(owners, local_experts * capacity, width)
 
     cosine, sine = rotary_tables(length, head_dim)
@@ -1088,10 +932,11 @@
 
     shared_share = spread(shared_pack)
     expert_share = spread(pack)
-    input_grad, attention_share, shared_share = settle(
-        grads, attention_weight, tokens, grad_first, gain_one, attention_pack, shared_share,
-        (lax.axis_size("dp"), lax.axis_size("shard"), owners),
-    )
+    input_grad, attention_share = settle(
+        grads, attention_weight, tokens, grad_first, gain_one, attention_pack,
+        (lax.axis_size("dp"), lax.axis_size("shard")),
+    )
+    shared_share = lax.psum(shared_share, "expert")
     returned = exchange(y)
     pieces = lax.all_to_all(
         attention_share.reshape(owners, -1, LANES), "expert", split_axis=0, concat_axis=0, tiled=True
@@ -1101,9 +946,8 @@
         jnp.broadcast_to(piece[None], pieces.shape), "expert", split_axis=0, concat_axis=0, tiled=True
     ).reshape(attention_share.shape)
     layer_out = combine(table, route_gates, live, first_sum, shared_out, returned.reshape(-1, width))
-    expert_gu, expert_down, shared_gu, shared_down = lay_out(
-        shared_share, expert_share, local_experts, own, width, shared_hidden, hidden
-    )
+    expert_gu, expert_down = lay_out(expert_share, local_experts, own, width, hidden)
+    shared_gu, shared_down = lay_out_shared(shared_share, own, width, shared_hidden)
     qkv_grad, out_grad, gain_rows = lay_out_attention(attention_share, own, width)
     grad_gain_one = jnp.sum(w_qkv.astype(F32) * qkv_grad, axis=1) / norm_gains[0].astype(F32)
     grad_gains = jnp.stack([grad_gain_one, gain_rows[0, :own]])

time: 666 us -> 694 us (1.042)
  blocking collectives: 26.8 us -> 51.6 us
  Pallas kernels: 388 us -> 410 us
  waiting for transfers between devices: 185 us -> 171 us
    pallas_call x1, Pallas kernels: 34.9 us -> 56.1 us  [add_part(): call(functools.partial(add_part_kernel, part, top, axis, count), (rows //...]
    pallas_call x1, Pallas kernels: 74.9 us -> 54.8 us  [settle(): call(functools.partial(settle_kernel, sizes), (rows // block,), [blocked]...]
    all_to_all x0 -> x1, blocking collectives: none -> 19.4 us  [local(): lax.all_to_all(jnp.broadcast_to(piece[None], pieces.shape), 'expert', spl...]
    pallas_call x3, Pallas kernels: 132 us -> 143 us  [ffn_both(): call(functools.partial(ffn_kernel, out_type, layout, block, axis, count),...]
    all_to_all x2, waiting for transfers between devices: 146 us -> 136 us  [exchange(): lax.all_to_all(rows.reshape(owners, -1, width), 'expert', split_axis=0, c...]
    pallas_call x3, Pallas kernels: 19.6 us -> 28.4 us  [dispatch(): call(functools.partial(dispatch_kernel, gated, first, base), (experts,),...]
  transfers between devices with their start and end apart: 7 -> 7, of which waited for: 5 -> 4; matrix products, arithmetic and copies ran while one was open for 3% -> 2% of each run, Pallas kernels for 52% -> 53%
where the time goes in v8:
time: 694 us; the launch traced here: 683 us
  Pallas kernels  410 us (59%)
  waiting for transfers between devices  171 us (25%)
  blocking collectives  51.6 us (7%)
  between operations  15.1 us (2%)
  starting transfers between devices  14.4 us (2%)
  local copies, waits for them, and re-layouts  11.3 us (2%)
  other arithmetic  9.47 us (1%)
    pallas_call x3, Pallas kernels, ffn_both(): call(functools.partial(ffn_kernel, out_type, layout, block, axis, count),...  143 us
    all_to_all x2, waiting for transfers between devices, exchange(): lax.all_to_all(rows.reshape(owners, -1, width), 'expert', split_axis=0, c...  136 us
    pallas_call x1, Pallas kernels, add_part(): call(functools.partial(add_part_kernel, part, top, axis, count), (rows //...  56.1 us
    pallas_call x1, Pallas kernels, settle(): call(functools.partial(settle_kernel, sizes), (rows // block,), [blocked]...  54.8 us
    pallas_call x1, Pallas kernels, attend_backward(): call(functools.partial(attend_backward_kernel, head_dim, block), (seqs, p...  34.8 us
    pallas_call x1, Pallas kernels, attend_forward(): call(functools.partial(attend_forward_kernel, head_dim, block), (seqs, pa...  33.1 us
    pallas_call x3, Pallas kernels, dispatch(): call(functools.partial(dispatch_kernel, gated, first, base), (experts,),...  28.4 us
    all_to_all x1, blocking collectives, local(): lax.all_to_all(attention_share.reshape(owners, -1, LANES), 'expert', spli...  21.9 us
  transfers between devices with their start and end apart: 7, of which 4 were waited for; matrix products, arithmetic and copies ran while one was open for 2% of the time, Pallas kernels for 53%

profile of v8, /device:TPU:0, one launch (start us, length us, event | category | flops | bytes accessed | tf_op | source)
XLA Modules:
  0.0 683.5 jit_solution(6890233272251152120)
XLA Ops:
  12.0 10.3 %all-gather.1 = bf16[8,96,2]{1,2,0:T(2,128)(2,1)S(1)} all-gather(bf16[1,96,2]{1,2,0:T(2,128)(2,1)S(1)} %bitcast.62), channel_id=1, replica_groups=mesh['dp'=2,'expert'=4,'shard'=4] {'dp','shard'}, dimensions={0}, use_global_device_ids=true | all-gather | bytes 3456 | tf_op jit(solution)/shard_map/all_gather | solution.py:863
  33.6 18.4 %all-gather.5.cloned.1.call-done.wq_ref.wk_ref.wv_ref.weight_ref = bf16[768,3072]{1,0:T(8,128)(2,1)} async-done(((bf16[96,3072]{1,0:T(8,128)(2,1)}), bf16[768,3072]{1,0:T(8,128)(2,1)}) %all-gather.5.cloned.1.call-update) | async-done | bytes 4718608 | tf_op jit(solution)/shard_map/all_gather | solution.py:864
  52.0 33.1 %shard_map.192 = (bf16[1024,768]{1,0:T(8,128)(2,1)}, bf16[1024,768]{1,0:T(8,128)(2,1)}, bf16[1024,768]{1,0:T(8,128)(2,1)}, bf16[1024,768]{1,0:T(8,128)(2,1)}, f32[96,1024]{1,0:T(8,128)}) custom-call(bf16[1024,768]{1,0:T(8,128)(2,1)} %shard_map.191.x_ref.normed_ref, bf16[768,3072]{1,0:T(8,128)(2,1)} %all-gather.5.cloned.1.call-done.wq_ref.wk_ref.wv_ref.weight_ref, ...), custom_call_target="tpu_custom_call" | custom-call | flops 6845104128 | bytes 12582912 | tf_op jit(solution)/shard_map/pallas_call | solution.py:140
  85.1 5.8 shard_map.193
  90.9 5.1 shard_map.194
  96.0 16.7 %all-gather.7.cloned.1.call-done = bf16[18432,256]{1,0:T(8,128)(2,1)} async-done(((bf16[2304,256]{1,0:T(8,128)(2,1)}), bf16[18432,256]{1,0:T(8,128)(2,1)}) %all-gather.7.cloned.1.call-update) | async-done | bytes 9437200 | tf_op jit(solution)/shard_map/all_gather | solution.py:865
  112.6 42.0 %shard_map.195 = (f32[1024,768]{1,0:T(8,128)}, f32[1024,768]{1,0:T(8,128)}, bf16[8,4608,128]{2,1,0:T(8,128)(2,1)}, bf16[4,288,768]{2,1,0:T(8,128)(2,1)}) custom-call(bf16[1024,768]{1,0:T(8,128)(2,1)} %get-tuple-element.53.x_ref, bf16[1024,768]{1,0:T(8,128)(2,1)} %broadcast_select_fusion.gy_ref, bf16[8,2304,256]{2,1,0:T(8,128)(2,1)} %bitcast.63, ...), custom_call_target="tpu_custom_call" | custom-call | flops 28991029248 | bytes 31457280 | tf_op jit(solution)/shard_map/pallas_call | solution.py:763
  154.7 8.6 %shard_map.196 = bf16[2304,768]{1,0:T(8,128)(2,1)} custom-call(s32[8,1024]{1,0:T(8,128)} %get-tuple-element.54.dest_ref, f32[2,1024]{1,0:T(2,128)} %bitcast.60, bf16[1024,768]{1,0:T(8,128)(2,1)} %cot_ref.1), custom_call_target="tpu_custom_call" | custom-call | flops 3623878656 | bytes 5111808 | tf_op jit(solution)/shard_map/pallas_call | solution.py:319
  163.3 10.1 %all-to-all-start = ((bf16[4,576,768]{2,1,0:T(8,128)(2,1)}), bf16[4,576,768]{2,1,0:T(8,128)(2,1)S(1)}, u32[]{:S(2)}, u32[]{:S(2)}) async-start(bf16[4,576,768]{2,1,0:T(8,128)(2,1)} %bitcast.43), calls=%async_computation | async-start | bytes 7077888 | tf_op jit(solution)/shard_map/all_to_all | solution.py:882
  173.4 14.7 %shard_map.197 = bf16[1152,768]{1,0:T(8,128)(2,1)} custom-call(s32[8,1024]{1,0:T(8,128)} %get-tuple-element.54.dest_ref, f32[2,1024]{1,0:T(2,128)} %bitcast.61, bf16[1024,768]{1,0:T(8,128)(2,1)} %get-tuple-element.53.x_ref), custom_call_target="tpu_custom_call" | custom-call | flops 1811939328 | bytes 3342336 | tf_op jit(solution)/shard_map/pallas_call | solution.py:319
  188.1 64.0 %all-to-all-done.gy_ref = bf16[4,576,768]{2,1,0:T(8,128)(2,1)S(1)} async-done(((bf16[4,576,768]{2,1,0:T(8,128)(2,1)}), bf16[4,576,768]{2,1,0:T(8,128)(2,1)S(1)}, u32[]{:S(2)}, u32[]{:S(2)}) %all-to-all-start) | async-done | bytes 3538976 | tf_op jit(solution)/shard_map/all_to_all | solution.py:882
  253.8 44.4 %shard_map.198 = (bf16[4,576,768]{2,1,0:T(8,128)(2,1)}, bf16[1152,768]{1,0:T(8,128)(2,1)}, bf16[8,9216,128]{2,1,0:T(8,128)(2,1)}, bf16[4,288,768]{2,1,0:T(8,128)(2,1)}) custom-call(bf16[1152,768]{1,0:T(8,128)(2,1)} %bitcast.67, bf16[4,576,768]{2,1,0:T(8,128)(2,1)} %copy-done.1, bf16[2,768,4096]{2,1,0:T(8,128)(2,1)} %wu_ref.3, bf16[2,768,4096]{2,1,0:T(8,128)(2,1)} %wu_ref.3, ...), custom_call_target="tpu_custom_call" | custom-call | flops 32614907904 | bytes 33030144 | tf_op jit(solution)/shard_map/pallas_call | solution.py:763
  298.3 56.6 %shard_map.199 = (bf16[4,576,768]{2,1,0:T(8,128)(2,1)}, bf16[1152,768]{1,0:T(8,128)(2,1)}, bf16[8,9216,128]{2,1,0:T(8,128)(2,1)}, bf16[4,288,768]{2,1,0:T(8,128)(2,1)}) custom-call(bf16[1152,768]{1,0:T(8,128)(2,1)} %bitcast.69, bf16[4,576,768]{2,1,0:T(8,128)(2,1)} %copy-done.1, ...), custom_call_target="tpu_custom_call", output_to_operand_aliasing={{0}: (6, {}), {2}: (7, {})} | custom-call | flops 32614907904 | bytes 33030144 | tf_op jit(solution)/shard_map/pallas_call | solution.py:763
  355.8 56.1 %shard_map.200 = (f32[1024,768]{1,0:T(8,128)}, bf16[4,288,768]{2,1,0:T(8,128)(2,1)}) custom-call(s32[1024,8]{1,0:T(8,128)} %get-tuple-element.50.dest_ref, f32[1024,768]{1,0:T(8,128)} %get-tuple-element.62.base_ref, bf16[1152,768]{1,0:T(8,128)(2,1)} %bitcast.51, bf16[4,288,768]{2,1,0:T(8,128)(2,1)} %bitcast.50), custom_call_target="tpu_custom_call" | custom-call | flops 1811939328 | bytes 6291456 | tf_op jit(solution)/shard_map/pallas_call | solution.py:491
  412.0 11.6 %shard_map.202 = (f32[1024,768]{1,0:T(8,128)}, bf16[1024,768]{1,0:T(8,128)(2,1)}, bf16[1024,768]{1,0:T(8,128)(2,1)}, f32[1,768]{1,0:T(1,128)}) custom-call(s32[1024,8]{1,0:T(8,128)} %get-tuple-element.50.dest_ref, f32[1024,1]{1,0:T(8,128)} %fusion.4.live_ref, bf16[1024,768]{1,0:T(8,128)(2,1)} %cot_ref.1, f32[1024,768]{1,0:T(8,128)} %get-tuple-element.52.sum_ref, ...), custom_call_target="tpu_custom_call" | custom-call | flops 3019898880 | bytes 14155776 | tf_op jit(solution)/shard_map/pallas_call | solution.py:527
  425.0 34.8 %shard_map.203 = (bf16[1024,768]{1,0:T(8,128)(2,1)}, bf16[1024,768]{1,0:T(8,128)(2,1)}, bf16[1024,768]{1,0:T(8,128)(2,1)}) custom-call(bf16[1024,768]{1,0:T(8,128)(2,1)} %get-tuple-element.67.q_ref, bf16[1024,768]{1,0:T(8,128)(2,1)} %get-tuple-element.68.k_ref, bf16[1024,768]{1,0:T(8,128)(2,1)} %get-tuple-element.69.v_ref, ...), custom_call_target="tpu_custom_call" | custom-call | flops 8053063680 | bytes 12582912 | tf_op jit(solution)/shard_map/pallas_call | solution.py:211
  459.8 14.9 %shard_map.204 = bf16[8,2496,128]{2,1,0:T(8,128)(2,1)} custom-call(bf16[1024,768]{1,0:T(8,128)(2,1)} %shard_map.191.x_ref.normed_ref, bf16[1024,768]{1,0:T(8,128)(2,1)} %get-tuple-element.51.mixed_ref.o_ref, bf16[1024,768]{1,0:T(8,128)(2,1)} %get-tuple-element.74.gq_ref, bf16[1024,768]{1,0:T(8,128)(2,1)} %get-tuple-element.75.gk_ref, ...), custom_call_target="tpu_custom_call" | custom-call | flops 4831838208 | bytes 12582912 | tf_op jit(solution)/shard_map/pallas_call | solution.py:825
  474.7 54.8 %shard_map.205 = (f32[1024,768]{1,0:T(8,128)}, bf16[2496,128]{1,0:T(8,128)(2,1)}) custom-call(bf16[1024,768]{1,0:T(8,128)(2,1)} %get-tuple-element.74.gq_ref, bf16[1024,768]{1,0:T(8,128)(2,1)} %get-tuple-element.75.gk_ref, bf16[1024,768]{1,0:T(8,128)(2,1)} %get-tuple-element.76.gv_ref, ...), custom_call_target="tpu_custom_call" | custom-call | flops 3623878656 | bytes 17301504 | tf_op jit(solution)/shard_map/pallas_call | solution.py:613
  529.6 21.9 %all_to_all.20 = bf16[4,624,128]{2,1,0:T(8,128)(2,1)S(1)} all-to-all(bf16[4,624,128]{2,1,0:T(8,128)(2,1)} %bitcast.57), channel_id=1, replica_groups=mesh['dp'=2,'expert'=4,'shard'=4] {'expert'}, dimensions={0} | all-to-all | bytes 1277952 | tf_op jit(solution)/shard_map/all_to_all | solution.py:941
  551.7 19.4 %all_to_all.21 = bf16[4,624,128]{2,1,0:T(8,128)(2,1)} all-to-all(bf16[4,624,128]{2,1,0:T(8,128)(2,1)S(1)} %broadcast_in_dim.30), channel_id=1, replica_groups=mesh['dp'=2,'expert'=4,'shard'=4] {'expert'}, dimensions={0} | all-to-all | bytes 1277952 | tf_op jit(solution)/shard_map/all_to_all | solution.py:945
  571.1 4.1 all-to-all-start.1
  581.1 72.3 %all-to-all-done.1 = bf16[4,576,768]{2,1,0:T(8,128)(2,1)S(1)} async-done(((bf16[4,576,768]{2,1,0:T(8,128)(2,1)}), bf16[4,576,768]{2,1,0:T(8,128)(2,1)S(1)}, u32[]{:S(2)}, u32[]{:S(2)}) %all-to-all-start.1) | async-done | bytes 3538976 | tf_op jit(solution)/shard_map/all_to_all | solution.py:882
  655.2 12.1 %shard_map.201 = bf16[1024,768]{1,0:T(8,128)(2,1)} custom-call(s32[1024,8]{1,0:T(8,128)} %get-tuple-element.50.dest_ref, f32[1024,2]{1,0:T(8,128)} %copy.62.gates_ref, f32[1024,1]{1,0:T(8,128)} %fusion.4.live_ref, f32[1024,768]{1,0:T(8,128)} %get-tuple-element.52.sum_ref, f32[1024,768]{1,0:T(8,128)} %get-tuple-element.55.shared_ref, bf16[2304,768]{1,0:T(8,128)(2,1)} %bitcast.42), custom_call_target="tpu_custom_call" | custom-call | flops 7247757312 | bytes 11403264 | tf_op jit(solution)/shard_map/pallas_call | solution.py:351
  670.3 4.5 shard_map.208
  (66 shorter events, 32.0 us)
Async XLA Ops:
  7.2 2.2 copy-start.5
  7.2 2.5 copy-start.4
  7.2 44.8 %all-gather.5.cloned.1.call-start = ((), (), s32[]{:S(2)}) async-start(), calls=%async_computation.6 | async-start | bytes 5308416 | tf_op jit(solution)/shard_map/all_gather | solution.py:864
  9.3 103.3 %all-gather.7.cloned.1.call-start = ((), (), s32[]{:S(2)}) async-start(), calls=%async_computation.10 | async-start | bytes 10616832 | tf_op jit(solution)/shard_map/all_gather | solution.py:865
  10.1 1.8 copy-start.7
  11.3 286.9 %reduce-scatter.3.cloned.1.call-start = ((), (), s32[]{:S(2)}) async-start(), calls=%async_computation.7 | async-start | bytes 10616832 | tf_op jit(solution)/shard_map/reduce_scatter | solution.py:931
  25.1 7.1 %copy-start = (bf16[1024,768]{1,0:T(8,128)(2,1)S(1)}, bf16[1024,768]{1,0:T(8,128)(2,1)}, u32[]{:S(2)}) copy-start(bf16[1024,768]{1,0:T(8,128)(2,1)} %cot_ref.1) | copy-start | bytes 4718596
  163.3 88.8 %all-to-all-start = ((bf16[4,576,768]{2,1,0:T(8,128)(2,1)}), bf16[4,576,768]{2,1,0:T(8,128)(2,1)S(1)}, u32[]{:S(2)}, u32[]{:S(2)}) async-start(bf16[4,576,768]{2,1,0:T(8,128)(2,1)} %bitcast.43), calls=%async_computation | async-start | bytes 7077888 | tf_op jit(solution)/shard_map/all_to_all | solution.py:882
  173.4 494.0 %all-reduce.3.cloned.1.call-start = ((), (), s32[]{:S(2)}) async-start(), calls=%async_computation.8 | async-start | bytes 2359296 | tf_op jit(solution)/shard_map/psum | solution.py:939
  252.0 1.7 copy-start.1
  298.3 372.1 %reduce-scatter.5.cloned.1.call-start = ((), (), s32[]{:S(2)}) async-start(), calls=%async_computation.9 | async-start | bytes 21233664 | tf_op jit(solution)/shard_map/reduce_scatter | solution.py:931
  571.1 4.1 copy-start.6
  571.1 82.4 %all-to-all-start.1 = ((bf16[4,576,768]{2,1,0:T(8,128)(2,1)}), bf16[4,576,768]{2,1,0:T(8,128)(2,1)S(1)}, u32[]{:S(2)}, u32[]{:S(2)}) async-start(bf16[4,576,768]{2,1,0:T(8,128)(2,1)} %get-tuple-element.66), calls=%async_computation.1 | async-start | bytes 7077888 | tf_op jit(solution)/shard_map/all_to_all | solution.py:882
  575.2 5.3 copy-start.8
  653.4 1.8 copy-start.2
  667.4 7.5 %copy-start.3 = (f32[1024,768]{1,0:T(8,128)S(1)}, f32[1024,768]{1,0:T(8,128)}, u32[]{:S(2)}) copy-start(f32[1024,768]{1,0:T(8,128)} %get-tuple-element.108) | copy-start | bytes 9437188
Sparse Core Ops, SparseCore 0:
  10.5 41.4 all-gather.4
  53.9 58.6 all-gather.6
  154.8 82.2 reduce-scatter.2
  298.4 109.6 all-reduce.2
  411.6 149.5 reduce-scatter.4

commit v9 on v7

--- a/solution.py
+++ b/solution.py
@@ -741,15 +741,15 @@
                 gathers[t - 1].relay(1)
             lines[t].finish(x_total)
             gathers[t].start(x_total[...].astype(BF16))
+        for k in range(1, count):
+            for t in range(turns):
+                if k > 1 or t == turns - 1:
+                    gathers[t].relay(k)
         total = own[place].astype(F32) + landed[place].astype(F32)
         for index in range(halves - 1):
             send(index).wait()
             total = total + arrived[index].astype(F32)
         share_ref[...] = total.astype(BF16)
-        for k in range(1, count):
-            for t in range(turns):
-                if k > 1 or t == turns - 1:
-                    gathers[t].relay(k)
         for gather in gathers:
             gather.finish()
         all_ref[...] = x_all[...]
@@ -823,8 +823,9 @@
     return 3 * width * hidden // owners // LANES
 
 
-def ffn_kernel(out_type, layout, block, axis, count, x_ref, gy_ref, wg_ref, wu_ref, wd_ref, sent_ref, *rest):
-    y_ref, gx_ref, packed_ref, kept_ref, xt, y_acc, gx_acc, stage_g, stage_u, stage_d, sems, *exchange_sems = rest[-14:]
+def ffn_kernel(out_type, layout, block, first, axis, count, x_ref, gy_ref, wg_ref, wu_ref, wd_ref, sent_ref, *rest):
+    (y_ref, gx_ref, packed_ref, kept_ref, x_own, gy_own, xt, y_acc, gx_acc, stage_g, stage_u, stage_d, sems, load_sems,
+     *exchange_sems) = rest[-17:]
     exchange = Exchange(axis, count, sent_ref, kept_ref, *exchange_sems)
     step = pl.program_id(0)
     steps = layout[2] // block
@@ -835,7 +836,16 @@
     @pl.when(step == 0)
     def _():
         exchange.start()
-        xt[...] = x_ref[...].T
+        gy_source = gy_ref if first is None else gy_ref.at[:, pl.ds(first, gy_own.shape[1]), :]
+        loads = [
+            pltpu.make_async_copy(x_ref, x_own, load_sems.at[0]),
+            pltpu.make_async_copy(gy_source, gy_own, load_sems.at[1]),
+        ]
+        for load in loads:
+            load.start()
+        for load in loads:
+            load.wait()
+        xt[...] = x_own[...].T
         y_acc[...] = jnp.zeros_like(y_acc)
         gx_acc[...] = jnp.zeros_like(gx_acc)
 
@@ -844,7 +854,7 @@
         for copy in copies(step - 2, stage_g, stage_u, stage_d, slot, packed_ref, sems):
             copy.wait()
 
-    x, gy = x_ref[...], gy_ref[...].reshape(x_ref.shape)
+    x, gy = x_own[...], gy_own[...].reshape(x_ref.shape)
     if layout[0]:
         wg, wu = wg_ref[...].reshape(width, block), wu_ref[...].reshape(width, block)
         rows = wd_ref.shape[1] // (width // block)
@@ -900,16 +910,14 @@
         down = pl.BlockSpec((None, block, width), lambda f: (expert, f, 0))
         stage = (2, width, block)
     if by_rows:
-        grads = whole((rows, width))
+        first, gy_shape = None, (rows, width)
         y_block, y_shape = whole((rows, width)), (rows, width)
     else:
         y_shape = (gy.shape[0], parts * (rows // gy.shape[0]), width)
         y_block = pl.BlockSpec(
             (gy.shape[0], rows // gy.shape[0], width), lambda f: (0, expert, 0), pipeline_mode=pl.Buffered(1)
         )
-        grads = pl.BlockSpec(
-            (gy.shape[0], rows // gy.shape[0], width), lambda f: (0, expert, 0), pipeline_mode=pl.Buffered(1)
-        )
+        first, gy_shape = expert * (rows // gy.shape[0]), (gy.shape[0], rows // gy.shape[0], width)
     out_rows = whole((rows, width))
     pack_rows = packed_rows(width, hidden, owners)
     layout = (by_rows, owners, hidden, (expert or 0) * pack_rows)
@@ -917,14 +925,15 @@
     sent = sent.reshape(count, -1, width)
     copies = 2 * (block // LANES) + block // (hidden // owners) * (width // LANES)
     y, gx, pack, kept = call(
-        functools.partial(ffn_kernel, out_type, layout, block, axis, count), (steps,),
-        [whole((rows, width)), grads, gate, up, down, hbm] + [hbm] * len(held),
+        functools.partial(ffn_kernel, out_type, layout, block, first, axis, count), (steps,),
+        [hbm, hbm, gate, up, down, hbm] + [hbm] * len(held),
         [y_block, out_rows, hbm, hbm],
         [shape_of(y_shape, out_type), shape_of((rows, width), out_type),
          shape_of((owners, parts * pack_rows, LANES), BF16), shape_of(sent.shape, BF16)],
-        scratch=[pltpu.VMEM((width, rows), BF16), pltpu.VMEM((rows, width), F32), pltpu.VMEM((rows, width), F32),
+        scratch=[pltpu.VMEM((rows, width), BF16), pltpu.VMEM(gy_shape, BF16),
+                 pltpu.VMEM((width, rows), BF16), pltpu.VMEM((rows, width), F32), pltpu.VMEM((rows, width), F32),
                  pltpu.VMEM(stage, BF16), pltpu.VMEM(stage, BF16), pltpu.VMEM((2, block, width), BF16),
-                 pltpu.SemaphoreType.DMA((2, copies))] + Exchange.scratch(count),
+                 pltpu.SemaphoreType.DMA((2, copies)), pltpu.SemaphoreType.DMA((2,))] + Exchange.scratch(count),
         flops=18 * rows * width * hidden, moved=12 * width * hidden + 16 * rows * width, trans=rows * hidden,
         aliases={6: 0, 7: 2} if held else None, collective_id=collective_id,
     )(x, gy, w_gu, w_gu, w_down, sent, *held)
@@ -1039,7 +1048,7 @@
             rows.reshape(owners, -1, width), "expert", split_axis=0, concat_axis=0, tiled=True
         ).reshape(rows.shape)
 
-    send_grad = dispatch(table_t, gates_t, grad_b, experts, capacity, True, 0, 0)
+    send_grad = dispatch(table_t, gates_t, cotangent, experts, capacity, True, 0, 0)
     received_grad = exchange(send_grad).reshape(owners, local_experts * capacity, width)
 
     cosine, sine = rotary_tables(length, head_dim)

time: 666 us -> 667 us (level)
  no operation moved by 1% of the time
where the time goes in v9:
time: 667 us; the launch traced here: 656 us
  Pallas kernels  390 us (58%)
  waiting for transfers between devices  185 us (28%)
  blocking collectives  26.7 us (4%)
  starting transfers between devices  16.2 us (2%)
  between operations  14.9 us (2%)
  local copies, waits for them, and re-layouts  11.5 us (2%)
  other arithmetic  11.2 us (2%)
    all_to_all x2, waiting for transfers between devices, exchange(): lax.all_to_all(rows.reshape(owners, -1, width), 'expert', split_axis=0, c...  146 us
    pallas_call x3, Pallas kernels, ffn_both(): call(functools.partial(ffn_kernel, out_type, layout, block, first, axis,...  134 us
    pallas_call x1, Pallas kernels, settle(): call(functools.partial(settle_kernel, sizes), (rows // block,), [blocked]...  75.6 us
    pallas_call x1, Pallas kernels, add_part(): call(functools.partial(add_part_kernel, part, top, axis, count), (rows //...  34.7 us
    pallas_call x1, Pallas kernels, attend_backward(): call(functools.partial(attend_backward_kernel, head_dim, block), (seqs, p...  34.4 us
    pallas_call x1, Pallas kernels, attend_forward(): call(functools.partial(attend_forward_kernel, head_dim, block), (seqs, pa...  33.1 us
    pallas_call x3, Pallas kernels, dispatch(): call(functools.partial(dispatch_kernel, gated, first, base), (experts,),...  19.6 us
    all_gather x1, waiting for transfers between devices, local(): lax.all_gather(jnp.concatenate([w_qkv, w_out], axis=1), GROUP, axis=0, ti...  18.4 us
  transfers between devices with their start and end apart: 7, of which 5 were waited for; matrix products, arithmetic and copies ran while one was open for 3% of the time, Pallas kernels for 52%

profile of v9, /device:TPU:0, one launch (start us, length us, event | category | flops | bytes accessed | tf_op | source)
XLA Modules:
  0.0 655.8 jit_solution(17218574779226084313)
XLA Ops:
  12.0 10.3 %all-gather.1 = bf16[8,96,2]{1,2,0:T(2,128)(2,1)S(1)} all-gather(bf16[1,96,2]{1,2,0:T(2,128)(2,1)S(1)} %bitcast.61), channel_id=1, replica_groups=mesh['dp'=2,'expert'=4,'shard'=4] {'dp','shard'}, dimensions={0}, use_global_device_ids=true | all-gather | bytes 3456 | tf_op jit(solution)/shard_map/all_gather | solution.py:1028
  25.7 3.9 shard_map.191.x_ref.normed_ref
  33.6 18.4 %all-gather.5.cloned.1.call-done.wq_ref.wk_ref.wv_ref.weight_ref = bf16[768,3072]{1,0:T(8,128)(2,1)} async-done(((bf16[96,3072]{1,0:T(8,128)(2,1)}), bf16[768,3072]{1,0:T(8,128)(2,1)}) %all-gather.5.cloned.1.call-update) | async-done | bytes 4718608 | tf_op jit(solution)/shard_map/all_gather | solution.py:1029
  52.0 33.1 %shard_map.192 = (bf16[1024,768]{1,0:T(8,128)(2,1)}, bf16[1024,768]{1,0:T(8,128)(2,1)}, bf16[1024,768]{1,0:T(8,128)(2,1)}, bf16[1024,768]{1,0:T(8,128)(2,1)}, f32[96,1024]{1,0:T(8,128)}) custom-call(bf16[1024,768]{1,0:T(8,128)(2,1)} %shard_map.191.x_ref.normed_ref, bf16[768,3072]{1,0:T(8,128)(2,1)} %all-gather.5.cloned.1.call-done.wq_ref.wk_ref.wv_ref.weight_ref, ...), custom_call_target="tpu_custom_call" | custom-call | flops 6845104128 | bytes 12582912 | tf_op jit(solution)/shard_map/pallas_call | solution.py:140
  85.1 5.8 shard_map.193
  90.8 5.1 shard_map.194
  95.9 16.7 %all-gather.7.cloned.1.call-done = bf16[18432,256]{1,0:T(8,128)(2,1)} async-done(((bf16[2304,256]{1,0:T(8,128)(2,1)}), bf16[18432,256]{1,0:T(8,128)(2,1)}) %all-gather.7.cloned.1.call-update) | async-done | bytes 9437200 | tf_op jit(solution)/shard_map/all_gather | solution.py:1030
  112.6 42.9 %shard_map.195 = (f32[1024,768]{1,0:T(8,128)}, f32[1024,768]{1,0:T(8,128)}, bf16[8,4608,128]{2,1,0:T(8,128)(2,1)}, bf16[4,288,768]{2,1,0:T(8,128)(2,1)}) custom-call(bf16[1024,768]{1,0:T(8,128)(2,1)} %get-tuple-element.54.x_ref, bf16[1024,768]{1,0:T(8,128)(2,1)} %broadcast_select_fusion.gy_ref, bf16[8,2304,256]{2,1,0:T(8,128)(2,1)} %bitcast.62, ...), custom_call_target="tpu_custom_call" | custom-call | flops 28991029248 | bytes 31457280 | tf_op jit(solution)/shard_map/pallas_call | solution.py:927
  155.6 8.6 %shard_map.196 = bf16[2304,768]{1,0:T(8,128)(2,1)} custom-call(s32[8,1024]{1,0:T(8,128)} %get-tuple-element.55.dest_ref, f32[2,1024]{1,0:T(2,128)} %bitcast.59, bf16[1024,768]{1,0:T(8,128)(2,1)} %cot_ref.1), custom_call_target="tpu_custom_call" | custom-call | flops 3623878656 | bytes 5111808 | tf_op jit(solution)/shard_map/pallas_call | solution.py:319
  164.2 8.2 %all-to-all-start = ((bf16[4,576,768]{2,1,0:T(8,128)(2,1)}), bf16[4,576,768]{2,1,0:T(8,128)(2,1)S(1)}, u32[]{:S(2)}, u32[]{:S(2)}) async-start(bf16[4,576,768]{2,1,0:T(8,128)(2,1)} %bitcast.43), calls=%async_computation | async-start | bytes 7077888 | tf_op jit(solution)/shard_map/all_to_all | solution.py:1047
  172.4 5.9 shard_map.197
  178.3 72.8 %all-to-all-done.gy_ref = bf16[4,576,768]{2,1,0:T(8,128)(2,1)S(1)} async-done(((bf16[4,576,768]{2,1,0:T(8,128)(2,1)}), bf16[4,576,768]{2,1,0:T(8,128)(2,1)S(1)}, u32[]{:S(2)}, u32[]{:S(2)}) %all-to-all-start) | async-done | bytes 3538976 | tf_op jit(solution)/shard_map/all_to_all | solution.py:1047
  252.8 45.3 %shard_map.198 = (bf16[4,576,768]{2,1,0:T(8,128)(2,1)}, bf16[1152,768]{1,0:T(8,128)(2,1)}, bf16[8,9216,128]{2,1,0:T(8,128)(2,1)}, bf16[4,288,768]{2,1,0:T(8,128)(2,1)}) custom-call(bf16[1152,768]{1,0:T(8,128)(2,1)} %bitcast.66, bf16[4,576,768]{2,1,0:T(8,128)(2,1)} %copy-done.1, bf16[2,768,4096]{2,1,0:T(8,128)(2,1)} %wu_ref.3, bf16[2,768,4096]{2,1,0:T(8,128)(2,1)} %wu_ref.3, ...), custom_call_target="tpu_custom_call" | custom-call | flops 32614907904 | bytes 33030144 | tf_op jit(solution)/shard_map/pallas_call | solution.py:927
  298.1 46.1 %shard_map.199 = (bf16[4,576,768]{2,1,0:T(8,128)(2,1)}, bf16[1152,768]{1,0:T(8,128)(2,1)}, bf16[8,9216,128]{2,1,0:T(8,128)(2,1)}, bf16[4,288,768]{2,1,0:T(8,128)(2,1)}) custom-call(bf16[1152,768]{1,0:T(8,128)(2,1)} %bitcast.69, bf16[4,576,768]{2,1,0:T(8,128)(2,1)} %copy-done.1, ...), custom_call_target="tpu_custom_call", output_to_operand_aliasing={{0}: (6, {}), {2}: (7, {})} | custom-call | flops 32614907904 | bytes 33030144 | tf_op jit(solution)/shard_map/pallas_call | solution.py:927
  345.1 34.7 %shard_map.200 = (f32[1024,768]{1,0:T(8,128)}, bf16[4,288,768]{2,1,0:T(8,128)(2,1)}) custom-call(s32[1024,8]{1,0:T(8,128)} %get-tuple-element.51.dest_ref, f32[1024,768]{1,0:T(8,128)} %get-tuple-element.63.base_ref, bf16[1152,768]{1,0:T(8,128)(2,1)} %bitcast.50, bf16[4,288,768]{2,1,0:T(8,128)(2,1)} %bitcast.49), custom_call_target="tpu_custom_call" | custom-call | flops 1811939328 | bytes 6291456 | tf_op jit(solution)/shard_map/pallas_call | solution.py:486
  379.8 11.9 %shard_map.202 = (f32[1024,768]{1,0:T(8,128)}, bf16[1024,768]{1,0:T(8,128)(2,1)}, bf16[1024,768]{1,0:T(8,128)(2,1)}, f32[1,768]{1,0:T(1,128)}) custom-call(s32[1024,8]{1,0:T(8,128)} %get-tuple-element.51.dest_ref, f32[1024,1]{1,0:T(8,128)} %fusion.4.live_ref, bf16[1024,768]{1,0:T(8,128)(2,1)} %cot_ref.1, f32[1024,768]{1,0:T(8,128)} %get-tuple-element.53.sum_ref, ...), custom_call_target="tpu_custom_call" | custom-call | flops 3019898880 | bytes 14155776 | tf_op jit(solution)/shard_map/pallas_call | solution.py:522
  393.1 34.4 %shard_map.203 = (bf16[1024,768]{1,0:T(8,128)(2,1)}, bf16[1024,768]{1,0:T(8,128)(2,1)}, bf16[1024,768]{1,0:T(8,128)(2,1)}) custom-call(bf16[1024,768]{1,0:T(8,128)(2,1)} %get-tuple-element.68.q_ref, bf16[1024,768]{1,0:T(8,128)(2,1)} %get-tuple-element.69.k_ref, bf16[1024,768]{1,0:T(8,128)(2,1)} %get-tuple-element.70.v_ref, ...), custom_call_target="tpu_custom_call" | custom-call | flops 8053063680 | bytes 12582912 | tf_op jit(solution)/shard_map/pallas_call | solution.py:211
  427.6 14.8 %shard_map.204 = bf16[8,2496,128]{2,1,0:T(8,128)(2,1)} custom-call(bf16[1024,768]{1,0:T(8,128)(2,1)} %shard_map.191.x_ref.normed_ref, bf16[1024,768]{1,0:T(8,128)(2,1)} %get-tuple-element.52.mixed_ref.o_ref, bf16[1024,768]{1,0:T(8,128)(2,1)} %get-tuple-element.75.gq_ref, bf16[1024,768]{1,0:T(8,128)(2,1)} %get-tuple-element.76.gk_ref, ...), custom_call_target="tpu_custom_call" | custom-call | flops 4831838208 | bytes 12582912 | tf_op jit(solution)/shard_map/pallas_call | solution.py:990
  442.4 75.6 %shard_map.205 = (f32[1024,768]{1,0:T(8,128)}, bf16[2496,128]{1,0:T(8,128)(2,1)}, bf16[4608,128]{1,0:T(8,128)(2,1)}) custom-call(bf16[1024,768]{1,0:T(8,128)(2,1)} %get-tuple-element.75.gq_ref, bf16[1024,768]{1,0:T(8,128)(2,1)} %get-tuple-element.76.gk_ref, bf16[1024,768]{1,0:T(8,128)(2,1)} %get-tuple-element.77.gv_ref, ...), custom_call_target="tpu_custom_call" | custom-call | flops 3623878656 | bytes 17301504 | tf_op jit(solution)/shard_map/pallas_call | solution.py:766
  518.0 16.4 %all_to_all.20 = bf16[4,624,128]{2,1,0:T(8,128)(2,1)} all-to-all(bf16[4,624,128]{2,1,0:T(8,128)(2,1)} %bitcast.56), channel_id=1, replica_groups=mesh['dp'=2,'expert'=4,'shard'=4] {'expert'}, dimensions={0} | all-to-all | bytes 1277952 | tf_op jit(solution)/shard_map/all_to_all | solution.py:1105
  540.1 73.7 %all-to-all-done.1 = bf16[4,576,768]{2,1,0:T(8,128)(2,1)S(1)} async-done(((bf16[4,576,768]{2,1,0:T(8,128)(2,1)}), bf16[4,576,768]{2,1,0:T(8,128)(2,1)S(1)}, u32[]{:S(2)}, u32[]{:S(2)}) %all-to-all-start.1) | async-done | bytes 3538976 | tf_op jit(solution)/shard_map/all_to_all | solution.py:1047
  615.8 4.2 all-to-all-start.3
  621.0 12.1 %shard_map.201 = bf16[1024,768]{1,0:T(8,128)(2,1)} custom-call(s32[1024,8]{1,0:T(8,128)} %get-tuple-element.51.dest_ref, f32[1024,2]{1,0:T(8,128)} %copy.62.gates_ref, f32[1024,1]{1,0:T(8,128)} %fusion.4.live_ref, f32[1024,768]{1,0:T(8,128)} %get-tuple-element.53.sum_ref, f32[1024,768]{1,0:T(8,128)} %get-tuple-element.56.shared_ref, bf16[2304,768]{1,0:T(8,128)(2,1)} %bitcast.42), custom_call_target="tpu_custom_call" | custom-call | flops 7247757312 | bytes 11403264 | tf_op jit(solution)/shard_map/pallas_call | solution.py:351
  641.4 5.9 shard_map.207
  (63 shorter events, 34.2 us)
Async XLA Ops:
  7.2 2.2 copy-start.5
  7.2 2.5 copy-start.4
  7.2 44.8 %all-gather.5.cloned.1.call-start = ((), (), s32[]{:S(2)}) async-start(), calls=%async_computation.6 | async-start | bytes 5308416 | tf_op jit(solution)/shard_map/all_gather | solution.py:1029
  9.3 103.3 %all-gather.7.cloned.1.call-start = ((), (), s32[]{:S(2)}) async-start(), calls=%async_computation.9 | async-start | bytes 10616832 | tf_op jit(solution)/shard_map/all_gather | solution.py:1030
  10.1 1.8 copy-start.7
  11.3 431.1 %reduce-scatter.3.cloned.1.call-start = ((), (), s32[]{:S(2)}) async-start(), calls=%async_computation.7 | async-start | bytes 10616832 | tf_op jit(solution)/shard_map/reduce_scatter | solution.py:1096
  25.1 7.1 %copy-start = (bf16[1024,768]{1,0:T(8,128)(2,1)S(1)}, bf16[1024,768]{1,0:T(8,128)(2,1)}, u32[]{:S(2)}) copy-start(bf16[1024,768]{1,0:T(8,128)(2,1)} %cot_ref.1) | copy-start | bytes 4718596
  164.2 86.8 %all-to-all-start = ((bf16[4,576,768]{2,1,0:T(8,128)(2,1)}), bf16[4,576,768]{2,1,0:T(8,128)(2,1)S(1)}, u32[]{:S(2)}, u32[]{:S(2)}) async-start(bf16[4,576,768]{2,1,0:T(8,128)(2,1)} %bitcast.43), calls=%async_computation | async-start | bytes 7077888 | tf_op jit(solution)/shard_map/all_to_all | solution.py:1047
  172.4 469.0 %reduce-scatter.5.cloned.1.call-start = ((), (), s32[]{:S(2)}) async-start(), calls=%async_computation.8 | async-start | bytes 21233664 | tf_op jit(solution)/shard_map/reduce_scatter | solution.py:1096
  251.1 1.7 copy-start.1
  534.4 79.3 %all-to-all-start.1 = ((bf16[4,576,768]{2,1,0:T(8,128)(2,1)}), bf16[4,576,768]{2,1,0:T(8,128)(2,1)S(1)}, u32[]{:S(2)}, u32[]{:S(2)}) async-start(bf16[4,576,768]{2,1,0:T(8,128)(2,1)} %get-tuple-element.67), calls=%async_computation.1 | async-start | bytes 7077888 | tf_op jit(solution)/shard_map/all_to_all | solution.py:1047
  538.2 81.8 %copy-start.6 = (f32[1024,2]{0,1:T(2,128)S(1)}, f32[1024,2]{0,1:T(2,128)}, u32[]{:S(2)}) copy-start(f32[1024,2]{0,1:T(2,128)} %param.15) | copy-start | bytes 24580
  613.7 7.3 %copy-start.2 = (bf16[4,576,768]{2,1,0:T(8,128)(2,1)}, bf16[4,576,768]{2,1,0:T(8,128)(2,1)S(1)}, u32[]{:S(2)}) copy-start(bf16[4,576,768]{2,1,0:T(8,128)(2,1)S(1)} %all-to-all-done.1) | copy-start | bytes 10616836
  615.8 20.7 %all-to-all-start.3 = ((bf16[4,624,128]{2,1,0:T(8,128)(2,1)}), bf16[4,624,128]{2,1,0:T(8,128)(2,1)}, u32[]{:S(2)}, u32[]{:S(2)}) async-start(bf16[4,624,128]{2,1,0:T(8,128)(2,1)} %broadcast_in_dim.30), calls=%async_computation.4 | async-start | bytes 1277952 | tf_op jit(solution)/shard_map/all_to_all | solution.py:1109
  633.1 7.7 %copy-start.8 = (bf16[2,96]{1,0:T(2,128)(2,1)S(1)}, bf16[2,96]{1,0:T(2,128)(2,1)}, u32[]{:S(2)}) copy-start(bf16[2,96]{1,0:T(2,128)(2,1)} %param.17) | copy-start | bytes 1156
  641.4 5.9 copy-start.3
Sparse Core Ops, SparseCore 0:
  10.5 41.4 all-gather.4
  53.9 58.6 all-gather.6
  155.7 80.3 reduce-scatter.2
  344.3 144.1 reduce-scatter.4

commit v10 on v7

--- a/solution.py
+++ b/solution.py
@@ -362,7 +362,40 @@
         target[:, pl.ds(p * LANES, LANES)] = source[pl.ds(start + p * rows, rows), :].astype(F32)
 
 
-def lay_out_kernel(parts, own, gu_panels, shared_ref, pack_ref, egu_ref, ed_ref, sgu_ref, sd_ref):
+def gather_kernel(axis, count, many, *refs):
+    pieces, outs, landed, sems = refs[:many], refs[many : 2 * many], refs[2 * many : 3 * many], refs[3 * many :]
+    barrier = pltpu.get_barrier_semaphore()
+    pl.semaphore_wait(barrier, greet_neighbours(barrier, axis, count))
+    gathers = [
+        LineGather(axis, count, landed[i], sems[2 * i], sems[2 * i + 1], 0, 1) for i in range(many)
+    ]
+    for gather, piece in zip(gathers, pieces):
+        gather.start(piece[...])
+    for k in range(1, count):
+        for gather in gathers:
+            gather.relay(k)
+    for gather, out, rows in zip(gathers, outs, landed):
+        gather.finish()
+        out[...] = rows[...]
+
+
+def gather_over(pieces, axis, count, collective_id):
+    shapes = [(count * piece.shape[0], LANES) for piece in pieces]
+    vmem = pl.BlockSpec(memory_space=pltpu.VMEM)
+    size = sum(shape[0] for shape in shapes) * LANES
+    return pl.pallas_call(
+        functools.partial(gather_kernel, axis, count, len(pieces)),
+        out_shape=[shape_of(shape, BF16) for shape in shapes],
+        in_specs=[vmem] * len(pieces),
+        out_specs=[vmem] * len(pieces),
+        scratch_shapes=[pltpu.VMEM(shape, BF16) for shape in shapes]
+        + [pltpu.SemaphoreType.DMA((2, count))] * (2 * len(pieces)),
+        compiler_params=pltpu.CompilerParams(collective_id=collective_id, has_side_effects=True),
+        cost_estimate=pl.CostEstimate(flops=size, bytes_accessed=40 * size, transcendentals=0),
+    )(*pieces)
+
+
+def lay_out_kernel(parts, pack_ref, egu_ref, ed_ref):
     step = pl.program_id(0)
     width = ed_ref.shape[2]
     packed = pack_ref.shape[0] // parts
@@ -377,40 +410,35 @@
         for e in range(parts):
             unpack(pack_ref, e * packed + e_panels * width, ed_ref.shape[1], width // LANES, ed_ref.at[e])
 
-    @pl.when(step == pl.num_programs(0) - 1)
-    def _():
-        unpack(shared_ref, 0, own, gu_panels, sgu_ref)
-        unpack(shared_ref, gu_panels * own, sd_ref.shape[0], width // LANES, sd_ref)
-
-
-def lay_out(shared, pack, parts, own, width, shared_hidden, hidden):
+
+def lay_out(pack, parts, own, width, hidden):
     group, steps = width // own, 4
     columns = 2 * hidden // group
-    outs = [
-        (parts, width, columns), (parts, hidden // group, width), (own, 2 * shared_hidden), (shared_hidden // group, width)
-    ]
+    outs = [(parts, width, columns), (parts, hidden // group, width)]
     return call(
-        functools.partial(lay_out_kernel, parts, own, 2 * shared_hidden // LANES), (steps,),
-        [whole(shared.shape), whole(pack.shape)],
-        [pl.BlockSpec((parts, width // steps, columns), lambda i: (0, i, 0))] + [whole(shape) for shape in outs[1:]],
+        functools.partial(lay_out_kernel, parts), (steps,), [whole(pack.shape)],
+        [pl.BlockSpec((parts, width // steps, columns), lambda i: (0, i, 0)), whole(outs[1])],
         [shape_of(shape, F32) for shape in outs],
-        flops=shared.size + pack.size, moved=6 * (shared.size + pack.size),
-    )(shared, pack)
-
-
-def lay_out_attention_kernel(own, x_ref, qkv_ref, wo_ref, gain_ref):
+        flops=pack.size, moved=6 * pack.size,
+    )(pack)
+
+
+def lay_out_last_kernel(own, gu_panels, x_ref, shared_ref, qkv_ref, wo_ref, gain_ref, sgu_ref, sd_ref):
     panels = wo_ref.shape[1] // LANES
     unpack(x_ref, 0, own, 3 * panels, qkv_ref)
     unpack(x_ref, 3 * panels * own, own, panels, wo_ref)
     gain_ref[...] = x_ref[pl.ds(4 * panels * own, gain_ref.shape[0]), :].astype(F32)
-
-
-def lay_out_attention(x, own, width):
-    outs = [(own, 3 * width), (own, width), (8, LANES)]
+    unpack(shared_ref, 0, own, gu_panels, sgu_ref)
+    unpack(shared_ref, gu_panels * own, sd_ref.shape[0], panels, sd_ref)
+
+
+def lay_out_last(x, shared, own, width, hidden):
+    outs = [(own, 3 * width), (own, width), (8, LANES), (own, 2 * hidden), (hidden // (width // own), width)]
     return call(
-        functools.partial(lay_out_attention_kernel, own), (1,), [whole(x.shape)], [whole(shape) for shape in outs],
-        [shape_of(shape, F32) for shape in outs], flops=x.size, moved=6 * x.size,
-    )(x)
+        functools.partial(lay_out_last_kernel, own, 2 * hidden // LANES), (1,), [whole(x.shape), whole(shared.shape)],
+        [whole(shape) for shape in outs], [shape_of(shape, F32) for shape in outs],
+        flops=x.size, moved=6 * (x.size + shared.size),
+    )(x, shared)
 
 
 def slot_numbers(block, slots, part):
@@ -663,8 +691,8 @@
 
 
 def settle_kernel(sizes, gq_ref, gk_ref, gv_ref, wq_ref, wk_ref, wv_ref, tokens_ref, first_ref, gain_ref, pack_ref,
-                  x_ref, out_ref, share_ref, all_ref, own, landed, chosen, arrived, sem, pair_send, pair_recv, send_sem,
-                  recv_sem, x_buffers, x_total, x_all, x_send, x_recv, g_send, g_recv):
+                  x_ref, out_ref, share_ref, piece_ref, own, landed, chosen, arrived, sem, pair_send, pair_recv, send_sem,
+                  recv_sem, x_buffers, x_total, x_send, x_recv):
     dp_size, shard_size, count = sizes
     spread = shard_size // 2
     halves = dp_size * spread
@@ -677,11 +705,7 @@
     def target(piece, bit):
         return {"dp": piece // spread, "shard": (piece % spread) * 2 + bit}
 
-    turns = x_buffers.shape[0]
-    lines = [
-        LineSum("expert", count, x_ref, x_buffers.at[t], x_send.at[t], x_recv.at[t], t, turns) for t in range(turns)
-    ]
-    gathers = [LineGather("expert", count, x_all, g_send.at[t], g_recv.at[t], t, turns) for t in range(turns)]
+    line = LineSum("expert", count, x_ref, x_buffers, x_send, x_recv, 0, 1)
 
     def pair_copy():
         return pltpu.make_async_remote_copy(
@@ -711,7 +735,7 @@
         pl.semaphore_wait(barrier, halves + neighbours)
         pair_copy().start()
         own_copy().start()
-        lines[0].start()
+        line.start()
 
     @pl.when(step == 1)
     def _():
@@ -733,26 +757,14 @@
 
     @pl.when(step == last)
     def _():
-        for t in range(turns):
-            if t:
-                lines[t].start()
-            lines[t].relay()
-            if t:
-                gathers[t - 1].relay(1)
-            lines[t].finish(x_total)
-            gathers[t].start(x_total[...].astype(BF16))
+        line.relay()
         total = own[place].astype(F32) + landed[place].astype(F32)
         for index in range(halves - 1):
             send(index).wait()
             total = total + arrived[index].astype(F32)
         share_ref[...] = total.astype(BF16)
-        for k in range(1, count):
-            for t in range(turns):
-                if k > 1 or t == turns - 1:
-                    gathers[t].relay(k)
-        for gather in gathers:
-            gather.finish()
-        all_ref[...] = x_all[...]
+        line.finish(x_total)
+        piece_ref[...] = x_total[...].astype(BF16)
 
 
 def settle(grads, w_qkv, tokens, grad_first, gain, pack, x, sizes):
@@ -761,20 +773,19 @@
     blocked = pl.BlockSpec((block, width), lambda i: (i, 0))
     halves, count = sizes[0] * sizes[1] // 2, pack.shape[1]
     piece = (count, LANES)
-    turns = 2 if x.shape[0] // sizes[2] % 32 == 0 else 1
-    x_piece = (x.shape[0] // sizes[2] // turns, LANES)
+    x_piece = (x.shape[0] // sizes[2], LANES)
     return call(
         functools.partial(settle_kernel, sizes), (rows // block,),
         [blocked] * 3 + [square(width, 0), square(width, 1), square(width, 2), blocked, blocked, whole((1, width)),
                          pl.BlockSpec(memory_space=pl.ANY), whole(x.shape)],
-        [blocked, whole(piece), whole(x.shape)],
-        [shape_of((rows, width), F32), shape_of(piece, BF16), shape_of(x.shape, BF16)],
+        [blocked, whole(piece), whole(x_piece)],
+        [shape_of((rows, width), F32), shape_of(piece, BF16), shape_of(x_piece, BF16)],
         scratch=[pltpu.VMEM((halves,) + piece, BF16), pltpu.VMEM((halves,) + piece, BF16),
                  pltpu.VMEM((halves - 1,) + piece, BF16), pltpu.VMEM((halves - 1,) + piece, BF16),
                  pltpu.SemaphoreType.DMA, pltpu.SemaphoreType.DMA, pltpu.SemaphoreType.DMA,
                  pltpu.SemaphoreType.DMA((halves - 1,)), pltpu.SemaphoreType.DMA((halves - 1,)),
-                 pltpu.VMEM((turns, 2, 2, sizes[2]) + x_piece, BF16), pltpu.VMEM(x_piece, F32), pltpu.VMEM(x.shape, BF16)]
-        + [pltpu.SemaphoreType.DMA((turns, 2, sizes[2]))] * 4,
+                 pltpu.VMEM((2, 2, sizes[2]) + x_piece, BF16), pltpu.VMEM(x_piece, F32)]
+        + [pltpu.SemaphoreType.DMA((2, sizes[2]))] * 2,
         flops=6 * rows * width * width, moved=22 * rows * width, collective_id=1,
     )(*grads, w_qkv, w_qkv, w_qkv, tokens, grad_first, gain, pack.reshape((halves, 2) + piece), x)
 
@@ -1039,7 +1050,7 @@
             rows.reshape(owners, -1, width), "expert", split_axis=0, concat_axis=0, tiled=True
         ).reshape(rows.shape)
 
-    send_grad = dispatch(table_t, gates_t, grad_b, experts, capacity, True, 0, 0)
+    send_grad = dispatch(table_t, gates_t, cotangent, experts, capacity, True, 0, 0)
     received_grad = exchange(send_grad).reshape(owners, local_experts * capacity, width)
 
     cosine, sine = rotary_tables(length, head_dim)
@@ -1088,7 +1099,7 @@
 
     shared_share = spread(shared_pack)
     expert_share = spread(pack)
-    input_grad, attention_share, shared_share = settle(
+    input_grad, attention_share, shared_piece = settle(
         grads, attention_weight, tokens, grad_first, gain_one, attention_pack, shared_share,
         (lax.axis_size("dp"), lax.axis_size("shard"), owners),
     )
@@ -1097,14 +1108,12 @@
         attention_share.reshape(owners, -1, LANES), "expert", split_axis=0, concat_axis=0, tiled=True
     )
     piece = jnp.sum(pieces.astype(F32), axis=0).astype(BF16)
-    attention_share = lax.all_to_all(
-        jnp.broadcast_to(piece[None], pieces.shape), "expert", split_axis=0, concat_axis=0, tiled=True
-    ).reshape(attention_share.shape)
     layer_out = combine(table, route_gates, live, first_sum, shared_out, returned.reshape(-1, width))
-    expert_gu, expert_down, shared_gu, shared_down = lay_out(
-        shared_share, expert_share, local_experts, own, width, shared_hidden, hidden
-    )
-    qkv_grad, out_grad, gain_rows = lay_out_attention(attention_share, own, width)
+    expert_gu, expert_down = lay_out(expert_share, local_experts, own, width, hidden)
+    attention_share, shared_share = gather_over([piece, shared_piece], "expert", owners, 2)
+    qkv_grad, out_grad, gain_rows, shared_gu, shared_down = lay_out_last(
+        attention_share, shared_share, own, width, shared_hidden
+    )
     grad_gain_one = jnp.sum(w_qkv.astype(F32) * qkv_grad, axis=1) / norm_gains[0].astype(F32)
     grad_gains = jnp.stack([grad_gain_one, gain_rows[0, :own]])
     return layer_out, input_grad, grad_gains, qkv_grad, out_grad, shared_gu, shared_down, expert_gu, expert_down

time: 666 us -> 584 us (0.88)
  waiting for transfers between devices: 185 us -> 112 us
  blocking collectives: 26.8 us -> 10.3 us
  starting transfers between devices: 18.1 us -> 26.2 us
    all_to_all x2, waiting for transfers between devices: 146 us -> 72.8 us  [exchange(): lax.all_to_all(rows.reshape(owners, -1, width), 'expert', split_axis=0, c...]
    pallas_call x2 -> x3, Pallas kernels: 8.02 us -> 41.4 us  [the longest x1 33.6 us: gather_over(): pl.pallas_call(functools.partial(gather_kernel, axis, count, len(pieces))...]
    pallas_call x1, Pallas kernels: 74.9 us -> 44.3 us  [settle(): call(functools.partial(settle_kernel, sizes), (rows // block,), [blocked]...]
    all_to_all x1 -> x0, blocking collectives: 16.5 us -> none  [local(): lax.all_to_all(attention_share.reshape(owners, -1, LANES), 'expert', spli...]
    all_to_all x2, starting transfers between devices: 13.8 us -> 21.4 us  [exchange(): lax.all_to_all(rows.reshape(owners, -1, width), 'expert', split_axis=0, c...]
  transfers between devices with their start and end apart: 7 -> 7, of which waited for: 5 -> 4; matrix products, arithmetic and copies ran while one was open for 3% -> 3% of each run, Pallas kernels for 52% -> 60%
where the time goes in v10:
time: 584 us; the launch traced here: 573 us
  Pallas kernels  389 us (67%)
  waiting for transfers between devices  112 us (19%)
  starting transfers between devices  26.2 us (4%)
  between operations  14.9 us (3%)
  other arithmetic  11.3 us (2%)
  blocking collectives  10.3 us (2%)
  local copies, waits for them, and re-layouts  9.41 us (2%)
    pallas_call x3, Pallas kernels, ffn_both(): call(functools.partial(ffn_kernel, out_type, layout, block, axis, count),...  132 us
    all_to_all x2, waiting for transfers between devices, exchange(): lax.all_to_all(rows.reshape(owners, -1, width), 'expert', split_axis=0, c...  72.8 us
    pallas_call x1, Pallas kernels, settle(): call(functools.partial(settle_kernel, sizes), (rows // block,), [blocked]...  44.3 us
    pallas_call x1, Pallas kernels, add_part(): call(functools.partial(add_part_kernel, part, top, axis, count), (rows //...  35 us
    pallas_call x1, Pallas kernels, attend_backward(): call(functools.partial(attend_backward_kernel, head_dim, block), (seqs, p...  34.2 us
    pallas_call x1, Pallas kernels, gather_over(): pl.pallas_call(functools.partial(gather_kernel, axis, count, len(pieces))...  33.6 us
    pallas_call x1, Pallas kernels, attend_forward(): call(functools.partial(attend_forward_kernel, head_dim, block), (seqs, pa...  33.1 us
    all_to_all x2, starting transfers between devices, exchange(): lax.all_to_all(rows.reshape(owners, -1, width), 'expert', split_axis=0, c...  21.4 us
  transfers between devices with their start and end apart: 7, of which 4 were waited for; matrix products, arithmetic and copies ran while one was open for 3% of the time, Pallas kernels for 60%

profile of v10, /device:TPU:0, one launch (start us, length us, event | category | flops | bytes accessed | tf_op | source)
XLA Modules:
  0.0 573.4 jit_solution(5225570435040492655)
XLA Ops:
  12.0 10.3 %all-gather.1 = bf16[8,96,2]{1,2,0:T(2,128)(2,1)S(1)} all-gather(bf16[1,96,2]{1,2,0:T(2,128)(2,1)S(1)} %bitcast.60), channel_id=1, replica_groups=mesh['dp'=2,'expert'=4,'shard'=4] {'dp','shard'}, dimensions={0}, use_global_device_ids=true | all-gather | bytes 3456 | tf_op jit(solution)/shard_map/all_gather | solution.py:1030
  33.6 18.4 %all-gather.5.cloned.1.call-done.wq_ref.wk_ref.wv_ref.weight_ref = bf16[768,3072]{1,0:T(8,128)(2,1)} async-done(((bf16[96,3072]{1,0:T(8,128)(2,1)}), bf16[768,3072]{1,0:T(8,128)(2,1)}) %all-gather.5.cloned.1.call-update) | async-done | bytes 4718608 | tf_op jit(solution)/shard_map/all_gather | solution.py:1031
  52.0 33.1 %shard_map.192 = (bf16[1024,768]{1,0:T(8,128)(2,1)}, bf16[1024,768]{1,0:T(8,128)(2,1)}, bf16[1024,768]{1,0:T(8,128)(2,1)}, bf16[1024,768]{1,0:T(8,128)(2,1)}, f32[96,1024]{1,0:T(8,128)}) custom-call(bf16[1024,768]{1,0:T(8,128)(2,1)} %shard_map.191.x_ref.normed_ref, bf16[768,3072]{1,0:T(8,128)(2,1)} %all-gather.5.cloned.1.call-done.wq_ref.wk_ref.wv_ref.weight_ref, ...), custom_call_target="tpu_custom_call" | custom-call | flops 6845104128 | bytes 12582912 | tf_op jit(solution)/shard_map/pallas_call | solution.py:140
  85.1 5.8 %shard_map.193 = (f32[1024,768]{1,0:T(8,128)}, bf16[1024,768]{1,0:T(8,128)(2,1)}) custom-call(bf16[1024,768]{1,0:T(8,128)(2,1)} %get-tuple-element.54.mixed_ref.o_ref, bf16[1024,768]{1,0:T(8,128)(2,1)} %tokens_ref.3, bf16[768,3072]{1,0:T(8,128)(2,1)} %all-gather.5.cloned.1.call-done.wq_ref.wk_ref.wv_ref.weight_ref, f32[1,768]{1,0:T(1,128)} %get-tuple-element.97.gain_ref), custom_call_target="tpu_custom_call" | custom-call | flops 1207959552 | bytes 7864320 | tf_op jit(solution)/shard_map/pallas_call | solution.py:255
  90.9 5.1 shard_map.194
  95.9 16.7 %all-gather.7.cloned.1.call-done = bf16[18432,256]{1,0:T(8,128)(2,1)} async-done(((bf16[2304,256]{1,0:T(8,128)(2,1)}), bf16[18432,256]{1,0:T(8,128)(2,1)}) %all-gather.7.cloned.1.call-update) | async-done | bytes 9437200 | tf_op jit(solution)/shard_map/all_gather | solution.py:1032
  112.6 42.0 %shard_map.195 = (f32[1024,768]{1,0:T(8,128)}, f32[1024,768]{1,0:T(8,128)}, bf16[8,4608,128]{2,1,0:T(8,128)(2,1)}, bf16[4,288,768]{2,1,0:T(8,128)(2,1)}) custom-call(bf16[1024,768]{1,0:T(8,128)(2,1)} %get-tuple-element.56.x_ref, bf16[1024,768]{1,0:T(8,128)(2,1)} %broadcast_select_fusion.gy_ref, bf16[8,2304,256]{2,1,0:T(8,128)(2,1)} %bitcast.61, ...), custom_call_target="tpu_custom_call" | custom-call | flops 28991029248 | bytes 31457280 | tf_op jit(solution)/shard_map/pallas_call | solution.py:930
  154.7 8.7 %shard_map.196 = bf16[2304,768]{1,0:T(8,128)(2,1)} custom-call(s32[8,1024]{1,0:T(8,128)} %get-tuple-element.57.dest_ref, f32[2,1024]{1,0:T(2,128)} %bitcast.58, bf16[1024,768]{1,0:T(8,128)(2,1)} %cot_ref.1), custom_call_target="tpu_custom_call" | custom-call | flops 3623878656 | bytes 5111808 | tf_op jit(solution)/shard_map/pallas_call | solution.py:319
  163.3 10.1 %all-to-all-start = ((bf16[4,576,768]{2,1,0:T(8,128)(2,1)}), bf16[4,576,768]{2,1,0:T(8,128)(2,1)S(1)}, u32[]{:S(2)}, u32[]{:S(2)}) async-start(bf16[4,576,768]{2,1,0:T(8,128)(2,1)} %bitcast.42), calls=%async_computation | async-start | bytes 7077888 | tf_op jit(solution)/shard_map/all_to_all | solution.py:1049
  173.4 5.9 %shard_map.197 = bf16[1152,768]{1,0:T(8,128)(2,1)} custom-call(s32[8,1024]{1,0:T(8,128)} %get-tuple-element.57.dest_ref, f32[2,1024]{1,0:T(2,128)} %bitcast.59, bf16[1024,768]{1,0:T(8,128)(2,1)} %get-tuple-element.56.x_ref), custom_call_target="tpu_custom_call" | custom-call | flops 1811939328 | bytes 3342336 | tf_op jit(solution)/shard_map/pallas_call | solution.py:319
  179.3 72.8 %all-to-all-done.gy_ref = bf16[4,576,768]{2,1,0:T(8,128)(2,1)S(1)} async-done(((bf16[4,576,768]{2,1,0:T(8,128)(2,1)}), bf16[4,576,768]{2,1,0:T(8,128)(2,1)S(1)}, u32[]{:S(2)}, u32[]{:S(2)}) %all-to-all-start) | async-done | bytes 3538976 | tf_op jit(solution)/shard_map/all_to_all | solution.py:1049
  253.8 44.4 %shard_map.198 = (bf16[4,576,768]{2,1,0:T(8,128)(2,1)}, bf16[1152,768]{1,0:T(8,128)(2,1)}, bf16[8,9216,128]{2,1,0:T(8,128)(2,1)}, bf16[4,288,768]{2,1,0:T(8,128)(2,1)}) custom-call(bf16[1152,768]{1,0:T(8,128)(2,1)} %bitcast.65, bf16[4,576,768]{2,1,0:T(8,128)(2,1)} %copy-done.2, bf16[2,768,4096]{2,1,0:T(8,128)(2,1)} %wu_ref.3, bf16[2,768,4096]{2,1,0:T(8,128)(2,1)} %wu_ref.3, ...), custom_call_target="tpu_custom_call" | custom-call | flops 32614907904 | bytes 33030144 | tf_op jit(solution)/shard_map/pallas_call | solution.py:930
  298.2 45.6 %shard_map.199 = (bf16[4,576,768]{2,1,0:T(8,128)(2,1)}, bf16[1152,768]{1,0:T(8,128)(2,1)}, bf16[8,9216,128]{2,1,0:T(8,128)(2,1)}, bf16[4,288,768]{2,1,0:T(8,128)(2,1)}) custom-call(bf16[1152,768]{1,0:T(8,128)(2,1)} %bitcast.68, bf16[4,576,768]{2,1,0:T(8,128)(2,1)} %copy-done.2, ...), custom_call_target="tpu_custom_call", output_to_operand_aliasing={{0}: (6, {}), {2}: (7, {})} | custom-call | flops 32614907904 | bytes 33030144 | tf_op jit(solution)/shard_map/pallas_call | solution.py:930
  343.9 35.0 %shard_map.200 = (f32[1024,768]{1,0:T(8,128)}, bf16[4,288,768]{2,1,0:T(8,128)(2,1)}) custom-call(s32[1024,8]{1,0:T(8,128)} %get-tuple-element.53.dest_ref, f32[1024,768]{1,0:T(8,128)} %get-tuple-element.65.base_ref, bf16[1152,768]{1,0:T(8,128)(2,1)} %bitcast.49, bf16[4,288,768]{2,1,0:T(8,128)(2,1)} %bitcast.48), custom_call_target="tpu_custom_call" | custom-call | flops 1811939328 | bytes 6291456 | tf_op jit(solution)/shard_map/pallas_call | solution.py:514
  378.9 11.4 %all-to-all-start.1 = ((bf16[4,576,768]{2,1,0:T(8,128)(2,1)}), bf16[4,576,768]{2,1,0:T(8,128)(2,1)S(1)}, u32[]{:S(2)}, u32[]{:S(2)}) async-start(bf16[4,576,768]{2,1,0:T(8,128)(2,1)} %get-tuple-element.69), calls=%async_computation.1 | async-start | bytes 7077888 | tf_op jit(solution)/shard_map/all_to_all | solution.py:1049
  391.1 11.1 %shard_map.202 = (f32[1024,768]{1,0:T(8,128)}, bf16[1024,768]{1,0:T(8,128)(2,1)}, bf16[1024,768]{1,0:T(8,128)(2,1)}, f32[1,768]{1,0:T(1,128)}) custom-call(s32[1024,8]{1,0:T(8,128)} %get-tuple-element.53.dest_ref, f32[1024,1]{1,0:T(8,128)} %fusion.4.live_ref, bf16[1024,768]{1,0:T(8,128)(2,1)} %cot_ref.1, f32[1024,768]{1,0:T(8,128)} %get-tuple-element.55.sum_ref, ...), custom_call_target="tpu_custom_call" | custom-call | flops 3019898880 | bytes 14155776 | tf_op jit(solution)/shard_map/pallas_call | solution.py:550
  403.6 34.2 %shard_map.203 = (bf16[1024,768]{1,0:T(8,128)(2,1)}, bf16[1024,768]{1,0:T(8,128)(2,1)}, bf16[1024,768]{1,0:T(8,128)(2,1)}) custom-call(bf16[1024,768]{1,0:T(8,128)(2,1)} %get-tuple-element.70.q_ref, bf16[1024,768]{1,0:T(8,128)(2,1)} %get-tuple-element.71.k_ref, bf16[1024,768]{1,0:T(8,128)(2,1)} %get-tuple-element.72.v_ref, ...), custom_call_target="tpu_custom_call" | custom-call | flops 8053063680 | bytes 12582912 | tf_op jit(solution)/shard_map/pallas_call | solution.py:211
  437.8 14.7 %shard_map.204 = bf16[8,2496,128]{2,1,0:T(8,128)(2,1)} custom-call(bf16[1024,768]{1,0:T(8,128)(2,1)} %shard_map.191.x_ref.normed_ref, bf16[1024,768]{1,0:T(8,128)(2,1)} %get-tuple-element.54.mixed_ref.o_ref, bf16[1024,768]{1,0:T(8,128)(2,1)} %get-tuple-element.77.gq_ref, bf16[1024,768]{1,0:T(8,128)(2,1)} %get-tuple-element.78.gk_ref, ...), custom_call_target="tpu_custom_call" | custom-call | flops 4831838208 | bytes 12582912 | tf_op jit(solution)/shard_map/pallas_call | solution.py:992
  452.6 44.3 %shard_map.205 = (f32[1024,768]{1,0:T(8,128)}, bf16[2496,128]{1,0:T(8,128)(2,1)}, bf16[1152,128]{1,0:T(8,128)(2,1)}) custom-call(bf16[1024,768]{1,0:T(8,128)(2,1)} %get-tuple-element.77.gq_ref, bf16[1024,768]{1,0:T(8,128)(2,1)} %get-tuple-element.78.gk_ref, bf16[1024,768]{1,0:T(8,128)(2,1)} %get-tuple-element.79.gv_ref, ...), custom_call_target="tpu_custom_call" | custom-call | flops 3623878656 | bytes 17301504 | tf_op jit(solution)/shard_map/pallas_call | solution.py:777
  496.9 4.6 all-to-all-start.2
  502.5 12.1 %shard_map.201 = bf16[1024,768]{1,0:T(8,128)(2,1)} custom-call(s32[1024,8]{1,0:T(8,128)} %get-tuple-element.53.dest_ref, f32[1024,2]{1,0:T(8,128)} %copy.62.gates_ref, f32[1024,1]{1,0:T(8,128)} %fusion.4.live_ref, f32[1024,768]{1,0:T(8,128)} %get-tuple-element.55.sum_ref, f32[1024,768]{1,0:T(8,128)} %get-tuple-element.58.shared_ref, bf16[2304,768]{1,0:T(8,128)(2,1)} %bitcast.41), custom_call_target="tpu_custom_call" | custom-call | flops 7247757312 | bytes 11403264 | tf_op jit(solution)/shard_map/pallas_call | solution.py:351
  514.7 4.1 all-to-all-done.2
  520.7 33.6 %shard_map.206 = (bf16[2496,128]{1,0:T(8,128)(2,1)}, bf16[4608,128]{1,0:T(8,128)(2,1)}) custom-call(bf16[624,128]{1,0:T(8,128)(2,1)} %reduce_sum.23.refs_0_, bf16[1152,128]{1,0:T(8,128)(2,1)} %get-tuple-element.86.refs_1_), custom_call_target="tpu_custom_call" | custom-call | flops 909312 | bytes 36372480 | tf_op jit(solution)/shard_map/pallas_call | solution.py:386
  560.5 4.5 shard_map.208
  (62 shorter events, 30.2 us)
Async XLA Ops:
  7.2 2.2 copy-start.5
  7.2 2.5 copy-start.4
  7.2 44.8 %all-gather.5.cloned.1.call-start = ((), (), s32[]{:S(2)}) async-start(), calls=%async_computation.5 | async-start | bytes 5308416 | tf_op jit(solution)/shard_map/all_gather | solution.py:1031
  9.3 103.3 %all-gather.7.cloned.1.call-start = ((), (), s32[]{:S(2)}) async-start(), calls=%async_computation.8 | async-start | bytes 10616832 | tf_op jit(solution)/shard_map/all_gather | solution.py:1032
  10.1 1.9 copy-start.7
  11.3 441.3 %reduce-scatter.3.cloned.1.call-start = ((), (), s32[]{:S(2)}) async-start(), calls=%async_computation.6 | async-start | bytes 10616832 | tf_op jit(solution)/shard_map/reduce_scatter | solution.py:1098
  25.1 7.1 %copy-start = (bf16[1024,768]{1,0:T(8,128)(2,1)S(1)}, bf16[1024,768]{1,0:T(8,128)(2,1)}, u32[]{:S(2)}) copy-start(bf16[1024,768]{1,0:T(8,128)(2,1)} %cot_ref.1) | copy-start | bytes 4718596
  163.3 88.7 %all-to-all-start = ((bf16[4,576,768]{2,1,0:T(8,128)(2,1)}), bf16[4,576,768]{2,1,0:T(8,128)(2,1)S(1)}, u32[]{:S(2)}, u32[]{:S(2)}) async-start(bf16[4,576,768]{2,1,0:T(8,128)(2,1)} %bitcast.42), calls=%async_computation | async-start | bytes 7077888 | tf_op jit(solution)/shard_map/all_to_all | solution.py:1049
  173.4 387.1 %reduce-scatter.5.cloned.1.call-start = ((), (), s32[]{:S(2)}) async-start(), calls=%async_computation.7 | async-start | bytes 21233664 | tf_op jit(solution)/shard_map/reduce_scatter | solution.py:1098
  252.1 1.7 copy-start.2
  378.9 118.0 %all-to-all-start.1 = ((bf16[4,576,768]{2,1,0:T(8,128)(2,1)}), bf16[4,576,768]{2,1,0:T(8,128)(2,1)S(1)}, u32[]{:S(2)}, u32[]{:S(2)}) async-start(bf16[4,576,768]{2,1,0:T(8,128)(2,1)} %get-tuple-element.69), calls=%async_computation.1 | async-start | bytes 7077888 | tf_op jit(solution)/shard_map/all_to_all | solution.py:1049
  452.6 48.9 %copy-start.6 = (f32[1024,2]{0,1:T(2,128)S(1)}, f32[1024,2]{0,1:T(2,128)}, u32[]{:S(2)}) copy-start(f32[1024,2]{0,1:T(2,128)} %param.15) | copy-start | bytes 24580
  496.9 5.7 copy-start.1
  496.9 21.9 %all-to-all-start.2 = ((bf16[4,624,128]{2,1,0:T(8,128)(2,1)}), bf16[4,624,128]{2,1,0:T(8,128)(2,1)}, u32[]{:S(2)}, u32[]{:S(2)}) async-start(bf16[4,624,128]{2,1,0:T(8,128)(2,1)} %bitcast.55), calls=%async_computation.3 | async-start | bytes 1277952 | tf_op jit(solution)/shard_map/all_to_all | solution.py:1107
  520.7 39.2 %copy-start.8 = (bf16[2,96]{1,0:T(2,128)(2,1)S(1)}, bf16[2,96]{1,0:T(2,128)(2,1)}, u32[]{:S(2)}) copy-start(bf16[2,96]{1,0:T(2,128)(2,1)} %param.17) | copy-start | bytes 1156
  558.3 6.7 %copy-start.3 = (f32[1024,768]{1,0:T(8,128)S(1)}, f32[1024,768]{1,0:T(8,128)}, u32[]{:S(2)}) copy-start(f32[1024,768]{1,0:T(8,128)} %get-tuple-element.114) | copy-start | bytes 9437188
Sparse Core Ops, SparseCore 0:
  10.5 41.4 all-gather.4
  53.9 58.6 all-gather.6
  154.8 82.2 reduce-scatter.2
  344.0 141.0 reduce-scatter.4

commit v11 on v10

--- a/solution.py
+++ b/solution.py
@@ -834,8 +834,9 @@
     return 3 * width * hidden // owners // LANES
 
 
-def ffn_kernel(out_type, layout, block, axis, count, x_ref, gy_ref, wg_ref, wu_ref, wd_ref, sent_ref, *rest):
-    y_ref, gx_ref, packed_ref, kept_ref, xt, y_acc, gx_acc, stage_g, stage_u, stage_d, sems, *exchange_sems = rest[-14:]
+def ffn_kernel(out_type, layout, block, first, axis, count, x_ref, gy_ref, wg_ref, wu_ref, wd_ref, sent_ref, *rest):
+    (y_ref, gx_ref, packed_ref, kept_ref, x_own, gy_own, xt, y_acc, gx_acc, stage_g, stage_u, stage_d, sems, load_sems,
+     *exchange_sems) = rest[-17:]
     exchange = Exchange(axis, count, sent_ref, kept_ref, *exchange_sems)
     step = pl.program_id(0)
     steps = layout[2] // block
@@ -846,7 +847,16 @@
     @pl.when(step == 0)
     def _():
         exchange.start()
-        xt[...] = x_ref[...].T
+        gy_source = gy_ref if first is None else gy_ref.at[:, pl.ds(first, gy_own.shape[1]), :]
+        loads = [
+            pltpu.make_async_copy(x_ref, x_own, load_sems.at[0]),
+            pltpu.make_async_copy(gy_source, gy_own, load_sems.at[1]),
+        ]
+        for load in loads:
+            load.start()
+        for load in loads:
+            load.wait()
+        xt[...] = x_own[...].T
         y_acc[...] = jnp.zeros_like(y_acc)
         gx_acc[...] = jnp.zeros_like(gx_acc)
 
@@ -855,7 +865,7 @@
         for copy in copies(step - 2, stage_g, stage_u, stage_d, slot, packed_ref, sems):
             copy.wait()
 
-    x, gy = x_ref[...], gy_ref[...].reshape(x_ref.shape)
+    x, gy = x_own[...], gy_own[...].reshape(x_ref.shape)
     if layout[0]:
         wg, wu = wg_ref[...].reshape(width, block), wu_ref[...].reshape(width, block)
         rows = wd_ref.shape[1] // (width // block)
@@ -911,16 +921,14 @@
         down = pl.BlockSpec((None, block, width), lambda f: (expert, f, 0))
         stage = (2, width, block)
     if by_rows:
-        grads = whole((rows, width))
+        first, gy_shape = None, (rows, width)
         y_block, y_shape = whole((rows, width)), (rows, width)
     else:
         y_shape = (gy.shape[0], parts * (rows // gy.shape[0]), width)
         y_block = pl.BlockSpec(
             (gy.shape[0], rows // gy.shape[0], width), lambda f: (0, expert, 0), pipeline_mode=pl.Buffered(1)
         )
-        grads = pl.BlockSpec(
-            (gy.shape[0], rows // gy.shape[0], width), lambda f: (0, expert, 0), pipeline_mode=pl.Buffered(1)
-        )
+        first, gy_shape = expert * (rows // gy.shape[0]), (gy.shape[0], rows // gy.shape[0], width)
     out_rows = whole((rows, width))
     pack_rows = packed_rows(width, hidden, owners)
     layout = (by_rows, owners, hidden, (expert or 0) * pack_rows)
@@ -928,14 +936,15 @@
     sent = sent.reshape(count, -1, width)
     copies = 2 * (block // LANES) + block // (hidden // owners) * (width // LANES)
     y, gx, pack, kept = call(
-        functools.partial(ffn_kernel, out_type, layout, block, axis, count), (steps,),
-        [whole((rows, width)), grads, gate, up, down, hbm] + [hbm] * len(held),
+        functools.partial(ffn_kernel, out_type, layout, block, first, axis, count), (steps,),
+        [hbm, hbm, gate, up, down, hbm] + [hbm] * len(held),
         [y_block, out_rows, hbm, hbm],
         [shape_of(y_shape, out_type), shape_of((rows, width), out_type),
          shape_of((owners, parts * pack_rows, LANES), BF16), shape_of(sent.shape, BF16)],
-        scratch=[pltpu.VMEM((width, rows), BF16), pltpu.VMEM((rows, width), F32), pltpu.VMEM((rows, width), F32),
+        scratch=[pltpu.VMEM((rows, width), BF16), pltpu.VMEM(gy_shape, BF16),
+                 pltpu.VMEM((width, rows), BF16), pltpu.VMEM((rows, width), F32), pltpu.VMEM((rows, width), F32),
                  pltpu.VMEM(stage, BF16), pltpu.VMEM(stage, BF16), pltpu.VMEM((2, block, width), BF16),
-                 pltpu.SemaphoreType.DMA((2, copies))] + Exchange.scratch(count),
+                 pltpu.SemaphoreType.DMA((2, copies)), pltpu.SemaphoreType.DMA((2,))] + Exchange.scratch(count),
         flops=18 * rows * width * hidden, moved=12 * width * hidden + 16 * rows * width, trans=rows * hidden,
         aliases={6: 0, 7: 2} if held else None, collective_id=collective_id,
     )(x, gy, w_gu, w_gu, w_down, sent, *held)

time: 584 us -> 584 us (level)
  no operation moved by 1% of the time
where the time goes in v11:
time: 584 us; the launch traced here: 573 us
  Pallas kernels  391 us (67%)
  waiting for transfers between devices  112 us (19%)
  starting transfers between devices  24.1 us (4%)
  between operations  14.9 us (3%)
  other arithmetic  11.3 us (2%)
  blocking collectives  10.3 us (2%)
  local copies, waits for them, and re-layouts  9.41 us (2%)
    pallas_call x3, Pallas kernels, ffn_both(): call(functools.partial(ffn_kernel, out_type, layout, block, first, axis,...  134 us
    all_to_all x2, waiting for transfers between devices, exchange(): lax.all_to_all(rows.reshape(owners, -1, width), 'expert', split_axis=0, c...  72.8 us
    pallas_call x1, Pallas kernels, settle(): call(functools.partial(settle_kernel, sizes), (rows // block,), [blocked]...  43.8 us
    pallas_call x1, Pallas kernels, add_part(): call(functools.partial(add_part_kernel, part, top, axis, count), (rows //...  34.8 us
    pallas_call x1, Pallas kernels, attend_backward(): call(functools.partial(attend_backward_kernel, head_dim, block), (seqs, p...  34.2 us
    pallas_call x1, Pallas kernels, gather_over(): pl.pallas_call(functools.partial(gather_kernel, axis, count, len(pieces))...  33.6 us
    pallas_call x1, Pallas kernels, attend_forward(): call(functools.partial(attend_forward_kernel, head_dim, block), (seqs, pa...  33.1 us
    pallas_call x3, Pallas kernels, dispatch(): call(functools.partial(dispatch_kernel, gated, first, base), (experts,),...  19.6 us
  transfers between devices with their start and end apart: 7, of which 4 were waited for; matrix products, arithmetic and copies ran while one was open for 3% of the time, Pallas kernels for 60%

profile of v11, /device:TPU:0, one launch (start us, length us, event | category | flops | bytes accessed | tf_op | source)
XLA Modules:
  0.0 573.1 jit_solution(8871693718019961692)
XLA Ops:
  12.0 10.3 %all-gather.1 = bf16[8,96,2]{1,2,0:T(2,128)(2,1)S(1)} all-gather(bf16[1,96,2]{1,2,0:T(2,128)(2,1)S(1)} %bitcast.60), channel_id=1, replica_groups=mesh['dp'=2,'expert'=4,'shard'=4] {'dp','shard'}, dimensions={0}, use_global_device_ids=true | all-gather | bytes 3456 | tf_op jit(solution)/shard_map/all_gather | solution.py:1039
  33.6 18.4 %all-gather.5.cloned.1.call-done.wq_ref.wk_ref.wv_ref.weight_ref = bf16[768,3072]{1,0:T(8,128)(2,1)} async-done(((bf16[96,3072]{1,0:T(8,128)(2,1)}), bf16[768,3072]{1,0:T(8,128)(2,1)}) %all-gather.5.cloned.1.call-update) | async-done | bytes 4718608 | tf_op jit(solution)/shard_map/all_gather | solution.py:1040
  52.0 33.1 %shard_map.192 = (bf16[1024,768]{1,0:T(8,128)(2,1)}, bf16[1024,768]{1,0:T(8,128)(2,1)}, bf16[1024,768]{1,0:T(8,128)(2,1)}, bf16[1024,768]{1,0:T(8,128)(2,1)}, f32[96,1024]{1,0:T(8,128)}) custom-call(bf16[1024,768]{1,0:T(8,128)(2,1)} %shard_map.191.x_ref.normed_ref, bf16[768,3072]{1,0:T(8,128)(2,1)} %all-gather.5.cloned.1.call-done.wq_ref.wk_ref.wv_ref.weight_ref, ...), custom_call_target="tpu_custom_call" | custom-call | flops 6845104128 | bytes 12582912 | tf_op jit(solution)/shard_map/pallas_call | solution.py:140
  85.1 5.8 %shard_map.193 = (f32[1024,768]{1,0:T(8,128)}, bf16[1024,768]{1,0:T(8,128)(2,1)}) custom-call(bf16[1024,768]{1,0:T(8,128)(2,1)} %get-tuple-element.54.mixed_ref.o_ref, bf16[1024,768]{1,0:T(8,128)(2,1)} %tokens_ref.3, bf16[768,3072]{1,0:T(8,128)(2,1)} %all-gather.5.cloned.1.call-done.wq_ref.wk_ref.wv_ref.weight_ref, f32[1,768]{1,0:T(1,128)} %get-tuple-element.97.gain_ref), custom_call_target="tpu_custom_call" | custom-call | flops 1207959552 | bytes 7864320 | tf_op jit(solution)/shard_map/pallas_call | solution.py:255
  90.9 5.1 shard_map.194
  95.9 16.7 %all-gather.7.cloned.1.call-done = bf16[18432,256]{1,0:T(8,128)(2,1)} async-done(((bf16[2304,256]{1,0:T(8,128)(2,1)}), bf16[18432,256]{1,0:T(8,128)(2,1)}) %all-gather.7.cloned.1.call-update) | async-done | bytes 9437200 | tf_op jit(solution)/shard_map/all_gather | solution.py:1041
  112.6 42.9 %shard_map.195 = (f32[1024,768]{1,0:T(8,128)}, f32[1024,768]{1,0:T(8,128)}, bf16[8,4608,128]{2,1,0:T(8,128)(2,1)}, bf16[4,288,768]{2,1,0:T(8,128)(2,1)}) custom-call(bf16[1024,768]{1,0:T(8,128)(2,1)} %get-tuple-element.56.x_ref, bf16[1024,768]{1,0:T(8,128)(2,1)} %broadcast_select_fusion.gy_ref, bf16[8,2304,256]{2,1,0:T(8,128)(2,1)} %bitcast.61, ...), custom_call_target="tpu_custom_call" | custom-call | flops 28991029248 | bytes 31457280 | tf_op jit(solution)/shard_map/pallas_call | solution.py:938
  155.6 8.7 %shard_map.196 = bf16[2304,768]{1,0:T(8,128)(2,1)} custom-call(s32[8,1024]{1,0:T(8,128)} %get-tuple-element.57.dest_ref, f32[2,1024]{1,0:T(2,128)} %bitcast.58, bf16[1024,768]{1,0:T(8,128)(2,1)} %cot_ref.1), custom_call_target="tpu_custom_call" | custom-call | flops 3623878656 | bytes 5111808 | tf_op jit(solution)/shard_map/pallas_call | solution.py:319
  164.2 8.2 %all-to-all-start = ((bf16[4,576,768]{2,1,0:T(8,128)(2,1)}), bf16[4,576,768]{2,1,0:T(8,128)(2,1)S(1)}, u32[]{:S(2)}, u32[]{:S(2)}) async-start(bf16[4,576,768]{2,1,0:T(8,128)(2,1)} %bitcast.42), calls=%async_computation | async-start | bytes 7077888 | tf_op jit(solution)/shard_map/all_to_all | solution.py:1058
  172.4 5.9 %shard_map.197 = bf16[1152,768]{1,0:T(8,128)(2,1)} custom-call(s32[8,1024]{1,0:T(8,128)} %get-tuple-element.57.dest_ref, f32[2,1024]{1,0:T(2,128)} %bitcast.59, bf16[1024,768]{1,0:T(8,128)(2,1)} %get-tuple-element.56.x_ref), custom_call_target="tpu_custom_call" | custom-call | flops 1811939328 | bytes 3342336 | tf_op jit(solution)/shard_map/pallas_call | solution.py:319
  178.3 72.8 %all-to-all-done.gy_ref = bf16[4,576,768]{2,1,0:T(8,128)(2,1)S(1)} async-done(((bf16[4,576,768]{2,1,0:T(8,128)(2,1)}), bf16[4,576,768]{2,1,0:T(8,128)(2,1)S(1)}, u32[]{:S(2)}, u32[]{:S(2)}) %all-to-all-start) | async-done | bytes 3538976 | tf_op jit(solution)/shard_map/all_to_all | solution.py:1058
  252.8 45.2 %shard_map.198 = (bf16[4,576,768]{2,1,0:T(8,128)(2,1)}, bf16[1152,768]{1,0:T(8,128)(2,1)}, bf16[8,9216,128]{2,1,0:T(8,128)(2,1)}, bf16[4,288,768]{2,1,0:T(8,128)(2,1)}) custom-call(bf16[1152,768]{1,0:T(8,128)(2,1)} %bitcast.65, bf16[4,576,768]{2,1,0:T(8,128)(2,1)} %copy-done.2, bf16[2,768,4096]{2,1,0:T(8,128)(2,1)} %wu_ref.3, bf16[2,768,4096]{2,1,0:T(8,128)(2,1)} %wu_ref.3, ...), custom_call_target="tpu_custom_call" | custom-call | flops 32614907904 | bytes 33030144 | tf_op jit(solution)/shard_map/pallas_call | solution.py:938
  298.0 46.0 %shard_map.199 = (bf16[4,576,768]{2,1,0:T(8,128)(2,1)}, bf16[1152,768]{1,0:T(8,128)(2,1)}, bf16[8,9216,128]{2,1,0:T(8,128)(2,1)}, bf16[4,288,768]{2,1,0:T(8,128)(2,1)}) custom-call(bf16[1152,768]{1,0:T(8,128)(2,1)} %bitcast.68, bf16[4,576,768]{2,1,0:T(8,128)(2,1)} %copy-done.2, ...), custom_call_target="tpu_custom_call", output_to_operand_aliasing={{0}: (6, {}), {2}: (7, {})} | custom-call | flops 32614907904 | bytes 33030144 | tf_op jit(solution)/shard_map/pallas_call | solution.py:938
  344.1 34.8 %shard_map.200 = (f32[1024,768]{1,0:T(8,128)}, bf16[4,288,768]{2,1,0:T(8,128)(2,1)}) custom-call(s32[1024,8]{1,0:T(8,128)} %get-tuple-element.53.dest_ref, f32[1024,768]{1,0:T(8,128)} %get-tuple-element.65.base_ref, bf16[1152,768]{1,0:T(8,128)(2,1)} %bitcast.49, bf16[4,288,768]{2,1,0:T(8,128)(2,1)} %bitcast.48), custom_call_target="tpu_custom_call" | custom-call | flops 1811939328 | bytes 6291456 | tf_op jit(solution)/shard_map/pallas_call | solution.py:514
  378.9 11.2 %all-to-all-start.1 = ((bf16[4,576,768]{2,1,0:T(8,128)(2,1)}), bf16[4,576,768]{2,1,0:T(8,128)(2,1)S(1)}, u32[]{:S(2)}, u32[]{:S(2)}) async-start(bf16[4,576,768]{2,1,0:T(8,128)(2,1)} %get-tuple-element.69), calls=%async_computation.1 | async-start | bytes 7077888 | tf_op jit(solution)/shard_map/all_to_all | solution.py:1058
  391.0 11.2 %shard_map.202 = (f32[1024,768]{1,0:T(8,128)}, bf16[1024,768]{1,0:T(8,128)(2,1)}, bf16[1024,768]{1,0:T(8,128)(2,1)}, f32[1,768]{1,0:T(1,128)}) custom-call(s32[1024,8]{1,0:T(8,128)} %get-tuple-element.53.dest_ref, f32[1024,1]{1,0:T(8,128)} %fusion.4.live_ref, bf16[1024,768]{1,0:T(8,128)(2,1)} %cot_ref.1, f32[1024,768]{1,0:T(8,128)} %get-tuple-element.55.sum_ref, ...), custom_call_target="tpu_custom_call" | custom-call | flops 3019898880 | bytes 14155776 | tf_op jit(solution)/shard_map/pallas_call | solution.py:550
  403.6 34.2 %shard_map.203 = (bf16[1024,768]{1,0:T(8,128)(2,1)}, bf16[1024,768]{1,0:T(8,128)(2,1)}, bf16[1024,768]{1,0:T(8,128)(2,1)}) custom-call(bf16[1024,768]{1,0:T(8,128)(2,1)} %get-tuple-element.70.q_ref, bf16[1024,768]{1,0:T(8,128)(2,1)} %get-tuple-element.71.k_ref, bf16[1024,768]{1,0:T(8,128)(2,1)} %get-tuple-element.72.v_ref, ...), custom_call_target="tpu_custom_call" | custom-call | flops 8053063680 | bytes 12582912 | tf_op jit(solution)/shard_map/pallas_call | solution.py:211
  437.8 14.9 %shard_map.204 = bf16[8,2496,128]{2,1,0:T(8,128)(2,1)} custom-call(bf16[1024,768]{1,0:T(8,128)(2,1)} %shard_map.191.x_ref.normed_ref, bf16[1024,768]{1,0:T(8,128)(2,1)} %get-tuple-element.54.mixed_ref.o_ref, bf16[1024,768]{1,0:T(8,128)(2,1)} %get-tuple-element.77.gq_ref, bf16[1024,768]{1,0:T(8,128)(2,1)} %get-tuple-element.78.gk_ref, ...), custom_call_target="tpu_custom_call" | custom-call | flops 4831838208 | bytes 12582912 | tf_op jit(solution)/shard_map/pallas_call | solution.py:1001
  452.7 43.8 %shard_map.205 = (f32[1024,768]{1,0:T(8,128)}, bf16[2496,128]{1,0:T(8,128)(2,1)}, bf16[1152,128]{1,0:T(8,128)(2,1)}) custom-call(bf16[1024,768]{1,0:T(8,128)(2,1)} %get-tuple-element.77.gq_ref, bf16[1024,768]{1,0:T(8,128)(2,1)} %get-tuple-element.78.gk_ref, bf16[1024,768]{1,0:T(8,128)(2,1)} %get-tuple-element.79.gv_ref, ...), custom_call_target="tpu_custom_call" | custom-call | flops 3623878656 | bytes 17301504 | tf_op jit(solution)/shard_map/pallas_call | solution.py:777
  496.5 4.6 all-to-all-start.2
  502.2 12.1 %shard_map.201 = bf16[1024,768]{1,0:T(8,128)(2,1)} custom-call(s32[1024,8]{1,0:T(8,128)} %get-tuple-element.53.dest_ref, f32[1024,2]{1,0:T(8,128)} %copy.62.gates_ref, f32[1024,1]{1,0:T(8,128)} %fusion.4.live_ref, f32[1024,768]{1,0:T(8,128)} %get-tuple-element.55.sum_ref, f32[1024,768]{1,0:T(8,128)} %get-tuple-element.58.shared_ref, bf16[2304,768]{1,0:T(8,128)(2,1)} %bitcast.41), custom_call_target="tpu_custom_call" | custom-call | flops 7247757312 | bytes 11403264 | tf_op jit(solution)/shard_map/pallas_call | solution.py:351
  514.3 4.2 all-to-all-done.2
  520.3 33.6 %shard_map.206 = (bf16[2496,128]{1,0:T(8,128)(2,1)}, bf16[4608,128]{1,0:T(8,128)(2,1)}) custom-call(bf16[624,128]{1,0:T(8,128)(2,1)} %reduce_sum.23.refs_0_, bf16[1152,128]{1,0:T(8,128)(2,1)} %get-tuple-element.86.refs_1_), custom_call_target="tpu_custom_call" | custom-call | flops 909312 | bytes 36372480 | tf_op jit(solution)/shard_map/pallas_call | solution.py:386
  560.2 4.5 shard_map.208
  (62 shorter events, 30.2 us)
Async XLA Ops:
  7.2 2.2 copy-start.5
  7.2 2.5 copy-start.4
  7.2 44.8 %all-gather.5.cloned.1.call-start = ((), (), s32[]{:S(2)}) async-start(), calls=%async_computation.5 | async-start | bytes 5308416 | tf_op jit(solution)/shard_map/all_gather | solution.py:1040
  9.3 103.3 %all-gather.7.cloned.1.call-start = ((), (), s32[]{:S(2)}) async-start(), calls=%async_computation.8 | async-start | bytes 10616832 | tf_op jit(solution)/shard_map/all_gather | solution.py:1041
  10.1 1.9 copy-start.7
  11.3 441.4 %reduce-scatter.3.cloned.1.call-start = ((), (), s32[]{:S(2)}) async-start(), calls=%async_computation.6 | async-start | bytes 10616832 | tf_op jit(solution)/shard_map/reduce_scatter | solution.py:1107
  25.1 7.1 %copy-start = (bf16[1024,768]{1,0:T(8,128)(2,1)S(1)}, bf16[1024,768]{1,0:T(8,128)(2,1)}, u32[]{:S(2)}) copy-start(bf16[1024,768]{1,0:T(8,128)(2,1)} %cot_ref.1) | copy-start | bytes 4718596
  164.2 86.8 %all-to-all-start = ((bf16[4,576,768]{2,1,0:T(8,128)(2,1)}), bf16[4,576,768]{2,1,0:T(8,128)(2,1)S(1)}, u32[]{:S(2)}, u32[]{:S(2)}) async-start(bf16[4,576,768]{2,1,0:T(8,128)(2,1)} %bitcast.42), calls=%async_computation | async-start | bytes 7077888 | tf_op jit(solution)/shard_map/all_to_all | solution.py:1058
  172.4 387.7 %reduce-scatter.5.cloned.1.call-start = ((), (), s32[]{:S(2)}) async-start(), calls=%async_computation.7 | async-start | bytes 21233664 | tf_op jit(solution)/shard_map/reduce_scatter | solution.py:1107
  251.1 1.7 copy-start.2
  378.9 117.6 %all-to-all-start.1 = ((bf16[4,576,768]{2,1,0:T(8,128)(2,1)}), bf16[4,576,768]{2,1,0:T(8,128)(2,1)S(1)}, u32[]{:S(2)}, u32[]{:S(2)}) async-start(bf16[4,576,768]{2,1,0:T(8,128)(2,1)} %get-tuple-element.69), calls=%async_computation.1 | async-start | bytes 7077888 | tf_op jit(solution)/shard_map/all_to_all | solution.py:1058
  452.7 48.5 %copy-start.6 = (f32[1024,2]{0,1:T(2,128)S(1)}, f32[1024,2]{0,1:T(2,128)}, u32[]{:S(2)}) copy-start(f32[1024,2]{0,1:T(2,128)} %param.15) | copy-start | bytes 24580
  496.5 5.7 copy-start.1
  496.5 21.9 %all-to-all-start.2 = ((bf16[4,624,128]{2,1,0:T(8,128)(2,1)}), bf16[4,624,128]{2,1,0:T(8,128)(2,1)}, u32[]{:S(2)}, u32[]{:S(2)}) async-start(bf16[4,624,128]{2,1,0:T(8,128)(2,1)} %bitcast.55), calls=%async_computation.3 | async-start | bytes 1277952 | tf_op jit(solution)/shard_map/all_to_all | solution.py:1116
  520.3 39.2 %copy-start.8 = (bf16[2,96]{1,0:T(2,128)(2,1)S(1)}, bf16[2,96]{1,0:T(2,128)(2,1)}, u32[]{:S(2)}) copy-start(bf16[2,96]{1,0:T(2,128)(2,1)} %param.17) | copy-start | bytes 1156
  557.9 6.7 %copy-start.3 = (f32[1024,768]{1,0:T(8,128)S(1)}, f32[1024,768]{1,0:T(8,128)}, u32[]{:S(2)}) copy-start(f32[1024,768]{1,0:T(8,128)} %get-tuple-element.114) | copy-start | bytes 9437188
Sparse Core Ops, SparseCore 0:
  10.5 41.4 all-gather.4
  53.9 58.6 all-gather.6
  155.7 80.3 reduce-scatter.2
  344.2 140.2 reduce-scatter.4
